TPU v7x, 32 devices: a whole 2x2x4 slice. The times are simulated.
32 devices in a mesh: dp: 4 (over y, core), cp: 8 (over z, x).
Axes of the slice: x: 2, y: 2, z: 4, core: 2. Of those that a mesh axis runs over, the one named last changes fastest.
Arguments:
- tokens: bfloat16 [8192, 1600], P(('dp', 'cp')), may hold values from -6 to 6
- params: bfloat16 [19456, 1600], P(('dp', 'cp')), as said below
- out_grad: bfloat16 [8192, 1600], P(('dp', 'cp')), may hold values from -6 to 6
- lengths: int32 [4, 2], P('dp'), may hold values from 1024 to 1024, as said below
Outputs:
- output: bfloat16 [8192, 1600], P(('dp', 'cp'))
- input_grad: bfloat16 [8192, 1600], P(('dp', 'cp'))
- param_grad: float32 [19456, 1600], P(('dp', 'cp'))
Inputs may be any that keep to these rules, and one draw needn't show every extreme that they name: Rows of params past the used ones are never read. Multiples of 128; a group's lengths sum to 2048; one of them is 1024 and one 1024.
All inputs are finite; a program needn't handle non-finite values.
Results may differ from a plain program's by a relative error of at most 0.028.
Values may be sent and summed in bfloat16 or wider, within the bound.
A program may use at most 832 MiB of HBM per device.

v0:
```python
import functools

import jax
import jax.numpy as jnp
from jax import lax
from jax.experimental import pallas as pl
from jax.experimental.pallas import tpu as pltpu
from jax.sharding import PartitionSpec as P


HEADS = 25
FF = 6400
HEAD_DIM = 64
TILE = 128
MIN_LEN = 1024
MAX_LEN = 4096


EPSILON = 1e-05
MASKED = -1e30
GELU_SCALE = 0.7978845608028654


def from_behind(value, axis, by):
    length = lax.axis_size(axis)
    pairs = [(i, i + by) for i in range(length) if 0 <= i + by < length]
    return lax.ppermute(value, axis, pairs)


def layer_norm(values, gain_row, bias_row):
    centre = values - jnp.mean(values, axis=-1, keepdims=True)
    spread = jnp.mean(centre * centre, axis=-1, keepdims=True)
    return centre * lax.rsqrt(spread + EPSILON) * gain_row + bias_row


def gelu_tanh(values):
    return (
        0.5 * values * (1.0 + jnp.tanh(GELU_SCALE * (values + 0.044715 * values * values * values)))
    )


def segment_of(position, seq_ends):
    return jnp.sum((position[:, None] >= seq_ends[None, :]).astype(jnp.int32), axis=1)


def unpack(gathered, model_width, hidden):
    out_end = 4 * model_width
    fc_end = out_end + hidden
    proj_end = fc_end + hidden
    vec_end = proj_end + 8
    return (
        gathered[0 : 3 * model_width],
        gathered[3 * model_width : out_end],
        gathered[out_end:fc_end],
        gathered[fc_end:proj_end],
        gathered[proj_end:vec_end].astype(jnp.float32),
        gathered[vec_end : vec_end + hidden // model_width].astype(jnp.float32).reshape(hidden),
    )


def matmul_nt(left_mat, right_mat):
    return lax.dot_general(
        left_mat, right_mat, (((1,), (1,)), ((), ())), preferred_element_type=jnp.float32
    )


def matmul_tn(left_mat, right_mat):
    return lax.dot_general(
        left_mat, right_mat, (((0,), (0,)), ((), ())), preferred_element_type=jnp.float32
    )


def matmul_nn(left_mat, right_mat):
    return jnp.dot(left_mat, right_mat, preferred_element_type=jnp.float32)


def per_device_general(tokens, params, out_grad, lengths):
    tok_rows, model_width = tokens.shape
    hidden = FF
    head_count = HEADS
    head_size = HEAD_DIM
    cp_count = lax.axis_size("cp")
    group_rows = tok_rows * cp_count
    seq_count = lengths.shape[1]
    longest = min(MAX_LEN, group_rows - (seq_count - 1) * MIN_LEN)
    reach_back = min(cp_count - 1, (longest + tok_rows - TILE - 1) // tok_rows)
    pair_count = (reach_back + 2) // 2
    score_scale = head_size ** (-0.5)
    gathered = lax.all_gather(params, ("dp", "cp"), axis=0, tiled=True)
    w_attn, w_out, w_fc, w_proj, vectors, fc_bias = unpack(gathered, model_width, hidden)
    inputs = tokens.astype(jnp.float32)
    act_one = layer_norm(inputs, vectors[0], vectors[1]).astype(jnp.bfloat16)
    qkv_bias = jnp.concatenate([vectors[2], jnp.zeros_like(vectors[2]), vectors[3]])
    qkv = (matmul_nt(act_one, w_attn) + qkv_bias).astype(jnp.bfloat16)
    queries = qkv[:, :model_width].reshape(tok_rows, head_count, head_size)
    key_value = qkv[:, model_width:]
    device = lax.axis_index("cp")
    seq_ends = jnp.cumsum(lengths[0])
    query_pos = device * tok_rows + jnp.arange(tok_rows, dtype=jnp.int32)
    query_seg = segment_of(query_pos, seq_ends)
    store = jnp.zeros((2 * pair_count, tok_rows, 2 * model_width), jnp.bfloat16)
    store = store.at[0].set(key_value)

    def fetch(step_index, state_pair):
        moving, held_rows = state_pair
        moving = from_behind(moving, "cp", 1)
        return (moving, lax.dynamic_update_index_in_dim(held_rows, moving, step_index, 0))

    _, store = lax.fori_loop(1, reach_back + 1, fetch, (key_value, store))

    def pair_mask(pair_index):
        owners = 2 * pair_index + jnp.arange(2, dtype=jnp.int32)
        key_pos = (
            (device - owners)[:, None] * tok_rows + jnp.arange(tok_rows, dtype=jnp.int32)[None, :]
        ).reshape(2 * tok_rows)
        usable = jnp.broadcast_to((owners <= reach_back)[:, None], (2, tok_rows)).reshape(
            2 * tok_rows
        ) & (key_pos >= 0)
        key_seg = segment_of(key_pos, seq_ends)
        return (
            (key_seg[None, :] == query_seg[:, None])
            & (key_pos[None, :] <= query_pos[:, None])
            & usable[None, :]
        )

    def pair_rows(pair_index):
        block_rows = lax.dynamic_slice_in_dim(store, 2 * pair_index, 2, 0).reshape(
            2 * tok_rows, 2 * model_width
        )
        return (
            block_rows[:, :model_width].reshape(2 * tok_rows, head_count, head_size),
            block_rows[:, model_width:].reshape(2 * tok_rows, head_count, head_size),
        )

    def pair_scores(key_rows, allowed):
        raw_scores = (
            jnp.einsum("qhd,khd->hqk", queries, key_rows, preferred_element_type=jnp.float32)
            * score_scale
        )
        return jnp.where(allowed[None], raw_scores, MASKED)

    def visit(work):

        def step_pair(pair_index, running):
            allowed = pair_mask(pair_index)
            result = work(pair_index, allowed, running)
            return result

        return step_pair

    def add_total(pair_index, allowed, running):
        row_top, summed = running
        key_rows, _ = pair_rows(pair_index)
        scores = pair_scores(key_rows, allowed)
        new_top = jnp.maximum(row_top, jnp.max(scores, axis=-1, keepdims=True))
        summed = summed * jnp.exp(row_top - new_top) + jnp.sum(
            jnp.exp(scores - new_top), axis=-1, keepdims=True
        )
        return (new_top, summed)

    start_top = jnp.full((head_count, tok_rows, 1), MASKED, jnp.float32)
    start_sum = jnp.zeros((head_count, tok_rows, 1), jnp.float32)
    row_top, summed = lax.fori_loop(0, pair_count, visit(add_total), (start_top, start_sum))
    log_total = row_top + jnp.log(summed)

    def add_mix(pair_index, allowed, running):
        key_rows, value_rows = pair_rows(pair_index)
        prob_rows = jnp.exp(pair_scores(key_rows, allowed) - log_total).astype(jnp.bfloat16)
        return running + jnp.einsum(
            "hqk,khd->qhd", prob_rows, value_rows, preferred_element_type=jnp.float32
        )

    mixed_full = lax.fori_loop(
        0, pair_count, visit(add_mix), jnp.zeros((tok_rows, head_count, head_size), jnp.float32)
    )
    mixed = mixed_full.reshape(tok_rows, model_width).astype(jnp.bfloat16)
    attn_out = matmul_nt(mixed, w_out) + vectors[4]
    residual = inputs + attn_out
    act_two = layer_norm(residual, vectors[5], vectors[6]).astype(jnp.bfloat16)
    pre_act = matmul_nt(act_two, w_fc) + fc_bias
    act_hidden = gelu_tanh(pre_act).astype(jnp.bfloat16)
    output = (residual + matmul_nn(act_hidden, w_proj) + vectors[7]).astype(jnp.bfloat16)
    gathered = lax.all_gather(params, ("dp", "cp"), axis=0, tiled=True)
    w_attn, w_out, w_fc, w_proj, vectors, fc_bias = unpack(gathered, model_width, hidden)
    grad_out_f = out_grad.astype(jnp.float32)
    grad_hidden = matmul_nt(out_grad, w_proj)
    _, pull_gelu = jax.vjp(gelu_tanh, pre_act)
    grad_fc = pull_gelu(grad_hidden)[0].astype(jnp.bfloat16)
    grad_act_two = matmul_nn(grad_fc, w_fc)
    _, pull_two = jax.vjp(layer_norm, residual, vectors[5], vectors[6])
    grad_res_norm, grad_gain_two, grad_bias_two = pull_two(grad_act_two)
    grad_res = grad_out_f + grad_res_norm
    grad_attn = grad_res.astype(jnp.bfloat16)
    grad_mix = (
        matmul_nn(grad_attn, w_out).astype(jnp.bfloat16).reshape(tok_rows, head_count, head_size)
    )
    grad_dot = jnp.transpose(jnp.sum(grad_mix.astype(jnp.float32) * mixed_full, axis=-1), (1, 0))[
        :, :, None
    ]

    def add_grads(pair_index, allowed, running):
        grad_query, grad_store = running
        key_rows, value_rows = pair_rows(pair_index)
        prob_rows = jnp.exp(pair_scores(key_rows, allowed) - log_total)
        grad_probs = jnp.einsum(
            "qhd,khd->hqk", grad_mix, value_rows, preferred_element_type=jnp.float32
        )
        grad_scores = (prob_rows * (grad_probs - grad_dot)).astype(jnp.bfloat16)
        grad_query = (
            grad_query
            + jnp.einsum("hqk,khd->qhd", grad_scores, key_rows, preferred_element_type=jnp.float32)
            * score_scale
        )
        grad_keys = (
            jnp.einsum("hqk,qhd->khd", grad_scores, queries, preferred_element_type=jnp.float32)
            * score_scale
        )
        grad_values = jnp.einsum(
            "hqk,qhd->khd",
            prob_rows.astype(jnp.bfloat16),
            grad_mix,
            preferred_element_type=jnp.float32,
        )
        pair_grad = jnp.concatenate(
            [
                grad_keys.reshape(2 * tok_rows, model_width),
                grad_values.reshape(2 * tok_rows, model_width),
            ],
            axis=1,
        )
        pair_grad = pair_grad.reshape(2, tok_rows, 2 * model_width)
        grad_store = lax.dynamic_update_slice_in_dim(grad_store, pair_grad, 2 * pair_index, 0)
        return (grad_query, grad_store)

    start_query = jnp.zeros((tok_rows, head_count, head_size), jnp.float32)
    start_store = jnp.zeros((2 * pair_count, tok_rows, 2 * model_width), jnp.float32)
    grad_query, grad_store = lax.fori_loop(
        0, pair_count, visit(add_grads), (start_query, start_store)
    )

    def send_back(step_index, moving):
        moving = moving + lax.dynamic_index_in_dim(
            grad_store, reach_back - step_index, 0, keepdims=False
        )
        return from_behind(moving.astype(jnp.bfloat16), "cp", -1).astype(moving.dtype)

    returned = lax.fori_loop(
        0, reach_back, send_back, jnp.zeros((tok_rows, 2 * model_width), jnp.float32)
    )
    grad_kv = returned + grad_store[0]
    grad_qkv = jnp.concatenate([grad_query.reshape(tok_rows, model_width), grad_kv], axis=1).astype(
        jnp.bfloat16
    )
    grad_qkv_f = grad_qkv.astype(jnp.float32)
    grad_act_one = matmul_nn(grad_qkv, w_attn)
    _, pull_one = jax.vjp(layer_norm, inputs, vectors[0], vectors[1])
    grad_in_norm, grad_gain_one, grad_bias_one = pull_one(grad_act_one)
    input_grad = (grad_res + grad_in_norm).astype(jnp.bfloat16)
    grad_vectors = jnp.stack(
        [
            grad_gain_one,
            grad_bias_one,
            jnp.sum(grad_qkv_f[:, :model_width], axis=0),
            jnp.sum(grad_qkv_f[:, 2 * model_width :], axis=0),
            jnp.sum(grad_attn.astype(jnp.float32), axis=0),
            grad_gain_two,
            grad_bias_two,
            jnp.sum(grad_out_f, axis=0),
        ]
    )
    grad_fc_bias = jnp.sum(grad_fc.astype(jnp.float32), axis=0).reshape(
        hidden // model_width, model_width
    )
    used_rows = 4 * model_width + 2 * hidden + 8 + hidden // model_width
    total_rows = gathered.shape[0]
    local_grad = jnp.concatenate(
        [
            matmul_tn(grad_qkv, act_one),
            matmul_tn(grad_attn, mixed),
            matmul_tn(grad_fc, act_two),
            matmul_tn(act_hidden, out_grad),
            grad_vectors,
            grad_fc_bias,
            jnp.zeros((total_rows - used_rows, model_width), jnp.float32),
        ],
        axis=0,
    )
    dp_count = lax.axis_size("dp")
    device_count = dp_count * cp_count
    share_rows = total_rows // device_count
    spread_rows = local_grad.reshape(device_count, 1, share_rows, model_width)
    received = lax.all_to_all(
        spread_rows.astype(jnp.bfloat16), ("dp", "cp"), split_axis=0, concat_axis=1, tiled=True
    ).astype(spread_rows.dtype)
    param_grad = jnp.sum(received, axis=1).reshape(share_rows, model_width)
    return (output, input_grad, param_grad)


MESH = pl.DeviceIdType.MESH
GRAIN = 8
NT = (((1,), (1,)), ((), ()))
TN = (((0,), (0,)), ((), ()))


def dot_nt(a, b):
    return lax.dot_general(a, b, NT, preferred_element_type=jnp.float32)


def dot_tn(a, b):
    return lax.dot_general(a, b, TN, preferred_element_type=jnp.float32)


def dot_nn(a, b):
    return jnp.dot(a, b, preferred_element_type=jnp.float32)


def flat_id(y, c, z, x):
    return ((y * 2 + c) * 4 + z) * 2 + x


def permute(value, move):
    pairs = []
    for y in range(2):
        for c in range(2):
            for z in range(4):
                for x in range(2):
                    to = move(y, c, z, x)
                    if to is not None:
                        pairs.append((flat_id(y, c, z, x), flat_id(*to)))
    return lax.ppermute(value, ("dp", "cp"), pairs)


def over_y(value):
    return permute(value, lambda y, c, z, x: (1 - y, c, z, x))


def over_z(value, by):
    return permute(value, lambda y, c, z, x: (y, c, (z + by) % 4, x))


class Sizes:
    def __init__(self, width, hidden, heads, head_size, rows):
        self.head_size = head_size
        self.quarter_heads = -(-heads // 4)
        self.part = self.quarter_heads * head_size
        self.part_grains = self.part // GRAIN
        self.width_grains = width // GRAIN
        self.spill = 4 * self.part_grains - self.width_grains
        self.qkv = 3 * self.part_grains // 8
        self.out = self.part_grains // 8
        self.mlp = hidden // 4 // 8 // GRAIN
        self.block = rows // GRAIN
        self.out_start = 3 * self.width_grains
        self.fc_start = 4 * self.width_grains
        self.proj_start = self.fc_start + hidden // GRAIN
        self.vec_start = self.proj_start + hidden // GRAIN
        self.vec = 2


def my_place():
    dp = lax.axis_index("dp")
    cp = lax.axis_index("cp")
    return dp // 2, dp % 2, cp // 2, cp % 2


def place_of(quarter, share):
    return (share // 4) * 2 + quarter // 2, (share % 4) * 2 + quarter % 2


class Wires:
    def __init__(self, send_sems, recv_sems):
        self.send_sems = send_sems
        self.recv_sems = recv_sems
        self.count = 0

    def to(self, src, dst, dp, cp):
        index = self.count
        self.count += 1
        return pltpu.make_async_remote_copy(
            src_ref=src,
            dst_ref=dst,
            send_sem=self.send_sems.at[index],
            recv_sem=self.recv_sems.at[index],
            device_id=(dp, cp),
            device_id_type=MESH,
        )


class PlaceGather:
    def __init__(self, wires, full):
        self.wires = wires
        self.full = full
        self.dp, self.cp = lax.axis_index("dp"), lax.axis_index("cp")
        self.y, self.z, self.x = self.dp // 2, self.cp // 2, self.cp % 2
        self.started = []

    def send(self, slot, dp, cp):
        view = self.full.at[slot]
        copy = self.wires.to(view, view, dp, cp)
        copy.start()
        self.started.append(copy)
        return copy

    def start(self):
        mine = self.y * 4 + self.z
        self.along = []
        for d in (1, 3, 2):
            self.along.append((d, self.send(mine, self.dp, ((self.z + d) % 4) * 2 + self.x)))
        self.over = [self.send(mine, (self.dp + 2) % 4, self.cp)]

    def forward(self):
        for d, copy in self.along:
            copy.wait_recv()
            self.over.append(self.send(self.y * 4 + (self.z - d + 4) % 4, (self.dp + 2) % 4, self.cp))

    def finish(self):
        for copy in self.over:
            copy.wait_recv()
        for copy in self.started:
            copy.wait_send()


class QuadGather:
    def __init__(self, wires, block, full, local_sem):
        self.wires = wires
        self.block = block
        self.full = full
        self.dp, self.cp = lax.axis_index("dp"), lax.axis_index("cp")
        self.c, self.x = self.dp % 2, self.cp % 2
        self.over_x = (self.dp, self.cp + 1 - 2 * self.x)
        self.over_c = (self.dp + 1 - 2 * self.c, self.cp)
        self.local_sem = local_sem

    def start(self):
        spot = self.full.at[self.c, self.x]
        self.by_x = self.wires.to(self.block, spot, *self.over_x)
        self.by_c = self.wires.to(self.block, spot, *self.over_c)
        self.by_x.start()
        self.by_c.start()
        self.local = pltpu.make_async_copy(self.block, spot, self.local_sem)
        self.local.start()

    def forward(self):
        self.by_x.wait_recv()
        spot = self.full.at[self.c, 1 - self.x]
        self.pass_on = self.wires.to(spot, spot, *self.over_c)
        self.pass_on.start()

    def finish(self):
        self.by_c.wait_recv()
        self.pass_on.wait_recv()
        self.by_x.wait_send()
        self.by_c.wait_send()
        self.pass_on.wait_send()
        self.local.wait()


def open_kernel(
    sz, p_ref, tok_ref, cot_ref, qkv_ref, out_ref, fc_ref, proj_ref, vec_ref, tok_all, cot_all,
    spread_sems, kind_sems, send_sems, recv_sems, local_sems,
):
    y, c, z, x = my_place()
    me = flat_id(y, c, z, x)
    wires = Wires(send_sems, recv_sems)
    tok = QuadGather(wires, tok_ref, tok_all, local_sems.at[0])
    cot = QuadGather(wires, cot_ref, cot_all, local_sems.at[1])

    def send(grain, ref, slot, quarter, share, sem, recv):
        dp, cp = place_of(quarter, share)
        mine = dp * 8 + cp == me

        @pl.when(mine)
        def _():
            pltpu.make_async_copy(p_ref.at[grain], ref.at[share, slot], recv).start()

        @pl.when(jnp.logical_not(mine))
        def _():
            pltpu.make_async_remote_copy(
                src_ref=p_ref.at[grain],
                dst_ref=ref.at[share, slot],
                send_sem=sem,
                recv_sem=recv,
                device_id=(dp, cp),
                device_id_type=MESH,
            ).start()

    def sent(grain, ref, slot, quarter, share, sem, recv):
        dp, cp = place_of(quarter, share)

        @pl.when(dp * 8 + cp != me)
        def _():
            pltpu.make_async_copy(p_ref.at[grain], p_ref.at[grain], sem).wait()

    def headed(act, grain, base, parts, ref, recv, share_size):
        offset = me * sz.block + grain - base
        part = offset // sz.width_grains
        local = offset % sz.width_grains

        def one(quarter, inner, sem):
            spot = part * sz.part_grains + inner
            act(grain, ref, spot % share_size, quarter, spot // share_size, sem, recv)

        @pl.when(jnp.logical_and(offset >= 0, offset < parts * sz.width_grains))
        def _():
            one(local // sz.part_grains, local % sz.part_grains, spread_sems.at[grain])

            @pl.when(local < sz.spill)
            def _():
                one(3, sz.part_grains - sz.spill + local, spread_sems.at[sz.block + grain])

    def plain(act, grain, base, ref, recv):
        offset = me * sz.block + grain - base

        @pl.when(jnp.logical_and(offset >= 0, offset < 32 * sz.mlp))
        def _():
            act(
                grain, ref, offset % sz.mlp, offset // (8 * sz.mlp), (offset // sz.mlp) % 8,
                spread_sems.at[grain], recv,
            )

    def heads(act):
        def one(grain, _):
            headed(act, grain, 0, 3, qkv_ref, kind_sems.at[0], sz.qkv)
            return 0

        lax.fori_loop(0, sz.block, one, 0)

    def others(act):
        def one(grain, _):
            headed(act, grain, sz.out_start, 1, out_ref, kind_sems.at[1], sz.out)
            plain(act, grain, sz.fc_start, fc_ref, kind_sems.at[2])
            plain(act, grain, sz.proj_start, proj_ref, kind_sems.at[3])
            return 0

        lax.fori_loop(0, sz.block, one, 0)

    owner = sz.vec_start // sz.block
    spot = sz.vec_start % sz.block

    def vector_sends(act):
        @pl.when(me == owner)
        def _():
            def to(device, _):
                @pl.when(device != me)
                def _():
                    act(
                        pltpu.make_async_remote_copy(
                            src_ref=p_ref.at[pl.ds(spot, sz.vec)],
                            dst_ref=vec_ref,
                            send_sem=spread_sems.at[2 * sz.block + device],
                            recv_sem=kind_sems.at[4],
                            device_id=(device // 8, device % 8),
                            device_id_type=MESH,
                        )
                    )

                return 0

            lax.fori_loop(0, 32, to, 0)

    heads(send)
    tok.start()
    cot.start()
    mine = y * 4 + z
    pltpu.make_async_copy(qkv_ref.at[mine], qkv_ref.at[mine], kind_sems.at[0]).wait()
    weights = PlaceGather(wires, qkv_ref)
    weights.start()
    others(send)
    vector_sends(lambda copy: copy.start())

    @pl.when(me == owner)
    def _():
        pltpu.make_async_copy(p_ref.at[pl.ds(spot, sz.vec)], vec_ref, kind_sems.at[4]).start()

    weights.forward()
    tok.forward()
    cot.forward()
    heads(sent)
    others(sent)
    vector_sends(lambda copy: copy.wait_send())
    for index, ref in enumerate((out_ref, fc_ref, proj_ref)):
        pltpu.make_async_copy(ref.at[mine], ref.at[mine], kind_sems.at[index + 1]).wait()
    pltpu.make_async_copy(vec_ref, vec_ref, kind_sems.at[4]).wait()
    tok.finish()
    cot.finish()
    weights.finish()


HBM = pl.BlockSpec(memory_space=pl.ANY)
VMEM = pl.BlockSpec(memory_space=pltpu.VMEM)
REMOTE = pltpu.CompilerParams(has_side_effects=True)


def remote_params(ident=None, vmem=None):
    return pltpu.CompilerParams(has_side_effects=True, collective_id=ident, vmem_limit_bytes=vmem)


def greet(partners):
    barrier = pltpu.get_barrier_semaphore()
    for dp, cp in partners:
        pl.semaphore_signal(barrier, inc=1, device_id=(dp, cp), device_id_type=MESH)
    pl.semaphore_wait(barrier, len(partners))


def cost(us):
    return pl.CostEstimate(flops=0, bytes_accessed=int(us * 3.0e6), transcendentals=0)


def wire_sems(count):
    return [pltpu.SemaphoreType.DMA((count,)), pltpu.SemaphoreType.DMA((count,))]


def open_call(sz, table, tokens, cotangent):
    rows, width = tokens.shape

    def like(*shape):
        return jax.ShapeDtypeStruct(shape + (width,), table.dtype)

    return pl.pallas_call(
        functools.partial(open_kernel, sz),
        out_shape=(
            like(8, sz.qkv, GRAIN),
            like(8, sz.out, GRAIN),
            like(8, sz.mlp, GRAIN),
            like(8, sz.mlp, GRAIN),
            like(sz.vec, GRAIN),
            like(2, 2, rows),
            like(2, 2, rows),
        ),
        in_specs=[HBM, VMEM, VMEM],
        out_specs=[HBM] * 7,
        scratch_shapes=[
            pltpu.SemaphoreType.DMA((2 * sz.block + 32,)),
            pltpu.SemaphoreType.DMA((5,)),
            *wire_sems(13),
            pltpu.SemaphoreType.DMA((2,)),
        ],
        compiler_params=REMOTE,
        name="open",
    )(table, tokens, cotangent)


def keys_kernel(kv_ref, out_in, fc_in, before_ref, out_ref, fc_ref, out_all, send_sems, recv_sems, local_sem):
    _, _, z, _ = my_place()
    dp, cp = lax.axis_index("dp"), lax.axis_index("cp")
    wires = Wires(send_sems, recv_sems)
    keys = wires.to(kv_ref, before_ref, dp, (cp + 2) % 8)

    @pl.when(z % 2 == 0)
    def _():
        keys.start()

    first = PlaceGather(wires, out_ref)
    second = PlaceGather(wires, fc_ref)
    first.start()
    second.start()
    first.forward()
    first.finish()
    quad = QuadGather(wires, out_ref, out_all, local_sem)
    quad.start()

    @pl.when(z % 2 == 1)
    def _():
        keys.wait_recv()

    second.forward()
    quad.forward()
    second.finish()
    quad.finish()

    @pl.when(z % 2 == 0)
    def _():
        keys.wait_send()


def keys_call(kv, w_out, w_fc):
    def like(value, *lead):
        return jax.ShapeDtypeStruct(lead + value.shape, value.dtype)

    return pl.pallas_call(
        keys_kernel,
        out_shape=(like(kv), like(w_out), like(w_fc), like(w_out, 2, 2)),
        in_specs=[HBM] * 3,
        out_specs=[HBM] * 4,
        input_output_aliases={1: 1, 2: 2},
        scratch_shapes=[*wire_sems(18), pltpu.SemaphoreType.DMA],
        compiler_params=REMOTE,
        name="keys",
    )(kv, w_out, w_fc)


def acts_kernel(act_ref, proj_in, act_all, proj_ref, send_sems, recv_sems, local_sem):
    wires = Wires(send_sems, recv_sems)
    quad = QuadGather(wires, act_ref, act_all, local_sem)
    places = PlaceGather(wires, proj_ref)
    quad.start()
    places.start()
    quad.forward()
    places.forward()
    quad.finish()
    places.finish()


def acts_call(act, w_proj):
    return pl.pallas_call(
        acts_kernel,
        out_shape=(
            jax.ShapeDtypeStruct((2, 2) + act.shape, act.dtype),
            jax.ShapeDtypeStruct(w_proj.shape, w_proj.dtype),
        ),
        in_specs=[VMEM, HBM],
        out_specs=[HBM] * 2,
        input_output_aliases={1: 1},
        scratch_shapes=[*wire_sems(10), pltpu.SemaphoreType.DMA],
        compiler_params=REMOTE,
        name="acts",
    )(act, w_proj)


def swap_kernel(in_ref, out_ref, send_sems, recv_sems, local_sem):
    y, c, z, x = my_place()
    wires = Wires(send_sems, recv_sems)
    mine = c * 2 + x
    others = [(1 - c, 1 - x), (c, 1 - x), (1 - c, x)]
    greet([(y * 2 + tc, z * 2 + tx) for tc, tx in others])
    copies = []
    for tc, tx in others:
        copies.append(wires.to(in_ref.at[tc * 2 + tx], out_ref.at[mine], y * 2 + tc, z * 2 + tx))
    for copy in copies:
        copy.start()
    local = pltpu.make_async_copy(in_ref.at[mine], out_ref.at[mine], local_sem)
    local.start()
    for copy in copies:
        copy.wait_recv()
    for copy in copies:
        copy.wait_send()
    local.wait()


def swap_call(value, ident):
    return pl.pallas_call(
        swap_kernel,
        out_shape=jax.ShapeDtypeStruct(value.shape, value.dtype),
        in_specs=[VMEM],
        out_specs=VMEM,
        scratch_shapes=[*wire_sems(3), pltpu.SemaphoreType.DMA],
        compiler_params=remote_params(ident),
        cost_estimate=cost(20),
        name="swap",
    )(value)


class QuadSum:
    step = 32

    def __init__(self, in_ref, out_ref, got_c, stage, got_x, send_sems, recv_sems):
        self.y, self.c, self.z, self.x = my_place()
        dp, cp = lax.axis_index("dp"), lax.axis_index("cp")
        wires = Wires(send_sems, recv_sems)
        self.in_ref, self.out_ref, self.got_c, self.stage, self.got_x = in_ref, out_ref, got_c, stage, got_x
        self.partners = [(dp + 1 - 2 * self.c, cp), (dp, cp + 1 - 2 * self.x)]
        self.by_c = wires.to(in_ref.at[1 - self.c], got_c, *self.partners[0])
        self.by_x = wires.to(stage, got_x, *self.partners[1])

    def each(self, act):
        def one(index, _):
            act(pl.ds(pl.multiple_of(index * self.step, self.step), self.step))
            return 0

        lax.fori_loop(0, self.out_ref.shape[0] // self.step, one, 0)

    def start(self):
        greet(self.partners)
        self.by_c.start()

    def middle(self):
        c, x = self.c, self.x
        self.by_c.wait_recv()

        def to_send(span):
            self.stage[span, :] = (
                self.in_ref[c, 1 - x, span, :].astype(jnp.float32) + self.got_c[1 - x, span, :].astype(jnp.float32)
            ).astype(self.stage.dtype)

        self.each(to_send)
        self.by_x.start()

    def finish(self):
        c, x = self.c, self.x
        self.by_x.wait_recv()

        def to_add(span):
            self.out_ref[span, :] = (
                self.in_ref[c, x, span, :].astype(jnp.float32)
                + self.got_c[x, span, :].astype(jnp.float32)
                + self.got_x[span, :].astype(jnp.float32)
            )

        self.each(to_add)
        self.by_c.wait_send()
        self.by_x.wait_send()


def quad_sum_kernel(*refs):
    quad = QuadSum(*refs)
    quad.start()
    quad.middle()
    quad.finish()


def quad_scratch(partial):
    rows, width = partial.shape[2:]
    return [
        pltpu.VMEM((2, rows, width), partial.dtype),
        pltpu.VMEM((rows, width), partial.dtype),
        pltpu.VMEM((rows, width), partial.dtype),
        *wire_sems(2),
    ]


def quad_sum(partial, ident):
    return pl.pallas_call(
        quad_sum_kernel,
        out_shape=jax.ShapeDtypeStruct(partial.shape[2:], jnp.float32),
        in_specs=[VMEM],
        out_specs=VMEM,
        scratch_shapes=quad_scratch(partial),
        compiler_params=remote_params(ident),
        cost_estimate=cost(30),
        name="quad_sum",
    )(partial)


def collect_kernel(sz, qkv_ref, out_ref, fc_ref, proj_ref, vec_ref, g_ref, vecs_ref, send_sems, recv_sem, vec_sems):
    y, c, z, x = my_place()
    me = flat_id(y, c, z, x)
    quarter = c * 2 + x
    share = y * 4 + z

    def send(ref, slot, table, sem):
        dest = table // sz.block
        mine = dest == me

        @pl.when(mine)
        def _():
            pltpu.make_async_copy(ref.at[slot], g_ref.at[table % sz.block], recv_sem).start()

        @pl.when(jnp.logical_not(mine))
        def _():
            pltpu.make_async_remote_copy(
                src_ref=ref.at[slot],
                dst_ref=g_ref.at[table % sz.block],
                send_sem=sem,
                recv_sem=recv_sem,
                device_id=(dest // 8, dest % 8),
                device_id_type=MESH,
            ).start()

    def sent(ref, slot, table, sem):
        @pl.when(table // sz.block != me)
        def _():
            pltpu.make_async_copy(ref.at[slot], ref.at[slot], sem).wait()

    def run(act):
        def headed(ref, size, base, first_sem):
            def one(slot, _):
                spot = share * size + slot
                part = spot // sz.part_grains
                local = quarter * sz.part_grains + spot % sz.part_grains

                @pl.when(local < sz.width_grains)
                def _():
                    act(ref, slot, base + part * sz.width_grains + local, send_sems.at[first_sem + slot])

                return 0

            lax.fori_loop(0, size, one, 0)

        def plain(ref, base, first_sem):
            def one(slot, _):
                table = base + (quarter * 8 + share) * sz.mlp + slot
                act(ref, slot, table, send_sems.at[first_sem + slot])
                return 0

            lax.fori_loop(0, sz.mlp, one, 0)

        headed(qkv_ref, sz.qkv, 0, 0)
        headed(out_ref, sz.out, sz.out_start, sz.qkv)
        plain(fc_ref, sz.fc_start, sz.qkv + sz.out)
        plain(proj_ref, sz.proj_start, sz.qkv + sz.out + sz.mlp)

    last = sz.vec_start // sz.block
    vec_copy = pltpu.make_async_remote_copy(
        src_ref=vec_ref,
        dst_ref=vecs_ref.at[me],
        send_sem=vec_sems.at[0],
        recv_sem=vec_sems.at[1],
        device_id=(last // 8, last % 8),
        device_id_type=MESH,
    )

    @pl.when(me != last)
    def _():
        vec_copy.start()

    @pl.when(me == last)
    def _():
        pltpu.make_async_copy(vec_ref, vecs_ref.at[me], vec_sems.at[1]).start()

    run(send)
    run(sent)

    @pl.when(me != last)
    def _():
        vec_copy.wait_send()

    @pl.when(me == last)
    def _():
        view = g_ref.at[pl.ds(0, sz.vec_start % sz.block)]
        pltpu.make_async_copy(view, view, recv_sem).wait()
        pltpu.make_async_copy(vecs_ref, vecs_ref, vec_sems.at[1]).wait()

    @pl.when(me != last)
    def _():
        pltpu.make_async_copy(g_ref, g_ref, recv_sem).wait()


def collect(sz, qkv, out, fc, proj, vectors):
    width = qkv.shape[-1]
    return pl.pallas_call(
        functools.partial(collect_kernel, sz),
        out_shape=(
            jax.ShapeDtypeStruct((sz.block, GRAIN, width), qkv.dtype),
            jax.ShapeDtypeStruct((32,) + vectors.shape, vectors.dtype),
        ),
        in_specs=[HBM] * 5,
        out_specs=[HBM] * 2,
        scratch_shapes=[
            pltpu.SemaphoreType.DMA((sz.qkv + sz.out + 2 * sz.mlp,)),
            pltpu.SemaphoreType.DMA,
            pltpu.SemaphoreType.DMA((2,)),
        ],
        compiler_params=REMOTE,
        name="collect",
    )(qkv, out, fc, proj, vectors)


def attend_kernel(heads, size, odd_ref, q_ref, kv_ref, before_ref, mix_ref, lse_ref):
    part = heads * size
    rows = q_ref.shape[0]
    blk = 128
    scale = size**-0.5
    lane = lax.broadcasted_iota(jnp.int32, (blk, rows), 1)
    line = lax.broadcasted_iota(jnp.int32, (blk, rows), 0)

    def block(index, _):
        first = pl.multiple_of(index * blk, blk)
        allowed = lane <= line + first

        def one(with_before):
            for h in range(heads):
                cols = slice(h * size, (h + 1) * size)
                vals = slice(part + h * size, part + (h + 1) * size)
                q = q_ref[pl.ds(first, blk), cols]
                s = dot_nt(q, kv_ref[:, cols]) * scale
                s = jnp.where(allowed, s, MASKED)
                top = jnp.max(s, axis=-1, keepdims=True)
                if with_before:
                    s_b = dot_nt(q, before_ref[:, cols]) * scale
                    top = jnp.maximum(top, jnp.max(s_b, axis=-1, keepdims=True))
                    p_b = jnp.exp(s_b - top)
                p = jnp.exp(s - top)
                total = jnp.sum(p, axis=-1, keepdims=True)
                mix = dot_nn(p.astype(jnp.bfloat16), kv_ref[:, vals])
                if with_before:
                    total = total + jnp.sum(p_b, axis=-1, keepdims=True)
                    mix = mix + dot_nn(p_b.astype(jnp.bfloat16), before_ref[:, vals])
                mix_ref[pl.ds(first, blk), cols] = mix / total
                lse_ref[pl.ds(first, blk), h : h + 1] = top + jnp.log(total)

        @pl.when(odd_ref[0] == 1)
        def _():
            one(True)

        @pl.when(odd_ref[0] == 0)
        def _():
            one(False)

        return 0

    lax.fori_loop(0, rows // blk, block, 0)


def attend(sz, odd, q, kv, before):
    rows = q.shape[0] // 2
    return pl.pallas_call(
        functools.partial(attend_kernel, sz.quarter_heads, sz.head_size),
        grid_spec=pltpu.PrefetchScalarGridSpec(
            num_scalar_prefetch=1,
            grid=(2,),
            in_specs=[
                pl.BlockSpec((rows, sz.part), lambda g, odd: (g, 0)),
                pl.BlockSpec((rows, 2 * sz.part), lambda g, odd: (g, 0)),
                pl.BlockSpec((rows, 2 * sz.part), lambda g, odd: (g, 0)),
            ],
            out_specs=[
                pl.BlockSpec((rows, sz.part), lambda g, odd: (g, 0)),
                pl.BlockSpec((rows, 8), lambda g, odd: (g, 0)),
            ],
        ),
        out_shape=(
            jax.ShapeDtypeStruct((2 * rows, sz.part), jnp.float32),
            jax.ShapeDtypeStruct((2 * rows, 8), jnp.float32),
        ),
        cost_estimate=pl.CostEstimate(
            flops=2 * 2 * 2 * rows * 2 * rows * sz.part,
            bytes_accessed=20 * rows * sz.part,
            transcendentals=4 * rows * rows * sz.quarter_heads,
        ),
        compiler_params=pltpu.CompilerParams(vmem_limit_bytes=40 << 20),
        name="attend",
    )(odd, q, kv, before)


def attend_back_kernel(heads, size, own, *refs):
    if own:
        q_ref, kv_ref, do_ref, mix_ref, lse_ref, seed_ref, term_ref, dq_ref, dkv_ref, sum_ref = refs[:10]
    else:
        q_ref, kv_ref, do_ref, mix_ref, lse_ref, term_ref, dq_ref, dkv_ref, sum_ref = refs[:9]
    quad = QuadSum(term_ref, sum_ref, *refs[-5:])
    quad.start()
    _, _, z, _ = my_place()
    part = heads * size
    rows = q_ref.shape[0] // 2
    blk = 128
    scale = size**-0.5
    lane = lax.broadcasted_iota(jnp.int32, (blk, rows), 1)
    line = lax.broadcasted_iota(jnp.int32, (blk, rows), 0)

    def group(start):
        keys_at = slice(start, start + rows)

        def block(index, _):
            first = pl.multiple_of(index * blk, blk)
            here = pl.ds(pl.multiple_of(start + first, blk), blk)
            if own:
                allowed = lane <= line + first
            for h in range(heads):
                cols = slice(h * size, (h + 1) * size)
                vals = slice(part + h * size, part + (h + 1) * size)
                q = q_ref[here, cols]
                k = kv_ref[keys_at, cols]
                do = do_ref[here, cols]
                s = dot_nt(q, k) * scale
                p = jnp.exp(s - lse_ref[here, h : h + 1])
                if own:
                    p = jnp.where(allowed, p, 0.0)
                dp = dot_nt(do, kv_ref[keys_at, vals])
                delta = jnp.sum(do.astype(jnp.float32) * mix_ref[here, cols], axis=-1, keepdims=True)
                ds = (p * (dp - delta)).astype(jnp.bfloat16)
                dq = dot_nn(ds, k) * scale
                if own:
                    dq = dq + seed_ref[here, cols]
                dq_ref[here, cols] = dq.astype(dq_ref.dtype)
                dkv_ref[keys_at, cols] += dot_tn(ds, q) * scale
                dkv_ref[keys_at, vals] += dot_tn(p.astype(jnp.bfloat16), do)
            return 0

        lax.fori_loop(0, rows // blk, block, 0)

    dkv_ref[...] = jnp.zeros_like(dkv_ref)
    if own:
        group(0)
        quad.middle()
        group(rows)
        quad.finish()
    else:
        odd = z % 2 == 1

        @pl.when(odd)
        def _():
            group(0)

        quad.middle()

        @pl.when(odd)
        def _():
            group(rows)

        @pl.when(jnp.logical_not(odd))
        def _():
            dq_ref[...] = jnp.zeros_like(dq_ref)

        quad.finish()


def attend_back(sz, own, q, kv, grad_mix, mix, lse, seed, term, ident):
    operands = [q, kv, grad_mix, mix, lse] + ([seed] if own else []) + [term]
    return pl.pallas_call(
        functools.partial(attend_back_kernel, sz.quarter_heads, sz.head_size, own),
        out_shape=(
            jax.ShapeDtypeStruct(q.shape, jnp.bfloat16 if own else jnp.float32),
            jax.ShapeDtypeStruct(kv.shape, jnp.float32),
            jax.ShapeDtypeStruct(term.shape[2:], jnp.float32),
        ),
        in_specs=[VMEM] * len(operands),
        out_specs=[VMEM] * 3,
        scratch_shapes=quad_scratch(term),
        cost_estimate=cost(35),
        compiler_params=remote_params(ident, 56 << 20),
        name="attend_back_own" if own else "attend_back_before",
    )(*operands)


def norm_parts(values):
    mean = jnp.mean(values, axis=-1, keepdims=True)
    centre = values - mean
    rs = lax.rsqrt(jnp.mean(centre * centre, axis=-1, keepdims=True) + EPSILON)
    return centre * rs, rs


def norm_back(normed, rs, grad, gain):
    e = grad * gain
    return rs * (
        e
        - jnp.mean(e, axis=-1, keepdims=True)
        - normed * jnp.mean(e * normed, axis=-1, keepdims=True)
    )


def per_device_quad(tokens, params, out_grad, lengths):
    rows, width = tokens.shape
    hidden = FF
    sz = Sizes(width, hidden, HEADS, HEAD_DIM, params.shape[0])
    y, c, z, x = my_place()
    quarter = c * 2 + x
    bf16, f32 = jnp.bfloat16, jnp.float32

    def pick(value, index):
        return lax.dynamic_index_in_dim(value, index, 0, keepdims=False)

    def halves_of(value):
        half = value.shape[1] // 2
        first, second = value[:, :half], value[:, half:]
        return jnp.where(y == 0, first, second), jnp.where(y == 0, second, first)

    def to_other_y(sent):
        return over_y(sent.astype(bf16))

    def to_places(kept, got):
        summed = kept + got.astype(f32)
        summed = summed.reshape(4, summed.shape[0] // 4, -1)
        total = pick(summed, z)
        for d in (1, 2, 3):
            got = over_z(pick(summed, (z + d) % 4).astype(bf16), d)
            total = total + got.astype(f32)
        return total

    w_qkv, w_out, w_fc, w_proj, vec, tok_all, cot_all = open_call(
        sz, params.reshape(sz.block, GRAIN, width), tokens, out_grad
    )
    flat = lambda value: value.reshape(-1, width)
    vectors = flat(vec).astype(f32)
    fc_bias = vectors[8 : 8 + hidden // width].reshape(hidden)
    w_qkv, cot_all = flat(w_qkv), flat(cot_all)
    normed_all, _ = norm_parts(flat(tok_all).astype(f32))
    act_one = (normed_all * vectors[0] + vectors[1]).astype(bf16)

    def quarter_of(vector):
        padded = jnp.pad(vector, (0, 4 * sz.part - width))
        return lax.dynamic_slice_in_dim(padded, quarter * sz.part, sz.part, 0)

    kv_bias = jnp.concatenate([jnp.zeros((sz.part,), f32), quarter_of(vectors[3])])
    kv = (dot_nt(act_one, w_qkv[sz.part :]) + kv_bias).astype(bf16)
    q = (dot_nt(act_one, w_qkv[: sz.part]) + quarter_of(vectors[2])).astype(bf16)
    before, _, w_fc, w_out = keys_call(kv, w_out, w_fc)
    w_fc, w_out = flat(w_fc), flat(w_out)[:width]
    odd = (z % 2).astype(jnp.int32).reshape(1)
    mix, lse = attend(sz, odd, q, kv, before)
    mixed = swap_call(mix.astype(bf16).reshape(4, rows, sz.part), 1)
    mixed = jnp.transpose(mixed, (1, 0, 2)).reshape(rows, 4 * sz.part)[:, :width]
    inputs = tokens.astype(f32)
    residual = inputs + (dot_nt(mixed, w_out) + vectors[4])
    normed_two, rs_two = norm_parts(residual)
    act_two, w_proj = acts_call((normed_two * vectors[5] + vectors[6]).astype(bf16), w_proj)
    act_two, w_proj = flat(act_two), flat(w_proj)
    bias = lax.dynamic_slice_in_dim(fc_bias, quarter * (hidden // 4), hidden // 4, 0)
    pre_act = dot_nt(act_two, w_fc) + bias
    act_hidden, pull_gelu = jax.vjp(gelu_tanh, pre_act)
    act_hidden = act_hidden.astype(bf16)
    hid_mine, hid_other = halves_of(act_hidden)
    got_proj = to_other_y(dot_tn(hid_other, cot_all))
    grad_fc = pull_gelu(dot_nt(cot_all, w_proj))[0].astype(bf16)
    fc_mine, fc_other = halves_of(grad_fc)
    got_fc = to_other_y(dot_tn(fc_other, act_two))
    grad_two = quad_sum(dot_nn(grad_fc, w_fc).astype(bf16).reshape(2, 2, rows, width), 2)

    cot = out_grad.astype(f32)
    grad_res = cot + norm_back(normed_two, rs_two, grad_two, vectors[5])
    grad_attn = grad_res.astype(bf16)
    grad_mix = dot_nn(grad_attn, w_out).astype(bf16)
    grad_mix = jnp.pad(grad_mix, ((0, 0), (0, 4 * sz.part - width)))
    grad_mix = jnp.transpose(grad_mix.reshape(rows, 4, sz.part), (1, 0, 2))
    grad_mix = swap_call(grad_mix, 3).reshape(4 * rows, sz.part)
    g_proj = to_places(dot_tn(hid_mine, cot_all), got_proj)
    g_out = jnp.pad(dot_tn(grad_attn, mixed).astype(bf16), ((0, 4 * sz.part - width), (0, 0)))
    dq_before, dkv_before, g_out = attend_back(
        sz, False, q, before, grad_mix, mix, lse, None, g_out.reshape(2, 2, sz.part, width), 4
    )
    returned = permute(
        dkv_before.astype(bf16), lambda py, pc, pz, px: (py, pc, pz - 1, px) if pz % 2 == 1 else None
    )
    g_fc = to_places(dot_tn(fc_mine, act_two), got_fc)
    g_out = g_out.reshape(2, sz.part // 2, width)
    got_out = to_other_y(pick(g_out, 1 - y))
    partial_out = dot_nn(act_hidden, w_proj).astype(bf16).reshape(2, 2, rows, width)
    dq, dkv, out_sum = attend_back(sz, True, q, kv, grad_mix, mix, lse, dq_before, partial_out, 5)
    output = (residual + out_sum + vectors[7]).astype(bf16)
    grad_qkv = jnp.concatenate([dq, (dkv + returned.astype(f32)).astype(bf16)], axis=1)
    qkv_mine, qkv_other = halves_of(grad_qkv)
    got_qkv = to_other_y(dot_tn(qkv_other, act_one))
    grad_one = quad_sum(dot_nn(grad_qkv, w_qkv).astype(bf16).reshape(2, 2, rows, width), 6)
    g_out = to_places(pick(g_out, y), got_out)
    g_qkv = to_places(dot_tn(qkv_mine, act_one), got_qkv)

    normed_one, rs_one = norm_parts(inputs)
    input_grad = (grad_res + norm_back(normed_one, rs_one, grad_one, vectors[0])).astype(bf16)

    def placed(vector):
        spot = lax.dynamic_update_slice_in_dim(jnp.zeros((4 * sz.part,), f32), vector, quarter * sz.part, 0)
        return spot[:width]

    sums = jnp.sum(grad_qkv.astype(f32), axis=0)
    bias_sum = jnp.sum(grad_fc.astype(f32), axis=0).reshape(1, hidden // 4)
    fc_rows = lax.dynamic_update_slice_in_dim(jnp.zeros((4, hidden // 4), f32), bias_sum, quarter, 0)
    grad_vectors = jnp.concatenate(
        [
            jnp.stack(
                [
                    jnp.sum(grad_one * normed_one, axis=0),
                    jnp.sum(grad_one, axis=0),
                    placed(sums[: sz.part]),
                    placed(sums[2 * sz.part :]),
                    jnp.sum(grad_attn.astype(f32), axis=0),
                    jnp.sum(grad_two * normed_two, axis=0),
                    jnp.sum(grad_two, axis=0),
                    jnp.sum(cot, axis=0),
                ]
            ),
            fc_rows.reshape(hidden // width, width),
        ]
    )
    count = grad_vectors.shape[0]
    grad_vectors = jnp.pad(grad_vectors, ((0, sz.vec * GRAIN - count), (0, 0)))
    grains = lambda value: value.astype(bf16).reshape(-1, GRAIN, width)
    table, all_vectors = collect(
        sz, grains(g_qkv), grains(g_out), grains(g_fc), grains(g_proj), grad_vectors.reshape(sz.vec, GRAIN, width)
    )
    grad_vectors = jnp.sum(all_vectors.reshape(32, sz.vec * GRAIN, width), axis=0)[:count]
    table = table.reshape(sz.block * GRAIN, width).astype(f32)
    used = (sz.vec_start % sz.block) * GRAIN
    tail = jnp.concatenate(
        [grad_vectors, jnp.zeros((sz.block * GRAIN - used - grad_vectors.shape[0], width), f32)]
    )
    last = flat_id(y, c, z, x) == sz.vec_start // sz.block
    tail = jnp.where(last, tail, table[used:])
    param_grad = jnp.concatenate([table[:used], tail])
    return (output, input_grad, param_grad)


def fits_quad(mesh, tokens, params, lengths):
    dp, cp = mesh.shape["dp"], mesh.shape["cp"]
    rows = tokens.shape[0] // (dp * cp)
    width = tokens.shape[1]
    blocks = params.shape[0] // (dp * cp)
    return (
        (dp, cp) == (4, 8)
        and lengths.shape[1] == 2
        and rows * cp == lengths.shape[1] * MIN_LEN
        and rows % 128 == 0
        and blocks % GRAIN == 0
        and (HEADS, HEAD_DIM, FF, width) == (25, 64, 6400, 1600)
    )


def solution(mesh):
    in_specs = (P(("dp", "cp"), None), P(("dp", "cp"), None), P(("dp", "cp"), None), P("dp", None))
    out_specs = (P(("dp", "cp"), None), P(("dp", "cp"), None), P(("dp", "cp"), None))

    def step(tokens, params, out_grad, lengths):
        body = per_device_quad if fits_quad(mesh, tokens, params, lengths) else per_device_general

        return jax.shard_map(
            body, mesh=mesh, in_specs=in_specs, out_specs=out_specs, check_vma=False
        )(tokens, params, out_grad, lengths)

    return step
```

profile of v0, /device:TPU:27, one launch (start us, length us, event | category | flops | bytes accessed | tf_op | source)
XLA Modules:
  0.0 1033.1 jit_solution(18191716452214810285)
XLA Ops:
  5.0 114.3 %open.1 = (bf16[8,21,8,1600]{3,2,1,0:T(8,128)(2,1)}, bf16[8,7,8,1600]{3,2,1,0:T(8,128)(2,1)}, bf16[8,25,8,1600]{3,2,1,0:T(8,128)(2,1)}, bf16[8,25,8,1600]{3,2,1,...) custom-call(bf16[76,8,1600]{2,1,0:T(8,128)(2,1)} %bitcast.169, ...), custom_call_target="tpu_custom_call" | custom-call | tf_op jit(solution)/shard_map/open/pallas_call | solution.py:619
  136.9 153.4 %keys.1 = (bf16[1024,896]{1,0:T(8,128)(2,1)}, bf16[8,7,8,1600]{3,2,1,0:T(8,128)(2,1)}, bf16[8,25,8,1600]{3,2,1,0:T(8,128)(2,1)}, bf16[2,2,8,7,8,1600]{5,4,3,2,1,0:T(8,128)(2,1)}) custom-call(bf16[1024,896]{1,0:T(8,128)(2,1)} %add_convert_fusion.1.kv_ref.refs_1_, ...), custom_call_target="tpu_custom_call", output_to_operand_aliasing={{1}: (1, {}), {2}: (2, {})} | custom-call | tf_op jit(solution)/shard_map/keys/pallas_call | solution.py:680
  293.3 22.5 %attend.1 = (f32[1024,448]{1,0:T(8,128)S(1)}, f32[1024,8]{1,0:T(8,128)S(1)}) custom-call(s32[1]{0:T(128)} %bitcast.odd_ref, bf16[1024,448]{1,0:T(8,128)(2,1)S(1)} %add_convert_fusion.2.q_ref.refs_0_, bf16[1024,896]{1,0:T(8,128)(2,1)S(1)} %copy-done.1, bf16[1024,896]{1,0:T(8,128)(2,1)S(1)} %copy-done.4), custom_call_target="tpu_custom_call" | custom-call | flops 1879048192 | bytes 4587520 | tf_op jit(solution)/shard_map/attend/pallas_call | solution.py:996
  317.8 17.1 %swap.2 = bf16[4,256,448]{2,1,0:T(8,128)(2,1)} custom-call(bf16[4,256,448]{2,1,0:T(8,128)(2,1)} %bitcast.159), custom_call_target="tpu_custom_call" | custom-call | bytes 60000000 | tf_op jit(solution)/shard_map/swap/pallas_call | solution.py:741
  343.8 81.0 %acts.1 = (bf16[2,2,256,1600]{3,2,1,0:T(8,128)(2,1)}, bf16[8,25,8,1600]{3,2,1,0:T(8,128)(2,1)}) custom-call(bf16[256,1600]{1,0:T(8,128)(2,1)} %add_convert_fusion.4.act_ref, bf16[8,25,8,1600]{3,2,1,0:T(8,128)(2,1)} %get-tuple-element.33.proj_in), custom_call_target="tpu_custom_call", output_to_operand_aliasing={{1}: (1, {})} | custom-call | tf_op jit(solution)/shard_map/acts/pallas_call | solution.py:705
  424.9 10.8 %fusion.112 = f32[1024,1600]{0,1:T(8,128)} fusion(bf16[1024,1600]{1,0:T(8,128)(2,1)} %bitcast.193, bf16[1600,1600]{1,0:T(8,128)(2,1)} %bitcast.157), kind=kOutput, calls=%fused_computation.179 | convolution fusion | flops 5242880000 | bytes 14950400 | tf_op jit(solution)/shard_map/dot_general | solution.py:306
  435.8 17.7 %convert_reduce_fusion = (f32[1600]{0:T(1024)S(1)}, bf16[1024,1600]{0,1:T(8,128)(2,1)S(1)}, bf16[1024,1600]{0,1:T(8,128)(2,1)}) fusion(f32[1024,1600]{0,1:T(8,128)} %fusion.112, f32[1600]{0:T(1024)S(1)} %dynamic_slice.69, bf16[1024,1600]{1,0:T(8,128)(2,1)} %bitcast.190, bf16[1600,1600]{1,0:T(8,128)(2,1)} %bitcast.155), kind=kOutput, calls=%fused_computation.17 | convolution fusion | flops 5290392064 | bytes 21516800 | tf_op jit(solution)/shard_map/dot_general | solution.py:306
  455.1 10.2 convolution_convert_fusion.3
  465.3 5.4 copy.28
  470.7 29.1 %quad_sum.2 = f32[256,1600]{1,0:T(8,128)} custom-call(bf16[2,2,256,1600]{3,2,1,0:T(8,128)(2,1)} %bitcast.148), custom_call_target="tpu_custom_call" | custom-call | bytes 90000000 | tf_op jit(solution)/shard_map/quad_sum/pallas_call | solution.py:822
  509.7 9.5 copy.37
  519.2 5.5 pad.24.clone
  526.0 16.2 %swap.3 = bf16[4,256,448]{2,1,0:T(8,128)(2,1)} custom-call(bf16[4,256,448]{2,1,0:T(8,128)(2,1)} %bitcast.161), custom_call_target="tpu_custom_call" | custom-call | bytes 60000000 | tf_op jit(solution)/shard_map/swap/pallas_call | solution.py:741
  542.3 58.5 %attend_back_before.1 = (f32[1024,448]{1,0:T(8,128)}, f32[1024,896]{1,0:T(8,128)}, f32[448,1600]{1,0:T(8,128)}) custom-call(bf16[1024,448]{1,0:T(8,128)(2,1)} %copy-done.2, bf16[1024,896]{1,0:T(8,128)(2,1)} %get-tuple-element.30.before_ref.refs_1_, bf16[1024,448]{1,0:T(8,128)(2,1)} %bitcast.151, f32[1024,448]{1,0:T(8,128)} %copy-done, f32[1024,8]{1,0:T(8,128)} %copy-done.3, ...), custom_call_target="tpu_custom_call" | custom-call | bytes 105000000 | tf_op jit(solution)/shard_map/attend_back_before/pallas_call | solution.py:1099
  606.9 7.7 convolution_convert_fusion.4
  618.4 11.4 %convolution_convert_fusion.2 = bf16[1024,1600]{0,1:T(8,128)(2,1)} fusion(bf16[1024,1600]{0,1:T(8,128)(2,1)} %get-tuple-element.73, bf16[1600,1600]{1,0:T(8,128)(2,1)} %bitcast.156), kind=kOutput, calls=%fused_computation.29 | convolution fusion | flops 5244518400 | bytes 11673600 | tf_op jit(solution)/shard_map/dot_general | solution.py:314
  634.3 5.4 copy.31
  639.7 43.1 %attend_back_own.1 = (bf16[1024,448]{1,0:T(8,128)(2,1)}, f32[1024,896]{1,0:T(8,128)}, f32[256,1600]{1,0:T(8,128)}) custom-call(bf16[1024,448]{1,0:T(8,128)(2,1)} %copy-done.2, bf16[1024,896]{1,0:T(8,128)(2,1)} %add_convert_fusion.1.kv_ref.refs_1_, bf16[1024,448]{1,0:T(8,128)(2,1)} %bitcast.152, f32[1024,448]{1,0:T(8,128)} %copy-done, f32[1024,8]{1,0:T(8,128)} %copy-done.3, ...), custom_call_target="tpu_custom_call" | custom-call | bytes 105000000 | tf_op jit(solution)/shard_map/attend_back_own/pallas_call | solution.py:1099
  692.9 5.3 collective-permute-done.6
  698.5 7.5 collective-permute-done.7
  710.0 7.5 convolution_convert_fusion.1
  719.0 5.4 copy.32
  724.4 29.3 %quad_sum.3 = f32[256,1600]{1,0:T(8,128)} custom-call(bf16[2,2,256,1600]{3,2,1,0:T(8,128)(2,1)} %bitcast.149), custom_call_target="tpu_custom_call" | custom-call | bytes 90000000 | tf_op jit(solution)/shard_map/quad_sum/pallas_call | solution.py:822
  753.6 6.8 convolution_convert_fusion.6
  767.6 7.0 convert_add_fusion
  788.2 24.9 %collective-permute-done.1 = bf16[672,1600]{1,0:T(8,128)(2,1)} collective-permute-done((bf16[672,1600]{1,0:T(8,128)(2,1)}, bf16[672,1600]{1,0:T(8,128)(2,1)}, u32[]{:S(2)}, u32[]{:S(2)}) %collective-permute-start.1) | collective-permute-done | bytes 2150432 | tf_op jit(solution)/shard_map/ppermute | solution.py:330
  821.7 14.9 %collective-permute-done.15 = bf16[200,1600]{1,0:T(8,128)(2,1)S(1)} collective-permute-done((bf16[200,1600]{1,0:T(8,128)(2,1)S(1)}, bf16[200,1600]{1,0:T(8,128)(2,1)S(1)}, u32[]{:S(2)}, u32[]{:S(2)}) %collective-permute-start.15) | collective-permute-done | bytes 640032 | tf_op jit(solution)/shard_map/ppermute | solution.py:330
  836.7 29.2 %collective-permute-start.3 = (bf16[168,1600]{1,0:T(8,128)(2,1)S(1)}, bf16[168,1600]{1,0:T(8,128)(2,1)S(1)}, u32[]{:S(2)}, u32[]{:S(2)}) collective-permute-start(bf16[168,1600]{1,0:T(8,128)(2,1)S(1)} %get-tuple-element.82), channel_id=1, source_target_pairs={{0,4},{1,5},{2,6},{3,7},{4,0},{5,1},{6,2},{7,3},{8,12},{9,13},{10,... | collective-permute-start | bytes 1612808 | tf_op jit(solution)/shard_map/ppermute | solution.py:330
  865.9 37.8 %collective-permute-start.4 = (bf16[168,1600]{1,0:T(8,128)(2,1)S(1)}, bf16[168,1600]{1,0:T(8,128)(2,1)S(1)}, u32[]{:S(2)}, u32[]{:S(2)}) collective-permute-start(bf16[168,1600]{1,0:T(8,128)(2,1)S(1)} %get-tuple-element.81), channel_id=1, source_target_pairs={{0,6},{1,7},{2,0},{3,1},{4,2},{5,3},{6,4},{7,5},{8,14},{9,15},{10,... | collective-permute-start | bytes 1612808 | tf_op jit(solution)/shard_map/ppermute | solution.py:330
  904.9 12.8 %collective-permute-done.11 = bf16[200,1600]{1,0:T(8,128)(2,1)S(1)} collective-permute-done((bf16[200,1600]{1,0:T(8,128)(2,1)S(1)}, bf16[200,1600]{1,0:T(8,128)(2,1)S(1)}, u32[]{:S(2)}, u32[]{:S(2)}) %collective-permute-start.11) | collective-permute-done | bytes 640032 | tf_op jit(solution)/shard_map/ppermute | solution.py:330
  918.9 22.8 %collective-permute-done.3 = bf16[168,1600]{1,0:T(8,128)(2,1)S(1)} collective-permute-done((bf16[168,1600]{1,0:T(8,128)(2,1)S(1)}, bf16[168,1600]{1,0:T(8,128)(2,1)S(1)}, u32[]{:S(2)}, u32[]{:S(2)}) %collective-permute-start.3) | collective-permute-done | bytes 537632 | tf_op jit(solution)/shard_map/ppermute | solution.py:330
  942.8 79.9 %collect.1 = (bf16[76,8,1600]{2,1,0:T(8,128)(2,1)}, f32[32,2,8,1600]{3,2,1,0:T(8,128)}) custom-call(bf16[21,8,1600]{2,1,0:T(8,128)(2,1)} %fusion.96.qkv_ref, bf16[7,8,1600]{2,1,0:T(8,128)(2,1)} %fusion.103.out_ref, bf16[25,8,1600]{2,1,0:T(8,128)(2,1)} %fusion.91.fc_ref, bf16[25,8,1600]{2,1,0:T(8,128)(2,1)} %fusion.92.proj_ref, ...), custom_call_target="tpu_custom_call" | custom-call | tf_op jit(solution)/shard_map/collect/pallas_call | solution.py:930
  (182 shorter events, 121.4 us)
Async XLA Ops:
  125.6 6.2 slice-start.3
  131.8 158.5 %copy-start.2 = (bf16[1024,448]{1,0:T(8,128)(2,1)}, bf16[1024,448]{1,0:T(8,128)(2,1)S(1)}, u32[]{:S(2)}) copy-start(bf16[1024,448]{1,0:T(8,128)(2,1)S(1)} %add_convert_fusion.2.q_ref.refs_0_) | copy-start | bytes 2752516
  316.6 20.6 %copy-start = (f32[1024,448]{1,0:T(8,128)}, f32[1024,448]{1,0:T(8,128)S(1)}, u32[]{:S(2)}) copy-start(f32[1024,448]{1,0:T(8,128)S(1)} %get-tuple-element.31.refs_3_) | copy-start | bytes 5505028
  316.6 20.6 %copy-start.23 = (f32[1600]{0:T(1024)S(1)}, f32[1600]{0:T(1024)}, u32[]{:S(2)}) copy-start(f32[1600]{0:T(1024)} %get-tuple-element.64) | copy-start | bytes 19204
  604.3 102.4 %collective-permute-start = (bf16[1024,896]{1,0:T(8,128)(2,1)}, bf16[1024,896]{1,0:T(8,128)(2,1)}, u32[]{:S(2)}, u32[]{:S(2)}) collective-permute-start(bf16[1024,896]{1,0:T(8,128)(2,1)} %convert_element_type.265), channel_id=1, source_target_pairs={{2,0},{3,1},{6,4},{7,5},{10,8},{11,9},{14,12},{15,13},{18,16},{19,... | collective-permute-start | bytes 5505032 | tf_op jit(solution)/shard_map/ppermute | solution.py:330
  614.6 153.0 %collective-permute-start.13 = (bf16[800,1600]{1,0:T(8,128)(2,1)}, bf16[800,1600]{1,0:T(8,128)(2,1)}, u32[]{:S(2)}, u32[]{:S(2)}) collective-permute-start(bf16[800,1600]{1,0:T(8,128)(2,1)} %convolution_convert_fusion.4), channel_id=1, source_target_pairs={{0,16},{1,17},{2,18},{3,19},{4,20},{5,21},{6,22},{7,23},{8,24},{9,... | collective-permute-start | bytes 7680008 | tf_op jit(solution)/shard_map/ppermute | solution.py:330
  617.2 12.6 %copy-start.24 = (bf16[2,2,256,1600]{3,2,1,0:T(8,128)(2,1)S(1)}, bf16[2,2,256,1600]{3,2,1,0:T(8,128)(2,1)}, u32[]{:S(2)}) copy-start(bf16[2,2,256,1600]{3,2,1,0:T(8,128)(2,1)} %get-tuple-element.34) | copy-start | bytes 9830404
  617.2 12.6 %copy-start.27 = (bf16[1024,1600]{0,1:T(8,128)(2,1)S(1)}, bf16[1024,1600]{0,1:T(8,128)(2,1)}, u32[]{:S(2)}) copy-start(bf16[1024,1600]{0,1:T(8,128)(2,1)} %copy-done.26) | copy-start | bytes 9830404
  617.2 72.0 %collective-permute-start.5 = (bf16[224,1600]{1,0:T(8,128)(2,1)}, bf16[224,1600]{1,0:T(8,128)(2,1)}, u32[]{:S(2)}, u32[]{:S(2)}) collective-permute-start(bf16[224,1600]{1,0:T(8,128)(2,1)} %fusion.82), channel_id=1, source_target_pairs={{0,16},{1,17},{2,18},{3,19},{4,20},{5,21},{6,22},{7,23},{8,24},{9,... | collective-permute-start | bytes 2150408 | tf_op jit(solution)/shard_map/ppermute | solution.py:330
  688.1 72.3 %copy-start.21 = (f32[256]{0:T(256)}, f32[256]{0:T(256)S(1)}, u32[]{:S(2)}) copy-start(f32[256]{0:T(256)S(1)} %broadcast_multiply_fusion.3) | copy-start | bytes 3076
  688.5 18.3 %copy-start.14 = (f32[1024,896]{1,0:T(8,128)S(1)}, f32[1024,896]{1,0:T(8,128)}, u32[]{:S(2)}) copy-start(f32[1024,896]{1,0:T(8,128)} %get-tuple-element.42) | copy-start | bytes 11010052
  689.2 20.8 %slice-start.5 = ((s8[4472832]{0:T(1024)(128)(4,1)}), s8[4194304]{0:T(1024)(128)(4,1)S(1)}, s32[]{:S(2)}) async-start(s8[4472832]{0:T(1024)(128)(4,1)} %bitcast.187), calls=%async_computation.5 | async-start | bytes 8388608
  691.4 6.8 collective-permute-start.6
  691.4 14.5 %collective-permute-start.7 = (bf16[56,1600]{1,0:T(8,128)(2,1)S(1)}, bf16[56,1600]{1,0:T(8,128)(2,1)S(1)}, u32[]{:S(2)}, u32[]{:S(2)}) collective-permute-start(bf16[56,1600]{1,0:T(8,128)(2,1)S(1)} %get-tuple-element.85), channel_id=1, source_target_pairs={{0,4},{1,5},{2,6},{3,7},{4,0},{5,1},{6,2},{7,3},{8,12},{9,13},{10,... | collective-permute-start | bytes 537608 | tf_op jit(solution)/shard_map/ppermute | solution.py:330
  691.5 14.5 %collective-permute-start.8 = (bf16[56,1600]{1,0:T(8,128)(2,1)S(1)}, bf16[56,1600]{1,0:T(8,128)(2,1)S(1)}, u32[]{:S(2)}, u32[]{:S(2)}) collective-permute-start(bf16[56,1600]{1,0:T(8,128)(2,1)S(1)} %get-tuple-element.84), channel_id=1, source_target_pairs={{0,6},{1,7},{2,0},{3,1},{4,2},{5,3},{6,4},{7,5},{8,14},{9,15},{10,... | collective-permute-start | bytes 537608 | tf_op jit(solution)/shard_map/ppermute | solution.py:330
  692.9 67.5 %copy-start.22 = (f32[256]{0:T(256)}, f32[256]{0:T(256)S(1)}, u32[]{:S(2)}) copy-start(f32[256]{0:T(256)S(1)} %add_rsqrt_fusion) | copy-start | bytes 3076
  698.2 82.5 %collective-permute-start.9 = (bf16[800,1600]{1,0:T(8,128)(2,1)}, bf16[800,1600]{1,0:T(8,128)(2,1)}, u32[]{:S(2)}, u32[]{:S(2)}) collective-permute-start(bf16[800,1600]{1,0:T(8,128)(2,1)} %convolution_convert_fusion.5), channel_id=1, source_target_pairs={{0,16},{1,17},{2,18},{3,19},{4,20},{5,21},{6,22},{7,23},{8,24},{9,... | collective-permute-start | bytes 7680008 | tf_op jit(solution)/shard_map/ppermute | solution.py:330
  753.6 6.8 copy-start.8
  762.4 50.7 %collective-permute-start.1 = (bf16[672,1600]{1,0:T(8,128)(2,1)}, bf16[672,1600]{1,0:T(8,128)(2,1)}, u32[]{:S(2)}, u32[]{:S(2)}) collective-permute-start(bf16[672,1600]{1,0:T(8,128)(2,1)} %convolution_convert_fusion.6), channel_id=1, source_target_pairs={{0,16},{1,17},{2,18},{3,19},{4,20},{5,21},{6,22},{7,23},{8,24},{9,... | collective-permute-start | bytes 6451208 | tf_op jit(solution)/shard_map/ppermute | solution.py:330
  767.6 13.1 %copy-start.28 = (bf16[1024,1600]{0,1:T(8,128)(2,1)S(1)}, bf16[1024,1600]{0,1:T(8,128)(2,1)}, u32[]{:S(2)}) copy-start(bf16[1024,1600]{0,1:T(8,128)(2,1)} %copy-done.26) | copy-start | bytes 9830404
  774.6 6.1 copy-start.25
  774.9 46.5 %collective-permute-start.14 = (bf16[200,1600]{1,0:T(8,128)(2,1)S(1)}, bf16[200,1600]{1,0:T(8,128)(2,1)S(1)}, u32[]{:S(2)}, u32[]{:S(2)}) collective-permute-start(bf16[200,1600]{1,0:T(8,128)(2,1)S(1)} %get-tuple-element.74), channel_id=1, source_target_pairs={{0,2},{1,3},{2,4},{3,5},{4,6},{5,7},{6,0},{7,1},{8,10},{9,11},{10,... | collective-permute-start | bytes 1920008 | tf_op jit(solution)/shard_map/ppermute | solution.py:330
  776.2 60.5 %collective-permute-start.15 = (bf16[200,1600]{1,0:T(8,128)(2,1)S(1)}, bf16[200,1600]{1,0:T(8,128)(2,1)S(1)}, u32[]{:S(2)}, u32[]{:S(2)}) collective-permute-start(bf16[200,1600]{1,0:T(8,128)(2,1)S(1)} %get-tuple-element.76), channel_id=1, source_target_pairs={{0,4},{1,5},{2,6},{3,7},{4,0},{5,1},{6,2},{7,3},{8,12},{9,13},{10,... | collective-permute-start | bytes 1920008 | tf_op jit(solution)/shard_map/ppermute | solution.py:330
  779.3 57.4 %collective-permute-start.16 = (bf16[200,1600]{1,0:T(8,128)(2,1)S(1)}, bf16[200,1600]{1,0:T(8,128)(2,1)S(1)}, u32[]{:S(2)}, u32[]{:S(2)}) collective-permute-start(bf16[200,1600]{1,0:T(8,128)(2,1)S(1)} %get-tuple-element.75), channel_id=1, source_target_pairs={{0,6},{1,7},{2,0},{3,1},{4,2},{5,3},{6,4},{7,5},{8,14},{9,15},{10,... | collective-permute-start | bytes 1920008 | tf_op jit(solution)/shard_map/ppermute | solution.py:330
  780.7 36.1 %copy-start.18 = (bf16[1024,448]{1,0:T(8,128)(2,1)S(1)}, bf16[1024,448]{1,0:T(8,128)(2,1)}, u32[]{:S(2)}) copy-start(bf16[1024,448]{1,0:T(8,128)(2,1)} %get-tuple-element.41) | copy-start | bytes 2752516
  785.7 31.1 %copy-start.16 = (bf16[1024,1600]{1,0:T(8,128)(2,1)S(1)}, bf16[1024,1600]{1,0:T(8,128)(2,1)}, u32[]{:S(2)}) copy-start(bf16[1024,1600]{1,0:T(8,128)(2,1)} %copy-done.15) | copy-start | bytes 9830404
  786.0 79.9 %collective-permute-start.10 = (bf16[200,1600]{1,0:T(8,128)(2,1)S(1)}, bf16[200,1600]{1,0:T(8,128)(2,1)S(1)}, u32[]{:S(2)}, u32[]{:S(2)}) collective-permute-start(bf16[200,1600]{1,0:T(8,128)(2,1)S(1)} %get-tuple-element.77), channel_id=1, source_target_pairs={{0,2},{1,3},{2,4},{3,5},{4,6},{5,7},{6,0},{7,1},{8,10},{9,11},{10,... | collective-permute-start | bytes 1920008 | tf_op jit(solution)/shard_map/ppermute | solution.py:330
  813.2 104.5 %collective-permute-start.11 = (bf16[200,1600]{1,0:T(8,128)(2,1)S(1)}, bf16[200,1600]{1,0:T(8,128)(2,1)S(1)}, u32[]{:S(2)}, u32[]{:S(2)}) collective-permute-start(bf16[200,1600]{1,0:T(8,128)(2,1)S(1)} %get-tuple-element.79), channel_id=1, source_target_pairs={{0,4},{1,5},{2,6},{3,7},{4,0},{5,1},{6,2},{7,3},{8,12},{9,13},{10,... | collective-permute-start | bytes 1920008 | tf_op jit(solution)/shard_map/ppermute | solution.py:330
  821.4 96.3 %collective-permute-start.12 = (bf16[200,1600]{1,0:T(8,128)(2,1)S(1)}, bf16[200,1600]{1,0:T(8,128)(2,1)S(1)}, u32[]{:S(2)}, u32[]{:S(2)}) collective-permute-start(bf16[200,1600]{1,0:T(8,128)(2,1)S(1)} %get-tuple-element.78), channel_id=1, source_target_pairs={{0,6},{1,7},{2,0},{3,1},{4,2},{5,3},{6,4},{7,5},{8,14},{9,15},{10,... | collective-permute-start | bytes 1920008 | tf_op jit(solution)/shard_map/ppermute | solution.py:330
  836.6 82.2 %collective-permute-start.2 = (bf16[168,1600]{1,0:T(8,128)(2,1)S(1)}, bf16[168,1600]{1,0:T(8,128)(2,1)S(1)}, u32[]{:S(2)}, u32[]{:S(2)}) collective-permute-start(bf16[168,1600]{1,0:T(8,128)(2,1)S(1)} %get-tuple-element.80), channel_id=1, source_target_pairs={{0,2},{1,3},{2,4},{3,5},{4,6},{5,7},{6,0},{7,1},{8,10},{9,11},{10,... | collective-permute-start | bytes 1612808 | tf_op jit(solution)/shard_map/ppermute | solution.py:330
  836.7 105.0 %collective-permute-start.3 = (bf16[168,1600]{1,0:T(8,128)(2,1)S(1)}, bf16[168,1600]{1,0:T(8,128)(2,1)S(1)}, u32[]{:S(2)}, u32[]{:S(2)}) collective-permute-start(bf16[168,1600]{1,0:T(8,128)(2,1)S(1)} %get-tuple-element.82), channel_id=1, source_target_pairs={{0,4},{1,5},{2,6},{3,7},{4,0},{5,1},{6,2},{7,3},{8,12},{9,13},{10,... | collective-permute-start | bytes 1612808 | tf_op jit(solution)/shard_map/ppermute | solution.py:330
  865.9 75.7 %collective-permute-start.4 = (bf16[168,1600]{1,0:T(8,128)(2,1)S(1)}, bf16[168,1600]{1,0:T(8,128)(2,1)S(1)}, u32[]{:S(2)}, u32[]{:S(2)}) collective-permute-start(bf16[168,1600]{1,0:T(8,128)(2,1)S(1)} %get-tuple-element.81), channel_id=1, source_target_pairs={{0,6},{1,7},{2,0},{3,1},{4,2},{5,3},{6,4},{7,5},{8,14},{9,15},{10,... | collective-permute-start | bytes 1612808 | tf_op jit(solution)/shard_map/ppermute | solution.py:330
  (21 other events, 66.0 us)
where the time goes:
time: 1040 us; the launch traced here: 1030 us
  Pallas kernels  644 us (62%)
  matrix products  114 us (11%)
  waiting for transfers between devices  88.9 us (9%)
  starting transfers between devices  84.7 us (8%)
  local copies, waits for them, and re-layouts  61.5 us (6%)
  other arithmetic  37.5 us (4%)
    pallas_call x1, Pallas kernels, keys_call(): pl.pallas_call(keys_kernel, out_shape=(like(kv), like(w_out), like(w_fc),...  153 us
    pallas_call x1, Pallas kernels, open_call(): pl.pallas_call(functools.partial(open_kernel, sz), out_shape=(like(8, sz....  114 us
    pallas_call x2, Pallas kernels, attend_back(): pl.pallas_call(functools.partial(attend_back_kernel, sz.quarter_heads, sz...  102 us
    ppermute x17, waiting for transfers between devices, permute(): return lax.ppermute(value, ('dp', 'cp'), pairs)  88.9 us
    ppermute x17, starting transfers between devices, permute(): return lax.ppermute(value, ('dp', 'cp'), pairs)  84.7 us
    pallas_call x1, Pallas kernels, acts_call(): pl.pallas_call(acts_kernel, out_shape=(jax.ShapeDtypeStruct((2, 2) + act....  81 us
    pallas_call x1, Pallas kernels, collect(): pl.pallas_call(functools.partial(collect_kernel, sz), out_shape=(jax.Shap...  79.9 us
    pallas_call x2, Pallas kernels, quad_sum(): pl.pallas_call(quad_sum_kernel, out_shape=jax.ShapeDtypeStruct(partial.sh...  58.3 us
  transfers between devices with their start and end apart: 17, of which 7 were waited for; matrix products, arithmetic and copies ran while one was open for 9% of the time, Pallas kernels for 7%

commit v1 on v0

--- a/solution.py
+++ b/solution.py
@@ -4,6 +4,7 @@
 import jax.numpy as jnp
 from jax import lax
 from jax.experimental import pallas as pl
+from jax.experimental.layout import Layout, with_layout_constraint
 from jax.experimental.pallas import tpu as pltpu
 from jax.sharding import PartitionSpec as P
 
@@ -401,12 +402,21 @@
         self.started.append(copy)
         return copy
 
-    def start(self):
+    def partners(self):
+        along = [(self.dp, ((self.z + d) % 4) * 2 + self.x) for d in (1, 2, 3)]
+        return along + [((self.dp + 2) % 4, self.cp)]
+
+    def start_over(self):
+        self.over = [self.send(self.y * 4 + self.z, (self.dp + 2) % 4, self.cp)]
+
+    def start(self, over=True):
         mine = self.y * 4 + self.z
         self.along = []
         for d in (1, 3, 2):
             self.along.append((d, self.send(mine, self.dp, ((self.z + d) % 4) * 2 + self.x)))
-        self.over = [self.send(mine, (self.dp + 2) % 4, self.cp)]
+        self.over = []
+        if over:
+            self.start_over()
 
     def forward(self):
         for d, copy in self.along:
@@ -640,61 +650,158 @@
     )(table, tokens, cotangent)
 
 
-def keys_kernel(kv_ref, out_in, fc_in, before_ref, out_ref, fc_ref, out_all, send_sems, recv_sems, local_sem):
-    _, _, z, _ = my_place()
+def forward_kernel(
+    heads, size, q_ref, kv_ref, out_in, fc_in, proj_in,
+    mix_ref, lse_ref, before_ref, mixed_ref, out_ref, fc_ref, proj_ref, out_all,
+    stage, send_sems, recv_sems, local_sems,
+):
+    y, c, z, x = my_place()
     dp, cp = lax.axis_index("dp"), lax.axis_index("cp")
     wires = Wires(send_sems, recv_sems)
+    part = heads * size
+    rows = q_ref.shape[0] // 2
+    blk = 128
+    scale = size**-0.5
+    odd = z % 2 == 1
+    w_out, w_fc, w_proj = [PlaceGather(wires, ref) for ref in (out_ref, fc_ref, proj_ref)]
+    others = [(c, 1 - x), (1 - c, x), (1 - c, 1 - x)]
+    quad = [(y * 2 + tc, z * 2 + tx) for tc, tx in others]
+    greet(w_out.partners() + quad)
     keys = wires.to(kv_ref, before_ref, dp, (cp + 2) % 8)
 
-    @pl.when(z % 2 == 0)
+    @pl.when(jnp.logical_not(odd))
     def _():
         keys.start()
 
-    first = PlaceGather(wires, out_ref)
-    second = PlaceGather(wires, fc_ref)
-    first.start()
-    second.start()
-    first.forward()
-    first.finish()
-    quad = QuadGather(wires, out_ref, out_all, local_sem)
-    quad.start()
-
-    @pl.when(z % 2 == 1)
+    w_out.start()
+    w_fc.start()
+
+    def own(group, _):
+        start = group * rows
+        for i in range(rows // blk):
+            here = pl.ds(pl.multiple_of(start + i * blk, blk), blk)
+            seen = (i + 1) * blk
+            keys_at = pl.ds(pl.multiple_of(start, rows), seen)
+            lane = lax.broadcasted_iota(jnp.int32, (blk, seen), 1)
+            line = lax.broadcasted_iota(jnp.int32, (blk, seen), 0)
+            allowed = lane <= line + i * blk
+            for h in range(heads):
+                cols = slice(h * size, (h + 1) * size)
+                vals = slice(part + h * size, part + (h + 1) * size)
+                s = dot_nt(q_ref[here, cols], kv_ref[keys_at, cols]) * scale
+                s = jnp.where(allowed, s, MASKED)
+                top = jnp.max(s, axis=-1, keepdims=True)
+                p = jnp.exp(s - top)
+                total = jnp.sum(p, axis=-1, keepdims=True)
+                mix_ref[here, cols] = dot_nn(p.astype(jnp.bfloat16), kv_ref[keys_at, vals]) / total
+                lse_ref[here, h : h + 1] = top + jnp.log(total)
+        return 0
+
+    lax.fori_loop(0, 2, own, 0)
+    w_out.forward()
+
+    def add_before(index, _):
+        here = pl.ds(pl.multiple_of(index * blk, blk), blk)
+        keys_at = pl.ds(pl.multiple_of((index * blk) // rows * rows, rows), rows)
+        for h in range(heads):
+            cols = slice(h * size, (h + 1) * size)
+            vals = slice(part + h * size, part + (h + 1) * size)
+            s = dot_nt(q_ref[here, cols], before_ref[keys_at, cols]) * scale
+            lse = lse_ref[here, h : h + 1]
+            top = jnp.maximum(lse, jnp.max(s, axis=-1, keepdims=True))
+            p = jnp.exp(s - top)
+            kept = jnp.exp(lse - top)
+            total = kept + jnp.sum(p, axis=-1, keepdims=True)
+            mix = mix_ref[here, cols] * kept + dot_nn(p.astype(jnp.bfloat16), before_ref[keys_at, vals])
+            mix_ref[here, cols] = mix / total
+            lse_ref[here, h : h + 1] = top + jnp.log(total)
+        return 0
+
+    w_out.finish()
+    whole = QuadGather(wires, out_ref, out_all, local_sems.at[0])
+    whole.start()
+
+    @pl.when(odd)
     def _():
         keys.wait_recv()
-
-    second.forward()
-    quad.forward()
-    second.finish()
-    quad.finish()
-
-    @pl.when(z % 2 == 0)
+        lax.fori_loop(0, 2 * rows // blk, add_before, 0)
+
+    def round_off(index, _):
+        here = pl.ds(pl.multiple_of(index * blk, blk), blk)
+        stage[here, :] = mix_ref[here, :].astype(stage.dtype)
+        return 0
+
+    lax.fori_loop(0, 2 * rows // blk, round_off, 0)
+    w_proj.start_over()
+    mine = c * 2 + x
+    each = rows // 2
+    swaps = []
+    for (tc, tx), (tdp, tcp) in zip(others, quad):
+        block = stage.at[pl.ds(pl.multiple_of((tc * 2 + tx) * each, each), each)]
+        swaps.append(wires.to(block, mixed_ref.at[mine], tdp, tcp))
+    for copy in swaps:
+        copy.start()
+    local = pltpu.make_async_copy(
+        stage.at[pl.ds(pl.multiple_of(mine * each, each), each)], mixed_ref.at[mine], local_sems.at[1]
+    )
+    local.start()
+    w_fc.forward()
+    whole.forward()
+    for copy in swaps:
+        copy.wait_recv()
+    whole.finish()
+    w_fc.finish()
+    w_proj.over[0].wait_recv()
+    w_proj.over[0].wait_send()
+    for copy in swaps:
+        copy.wait_send()
+    local.wait()
+
+    @pl.when(jnp.logical_not(odd))
     def _():
         keys.wait_send()
 
 
-def keys_call(kv, w_out, w_fc):
+def forward_call(sz, q, kv, w_out, w_fc, w_proj):
+    part = sz.part
+    rows = q.shape[0]
+
     def like(value, *lead):
         return jax.ShapeDtypeStruct(lead + value.shape, value.dtype)
 
     return pl.pallas_call(
-        keys_kernel,
-        out_shape=(like(kv), like(w_out), like(w_fc), like(w_out, 2, 2)),
-        in_specs=[HBM] * 3,
-        out_specs=[HBM] * 4,
-        input_output_aliases={1: 1, 2: 2},
-        scratch_shapes=[*wire_sems(18), pltpu.SemaphoreType.DMA],
-        compiler_params=REMOTE,
-        name="keys",
-    )(kv, w_out, w_fc)
+        functools.partial(forward_kernel, sz.quarter_heads, sz.head_size),
+        out_shape=(
+            jax.ShapeDtypeStruct((rows, part), jnp.float32),
+            jax.ShapeDtypeStruct((rows, 8), jnp.float32),
+            like(kv),
+            jax.ShapeDtypeStruct((4, rows // 4, part), jnp.bfloat16),
+            like(w_out),
+            like(w_fc),
+            like(w_proj),
+            like(w_out, 2, 2),
+        ),
+        in_specs=[VMEM, VMEM, HBM, HBM, HBM],
+        out_specs=[VMEM] * 4 + [HBM] * 4,
+        input_output_aliases={2: 4, 3: 5, 4: 6},
+        scratch_shapes=[
+            pltpu.VMEM((rows, part), jnp.bfloat16),
+            *wire_sems(22),
+            pltpu.SemaphoreType.DMA((2,)),
+        ],
+        cost_estimate=cost(120),
+        compiler_params=remote_params(1, 56 << 20),
+        name="forward",
+    )(q, kv, w_out, w_fc, w_proj)
 
 
 def acts_kernel(act_ref, proj_in, act_all, proj_ref, send_sems, recv_sems, local_sem):
     wires = Wires(send_sems, recv_sems)
     quad = QuadGather(wires, act_ref, act_all, local_sem)
     places = PlaceGather(wires, proj_ref)
+    greet(places.partners() + [quad.over_x, quad.over_c])
     quad.start()
-    places.start()
+    places.start(False)
     quad.forward()
     places.forward()
     quad.finish()
@@ -711,8 +818,9 @@
         in_specs=[VMEM, HBM],
         out_specs=[HBM] * 2,
         input_output_aliases={1: 1},
-        scratch_shapes=[*wire_sems(10), pltpu.SemaphoreType.DMA],
-        compiler_params=REMOTE,
+        scratch_shapes=[*wire_sems(9), pltpu.SemaphoreType.DMA],
+        cost_estimate=cost(60),
+        compiler_params=remote_params(2),
         name="acts",
     )(act, w_proj)
 
@@ -945,83 +1053,6 @@
     )(qkv, out, fc, proj, vectors)
 
 
-def attend_kernel(heads, size, odd_ref, q_ref, kv_ref, before_ref, mix_ref, lse_ref):
-    part = heads * size
-    rows = q_ref.shape[0]
-    blk = 128
-    scale = size**-0.5
-    lane = lax.broadcasted_iota(jnp.int32, (blk, rows), 1)
-    line = lax.broadcasted_iota(jnp.int32, (blk, rows), 0)
-
-    def block(index, _):
-        first = pl.multiple_of(index * blk, blk)
-        allowed = lane <= line + first
-
-        def one(with_before):
-            for h in range(heads):
-                cols = slice(h * size, (h + 1) * size)
-                vals = slice(part + h * size, part + (h + 1) * size)
-                q = q_ref[pl.ds(first, blk), cols]
-                s = dot_nt(q, kv_ref[:, cols]) * scale
-                s = jnp.where(allowed, s, MASKED)
-                top = jnp.max(s, axis=-1, keepdims=True)
-                if with_before:
-                    s_b = dot_nt(q, before_ref[:, cols]) * scale
-                    top = jnp.maximum(top, jnp.max(s_b, axis=-1, keepdims=True))
-                    p_b = jnp.exp(s_b - top)
-                p = jnp.exp(s - top)
-                total = jnp.sum(p, axis=-1, keepdims=True)
-                mix = dot_nn(p.astype(jnp.bfloat16), kv_ref[:, vals])
-                if with_before:
-                    total = total + jnp.sum(p_b, axis=-1, keepdims=True)
-                    mix = mix + dot_nn(p_b.astype(jnp.bfloat16), before_ref[:, vals])
-                mix_ref[pl.ds(first, blk), cols] = mix / total
-                lse_ref[pl.ds(first, blk), h : h + 1] = top + jnp.log(total)
-
-        @pl.when(odd_ref[0] == 1)
-        def _():
-            one(True)
-
-        @pl.when(odd_ref[0] == 0)
-        def _():
-            one(False)
-
-        return 0
-
-    lax.fori_loop(0, rows // blk, block, 0)
-
-
-def attend(sz, odd, q, kv, before):
-    rows = q.shape[0] // 2
-    return pl.pallas_call(
-        functools.partial(attend_kernel, sz.quarter_heads, sz.head_size),
-        grid_spec=pltpu.PrefetchScalarGridSpec(
-            num_scalar_prefetch=1,
-            grid=(2,),
-            in_specs=[
-                pl.BlockSpec((rows, sz.part), lambda g, odd: (g, 0)),
-                pl.BlockSpec((rows, 2 * sz.part), lambda g, odd: (g, 0)),
-                pl.BlockSpec((rows, 2 * sz.part), lambda g, odd: (g, 0)),
-            ],
-            out_specs=[
-                pl.BlockSpec((rows, sz.part), lambda g, odd: (g, 0)),
-                pl.BlockSpec((rows, 8), lambda g, odd: (g, 0)),
-            ],
-        ),
-        out_shape=(
-            jax.ShapeDtypeStruct((2 * rows, sz.part), jnp.float32),
-            jax.ShapeDtypeStruct((2 * rows, 8), jnp.float32),
-        ),
-        cost_estimate=pl.CostEstimate(
-            flops=2 * 2 * 2 * rows * 2 * rows * sz.part,
-            bytes_accessed=20 * rows * sz.part,
-            transcendentals=4 * rows * rows * sz.quarter_heads,
-        ),
-        compiler_params=pltpu.CompilerParams(vmem_limit_bytes=40 << 20),
-        name="attend",
-    )(odd, q, kv, before)
-
-
 def attend_back_kernel(heads, size, own, *refs):
     if own:
         q_ref, kv_ref, do_ref, mix_ref, lse_ref, seed_ref, term_ref, dq_ref, dkv_ref, sum_ref = refs[:10]
@@ -1034,64 +1065,71 @@
     rows = q_ref.shape[0] // 2
     blk = 128
     scale = size**-0.5
-    lane = lax.broadcasted_iota(jnp.int32, (blk, rows), 1)
-    line = lax.broadcasted_iota(jnp.int32, (blk, rows), 0)
-
-    def group(start):
-        keys_at = slice(start, start + rows)
-
-        def block(index, _):
-            first = pl.multiple_of(index * blk, blk)
-            here = pl.ds(pl.multiple_of(start + first, blk), blk)
+
+    def visit(here, start, seen, allowed):
+        keys_at = pl.ds(start, seen)
+        for h in range(heads):
+            cols = slice(h * size, (h + 1) * size)
+            vals = slice(part + h * size, part + (h + 1) * size)
+            q = q_ref[here, cols]
+            k = kv_ref[keys_at, cols]
+            do = do_ref[here, cols]
+            s = dot_nt(q, k) * scale
+            p = jnp.exp(s - lse_ref[here, h : h + 1])
             if own:
-                allowed = lane <= line + first
-            for h in range(heads):
-                cols = slice(h * size, (h + 1) * size)
-                vals = slice(part + h * size, part + (h + 1) * size)
-                q = q_ref[here, cols]
-                k = kv_ref[keys_at, cols]
-                do = do_ref[here, cols]
-                s = dot_nt(q, k) * scale
-                p = jnp.exp(s - lse_ref[here, h : h + 1])
-                if own:
-                    p = jnp.where(allowed, p, 0.0)
-                dp = dot_nt(do, kv_ref[keys_at, vals])
-                delta = jnp.sum(do.astype(jnp.float32) * mix_ref[here, cols], axis=-1, keepdims=True)
-                ds = (p * (dp - delta)).astype(jnp.bfloat16)
-                dq = dot_nn(ds, k) * scale
-                if own:
-                    dq = dq + seed_ref[here, cols]
-                dq_ref[here, cols] = dq.astype(dq_ref.dtype)
-                dkv_ref[keys_at, cols] += dot_tn(ds, q) * scale
-                dkv_ref[keys_at, vals] += dot_tn(p.astype(jnp.bfloat16), do)
-            return 0
-
-        lax.fori_loop(0, rows // blk, block, 0)
-
-    dkv_ref[...] = jnp.zeros_like(dkv_ref)
-    if own:
-        group(0)
-        quad.middle()
-        group(rows)
-        quad.finish()
-    else:
-        odd = z % 2 == 1
-
-        @pl.when(odd)
+                p = jnp.where(allowed, p, 0.0)
+            dp = dot_nt(do, kv_ref[keys_at, vals])
+            delta = jnp.sum(do.astype(jnp.float32) * mix_ref[here, cols], axis=-1, keepdims=True)
+            ds = (p * (dp - delta)).astype(jnp.bfloat16)
+            dq = dot_nn(ds, k) * scale
+            if own:
+                dq = dq + seed_ref[here, cols]
+            dq_ref[here, cols] = dq.astype(dq_ref.dtype)
+            dkv_ref[keys_at, cols] += dot_tn(ds, q) * scale
+            dkv_ref[keys_at, vals] += dot_tn(p.astype(jnp.bfloat16), do)
+
+    def group(index):
+        start = pl.multiple_of(index * rows, rows)
+        if not own:
+
+            def block(i, _):
+                visit(pl.ds(pl.multiple_of(start + i * blk, blk), blk), start, rows, None)
+                return 0
+
+            lax.fori_loop(0, rows // blk, block, 0)
+            return
+        for i in range(rows // blk):
+            seen = (i + 1) * blk
+            lane = lax.broadcasted_iota(jnp.int32, (blk, seen), 1)
+            line = lax.broadcasted_iota(jnp.int32, (blk, seen), 0)
+            visit(pl.ds(pl.multiple_of(start + i * blk, blk), blk), start, seen, lane <= line + i * blk)
+
+    def clear(index, _):
+        here = pl.ds(pl.multiple_of(index * blk, blk), blk)
+        dkv_ref[here, :] = jnp.zeros((blk, dkv_ref.shape[1]), dkv_ref.dtype)
+        if not own:
+            dq_ref[here, :] = jnp.zeros((blk, dq_ref.shape[1]), dq_ref.dtype)
+        return 0
+
+    lax.fori_loop(0, 2 * rows // blk, clear, 0)
+
+    def one(index, _):
+        if own:
+            group(index)
+        else:
+
+            @pl.when(z % 2 == 1)
+            def _():
+                group(index)
+
+        @pl.when(index == 0)
         def _():
-            group(0)
-
-        quad.middle()
-
-        @pl.when(odd)
-        def _():
-            group(rows)
-
-        @pl.when(jnp.logical_not(odd))
-        def _():
-            dq_ref[...] = jnp.zeros_like(dq_ref)
-
-        quad.finish()
+            quad.middle()
+
+        return 0
+
+    lax.fori_loop(0, 2, one, 0)
+    quad.finish()
 
 
 def attend_back(sz, own, q, kv, grad_mix, mix, lse, seed, term, ident):
@@ -1112,6 +1150,10 @@
     )(*operands)
 
 
+def rowwise(value):
+    return with_layout_constraint(value, Layout(major_to_minor=(0, 1)))
+
+
 def norm_parts(values):
     mean = jnp.mean(values, axis=-1, keepdims=True)
     centre = values - mean
@@ -1173,11 +1215,8 @@
     kv_bias = jnp.concatenate([jnp.zeros((sz.part,), f32), quarter_of(vectors[3])])
     kv = (dot_nt(act_one, w_qkv[sz.part :]) + kv_bias).astype(bf16)
     q = (dot_nt(act_one, w_qkv[: sz.part]) + quarter_of(vectors[2])).astype(bf16)
-    before, _, w_fc, w_out = keys_call(kv, w_out, w_fc)
+    mix, lse, before, mixed, _, w_fc, w_proj, w_out = forward_call(sz, q, kv, w_out, w_fc, w_proj)
     w_fc, w_out = flat(w_fc), flat(w_out)[:width]
-    odd = (z % 2).astype(jnp.int32).reshape(1)
-    mix, lse = attend(sz, odd, q, kv, before)
-    mixed = swap_call(mix.astype(bf16).reshape(4, rows, sz.part), 1)
     mixed = jnp.transpose(mixed, (1, 0, 2)).reshape(rows, 4 * sz.part)[:, :width]
     inputs = tokens.astype(f32)
     residual = inputs + (dot_nt(mixed, w_out) + vectors[4])
@@ -1193,7 +1232,7 @@
     grad_fc = pull_gelu(dot_nt(cot_all, w_proj))[0].astype(bf16)
     fc_mine, fc_other = halves_of(grad_fc)
     got_fc = to_other_y(dot_tn(fc_other, act_two))
-    grad_two = quad_sum(dot_nn(grad_fc, w_fc).astype(bf16).reshape(2, 2, rows, width), 2)
+    grad_two = quad_sum(rowwise(dot_nn(grad_fc, w_fc).astype(bf16)).reshape(2, 2, rows, width), 7)
 
     cot = out_grad.astype(f32)
     grad_res = cot + norm_back(normed_two, rs_two, grad_two, vectors[5])
@@ -1203,23 +1242,25 @@
     grad_mix = jnp.transpose(grad_mix.reshape(rows, 4, sz.part), (1, 0, 2))
     grad_mix = swap_call(grad_mix, 3).reshape(4 * rows, sz.part)
     g_proj = to_places(dot_tn(hid_mine, cot_all), got_proj)
-    g_out = jnp.pad(dot_tn(grad_attn, mixed).astype(bf16), ((0, 4 * sz.part - width), (0, 0)))
-    dq_before, dkv_before, g_out = attend_back(
-        sz, False, q, before, grad_mix, mix, lse, None, g_out.reshape(2, 2, sz.part, width), 4
-    )
+    partial_out = rowwise(dot_nn(act_hidden, w_proj).astype(bf16)).reshape(2, 2, rows, width)
+    dq_before, dkv_before, out_sum = attend_back(
+        sz, False, q, before, grad_mix, mix, lse, None, partial_out, 4
+    )
+    output = (residual + out_sum + vectors[7]).astype(bf16)
     returned = permute(
         dkv_before.astype(bf16), lambda py, pc, pz, px: (py, pc, pz - 1, px) if pz % 2 == 1 else None
     )
     g_fc = to_places(dot_tn(fc_mine, act_two), got_fc)
+    g_out = rowwise(dot_tn(jnp.pad(grad_attn, ((0, 0), (0, 4 * sz.part - width))), mixed).astype(bf16))
+    dq, dkv, g_out = attend_back(
+        sz, True, q, kv, grad_mix, mix, lse, dq_before, g_out.reshape(2, 2, sz.part, width), 5
+    )
     g_out = g_out.reshape(2, sz.part // 2, width)
     got_out = to_other_y(pick(g_out, 1 - y))
-    partial_out = dot_nn(act_hidden, w_proj).astype(bf16).reshape(2, 2, rows, width)
-    dq, dkv, out_sum = attend_back(sz, True, q, kv, grad_mix, mix, lse, dq_before, partial_out, 5)
-    output = (residual + out_sum + vectors[7]).astype(bf16)
     grad_qkv = jnp.concatenate([dq, (dkv + returned.astype(f32)).astype(bf16)], axis=1)
     qkv_mine, qkv_other = halves_of(grad_qkv)
     got_qkv = to_other_y(dot_tn(qkv_other, act_one))
-    grad_one = quad_sum(dot_nn(grad_qkv, w_qkv).astype(bf16).reshape(2, 2, rows, width), 6)
+    grad_one = quad_sum(rowwise(dot_nn(grad_qkv, w_qkv).astype(bf16)).reshape(2, 2, rows, width), 6)
     g_out = to_places(pick(g_out, y), got_out)
     g_qkv = to_places(dot_tn(qkv_mine, act_one), got_qkv)
 

time: 1040 us -> 1000 us (0.962)
  local copies, waits for them, and re-layouts: 61.5 us -> 17 us
    pallas_call x2 -> x1, Pallas kernels: 33.3 us -> 16.6 us  [swap_call(): pl.pallas_call(swap_kernel, out_shape=jax.ShapeDtypeStruct(value.shape, v...]
    unnamed x77 -> x58, local copies, waits for them, and re-layouts: 24 us -> 7.42 us
    convert_element_type x3 -> x0, local copies, waits for them, and re-layouts: 16.2 us -> none  [the longest x1 5.4 us: per_device_quad(): dot_nn(grad_fc, w_fc).astype(bf16).reshape(2, 2, rows, width)]
    pallas_call x2 -> x1, Pallas kernels: 176 us -> 189 us  [forward_call(): pl.pallas_call(functools.partial(forward_kernel, sz.quarter_heads, sz.hea...]
    pallas_call x1, Pallas kernels: 81 us -> 70.5 us  [acts_call(): pl.pallas_call(acts_kernel, out_shape=(jax.ShapeDtypeStruct((2, 2) + act....]
  transfers between devices with their start and end apart: 17 -> 17, of which waited for: 7 -> 7; matrix products, arithmetic and copies ran while one was open for 9% -> 7% of each run, Pallas kernels for 7% -> 9%
where the time goes in v1:
time: 1000 us; the launch traced here: 994 us
  Pallas kernels  635 us (64%)
  matrix products  123 us (12%)
  waiting for transfers between devices  93.3 us (9%)
  starting transfers between devices  87.5 us (9%)
  other arithmetic  37.1 us (4%)
  local copies, waits for them, and re-layouts  17 us (2%)
    pallas_call x1, Pallas kernels, forward_call(): pl.pallas_call(functools.partial(forward_kernel, sz.quarter_heads, sz.hea...  189 us
    pallas_call x1, Pallas kernels, open_call(): pl.pallas_call(functools.partial(open_kernel, sz), out_shape=(like(8, sz....  114 us
    pallas_call x2, Pallas kernels, attend_back(): pl.pallas_call(functools.partial(attend_back_kernel, sz.quarter_heads, sz...  100 us
    ppermute x17, waiting for transfers between devices, permute(): return lax.ppermute(value, ('dp', 'cp'), pairs)  93.3 us
    ppermute x17, starting transfers between devices, permute(): return lax.ppermute(value, ('dp', 'cp'), pairs)  87.5 us
    pallas_call x1, Pallas kernels, collect(): pl.pallas_call(functools.partial(collect_kernel, sz), out_shape=(jax.Shap...  79.2 us
    pallas_call x1, Pallas kernels, acts_call(): pl.pallas_call(acts_kernel, out_shape=(jax.ShapeDtypeStruct((2, 2) + act....  70.5 us
    pallas_call x2, Pallas kernels, quad_sum(): pl.pallas_call(quad_sum_kernel, out_shape=jax.ShapeDtypeStruct(partial.sh...  65.2 us
  transfers between devices with their start and end apart: 17, of which 7 were waited for; matrix products, arithmetic and copies ran while one was open for 7% of the time, Pallas kernels for 9%

profile of v1, /device:TPU:27, one launch (start us, length us, event | category | flops | bytes accessed | tf_op | source)
XLA Modules:
  0.0 994.0 jit_solution(4480707788626089724)
XLA Ops:
  5.0 114.3 %open.1 = (bf16[8,21,8,1600]{3,2,1,0:T(8,128)(2,1)}, bf16[8,7,8,1600]{3,2,1,0:T(8,128)(2,1)}, bf16[8,25,8,1600]{3,2,1,0:T(8,128)(2,1)}, bf16[8,25,8,1600]{3,2,1,...) custom-call(bf16[76,8,1600]{2,1,0:T(8,128)(2,1)} %bitcast.166, ...), custom_call_target="tpu_custom_call" | custom-call | tf_op jit(solution)/shard_map/open/pallas_call | solution.py:629
  126.3 8.1 add_convert_fusion.1.kv_ref.refs_1_
  134.5 4.5 add_convert_fusion.2.q_ref.refs_0_
  138.9 188.5 %forward.1 = (f32[1024,448]{1,0:T(8,128)}, f32[1024,8]{1,0:T(8,128)}, bf16[1024,896]{1,0:T(8,128)(2,1)}, bf16[4,256,448]{2,1,0:T(8,128)(2,1)}, bf16[8,7,8,1600]{...) custom-call(bf16[1024,448]{1,0:T(8,128)(2,1)} %add_convert_fusion.2., ...), custom_call_target="tpu_custom_call", output_to_operand_aliasing={{4}: (2, {}), {5}: (3, {}), {6}: (4, {})} | custom-call | bytes 360000000 | tf_op jit(solution)/shard_map/forward/pallas_call | solution.py:772
  329.0 4.8 fusion.111
  335.6 70.5 %acts.1 = (bf16[2,2,256,1600]{3,2,1,0:T(8,128)(2,1)}, bf16[8,25,8,1600]{3,2,1,0:T(8,128)(2,1)}) custom-call(bf16[256,1600]{1,0:T(8,128)(2,1)} %add_convert_fusion.4.act_ref, bf16[8,25,8,1600]{3,2,1,0:T(8,128)(2,1)} %get-tuple-element.36.proj_in), custom_call_target="tpu_custom_call", output_to_operand_aliasing={{1}: (1, {})} | custom-call | bytes 180000000 | tf_op jit(solution)/shard_map/acts/pallas_call | solution.py:812
  406.1 10.8 %fusion.112 = f32[1024,1600]{0,1:T(8,128)} fusion(bf16[1024,1600]{1,0:T(8,128)(2,1)} %bitcast.189, bf16[1600,1600]{1,0:T(8,128)(2,1)} %bitcast.151), kind=kOutput, calls=%fused_computation.179 | convolution fusion | flops 5242880000 | bytes 14950400 | tf_op jit(solution)/shard_map/dot_general | solution.py:307
  417.0 17.7 %convert_reduce_fusion = (f32[1600]{0:T(1024)S(1)}, bf16[1024,1600]{0,1:T(8,128)(2,1)S(1)}, bf16[1024,1600]{0,1:T(8,128)(2,1)}) fusion(f32[1024,1600]{0,1:T(8,128)} %fusion.112, f32[1600]{0:T(1024)S(1)} %dynamic_slice.69, bf16[1024,1600]{1,0:T(8,128)(2,1)} %bitcast.186, bf16[1600,1600]{1,0:T(8,128)(2,1)} %bitcast.147), kind=kOutput, calls=%fused_computation.17 | convolution fusion | flops 5290392064 | bytes 21516800 | tf_op jit(solution)/shard_map/dot_general | solution.py:307
  434.7 12.0 %convolution_convert_fusion.3 = bf16[1024,1600]{1,0:T(8,128)(2,1)} fusion(bf16[1024,1600]{0,1:T(8,128)(2,1)S(1)} %get-tuple-element.74, bf16[1600,1600]{1,0:T(8,128)(2,1)} %bitcast.152), kind=kOutput, calls=%fused_computation.30 | convolution fusion | flops 5244518400 | bytes 11673600 | tf_op jit(solution)/shard_map/dot_general | solution.py:315
  446.7 36.2 %quad_sum.2 = f32[256,1600]{1,0:T(8,128)} custom-call(bf16[2,2,256,1600]{3,2,1,0:T(8,128)(2,1)} %bitcast.158), custom_call_target="tpu_custom_call" | custom-call | bytes 90000000 | tf_op jit(solution)/shard_map/quad_sum/pallas_call | solution.py:930
  485.2 11.4 %convolution_convert_fusion.2 = bf16[1024,1600]{1,0:T(8,128)(2,1)} fusion(bf16[1024,1600]{0,1:T(8,128)(2,1)} %get-tuple-element.78, bf16[1600,1600]{1,0:T(8,128)(2,1)} %bitcast.148), kind=kOutput, calls=%fused_computation.29 | convolution fusion | flops 5244518400 | bytes 11673600 | tf_op jit(solution)/shard_map/dot_general | solution.py:315
  502.6 16.6 %swap.1 = bf16[4,256,448]{2,1,0:T(8,128)(2,1)} custom-call(bf16[4,256,448]{2,1,0:T(8,128)(2,1)} %bitcast.153), custom_call_target="tpu_custom_call" | custom-call | bytes 60000000 | tf_op jit(solution)/shard_map/swap/pallas_call | solution.py:849
  519.3 42.5 %attend_back_before.1 = (f32[1024,448]{1,0:T(8,128)}, f32[1024,896]{1,0:T(8,128)}, f32[256,1600]{1,0:T(8,128)}) custom-call(bf16[1024,448]{1,0:T(8,128)(2,1)} %add_convert_fusion.2.q_ref.refs_0_, bf16[1024,896]{1,0:T(8,128)(2,1)} %get-tuple-element.35.refs_1_, bf16[1024,448]{1,0:T(8,128)(2,1)} %bitcast.149, f32[1024,448]{1,0:T(8,128)} %get-tuple-element.41.refs_3_, ...), custom_call_target="tpu_custom_call" | custom-call | bytes 105000000 | tf_op jit(solution)/shard_map/attend_back_before/pallas_call | solution.py:1137
  567.8 7.7 convolution_convert_fusion.4
  580.0 57.6 %attend_back_own.1 = (bf16[1024,448]{1,0:T(8,128)(2,1)}, f32[1024,896]{1,0:T(8,128)}, f32[448,1600]{1,0:T(8,128)}) custom-call(bf16[1024,448]{1,0:T(8,128)(2,1)} %add_convert_fusion.2.q_ref.refs_0_, bf16[1024,896]{1,0:T(8,128)(2,1)} %add_convert_fusion.1.kv_ref.refs_1_, bf16[1024,448]{1,0:T(8,128)(2,1)} %bitcast.150, f32[1024,448]{1,0:T(8,128)} %get-tuple-element.41.refs_3_, ...), custom_call_target="tpu_custom_call" | custom-call | bytes 105000000 | tf_op jit(solution)/shard_map/attend_back_own/pallas_call | solution.py:1137
  641.6 7.6 convolution_convert_fusion.5
  651.5 6.1 collective-permute-done.5
  661.1 5.1 collective-permute-done.6
  667.2 7.0 collective-permute-done.7
  678.3 7.4 convolution_convert_fusion.1
  685.9 29.1 %quad_sum.3 = f32[256,1600]{1,0:T(8,128)} custom-call(bf16[2,2,256,1600]{3,2,1,0:T(8,128)(2,1)} %bitcast.157), custom_call_target="tpu_custom_call" | custom-call | bytes 90000000 | tf_op jit(solution)/shard_map/quad_sum/pallas_call | solution.py:930
  715.0 7.2 convolution_convert_fusion.6
  727.0 7.0 convert_add_fusion
  740.6 5.0 convert_add_fusion.1
  748.2 25.9 %collective-permute-done.1 = bf16[672,1600]{1,0:T(8,128)(2,1)} collective-permute-done((bf16[672,1600]{1,0:T(8,128)(2,1)}, bf16[672,1600]{1,0:T(8,128)(2,1)}, u32[]{:S(2)}, u32[]{:S(2)}) %collective-permute-start.1) | collective-permute-done | bytes 2150432 | tf_op jit(solution)/shard_map/ppermute | solution.py:331
  778.1 4.6 convert_add_fusion.2
  783.0 13.6 %collective-permute-done.15 = bf16[200,1600]{1,0:T(8,128)(2,1)S(1)} collective-permute-done((bf16[200,1600]{1,0:T(8,128)(2,1)S(1)}, bf16[200,1600]{1,0:T(8,128)(2,1)S(1)}, u32[]{:S(2)}, u32[]{:S(2)}) %collective-permute-start.15) | collective-permute-done | bytes 640032 | tf_op jit(solution)/shard_map/ppermute | solution.py:331
  796.7 29.0 %collective-permute-start.3 = (bf16[168,1600]{1,0:T(8,128)(2,1)S(1)}, bf16[168,1600]{1,0:T(8,128)(2,1)S(1)}, u32[]{:S(2)}, u32[]{:S(2)}) collective-permute-start(bf16[168,1600]{1,0:T(8,128)(2,1)S(1)} %get-tuple-element.87), channel_id=1, source_target_pairs={{0,4},{1,5},{2,6},{3,7},{4,0},{5,1},{6,2},{7,3},{8,12},{9,13},{10,... | collective-permute-start | bytes 1612808 | tf_op jit(solution)/shard_map/ppermute | solution.py:331
  825.7 38.0 %collective-permute-start.4 = (bf16[168,1600]{1,0:T(8,128)(2,1)S(1)}, bf16[168,1600]{1,0:T(8,128)(2,1)S(1)}, u32[]{:S(2)}, u32[]{:S(2)}) collective-permute-start(bf16[168,1600]{1,0:T(8,128)(2,1)S(1)} %get-tuple-element.86), channel_id=1, source_target_pairs={{0,6},{1,7},{2,0},{3,1},{4,2},{5,3},{6,4},{7,5},{8,14},{9,15},{10,... | collective-permute-start | bytes 1612808 | tf_op jit(solution)/shard_map/ppermute | solution.py:331
  864.9 12.8 %collective-permute-done.11 = bf16[200,1600]{1,0:T(8,128)(2,1)S(1)} collective-permute-done((bf16[200,1600]{1,0:T(8,128)(2,1)S(1)}, bf16[200,1600]{1,0:T(8,128)(2,1)S(1)}, u32[]{:S(2)}, u32[]{:S(2)}) %collective-permute-start.11) | collective-permute-done | bytes 640032 | tf_op jit(solution)/shard_map/ppermute | solution.py:331
  878.9 22.8 %collective-permute-done.3 = bf16[168,1600]{1,0:T(8,128)(2,1)S(1)} collective-permute-done((bf16[168,1600]{1,0:T(8,128)(2,1)S(1)}, bf16[168,1600]{1,0:T(8,128)(2,1)S(1)}, u32[]{:S(2)}, u32[]{:S(2)}) %collective-permute-start.3) | collective-permute-done | bytes 537632 | tf_op jit(solution)/shard_map/ppermute | solution.py:331
  902.8 79.2 %collect.1 = (bf16[76,8,1600]{2,1,0:T(8,128)(2,1)}, f32[32,2,8,1600]{3,2,1,0:T(8,128)}) custom-call(bf16[21,8,1600]{2,1,0:T(8,128)(2,1)} %fusion.97.qkv_ref, bf16[7,8,1600]{2,1,0:T(8,128)(2,1)} %fusion.104.out_ref, bf16[25,8,1600]{2,1,0:T(8,128)(2,1)} %fusion.92.fc_ref, bf16[25,8,1600]{2,1,0:T(8,128)(2,1)} %fusion.93.proj_ref, ...), custom_call_target="tpu_custom_call" | custom-call | tf_op jit(solution)/shard_map/collect/pallas_call | solution.py:1038
  (155 shorter events, 81.4 us)
Async XLA Ops:
  126.3 8.1 copy-start.11
  138.9 190.0 %copy-start = (bf16[256,1600]{1,0:T(8,128)(2,1)S(1)}, bf16[256,1600]{1,0:T(8,128)(2,1)}, u32[]{:S(2)}) copy-start(bf16[256,1600]{1,0:T(8,128)(2,1)} %copy.18.tok_ref) | copy-start | bytes 2457604
  434.7 12.0 %copy-start.20 = (bf16[1024,1600]{0,1:T(8,128)(2,1)}, bf16[1024,1600]{0,1:T(8,128)(2,1)S(1)}, u32[]{:S(2)}) copy-start(bf16[1024,1600]{0,1:T(8,128)(2,1)S(1)} %get-tuple-element.74) | copy-start | bytes 9830404
  482.8 16.0 %slice-start.1 = ((s8[5963776]{0:T(1024)(128)(4,1)}), s8[4194304]{0:T(1024)(128)(4,1)S(1)}, s32[]{:S(2)}) async-start(s8[5963776]{0:T(1024)(128)(4,1)} %bitcast.178), calls=%async_computation.1 | async-start | bytes 8388608
  485.2 11.4 %copy-start.3 = (f32[256,1600]{1,0:T(8,128)S(1)}, f32[256,1600]{1,0:T(8,128)}, u32[]{:S(2)}) copy-start(f32[256,1600]{1,0:T(8,128)} %quad_sum.2) | copy-start | bytes 4915204
  485.2 11.4 %copy-start.4 = (bf16[256,1600]{1,0:T(8,128)(2,1)S(1)}, bf16[256,1600]{1,0:T(8,128)(2,1)}, u32[]{:S(2)}) copy-start(bf16[256,1600]{1,0:T(8,128)(2,1)} %copy.20.cot_ref) | copy-start | bytes 2457604
  485.2 13.6 %slice-start.2 = ((s8[5963776]{0:T(1024)(128)(4,1)}), s8[1769472]{0:T(1024)(128)(4,1)S(1)}, s32[]{:S(2)}) async-start(s8[5963776]{0:T(1024)(128)(4,1)} %bitcast.178), calls=%async_computation.2 | async-start | bytes 3538944
  565.2 109.8 %collective-permute-start = (bf16[1024,896]{1,0:T(8,128)(2,1)}, bf16[1024,896]{1,0:T(8,128)(2,1)}, u32[]{:S(2)}, u32[]{:S(2)}) collective-permute-start(bf16[1024,896]{1,0:T(8,128)(2,1)} %convert_element_type.260), channel_id=1, source_target_pairs={{2,0},{3,1},{6,4},{7,5},{10,8},{11,9},{14,12},{15,13},{18,16},{19,... | collective-permute-start | bytes 5505032 | tf_op jit(solution)/shard_map/ppermute | solution.py:331
  575.5 151.5 %collective-permute-start.13 = (bf16[800,1600]{1,0:T(8,128)(2,1)}, bf16[800,1600]{1,0:T(8,128)(2,1)}, u32[]{:S(2)}, u32[]{:S(2)}) collective-permute-start(bf16[800,1600]{1,0:T(8,128)(2,1)} %convolution_convert_fusion.4), channel_id=1, source_target_pairs={{0,16},{1,17},{2,18},{3,19},{4,20},{5,21},{6,22},{7,23},{8,24},{9,... | collective-permute-start | bytes 7680008 | tf_op jit(solution)/shard_map/ppermute | solution.py:331
  639.9 9.4 copy-start.15
  639.9 17.7 %collective-permute-start.5 = (bf16[224,1600]{1,0:T(8,128)(2,1)}, bf16[224,1600]{1,0:T(8,128)(2,1)}, u32[]{:S(2)}, u32[]{:S(2)}) collective-permute-start(bf16[224,1600]{1,0:T(8,128)(2,1)} %fusion.83), channel_id=1, source_target_pairs={{0,16},{1,17},{2,18},{3,19},{4,20},{5,21},{6,22},{7,23},{8,24},{9,... | collective-permute-start | bytes 2150408 | tf_op jit(solution)/shard_map/ppermute | solution.py:331
  651.5 23.5 %copy-start.8 = (f32[1024,896]{1,0:T(8,128)S(1)}, f32[1024,896]{1,0:T(8,128)}, u32[]{:S(2)}) copy-start(f32[1024,896]{1,0:T(8,128)} %get-tuple-element.46) | copy-start | bytes 11010052
  657.6 20.6 %slice-start.3 = ((s8[4472832]{0:T(1024)(128)(4,1)}), s8[4194304]{0:T(1024)(128)(4,1)S(1)}, s32[]{:S(2)}) async-start(s8[4472832]{0:T(1024)(128)(4,1)} %bitcast.183), calls=%async_computation.3 | async-start | bytes 8388608
  659.6 6.7 collective-permute-start.6
  659.7 14.5 %collective-permute-start.7 = (bf16[56,1600]{1,0:T(8,128)(2,1)S(1)}, bf16[56,1600]{1,0:T(8,128)(2,1)S(1)}, u32[]{:S(2)}, u32[]{:S(2)}) collective-permute-start(bf16[56,1600]{1,0:T(8,128)(2,1)S(1)} %get-tuple-element.90), channel_id=1, source_target_pairs={{0,4},{1,5},{2,6},{3,7},{4,0},{5,1},{6,2},{7,3},{8,12},{9,13},{10,... | collective-permute-start | bytes 537608 | tf_op jit(solution)/shard_map/ppermute | solution.py:331
  659.7 14.5 %collective-permute-start.8 = (bf16[56,1600]{1,0:T(8,128)(2,1)S(1)}, bf16[56,1600]{1,0:T(8,128)(2,1)S(1)}, u32[]{:S(2)}, u32[]{:S(2)}) collective-permute-start(bf16[56,1600]{1,0:T(8,128)(2,1)S(1)} %get-tuple-element.89), channel_id=1, source_target_pairs={{0,6},{1,7},{2,0},{3,1},{4,2},{5,3},{6,4},{7,5},{8,14},{9,15},{10,... | collective-permute-start | bytes 537608 | tf_op jit(solution)/shard_map/ppermute | solution.py:331
  666.2 74.3 %collective-permute-start.9 = (bf16[800,1600]{1,0:T(8,128)(2,1)}, bf16[800,1600]{1,0:T(8,128)(2,1)}, u32[]{:S(2)}, u32[]{:S(2)}) collective-permute-start(bf16[800,1600]{1,0:T(8,128)(2,1)} %convolution_convert_fusion.5), channel_id=1, source_target_pairs={{0,16},{1,17},{2,18},{3,19},{4,20},{5,21},{6,22},{7,23},{8,24},{9,... | collective-permute-start | bytes 7680008 | tf_op jit(solution)/shard_map/ppermute | solution.py:331
  677.0 8.8 copy-start.5
  723.1 51.0 %collective-permute-start.1 = (bf16[672,1600]{1,0:T(8,128)(2,1)}, bf16[672,1600]{1,0:T(8,128)(2,1)}, u32[]{:S(2)}, u32[]{:S(2)}) collective-permute-start(bf16[672,1600]{1,0:T(8,128)(2,1)} %convolution_convert_fusion.6), channel_id=1, source_target_pairs={{0,16},{1,17},{2,18},{3,19},{4,20},{5,21},{6,22},{7,23},{8,24},{9,... | collective-permute-start | bytes 6451208 | tf_op jit(solution)/shard_map/ppermute | solution.py:331
  727.0 13.6 %copy-start.21 = (bf16[1024,1600]{0,1:T(8,128)(2,1)S(1)}, bf16[1024,1600]{0,1:T(8,128)(2,1)}, u32[]{:S(2)}) copy-start(bf16[1024,1600]{0,1:T(8,128)(2,1)} %copy-done.20) | copy-start | bytes 9830404
  734.4 48.3 %collective-permute-start.14 = (bf16[200,1600]{1,0:T(8,128)(2,1)S(1)}, bf16[200,1600]{1,0:T(8,128)(2,1)S(1)}, u32[]{:S(2)}, u32[]{:S(2)}) collective-permute-start(bf16[200,1600]{1,0:T(8,128)(2,1)S(1)} %get-tuple-element.79), channel_id=1, source_target_pairs={{0,2},{1,3},{2,4},{3,5},{4,6},{5,7},{6,0},{7,1},{8,10},{9,11},{10,... | collective-permute-start | bytes 1920008 | tf_op jit(solution)/shard_map/ppermute | solution.py:331
  736.0 60.7 %collective-permute-start.15 = (bf16[200,1600]{1,0:T(8,128)(2,1)S(1)}, bf16[200,1600]{1,0:T(8,128)(2,1)S(1)}, u32[]{:S(2)}, u32[]{:S(2)}) collective-permute-start(bf16[200,1600]{1,0:T(8,128)(2,1)S(1)} %get-tuple-element.81), channel_id=1, source_target_pairs={{0,4},{1,5},{2,6},{3,7},{4,0},{5,1},{6,2},{7,3},{8,12},{9,13},{10,... | collective-permute-start | bytes 1920008 | tf_op jit(solution)/shard_map/ppermute | solution.py:331
  739.2 57.5 %collective-permute-start.16 = (bf16[200,1600]{1,0:T(8,128)(2,1)S(1)}, bf16[200,1600]{1,0:T(8,128)(2,1)S(1)}, u32[]{:S(2)}, u32[]{:S(2)}) collective-permute-start(bf16[200,1600]{1,0:T(8,128)(2,1)S(1)} %get-tuple-element.80), channel_id=1, source_target_pairs={{0,6},{1,7},{2,0},{3,1},{4,2},{5,3},{6,4},{7,5},{8,14},{9,15},{10,... | collective-permute-start | bytes 1920008 | tf_op jit(solution)/shard_map/ppermute | solution.py:331
  740.6 37.4 %copy-start.12 = (bf16[1024,1600]{1,0:T(8,128)(2,1)S(1)}, bf16[1024,1600]{1,0:T(8,128)(2,1)}, u32[]{:S(2)}) copy-start(bf16[1024,1600]{1,0:T(8,128)(2,1)} %copy-done.11) | copy-start | bytes 9830404
  745.7 32.4 %copy-start.6 = (bf16[1024,896]{1,0:T(8,128)(2,1)S(1)}, bf16[1024,896]{1,0:T(8,128)(2,1)}, u32[]{:S(2)}) copy-start(bf16[1024,896]{1,0:T(8,128)(2,1)} %copy-done.5) | copy-start | bytes 5505028
  745.7 32.4 %copy-start.17 = (bf16[1024,448]{1,0:T(8,128)(2,1)S(1)}, bf16[1024,448]{1,0:T(8,128)(2,1)}, u32[]{:S(2)}) copy-start(bf16[1024,448]{1,0:T(8,128)(2,1)} %get-tuple-element.45) | copy-start | bytes 2752516
  746.0 79.7 %collective-permute-start.10 = (bf16[200,1600]{1,0:T(8,128)(2,1)S(1)}, bf16[200,1600]{1,0:T(8,128)(2,1)S(1)}, u32[]{:S(2)}, u32[]{:S(2)}) collective-permute-start(bf16[200,1600]{1,0:T(8,128)(2,1)S(1)} %get-tuple-element.82), channel_id=1, source_target_pairs={{0,2},{1,3},{2,4},{3,5},{4,6},{5,7},{6,0},{7,1},{8,10},{9,11},{10,... | collective-permute-start | bytes 1920008 | tf_op jit(solution)/shard_map/ppermute | solution.py:331
  774.1 103.6 %collective-permute-start.11 = (bf16[200,1600]{1,0:T(8,128)(2,1)S(1)}, bf16[200,1600]{1,0:T(8,128)(2,1)S(1)}, u32[]{:S(2)}, u32[]{:S(2)}) collective-permute-start(bf16[200,1600]{1,0:T(8,128)(2,1)S(1)} %get-tuple-element.84), channel_id=1, source_target_pairs={{0,4},{1,5},{2,6},{3,7},{4,0},{5,1},{6,2},{7,3},{8,12},{9,13},{10,... | collective-permute-start | bytes 1920008 | tf_op jit(solution)/shard_map/ppermute | solution.py:331
  782.7 95.0 %collective-permute-start.12 = (bf16[200,1600]{1,0:T(8,128)(2,1)S(1)}, bf16[200,1600]{1,0:T(8,128)(2,1)S(1)}, u32[]{:S(2)}, u32[]{:S(2)}) collective-permute-start(bf16[200,1600]{1,0:T(8,128)(2,1)S(1)} %get-tuple-element.83), channel_id=1, source_target_pairs={{0,6},{1,7},{2,0},{3,1},{4,2},{5,3},{6,4},{7,5},{8,14},{9,15},{10,... | collective-permute-start | bytes 1920008 | tf_op jit(solution)/shard_map/ppermute | solution.py:331
  796.7 82.2 %collective-permute-start.2 = (bf16[168,1600]{1,0:T(8,128)(2,1)S(1)}, bf16[168,1600]{1,0:T(8,128)(2,1)S(1)}, u32[]{:S(2)}, u32[]{:S(2)}) collective-permute-start(bf16[168,1600]{1,0:T(8,128)(2,1)S(1)} %get-tuple-element.85), channel_id=1, source_target_pairs={{0,2},{1,3},{2,4},{3,5},{4,6},{5,7},{6,0},{7,1},{8,10},{9,11},{10,... | collective-permute-start | bytes 1612808 | tf_op jit(solution)/shard_map/ppermute | solution.py:331
  796.7 105.0 %collective-permute-start.3 = (bf16[168,1600]{1,0:T(8,128)(2,1)S(1)}, bf16[168,1600]{1,0:T(8,128)(2,1)S(1)}, u32[]{:S(2)}, u32[]{:S(2)}) collective-permute-start(bf16[168,1600]{1,0:T(8,128)(2,1)S(1)} %get-tuple-element.87), channel_id=1, source_target_pairs={{0,4},{1,5},{2,6},{3,7},{4,0},{5,1},{6,2},{7,3},{8,12},{9,13},{10,... | collective-permute-start | bytes 1612808 | tf_op jit(solution)/shard_map/ppermute | solution.py:331
  825.7 75.9 %collective-permute-start.4 = (bf16[168,1600]{1,0:T(8,128)(2,1)S(1)}, bf16[168,1600]{1,0:T(8,128)(2,1)S(1)}, u32[]{:S(2)}, u32[]{:S(2)}) collective-permute-start(bf16[168,1600]{1,0:T(8,128)(2,1)S(1)} %get-tuple-element.86), channel_id=1, source_target_pairs={{0,6},{1,7},{2,0},{3,1},{4,2},{5,3},{6,4},{7,5},{8,14},{9,15},{10,... | collective-permute-start | bytes 1612808 | tf_op jit(solution)/shard_map/ppermute | solution.py:331
  (12 other events, 53.8 us)

commit v2 on v1

--- a/solution.py
+++ b/solution.py
@@ -341,6 +341,7 @@
 
 class Sizes:
     def __init__(self, width, hidden, heads, head_size, rows):
+        self.heads = heads
         self.head_size = head_size
         self.quarter_heads = -(-heads // 4)
         self.part = self.quarter_heads * head_size
@@ -356,6 +357,40 @@
         self.proj_start = self.fc_start + hidden // GRAIN
         self.vec_start = self.proj_start + hidden // GRAIN
         self.vec = 2
+        self.head_grains = head_size // GRAIN
+        self.fc_turn = self.turn(self.fc_start)
+        self.proj_turn = self.turn(self.proj_start)
+
+    def turn(self, start):
+        return start // (2 * self.block) % 4
+
+
+def spot_of_range(r):
+    y = r // 6 + (r % 2) * ((r // 3) % 2)
+    u = (r - (r + 5) // 8 - (r + 3) // 8) % 4
+    return y, u
+
+
+def range_of_spot(y, u):
+    first = u + u // 3
+    second = (1 - u // 2) * (u + 6) + (u // 2) * (2 * u - 1)
+    return (1 - y) * first + y * second
+
+
+RANGES = (0, 1, 2, 4, 6, 7, 3, 5)
+SPOTS = (0, 1, 2, 6, 3, 7, 4, 5)
+
+
+def slot_qkv(y, z):
+    return 2 * z + y
+
+
+def slot_out(y, z):
+    return 4 * y + z
+
+
+def slot_turned(turn):
+    return lambda y, z: 4 * y + (z + 4 - turn) % 4
 
 
 def my_place():
@@ -364,8 +399,8 @@
     return dp // 2, dp % 2, cp // 2, cp % 2
 
 
-def place_of(quarter, share):
-    return (share // 4) * 2 + quarter // 2, (share % 4) * 2 + quarter % 2
+def device_of(quarter, y, z):
+    return y * 2 + quarter // 2, z * 2 + quarter % 2
 
 
 class Wires:
@@ -388,9 +423,10 @@
 
 
 class PlaceGather:
-    def __init__(self, wires, full):
+    def __init__(self, wires, full, slot):
         self.wires = wires
         self.full = full
+        self.slot = slot
         self.dp, self.cp = lax.axis_index("dp"), lax.axis_index("cp")
         self.y, self.z, self.x = self.dp // 2, self.cp // 2, self.cp % 2
         self.started = []
@@ -407,10 +443,10 @@
         return along + [((self.dp + 2) % 4, self.cp)]
 
     def start_over(self):
-        self.over = [self.send(self.y * 4 + self.z, (self.dp + 2) % 4, self.cp)]
+        self.over = [self.send(self.slot(self.y, self.z), (self.dp + 2) % 4, self.cp)]
 
     def start(self, over=True):
-        mine = self.y * 4 + self.z
+        mine = self.slot(self.y, self.z)
         self.along = []
         for d in (1, 3, 2):
             self.along.append((d, self.send(mine, self.dp, ((self.z + d) % 4) * 2 + self.x)))
@@ -421,7 +457,7 @@
     def forward(self):
         for d, copy in self.along:
             copy.wait_recv()
-            self.over.append(self.send(self.y * 4 + (self.z - d + 4) % 4, (self.dp + 2) % 4, self.cp))
+            self.over.append(self.send(self.slot(self.y, (self.z - d + 4) % 4), (self.dp + 2) % 4, self.cp))
 
     def finish(self):
         for copy in self.over:
@@ -475,71 +511,92 @@
     tok = QuadGather(wires, tok_ref, tok_all, local_sems.at[0])
     cot = QuadGather(wires, cot_ref, cot_all, local_sems.at[1])
 
-    def send(grain, ref, slot, quarter, share, sem, recv):
-        dp, cp = place_of(quarter, share)
+    def send(grain, ref, spot, slot, quarter, py, pz, sem, recv):
+        dp, cp = device_of(quarter, py, pz)
         mine = dp * 8 + cp == me
 
         @pl.when(mine)
         def _():
-            pltpu.make_async_copy(p_ref.at[grain], ref.at[share, slot], recv).start()
+            pltpu.make_async_copy(p_ref.at[grain], ref.at[spot, slot], recv).start()
 
         @pl.when(jnp.logical_not(mine))
         def _():
             pltpu.make_async_remote_copy(
                 src_ref=p_ref.at[grain],
-                dst_ref=ref.at[share, slot],
+                dst_ref=ref.at[spot, slot],
                 send_sem=sem,
                 recv_sem=recv,
                 device_id=(dp, cp),
                 device_id_type=MESH,
             ).start()
 
-    def sent(grain, ref, slot, quarter, share, sem, recv):
-        dp, cp = place_of(quarter, share)
+    def sent(grain, ref, spot, slot, quarter, py, pz, sem, recv):
+        dp, cp = device_of(quarter, py, pz)
 
         @pl.when(dp * 8 + cp != me)
         def _():
             pltpu.make_async_copy(p_ref.at[grain], p_ref.at[grain], sem).wait()
 
-    def headed(act, grain, base, parts, ref, recv, share_size):
-        offset = me * sz.block + grain - base
-        part = offset // sz.width_grains
-        local = offset % sz.width_grains
+    def headed(act, grain):
+        table = me * sz.block + grain
+        part = table // sz.width_grains
+        inner = table % sz.width_grains
+        head = inner // sz.head_grains
+        rest = inner % sz.head_grains
+
+        def one(quarter, sem):
+            local = part * sz.part_grains + (head // 4) * sz.head_grains + rest
+            spot = local // sz.qkv
+            act(grain, qkv_ref, spot, local % sz.qkv, quarter, spot % 2, spot // 2, sem, kind_sems.at[0])
+
+        @pl.when(table < sz.out_start)
+        def _():
+            one(head % 4, spread_sems.at[grain])
+
+            @pl.when(head == sz.heads - 1)
+            def _():
+                for quarter in range(1, 4):
+                    one(quarter, spread_sems.at[sz.block + (quarter - 1) * sz.head_grains + rest])
+
+    def outward(act, grain):
+        local = me * sz.block + grain - sz.out_start
 
         def one(quarter, inner, sem):
-            spot = part * sz.part_grains + inner
-            act(grain, ref, spot % share_size, quarter, spot // share_size, sem, recv)
-
-        @pl.when(jnp.logical_and(offset >= 0, offset < parts * sz.width_grains))
+            spot = inner // sz.out
+            act(grain, out_ref, spot, inner % sz.out, quarter, spot // 4, spot % 4, sem, kind_sems.at[1])
+
+        @pl.when(jnp.logical_and(local >= 0, local < sz.width_grains))
         def _():
             one(local // sz.part_grains, local % sz.part_grains, spread_sems.at[grain])
 
             @pl.when(local < sz.spill)
             def _():
-                one(3, sz.part_grains - sz.spill + local, spread_sems.at[sz.block + grain])
-
-    def plain(act, grain, base, ref, recv):
+                one(3, sz.part_grains - sz.spill + local, spread_sems.at[sz.block + 3 * sz.head_grains + local])
+
+    def plain(act, grain, base, turn, ref, recv):
         offset = me * sz.block + grain - base
 
         @pl.when(jnp.logical_and(offset >= 0, offset < 32 * sz.mlp))
         def _():
+            local = offset // 4
+            py, u = spot_of_range(local // sz.mlp)
             act(
-                grain, ref, offset % sz.mlp, offset // (8 * sz.mlp), (offset // sz.mlp) % 8,
+                grain, ref, py * 4 + u, local % sz.mlp, offset % 4, py, (u + turn) % 4,
                 spread_sems.at[grain], recv,
             )
 
     def heads(act):
         def one(grain, _):
-            headed(act, grain, 0, 3, qkv_ref, kind_sems.at[0], sz.qkv)
+            headed(act, grain)
             return 0
 
         lax.fori_loop(0, sz.block, one, 0)
 
     def others(act):
         def one(grain, _):
-            headed(act, grain, sz.out_start, 1, out_ref, kind_sems.at[1], sz.out)
-            plain(act, grain, sz.fc_start, fc_ref, kind_sems.at[2])
-            plain(act, grain, sz.proj_start, proj_ref, kind_sems.at[3])
+            outward(act, grain)
+            plain(act, grain, sz.fc_start, sz.fc_turn, fc_ref, kind_sems.at[2])
+            plain(act, grain, sz.proj_start, sz.proj_turn, proj_ref, kind_sems.at[3])
             return 0
 
         lax.fori_loop(0, sz.block, one, 0)
@@ -557,7 +614,7 @@
                         pltpu.make_async_remote_copy(
                             src_ref=p_ref.at[pl.ds(spot, sz.vec)],
                             dst_ref=vec_ref,
-                            send_sem=spread_sems.at[2 * sz.block + device],
+                            send_sem=spread_sems.at[sz.block + 3 * sz.head_grains + sz.spill + device],
                             recv_sem=kind_sems.at[4],
                             device_id=(device // 8, device % 8),
                             device_id_type=MESH,
@@ -570,26 +627,29 @@
 
     heads(send)
     tok.start()
-    cot.start()
-    mine = y * 4 + z
+    mine = slot_qkv(y, z)
     pltpu.make_async_copy(qkv_ref.at[mine], qkv_ref.at[mine], kind_sems.at[0]).wait()
-    weights = PlaceGather(wires, qkv_ref)
+    weights = PlaceGather(wires, qkv_ref, slot_qkv)
     weights.start()
-    others(send)
     vector_sends(lambda copy: copy.start())
 
     @pl.when(me == owner)
     def _():
         pltpu.make_async_copy(p_ref.at[pl.ds(spot, sz.vec)], vec_ref, kind_sems.at[4]).start()
 
+    others(send)
+    cot.start()
     weights.forward()
     tok.forward()
     cot.forward()
     heads(sent)
     others(sent)
     vector_sends(lambda copy: copy.wait_send())
-    for index, ref in enumerate((out_ref, fc_ref, proj_ref)):
-        pltpu.make_async_copy(ref.at[mine], ref.at[mine], kind_sems.at[index + 1]).wait()
+    for index, (ref, slot) in enumerate(
+        ((out_ref, slot_out), (fc_ref, slot_turned(sz.fc_turn)), (proj_ref, slot_turned(sz.proj_turn)))
+    ):
+        view = ref.at[slot(y, z)]
+        pltpu.make_async_copy(view, view, kind_sems.at[index + 1]).wait()
     pltpu.make_async_copy(vec_ref, vec_ref, kind_sems.at[4]).wait()
     tok.finish()
     cot.finish()
@@ -640,7 +700,7 @@
         in_specs=[HBM, VMEM, VMEM],
         out_specs=[HBM] * 7,
         scratch_shapes=[
-            pltpu.SemaphoreType.DMA((2 * sz.block + 32,)),
+            pltpu.SemaphoreType.DMA((sz.block + 3 * sz.head_grains + sz.spill + 32,)),
             pltpu.SemaphoreType.DMA((5,)),
             *wire_sems(13),
             pltpu.SemaphoreType.DMA((2,)),
@@ -651,7 +711,7 @@
 
 
 def forward_kernel(
-    heads, size, q_ref, kv_ref, out_in, fc_in, proj_in,
+    heads, size, fc_turn, proj_turn, q_ref, kv_ref, out_in, fc_in, proj_in,
     mix_ref, lse_ref, before_ref, mixed_ref, out_ref, fc_ref, proj_ref, out_all,
     stage, send_sems, recv_sems, local_sems,
 ):
@@ -663,7 +723,9 @@
     blk = 128
     scale = size**-0.5
     odd = z % 2 == 1
-    w_out, w_fc, w_proj = [PlaceGather(wires, ref) for ref in (out_ref, fc_ref, proj_ref)]
+    w_out = PlaceGather(wires, out_ref, slot_out)
+    w_fc = PlaceGather(wires, fc_ref, slot_turned(fc_turn))
+    w_proj = PlaceGather(wires, proj_ref, slot_turned(proj_turn))
     others = [(c, 1 - x), (1 - c, x), (1 - c, 1 - x)]
     quad = [(y * 2 + tc, z * 2 + tx) for tc, tx in others]
     greet(w_out.partners() + quad)
@@ -770,7 +832,7 @@
         return jax.ShapeDtypeStruct(lead + value.shape, value.dtype)
 
     return pl.pallas_call(
-        functools.partial(forward_kernel, sz.quarter_heads, sz.head_size),
+        functools.partial(forward_kernel, sz.quarter_heads, sz.head_size, sz.fc_turn, sz.proj_turn),
         out_shape=(
             jax.ShapeDtypeStruct((rows, part), jnp.float32),
             jax.ShapeDtypeStruct((rows, 8), jnp.float32),
@@ -795,10 +857,10 @@
     )(q, kv, w_out, w_fc, w_proj)
 
 
-def acts_kernel(act_ref, proj_in, act_all, proj_ref, send_sems, recv_sems, local_sem):
+def acts_kernel(proj_turn, act_ref, proj_in, act_all, proj_ref, send_sems, recv_sems, local_sem):
     wires = Wires(send_sems, recv_sems)
     quad = QuadGather(wires, act_ref, act_all, local_sem)
-    places = PlaceGather(wires, proj_ref)
+    places = PlaceGather(wires, proj_ref, slot_turned(proj_turn))
     greet(places.partners() + [quad.over_x, quad.over_c])
     quad.start()
     places.start(False)
@@ -808,9 +870,9 @@
     places.finish()
 
 
-def acts_call(act, w_proj):
+def acts_call(sz, act, w_proj):
     return pl.pallas_call(
-        acts_kernel,
+        functools.partial(acts_kernel, sz.proj_turn),
         out_shape=(
             jax.ShapeDtypeStruct((2, 2) + act.shape, act.dtype),
             jax.ShapeDtypeStruct(w_proj.shape, w_proj.dtype),
@@ -943,7 +1005,6 @@
     y, c, z, x = my_place()
     me = flat_id(y, c, z, x)
     quarter = c * 2 + x
-    share = y * 4 + z
 
     def send(ref, slot, table, sem):
         dest = table // sz.block
@@ -970,32 +1031,43 @@
             pltpu.make_async_copy(ref.at[slot], ref.at[slot], sem).wait()
 
     def run(act):
-        def headed(ref, size, base, first_sem):
+        def heads(slot, _):
+            local = slot_qkv(y, z) * sz.qkv + slot
+            inner = local % sz.part_grains
+            head = 4 * (inner // sz.head_grains) + quarter
+
+            @pl.when(head < sz.heads)
+            def _():
+                table = (local // sz.part_grains) * sz.width_grains + head * sz.head_grains + inner % sz.head_grains
+                act(qkv_ref, slot, table, send_sems.at[slot])
+
+            return 0
+
+        lax.fori_loop(0, sz.qkv, heads, 0)
+
+        def outward(slot, _):
+            local = quarter * sz.part_grains + slot_out(y, z) * sz.out + slot
+
+            @pl.when(local < sz.width_grains)
+            def _():
+                act(out_ref, slot, sz.out_start + local, send_sems.at[sz.qkv + slot])
+
+            return 0
+
+        lax.fori_loop(0, sz.out, outward, 0)
+
+        def plain(ref, base, turn, first_sem):
+            r = range_of_spot(y, (z + 4 - turn) % 4)
+
             def one(slot, _):
-                spot = share * size + slot
-                part = spot // sz.part_grains
-                local = quarter * sz.part_grains + spot % sz.part_grains
-
-                @pl.when(local < sz.width_grains)
-                def _():
-                    act(ref, slot, base + part * sz.width_grains + local, send_sems.at[first_sem + slot])
-
-                return 0
-
-            lax.fori_loop(0, size, one, 0)
-
-        def plain(ref, base, first_sem):
-            def one(slot, _):
-                table = base + (quarter * 8 + share) * sz.mlp + slot
+                table = base + 4 * (r * sz.mlp + slot) + quarter
                 act(ref, slot, table, send_sems.at[first_sem + slot])
                 return 0
 
             lax.fori_loop(0, sz.mlp, one, 0)
 
-        headed(qkv_ref, sz.qkv, 0, 0)
-        headed(out_ref, sz.out, sz.out_start, sz.qkv)
-        plain(fc_ref, sz.fc_start, sz.qkv + sz.out)
-        plain(proj_ref, sz.proj_start, sz.qkv + sz.out + sz.mlp)
+        plain(fc_ref, sz.fc_start, sz.fc_turn, sz.qkv + sz.out)
+        plain(proj_ref, sz.proj_start, sz.proj_turn, sz.qkv + sz.out + sz.mlp)
 
     last = sz.vec_start // sz.block
     vec_copy = pltpu.make_async_remote_copy(
@@ -1189,12 +1261,12 @@
     def to_other_y(sent):
         return over_y(sent.astype(bf16))
 
-    def to_places(kept, got):
-        summed = kept + got.astype(f32)
+    def to_places(kept, got, turn=0):
+        summed = kept.astype(f32) + got.astype(f32)
         summed = summed.reshape(4, summed.shape[0] // 4, -1)
-        total = pick(summed, z)
+        total = pick(summed, (z + 4 - turn) % 4)
         for d in (1, 2, 3):
-            got = over_z(pick(summed, (z + d) % 4).astype(bf16), d)
+            got = over_z(pick(summed, (z + d + 4 - turn) % 4).astype(bf16), d)
             total = total + got.astype(f32)
         return total
 
@@ -1209,21 +1281,23 @@
     act_one = (normed_all * vectors[0] + vectors[1]).astype(bf16)
 
     def quarter_of(vector):
-        padded = jnp.pad(vector, (0, 4 * sz.part - width))
-        return lax.dynamic_slice_in_dim(padded, quarter * sz.part, sz.part, 0)
+        padded = jnp.pad(vector, (0, 4 * sz.part - width)).reshape(sz.quarter_heads, 4, sz.head_size)
+        return lax.dynamic_index_in_dim(padded, quarter, 1, keepdims=False).reshape(sz.part)
 
     kv_bias = jnp.concatenate([jnp.zeros((sz.part,), f32), quarter_of(vectors[3])])
     kv = (dot_nt(act_one, w_qkv[sz.part :]) + kv_bias).astype(bf16)
     q = (dot_nt(act_one, w_qkv[: sz.part]) + quarter_of(vectors[2])).astype(bf16)
     mix, lse, before, mixed, _, w_fc, w_proj, w_out = forward_call(sz, q, kv, w_out, w_fc, w_proj)
     w_fc, w_out = flat(w_fc), flat(w_out)[:width]
-    mixed = jnp.transpose(mixed, (1, 0, 2)).reshape(rows, 4 * sz.part)[:, :width]
+    by_head = (sz.quarter_heads, sz.head_size)
+    mixed = jnp.transpose(mixed.reshape((4, rows) + by_head), (1, 2, 0, 3)).reshape(rows, 4 * sz.part)[:, :width]
     inputs = tokens.astype(f32)
     residual = inputs + (dot_nt(mixed, w_out) + vectors[4])
     normed_two, rs_two = norm_parts(residual)
-    act_two, w_proj = acts_call((normed_two * vectors[5] + vectors[6]).astype(bf16), w_proj)
+    act_two, w_proj = acts_call(sz, (normed_two * vectors[5] + vectors[6]).astype(bf16), w_proj)
     act_two, w_proj = flat(act_two), flat(w_proj)
-    bias = lax.dynamic_slice_in_dim(fc_bias, quarter * (hidden // 4), hidden // 4, 0)
+    bias = lax.dynamic_index_in_dim(fc_bias.reshape(-1, 4, GRAIN), quarter, 1, keepdims=False)
+    bias = bias.reshape(8, hidden // 32)[jnp.array(RANGES)].reshape(hidden // 4)
     pre_act = dot_nt(act_two, w_fc) + bias
     act_hidden, pull_gelu = jax.vjp(gelu_tanh, pre_act)
     act_hidden = act_hidden.astype(bf16)
@@ -1239,41 +1313,42 @@
     grad_attn = grad_res.astype(bf16)
     grad_mix = dot_nn(grad_attn, w_out).astype(bf16)
     grad_mix = jnp.pad(grad_mix, ((0, 0), (0, 4 * sz.part - width)))
-    grad_mix = jnp.transpose(grad_mix.reshape(rows, 4, sz.part), (1, 0, 2))
+    grad_mix = jnp.transpose(grad_mix.reshape(rows, sz.quarter_heads, 4, sz.head_size), (2, 0, 1, 3))
+    grad_mix = grad_mix.reshape(4, rows, sz.part)
     grad_mix = swap_call(grad_mix, 3).reshape(4 * rows, sz.part)
-    g_proj = to_places(dot_tn(hid_mine, cot_all), got_proj)
+    g_proj = to_places(dot_tn(hid_mine, cot_all), got_proj, sz.proj_turn)
     partial_out = rowwise(dot_nn(act_hidden, w_proj).astype(bf16)).reshape(2, 2, rows, width)
     dq_before, dkv_before, out_sum = attend_back(
         sz, False, q, before, grad_mix, mix, lse, None, partial_out, 4
     )
     output = (residual + out_sum + vectors[7]).astype(bf16)
-    returned = permute(
-        dkv_before.astype(bf16), lambda py, pc, pz, px: (py, pc, pz - 1, px) if pz % 2 == 1 else None
-    )
-    g_fc = to_places(dot_tn(fc_mine, act_two), got_fc)
+    returned = permute(dkv_before.astype(bf16), lambda py, pc, pz, px: (py, pc, pz - 1, px) if pz % 2 == 1 else None)
+    g_fc = to_places(dot_tn(fc_mine, act_two), got_fc, sz.fc_turn)
     g_out = rowwise(dot_tn(jnp.pad(grad_attn, ((0, 0), (0, 4 * sz.part - width))), mixed).astype(bf16))
-    dq, dkv, g_out = attend_back(
-        sz, True, q, kv, grad_mix, mix, lse, dq_before, g_out.reshape(2, 2, sz.part, width), 5
-    )
+    dq, dkv, g_out = attend_back(sz, True, q, kv, grad_mix, mix, lse, dq_before, g_out.reshape(2, 2, sz.part, width), 5)
     g_out = g_out.reshape(2, sz.part // 2, width)
     got_out = to_other_y(pick(g_out, 1 - y))
     grad_qkv = jnp.concatenate([dq, (dkv + returned.astype(f32)).astype(bf16)], axis=1)
-    qkv_mine, qkv_other = halves_of(grad_qkv)
-    got_qkv = to_other_y(dot_tn(qkv_other, act_one))
+    g_qkv = rowwise(dot_tn(grad_qkv, act_one).astype(bf16)).reshape(4, 2, 3 * sz.part // 8, width)
+    half_qkv = lambda index: lax.dynamic_index_in_dim(g_qkv, index, 1, keepdims=False).reshape(-1, width)
+    got_qkv = to_other_y(half_qkv(1 - y))
     grad_one = quad_sum(rowwise(dot_nn(grad_qkv, w_qkv).astype(bf16)).reshape(2, 2, rows, width), 6)
     g_out = to_places(pick(g_out, y), got_out)
-    g_qkv = to_places(dot_tn(qkv_mine, act_one), got_qkv)
+    g_qkv = to_places(half_qkv(y), got_qkv)
 
     normed_one, rs_one = norm_parts(inputs)
     input_grad = (grad_res + norm_back(normed_one, rs_one, grad_one, vectors[0])).astype(bf16)
 
     def placed(vector):
-        spot = lax.dynamic_update_slice_in_dim(jnp.zeros((4 * sz.part,), f32), vector, quarter * sz.part, 0)
-        return spot[:width]
+        spread = jnp.zeros((sz.quarter_heads, 4, sz.head_size), f32)
+        spread = lax.dynamic_update_slice_in_dim(spread, vector.reshape(-1, 1, sz.head_size), quarter, 1)
+        return spread.reshape(4 * sz.part)[:width]
 
     sums = jnp.sum(grad_qkv.astype(f32), axis=0)
-    bias_sum = jnp.sum(grad_fc.astype(f32), axis=0).reshape(1, hidden // 4)
-    fc_rows = lax.dynamic_update_slice_in_dim(jnp.zeros((4, hidden // 4), f32), bias_sum, quarter, 0)
+    bias_sum = jnp.sum(grad_fc.astype(f32), axis=0).reshape(8, hidden // 32)[jnp.array(SPOTS)]
+    fc_rows = lax.dynamic_update_slice_in_dim(
+        jnp.zeros((hidden // 4 // GRAIN, 4, GRAIN), f32), bias_sum.reshape(-1, 1, GRAIN), quarter, 1
+    )
     grad_vectors = jnp.concatenate(
         [
             jnp.stack(

time: 1000 us -> 954 us (0.954)
  the two profiles are of different devices: /device:TPU:27 before, /device:TPU:0 now
where the time goes in v2:
time: 954 us; the launch traced here: 944 us
  Pallas kernels  575 us (60%)
  starting transfers between devices  119 us (12%)
  matrix products  113 us (12%)
  waiting for transfers between devices  60.4 us (6%)
  other arithmetic  39.2 us (4%)
  local copies, waits for them, and re-layouts  35.1 us (4%)
    ppermute x17, starting transfers between devices, permute(): return lax.ppermute(value, ('dp', 'cp'), pairs)  119 us
    pallas_call x1, Pallas kernels, forward_call(): pl.pallas_call(functools.partial(forward_kernel, sz.quarter_heads, sz.hea...  118 us
    pallas_call x1, Pallas kernels, acts_call(): pl.pallas_call(functools.partial(acts_kernel, sz.proj_turn), out_shape=(j...  117 us
    pallas_call x1, Pallas kernels, open_call(): pl.pallas_call(functools.partial(open_kernel, sz), out_shape=(like(8, sz....  108 us
    pallas_call x2, Pallas kernels, attend_back(): pl.pallas_call(functools.partial(attend_back_kernel, sz.quarter_heads, sz...  88.8 us
    pallas_call x2, Pallas kernels, quad_sum(): pl.pallas_call(quad_sum_kernel, out_shape=jax.ShapeDtypeStruct(partial.sh...  64.1 us
    pallas_call x1, Pallas kernels, collect(): pl.pallas_call(functools.partial(collect_kernel, sz), out_shape=(jax.Shap...  61.7 us
    ppermute x17, waiting for transfers between devices, permute(): return lax.ppermute(value, ('dp', 'cp'), pairs)  60.4 us
  transfers between devices with their start and end apart: 17, of which 6 were waited for; matrix products, arithmetic and copies ran while one was open for 8% of the time, Pallas kernels for 9%

profile of v2, /device:TPU:0, one launch (start us, length us, event | category | flops | bytes accessed | tf_op | source)
XLA Modules:
  0.0 943.8 jit_solution(15305265866585815045)
XLA Ops:
  5.0 107.9 %open.1 = (bf16[8,21,8,1600]{3,2,1,0:T(8,128)(2,1)}, bf16[8,7,8,1600]{3,2,1,0:T(8,128)(2,1)}, bf16[8,25,8,1600]{3,2,1,0:T(8,128)(2,1)}, bf16[8,25,8,1600]{3,2,1,...) custom-call(bf16[76,8,1600]{2,1,0:T(8,128)(2,1)} %bitcast.181, ...), custom_call_target="tpu_custom_call" | custom-call | tf_op jit(solution)/shard_map/open/pallas_call | solution.py:689
  129.4 8.1 add_convert_fusion.1.kv_ref.refs_1_
  137.5 4.4 add_convert_fusion.2.q_ref.refs_0_
  141.9 118.0 %forward.1 = (f32[1024,448]{1,0:T(8,128)}, f32[1024,8]{1,0:T(8,128)}, bf16[1024,896]{1,0:T(8,128)(2,1)}, bf16[4,256,448]{2,1,0:T(8,128)(2,1)}, bf16[8,7,8,1600]{...) custom-call(bf16[1024,448]{1,0:T(8,128)(2,1)} %add_convert_fusion.2., ...), custom_call_target="tpu_custom_call", output_to_operand_aliasing={{4}: (2, {}), {5}: (3, {}), {6}: (4, {})} | custom-call | bytes 360000000 | tf_op jit(solution)/shard_map/forward/pallas_call | solution.py:834
  261.7 4.9 fusion.103
  269.6 117.5 %acts.1 = (bf16[2,2,256,1600]{3,2,1,0:T(8,128)(2,1)}, bf16[8,25,8,1600]{3,2,1,0:T(8,128)(2,1)}) custom-call(bf16[256,1600]{1,0:T(8,128)(2,1)} %add_convert_fusion.4.act_ref, bf16[8,25,8,1600]{3,2,1,0:T(8,128)(2,1)} %get-tuple-element.36.proj_in), custom_call_target="tpu_custom_call", output_to_operand_aliasing={{1}: (1, {})} | custom-call | bytes 180000000 | tf_op jit(solution)/shard_map/acts/pallas_call | solution.py:874
  387.1 10.9 %fusion.104 = f32[1024,1600]{0,1:T(8,128)} fusion(bf16[1024,1600]{1,0:T(8,128)(2,1)} %bitcast.202, bf16[1600,1600]{1,0:T(8,128)(2,1)} %bitcast.162), kind=kOutput, calls=%fused_computation.178 | convolution fusion | flops 5242880000 | bytes 14950400 | tf_op jit(solution)/shard_map/dot_general | solution.py:307
  398.0 15.6 %convert_reduce_fusion = (f32[1600]{0:T(1024)S(1)}, bf16[1024,1600]{0,1:T(8,128)(2,1)S(1)}, bf16[1024,1600]{0,1:T(8,128)(2,1)}) fusion(f32[1024,1600]{0,1:T(8,128)} %fusion.104, f32[1600]{0:T(1024)S(1)} %add.376, bf16[1024,1600]{1,0:T(8,128)(2,1)S(1)} %bitcast.201, bf16[1600,1600]{1,0:T(8,128)(2,1)S(1)} %bitcast.157), kind=kOutput, calls=%fused_computation.20 | convolution fusion | flops 5290392064 | bytes 21516800 | tf_op jit(solution)/shard_map/dot_general | solution.py:307
  413.7 8.5 convolution_convert_fusion.4
  422.2 35.7 %quad_sum.2 = f32[256,1600]{1,0:T(8,128)} custom-call(bf16[2,2,256,1600]{3,2,1,0:T(8,128)(2,1)} %bitcast.173), custom_call_target="tpu_custom_call" | custom-call | bytes 90000000 | tf_op jit(solution)/shard_map/quad_sum/pallas_call | solution.py:992
  460.3 11.4 %convolution_convert_fusion.3 = bf16[1024,1600]{1,0:T(8,128)(2,1)} fusion(bf16[1024,1600]{0,1:T(8,128)(2,1)} %get-tuple-element.78, bf16[1600,1600]{1,0:T(8,128)(2,1)} %bitcast.156), kind=kOutput, calls=%fused_computation.32 | convolution fusion | flops 5244518400 | bytes 11673600 | tf_op jit(solution)/shard_map/dot_general | solution.py:315
  477.8 16.5 %swap.1 = bf16[4,256,448]{2,1,0:T(8,128)(2,1)} custom-call(bf16[4,256,448]{2,1,0:T(8,128)(2,1)} %copy.32.in_ref), custom_call_target="tpu_custom_call" | custom-call | bytes 60000000 | tf_op jit(solution)/shard_map/swap/pallas_call | solution.py:911
  494.4 31.2 %attend_back_before.1 = (f32[1024,448]{1,0:T(8,128)}, f32[1024,896]{1,0:T(8,128)}, f32[256,1600]{1,0:T(8,128)}) custom-call(bf16[1024,448]{1,0:T(8,128)(2,1)} %add_convert_fusion.2.q_ref.refs_0_, bf16[1024,896]{1,0:T(8,128)(2,1)} %get-tuple-element.35.refs_1_, bf16[1024,448]{1,0:T(8,128)(2,1)} %bitcast.160, f32[1024,448]{1,0:T(8,128)} %get-tuple-element.41.refs_3_, ...), custom_call_target="tpu_custom_call" | custom-call | bytes 105000000 | tf_op jit(solution)/shard_map/attend_back_before/pallas_call | solution.py:1209
  530.3 7.8 convolution_convert_fusion.5
  540.6 4.4 convolution_convert_fusion.1
  545.0 57.7 %attend_back_own.1 = (bf16[1024,448]{1,0:T(8,128)(2,1)}, f32[1024,896]{1,0:T(8,128)}, f32[448,1600]{1,0:T(8,128)}) custom-call(bf16[1024,448]{1,0:T(8,128)(2,1)} %add_convert_fusion.2.q_ref.refs_0_, bf16[1024,896]{1,0:T(8,128)(2,1)} %add_convert_fusion.1.kv_ref.refs_1_, bf16[1024,448]{1,0:T(8,128)(2,1)} %bitcast.161, f32[1024,448]{1,0:T(8,128)} %get-tuple-element.41.refs_3_, ...), custom_call_target="tpu_custom_call" | custom-call | bytes 105000000 | tf_op jit(solution)/shard_map/attend_back_own/pallas_call | solution.py:1209
  605.1 7.8 convolution_convert_fusion.6
  629.2 11.4 %collective-permute-start.7 = (bf16[56,1600]{1,0:T(8,128)(2,1)S(1)}, bf16[56,1600]{1,0:T(8,128)(2,1)S(1)}, u32[]{:S(2)}, u32[]{:S(2)}) collective-permute-start(bf16[56,1600]{1,0:T(8,128)(2,1)S(1)} %get-tuple-element.92), channel_id=1, source_target_pairs={{0,4},{1,5},{2,6},{3,7},{4,0},{5,1},{6,2},{7,3},{8,12},{9,13},{10,... | collective-permute-start | bytes 537608 | tf_op jit(solution)/shard_map/ppermute | solution.py:331
  640.6 5.0 collective-permute-done.6
  645.9 5.4 collective-permute-done.7
  655.3 7.4 convolution_convert_fusion.2
  663.2 28.4 %quad_sum.3 = f32[256,1600]{1,0:T(8,128)} custom-call(bf16[2,2,256,1600]{3,2,1,0:T(8,128)(2,1)} %bitcast.172), custom_call_target="tpu_custom_call" | custom-call | bytes 90000000 | tf_op jit(solution)/shard_map/quad_sum/pallas_call | solution.py:992
  691.5 8.0 convolution_convert_fusion
  706.2 7.0 convert_add_fusion
  713.6 5.1 collective-permute-start.14
  718.7 4.9 convert_add_fusion.1
  727.0 27.3 %collective-permute-done.1 = bf16[672,1600]{1,0:T(8,128)(2,1)} collective-permute-done((bf16[672,1600]{1,0:T(8,128)(2,1)}, bf16[672,1600]{1,0:T(8,128)(2,1)}, u32[]{:S(2)}, u32[]{:S(2)}) %collective-permute-start.1) | collective-permute-done | bytes 2150432 | tf_op jit(solution)/shard_map/ppermute | solution.py:331
  757.3 4.1 collective-permute-start.16
  762.6 57.0 %collective-permute-start.2 = (bf16[168,1600]{1,0:T(8,128)(2,1)S(1)}, bf16[168,1600]{1,0:T(8,128)(2,1)S(1)}, u32[]{:S(2)}, u32[]{:S(2)}) collective-permute-start(bf16[168,1600]{1,0:T(8,128)(2,1)S(1)} %get-tuple-element.85), channel_id=1, source_target_pairs={{0,2},{1,3},{2,4},{3,5},{4,6},{5,7},{6,0},{7,1},{8,10},{9,11},{10,... | collective-permute-start | bytes 1612808 | tf_op jit(solution)/shard_map/ppermute | solution.py:331
  821.6 27.2 %collective-permute-start.4 = (bf16[168,1600]{1,0:T(8,128)(2,1)S(1)}, bf16[168,1600]{1,0:T(8,128)(2,1)S(1)}, u32[]{:S(2)}, u32[]{:S(2)}) collective-permute-start(bf16[168,1600]{1,0:T(8,128)(2,1)S(1)} %get-tuple-element.86), channel_id=1, source_target_pairs={{0,6},{1,7},{2,0},{3,1},{4,2},{5,3},{6,4},{7,5},{8,14},{9,15},{10,... | collective-permute-start | bytes 1612808 | tf_op jit(solution)/shard_map/ppermute | solution.py:331
  851.1 17.8 %collective-permute-done.3 = bf16[168,1600]{1,0:T(8,128)(2,1)S(1)} collective-permute-done((bf16[168,1600]{1,0:T(8,128)(2,1)S(1)}, bf16[168,1600]{1,0:T(8,128)(2,1)S(1)}, u32[]{:S(2)}, u32[]{:S(2)}) %collective-permute-start.3) | collective-permute-done | bytes 537632 | tf_op jit(solution)/shard_map/ppermute | solution.py:331
  870.1 61.7 %collect.1 = (bf16[76,8,1600]{2,1,0:T(8,128)(2,1)}, f32[32,2,8,1600]{3,2,1,0:T(8,128)}) custom-call(bf16[21,8,1600]{2,1,0:T(8,128)(2,1)} %fusion.87.qkv_ref, bf16[7,8,1600]{2,1,0:T(8,128)(2,1)} %fusion.94.out_ref, bf16[25,8,1600]{2,1,0:T(8,128)(2,1)} %fusion.82.fc_ref, bf16[25,8,1600]{2,1,0:T(8,128)(2,1)} %fusion.83.proj_ref, ...), custom_call_target="tpu_custom_call" | custom-call | tf_op jit(solution)/shard_map/collect/pallas_call | solution.py:1110
  (188 shorter events, 96.1 us)
Async XLA Ops:
  113.0 12.2 %copy-start.1 = (bf16[2,2,256,1600]{3,2,1,0:T(8,128)(2,1)S(1)}, bf16[2,2,256,1600]{3,2,1,0:T(8,128)(2,1)}, u32[]{:S(2)}) copy-start(bf16[2,2,256,1600]{3,2,1,0:T(8,128)(2,1)} %get-tuple-element.27) | copy-start | bytes 9830404
  114.0 12.3 %copy-start.17 = (f32[16,1600]{1,0:T(8,128)}, f32[16,1600]{1,0:T(8,128)S(1)}, u32[]{:S(2)}) copy-start(f32[16,1600]{1,0:T(8,128)S(1)} %bitcast_convert_fusion) | copy-start | bytes 307204
  387.1 10.9 %copy-start.2 = (bf16[8,25,8,1600]{3,2,1,0:T(8,128)(2,1)S(1)}, bf16[8,25,8,1600]{3,2,1,0:T(8,128)(2,1)}, u32[]{:S(2)}) copy-start(bf16[8,25,8,1600]{3,2,1,0:T(8,128)(2,1)} %get-tuple-element.40) | copy-start | bytes 15360004
  387.1 10.9 %copy-start.21 = (bf16[2,2,256,1600]{3,2,1,0:T(8,128)(2,1)S(1)}, bf16[2,2,256,1600]{3,2,1,0:T(8,128)(2,1)}, u32[]{:S(2)}) copy-start(bf16[2,2,256,1600]{3,2,1,0:T(8,128)(2,1)} %get-tuple-element.39) | copy-start | bytes 9830404
  387.1 26.6 %slice-start = ((s8[5324800]{0:T(1024)(128)(4,1)}), s8[4194304]{0:T(1024)(128)(4,1)S(1)}, s32[]{:S(2)}) async-start(s8[5324800]{0:T(1024)(128)(4,1)} %bitcast.163), calls=%async_computation | async-start | bytes 8388608
  398.0 15.7 %slice-start.1 = ((s8[5324800]{0:T(1024)(128)(4,1)}), s8[1130496]{0:T(1024)(128)(4,1)S(1)}, s32[]{:S(2)}) async-start(s8[5324800]{0:T(1024)(128)(4,1)} %bitcast.163), calls=%async_computation.1 | async-start | bytes 2260992
  457.9 16.1 %slice-start.3 = ((s8[5963776]{0:T(1024)(128)(4,1)}), s8[4194304]{0:T(1024)(128)(4,1)S(1)}, s32[]{:S(2)}) async-start(s8[5963776]{0:T(1024)(128)(4,1)} %bitcast.191), calls=%async_computation.3 | async-start | bytes 8388608
  460.2 11.4 %copy-start.4 = (f32[256,1600]{1,0:T(8,128)S(1)}, f32[256,1600]{1,0:T(8,128)}, u32[]{:S(2)}) copy-start(f32[256,1600]{1,0:T(8,128)} %quad_sum.2) | copy-start | bytes 4915204
  460.2 11.4 %copy-start.6 = (bf16[256,1600]{1,0:T(8,128)(2,1)S(1)}, bf16[256,1600]{1,0:T(8,128)(2,1)}, u32[]{:S(2)}) copy-start(bf16[256,1600]{1,0:T(8,128)(2,1)} %copy.25.cot_ref) | copy-start | bytes 2457604
  460.2 13.7 %slice-start.4 = ((s8[5963776]{0:T(1024)(128)(4,1)}), s8[1769472]{0:T(1024)(128)(4,1)S(1)}, s32[]{:S(2)}) async-start(s8[5963776]{0:T(1024)(128)(4,1)} %bitcast.191), calls=%async_computation.4 | async-start | bytes 3538944
  529.0 123.0 %collective-permute-start = (bf16[1024,896]{1,0:T(8,128)(2,1)}, bf16[1024,896]{1,0:T(8,128)(2,1)}, u32[]{:S(2)}, u32[]{:S(2)}) collective-permute-start(bf16[1024,896]{1,0:T(8,128)(2,1)} %convert_element_type.266), channel_id=1, source_target_pairs={{2,0},{3,1},{6,4},{7,5},{10,8},{11,9},{14,12},{15,13},{18,16},{19,... | collective-permute-start | bytes 5505032 | tf_op jit(solution)/shard_map/ppermute | solution.py:331
  530.3 10.3 %copy-start.11 = (bf16[256,1600]{1,0:T(8,128)(2,1)S(1)}, bf16[256,1600]{1,0:T(8,128)(2,1)}, u32[]{:S(2)}) copy-start(bf16[256,1600]{1,0:T(8,128)(2,1)} %copy-done.10) | copy-start | bytes 2457604
  538.1 168.1 %collective-permute-start.13 = (bf16[800,1600]{1,0:T(8,128)(2,1)}, bf16[800,1600]{1,0:T(8,128)(2,1)}, u32[]{:S(2)}, u32[]{:S(2)}) collective-permute-start(bf16[800,1600]{1,0:T(8,128)(2,1)} %convolution_convert_fusion.5), channel_id=1, source_target_pairs={{0,16},{1,17},{2,18},{3,19},{4,20},{5,21},{6,22},{7,23},{8,24},{9,... | collective-permute-start | bytes 7680008 | tf_op jit(solution)/shard_map/ppermute | solution.py:331
  605.0 18.4 %collective-permute-start.5 = (bf16[224,1600]{1,0:T(8,128)(2,1)}, bf16[224,1600]{1,0:T(8,128)(2,1)}, u32[]{:S(2)}, u32[]{:S(2)}) collective-permute-start(bf16[224,1600]{1,0:T(8,128)(2,1)} %fusion.73), channel_id=1, source_target_pairs={{0,16},{1,17},{2,18},{3,19},{4,20},{5,21},{6,22},{7,23},{8,24},{9,... | collective-permute-start | bytes 2150408 | tf_op jit(solution)/shard_map/ppermute | solution.py:331
  619.2 32.9 %copy-start.9 = (f32[1024,896]{1,0:T(8,128)S(1)}, f32[1024,896]{1,0:T(8,128)}, u32[]{:S(2)}) copy-start(f32[1024,896]{1,0:T(8,128)} %get-tuple-element.46) | copy-start | bytes 11010052
  623.4 31.9 %slice-start.5 = ((s8[4472832]{0:T(1024)(128)(4,1)}), s8[4194304]{0:T(1024)(128)(4,1)S(1)}, s32[]{:S(2)}) async-start(s8[4472832]{0:T(1024)(128)(4,1)} %bitcast.196), calls=%async_computation.5 | async-start | bytes 8388608
  625.4 20.2 %collective-permute-start.6 = (bf16[56,1600]{1,0:T(8,128)(2,1)S(1)}, bf16[56,1600]{1,0:T(8,128)(2,1)S(1)}, u32[]{:S(2)}, u32[]{:S(2)}) collective-permute-start(bf16[56,1600]{1,0:T(8,128)(2,1)S(1)} %get-tuple-element.90), channel_id=1, source_target_pairs={{0,2},{1,3},{2,4},{3,5},{4,6},{5,7},{6,0},{7,1},{8,10},{9,11},{10,... | collective-permute-start | bytes 537608 | tf_op jit(solution)/shard_map/ppermute | solution.py:331
  629.2 22.0 %collective-permute-start.7 = (bf16[56,1600]{1,0:T(8,128)(2,1)S(1)}, bf16[56,1600]{1,0:T(8,128)(2,1)S(1)}, u32[]{:S(2)}, u32[]{:S(2)}) collective-permute-start(bf16[56,1600]{1,0:T(8,128)(2,1)S(1)} %get-tuple-element.92), channel_id=1, source_target_pairs={{0,4},{1,5},{2,6},{3,7},{4,0},{5,1},{6,2},{7,3},{8,12},{9,13},{10,... | collective-permute-start | bytes 537608 | tf_op jit(solution)/shard_map/ppermute | solution.py:331
  640.6 10.7 %collective-permute-start.8 = (bf16[56,1600]{1,0:T(8,128)(2,1)S(1)}, bf16[56,1600]{1,0:T(8,128)(2,1)S(1)}, u32[]{:S(2)}, u32[]{:S(2)}) collective-permute-start(bf16[56,1600]{1,0:T(8,128)(2,1)S(1)} %get-tuple-element.91), channel_id=1, source_target_pairs={{0,6},{1,7},{2,0},{3,1},{4,2},{5,3},{6,4},{7,5},{8,14},{9,15},{10,... | collective-permute-start | bytes 537608 | tf_op jit(solution)/shard_map/ppermute | solution.py:331
  645.6 73.1 %collective-permute-start.9 = (bf16[800,1600]{1,0:T(8,128)(2,1)}, bf16[800,1600]{1,0:T(8,128)(2,1)}, u32[]{:S(2)}, u32[]{:S(2)}) collective-permute-start(bf16[800,1600]{1,0:T(8,128)(2,1)} %convolution_convert_fusion.6), channel_id=1, source_target_pairs={{0,16},{1,17},{2,18},{3,19},{4,20},{5,21},{6,22},{7,23},{8,24},{9,... | collective-permute-start | bytes 7680008 | tf_op jit(solution)/shard_map/ppermute | solution.py:331
  703.0 51.3 %collective-permute-start.1 = (bf16[672,1600]{1,0:T(8,128)(2,1)}, bf16[672,1600]{1,0:T(8,128)(2,1)}, u32[]{:S(2)}, u32[]{:S(2)}) collective-permute-start(bf16[672,1600]{1,0:T(8,128)(2,1)} %bitcast.23), channel_id=1, source_target_pairs={{0,16},{1,17},{2,18},{3,19},{4,20},{5,21},{6,22},{7,23},{8,24},{9,... | collective-permute-start | bytes 6451208 | tf_op jit(solution)/shard_map/ppermute | solution.py:331
  706.2 12.5 %copy-start.24 = (bf16[1024,1600]{0,1:T(8,128)(2,1)S(1)}, bf16[1024,1600]{0,1:T(8,128)(2,1)}, u32[]{:S(2)}) copy-start(bf16[1024,1600]{0,1:T(8,128)(2,1)} %copy-done.23) | copy-start | bytes 9830404
  713.6 43.7 %collective-permute-start.14 = (bf16[200,1600]{1,0:T(8,128)(2,1)S(1)}, bf16[200,1600]{1,0:T(8,128)(2,1)S(1)}, u32[]{:S(2)}, u32[]{:S(2)}) collective-permute-start(bf16[200,1600]{1,0:T(8,128)(2,1)S(1)} %get-tuple-element.79), channel_id=1, source_target_pairs={{0,2},{1,3},{2,4},{3,5},{4,6},{5,7},{6,0},{7,1},{8,10},{9,11},{10,... | collective-permute-start | bytes 1920008 | tf_op jit(solution)/shard_map/ppermute | solution.py:331
  718.7 131.2 %collective-permute-start.15 = (bf16[200,1600]{1,0:T(8,128)(2,1)S(1)}, bf16[200,1600]{1,0:T(8,128)(2,1)S(1)}, u32[]{:S(2)}, u32[]{:S(2)}) collective-permute-start(bf16[200,1600]{1,0:T(8,128)(2,1)S(1)} %get-tuple-element.81), channel_id=1, source_target_pairs={{0,4},{1,5},{2,6},{3,7},{4,0},{5,1},{6,2},{7,3},{8,12},{9,13},{10,... | collective-permute-start | bytes 1920008 | tf_op jit(solution)/shard_map/ppermute | solution.py:331
  723.6 31.6 %copy-start.5 = (bf16[4,1,168,1600]{3,2,1,0:T(8,128)(2,1)S(1)}, bf16[4,1,168,1600]{3,2,1,0:T(8,128)(2,1)}, u32[]{:S(2)}) copy-start(bf16[4,1,168,1600]{3,2,1,0:T(8,128)(2,1)} %get-tuple-element.88) | copy-start | bytes 6451204
  723.9 38.7 %collective-permute-start.10 = (bf16[200,1600]{1,0:T(8,128)(2,1)S(1)}, bf16[200,1600]{1,0:T(8,128)(2,1)S(1)}, u32[]{:S(2)}, u32[]{:S(2)}) collective-permute-start(bf16[200,1600]{1,0:T(8,128)(2,1)S(1)} %get-tuple-element.82), channel_id=1, source_target_pairs={{0,2},{1,3},{2,4},{3,5},{4,6},{5,7},{6,0},{7,1},{8,10},{9,11},{10,... | collective-permute-start | bytes 1920008 | tf_op jit(solution)/shard_map/ppermute | solution.py:331
  725.3 94.3 %collective-permute-start.11 = (bf16[200,1600]{1,0:T(8,128)(2,1)S(1)}, bf16[200,1600]{1,0:T(8,128)(2,1)S(1)}, u32[]{:S(2)}, u32[]{:S(2)}) collective-permute-start(bf16[200,1600]{1,0:T(8,128)(2,1)S(1)} %get-tuple-element.84), channel_id=1, source_target_pairs={{0,4},{1,5},{2,6},{3,7},{4,0},{5,1},{6,2},{7,3},{8,12},{9,13},{10,... | collective-permute-start | bytes 1920008 | tf_op jit(solution)/shard_map/ppermute | solution.py:331
  754.3 67.2 %collective-permute-start.12 = (bf16[200,1600]{1,0:T(8,128)(2,1)S(1)}, bf16[200,1600]{1,0:T(8,128)(2,1)S(1)}, u32[]{:S(2)}, u32[]{:S(2)}) collective-permute-start(bf16[200,1600]{1,0:T(8,128)(2,1)S(1)} %get-tuple-element.83), channel_id=1, source_target_pairs={{0,6},{1,7},{2,0},{3,1},{4,2},{5,3},{6,4},{7,5},{8,14},{9,15},{10,... | collective-permute-start | bytes 1920008 | tf_op jit(solution)/shard_map/ppermute | solution.py:331
  757.3 92.6 %collective-permute-start.16 = (bf16[200,1600]{1,0:T(8,128)(2,1)S(1)}, bf16[200,1600]{1,0:T(8,128)(2,1)S(1)}, u32[]{:S(2)}, u32[]{:S(2)}) collective-permute-start(bf16[200,1600]{1,0:T(8,128)(2,1)S(1)} %get-tuple-element.80), channel_id=1, source_target_pairs={{0,6},{1,7},{2,0},{3,1},{4,2},{5,3},{6,4},{7,5},{8,14},{9,15},{10,... | collective-permute-start | bytes 1920008 | tf_op jit(solution)/shard_map/ppermute | solution.py:331
  762.6 88.5 %collective-permute-start.2 = (bf16[168,1600]{1,0:T(8,128)(2,1)S(1)}, bf16[168,1600]{1,0:T(8,128)(2,1)S(1)}, u32[]{:S(2)}, u32[]{:S(2)}) collective-permute-start(bf16[168,1600]{1,0:T(8,128)(2,1)S(1)} %get-tuple-element.85), channel_id=1, source_target_pairs={{0,2},{1,3},{2,4},{3,5},{4,6},{5,7},{6,0},{7,1},{8,10},{9,11},{10,... | collective-permute-start | bytes 1612808 | tf_op jit(solution)/shard_map/ppermute | solution.py:331
  819.6 49.3 %collective-permute-start.3 = (bf16[168,1600]{1,0:T(8,128)(2,1)S(1)}, bf16[168,1600]{1,0:T(8,128)(2,1)S(1)}, u32[]{:S(2)}, u32[]{:S(2)}) collective-permute-start(bf16[168,1600]{1,0:T(8,128)(2,1)S(1)} %get-tuple-element.87), channel_id=1, source_target_pairs={{0,4},{1,5},{2,6},{3,7},{4,0},{5,1},{6,2},{7,3},{8,12},{9,13},{10,... | collective-permute-start | bytes 1612808 | tf_op jit(solution)/shard_map/ppermute | solution.py:331
  821.6 47.4 %collective-permute-start.4 = (bf16[168,1600]{1,0:T(8,128)(2,1)S(1)}, bf16[168,1600]{1,0:T(8,128)(2,1)S(1)}, u32[]{:S(2)}, u32[]{:S(2)}) collective-permute-start(bf16[168,1600]{1,0:T(8,128)(2,1)S(1)} %get-tuple-element.86), channel_id=1, source_target_pairs={{0,6},{1,7},{2,0},{3,1},{4,2},{5,3},{6,4},{7,5},{8,14},{9,15},{10,... | collective-permute-start | bytes 1612808 | tf_op jit(solution)/shard_map/ppermute | solution.py:331
  (17 other events, 80.8 us)

commit v3 on v2

--- a/solution.py
+++ b/solution.py
@@ -423,47 +423,82 @@
 
 
 class PlaceGather:
-    def __init__(self, wires, full, slot):
-        self.wires = wires
+    def __init__(self, wires, full, slot, along=True, over=True):
         self.full = full
-        self.slot = slot
         self.dp, self.cp = lax.axis_index("dp"), lax.axis_index("cp")
         self.y, self.z, self.x = self.dp // 2, self.cp // 2, self.cp % 2
-        self.started = []
-
-    def send(self, slot, dp, cp):
-        view = self.full.at[slot]
-        copy = self.wires.to(view, view, dp, cp)
-        copy.start()
-        self.started.append(copy)
-        return copy
+        self.above = (self.dp, ((self.z + 1) % 4) * 2 + self.x)
+        self.below = (self.dp, ((self.z + 3) % 4) * 2 + self.x)
+        self.across = ((self.dp + 2) % 4, self.cp)
+
+        def share(by, to):
+            view = full.at[slot(self.y, (self.z + 4 + by) % 4)]
+            return wires.to(view, view, *to)
+
+        if along:
+            self.up = [share(1 - k, self.above) for k in (1, 2, 3)]
+            self.down = [share(k - 1, self.below) for k in (1, 2, 3)]
+        self.own_over = share(0, self.across) if over else None
+        self.over = [self.own_over] + [share(d, self.across) if along else None for d in (1, 2, 3)]
 
     def partners(self):
-        along = [(self.dp, ((self.z + d) % 4) * 2 + self.x) for d in (1, 2, 3)]
-        return along + [((self.dp + 2) % 4, self.cp)]
+        return [self.above, self.below, self.across]
 
     def start_over(self):
-        self.over = [self.send(self.slot(self.y, self.z), (self.dp + 2) % 4, self.cp)]
-
-    def start(self, over=True):
-        mine = self.slot(self.y, self.z)
-        self.along = []
-        for d in (1, 3, 2):
-            self.along.append((d, self.send(mine, self.dp, ((self.z + d) % 4) * 2 + self.x)))
-        self.over = []
-        if over:
+        self.own_over.start()
+
+    def start(self):
+        @pl.when(self.z < 3)
+        def _():
+            self.up[0].start()
+
+        @pl.when(self.z > 0)
+        def _():
+            self.down[0].start()
+
+        if self.own_over is not None:
             self.start_over()
 
-    def forward(self):
-        for d, copy in self.along:
+    def forward(self, steps=(1, 2, 3)):
+        for k in steps:
+
+            @pl.when(self.z >= k)
+            def _():
+                self.up[k - 1].wait_recv()
+                if k < 3:
+
+                    @pl.when(self.z < 3)
+                    def _():
+                        self.up[k].start()
+
+                self.over[4 - k].start()
+
+            @pl.when(self.z <= 3 - k)
+            def _():
+                self.down[k - 1].wait_recv()
+                if k < 3:
+
+                    @pl.when(self.z > 0)
+                    def _():
+                        self.down[k].start()
+
+                self.over[k].start()
+
+    def finish(self):
+        sent_over = [copy for copy in self.over if copy is not None]
+        for copy in sent_over:
             copy.wait_recv()
-            self.over.append(self.send(self.slot(self.y, (self.z - d + 4) % 4), (self.dp + 2) % 4, self.cp))
-
-    def finish(self):
-        for copy in self.over:
-            copy.wait_recv()
-        for copy in self.started:
+        for copy in sent_over:
             copy.wait_send()
+        for k in (1, 2, 3):
+
+            @pl.when(jnp.logical_and(self.z >= k - 1, self.z < 3))
+            def _():
+                self.up[k - 1].wait_send()
+
+            @pl.when(jnp.logical_and(self.z <= 4 - k, self.z > 0))
+            def _():
+                self.down[k - 1].wait_send()
 
 
 class QuadGather:
@@ -702,7 +737,7 @@
         scratch_shapes=[
             pltpu.SemaphoreType.DMA((sz.block + 3 * sz.head_grains + sz.spill + 32,)),
             pltpu.SemaphoreType.DMA((5,)),
-            *wire_sems(13),
+            *wire_sems(16),
             pltpu.SemaphoreType.DMA((2,)),
         ],
         compiler_params=REMOTE,
@@ -725,15 +760,11 @@
     odd = z % 2 == 1
     w_out = PlaceGather(wires, out_ref, slot_out)
     w_fc = PlaceGather(wires, fc_ref, slot_turned(fc_turn))
-    w_proj = PlaceGather(wires, proj_ref, slot_turned(proj_turn))
+    w_proj = PlaceGather(wires, proj_ref, slot_turned(proj_turn), along=False)
     others = [(c, 1 - x), (1 - c, x), (1 - c, 1 - x)]
     quad = [(y * 2 + tc, z * 2 + tx) for tc, tx in others]
     greet(w_out.partners() + quad)
     keys = wires.to(kv_ref, before_ref, dp, (cp + 2) % 8)
-
-    @pl.when(jnp.logical_not(odd))
-    def _():
-        keys.start()
 
     w_out.start()
     w_fc.start()
@@ -762,6 +793,12 @@
     lax.fori_loop(0, 2, own, 0)
     w_out.forward()
 
+    @pl.when(jnp.logical_not(odd))
+    def _():
+        keys.start()
+
+    w_fc.forward((1,))
+
     def add_before(index, _):
         here = pl.ds(pl.multiple_of(index * blk, blk), blk)
         keys_at = pl.ds(pl.multiple_of((index * blk) // rows * rows, rows), rows)
@@ -783,6 +820,10 @@
     whole = QuadGather(wires, out_ref, out_all, local_sems.at[0])
     whole.start()
 
+    @pl.when(z < 3)
+    def _():
+        w_fc.forward((2,))
+
     @pl.when(odd)
     def _():
         keys.wait_recv()
@@ -794,6 +835,11 @@
         return 0
 
     lax.fori_loop(0, 2 * rows // blk, round_off, 0)
+
+    @pl.when(z == 3)
+    def _():
+        w_fc.forward((2,))
+
     w_proj.start_over()
     mine = c * 2 + x
     each = rows // 2
@@ -807,7 +853,7 @@
         stage.at[pl.ds(pl.multiple_of(mine * each, each), each)], mixed_ref.at[mine], local_sems.at[1]
     )
     local.start()
-    w_fc.forward()
+    w_fc.forward((3,))
     whole.forward()
     for copy in swaps:
         copy.wait_recv()
@@ -848,7 +894,7 @@
         input_output_aliases={2: 4, 3: 5, 4: 6},
         scratch_shapes=[
             pltpu.VMEM((rows, part), jnp.bfloat16),
-            *wire_sems(22),
+            *wire_sems(37),
             pltpu.SemaphoreType.DMA((2,)),
         ],
         cost_estimate=cost(120),
@@ -860,14 +906,36 @@
 def acts_kernel(proj_turn, act_ref, proj_in, act_all, proj_ref, send_sems, recv_sems, local_sem):
     wires = Wires(send_sems, recv_sems)
     quad = QuadGather(wires, act_ref, act_all, local_sem)
-    places = PlaceGather(wires, proj_ref, slot_turned(proj_turn))
+    places = PlaceGather(wires, proj_ref, slot_turned(proj_turn), over=False)
     greet(places.partners() + [quad.over_x, quad.over_c])
     quad.start()
-    places.start(False)
+    places.start()
     quad.forward()
     places.forward()
     quad.finish()
     places.finish()
+
+
+def grads_kernel(act_ref, act_all, send_sems, recv_sems, local_sem):
+    wires = Wires(send_sems, recv_sems)
+    quad = QuadGather(wires, act_ref, act_all, local_sem)
+    greet([quad.over_x, quad.over_c])
+    quad.start()
+    quad.forward()
+    quad.finish()
+
+
+def grads_call(act, ident):
+    return pl.pallas_call(
+        grads_kernel,
+        out_shape=jax.ShapeDtypeStruct((2, 2) + act.shape, act.dtype),
+        in_specs=[VMEM],
+        out_specs=HBM,
+        scratch_shapes=[*wire_sems(3), pltpu.SemaphoreType.DMA],
+        cost_estimate=cost(25),
+        compiler_params=remote_params(ident),
+        name="grads",
+    )(act)
 
 
 def acts_call(sz, act, w_proj):
@@ -880,44 +948,11 @@
         in_specs=[VMEM, HBM],
         out_specs=[HBM] * 2,
         input_output_aliases={1: 1},
-        scratch_shapes=[*wire_sems(9), pltpu.SemaphoreType.DMA],
+        scratch_shapes=[*wire_sems(13), pltpu.SemaphoreType.DMA],
         cost_estimate=cost(60),
         compiler_params=remote_params(2),
         name="acts",
     )(act, w_proj)
-
-
-def swap_kernel(in_ref, out_ref, send_sems, recv_sems, local_sem):
-    y, c, z, x = my_place()
-    wires = Wires(send_sems, recv_sems)
-    mine = c * 2 + x
-    others = [(1 - c, 1 - x), (c, 1 - x), (1 - c, x)]
-    greet([(y * 2 + tc, z * 2 + tx) for tc, tx in others])
-    copies = []
-    for tc, tx in others:
-        copies.append(wires.to(in_ref.at[tc * 2 + tx], out_ref.at[mine], y * 2 + tc, z * 2 + tx))
-    for copy in copies:
-        copy.start()
-    local = pltpu.make_async_copy(in_ref.at[mine], out_ref.at[mine], local_sem)
-    local.start()
-    for copy in copies:
-        copy.wait_recv()
-    for copy in copies:
-        copy.wait_send()
-    local.wait()
-
-
-def swap_call(value, ident):
-    return pl.pallas_call(
-        swap_kernel,
-        out_shape=jax.ShapeDtypeStruct(value.shape, value.dtype),
-        in_specs=[VMEM],
-        out_specs=VMEM,
-        scratch_shapes=[*wire_sems(3), pltpu.SemaphoreType.DMA],
-        compiler_params=remote_params(ident),
-        cost_estimate=cost(20),
-        name="swap",
-    )(value)
 
 
 class QuadSum:
@@ -1001,137 +1036,170 @@
     )(partial)
 
 
-def collect_kernel(sz, qkv_ref, out_ref, fc_ref, proj_ref, vec_ref, g_ref, vecs_ref, send_sems, recv_sem, vec_sems):
-    y, c, z, x = my_place()
-    me = flat_id(y, c, z, x)
-    quarter = c * 2 + x
-
-    def send(ref, slot, table, sem):
-        dest = table // sz.block
-        mine = dest == me
-
-        @pl.when(mine)
+class Collector:
+    def __init__(self, sz):
+        self.sz = sz
+        self.y, self.c, self.z, self.x = my_place()
+        self.me = flat_id(self.y, self.c, self.z, self.x)
+        self.quarter = self.c * 2 + self.x
+
+    def send(self, src, dst, table, sem, recv):
+        dest = table // self.sz.block
+
+        @pl.when(dest == self.me)
         def _():
-            pltpu.make_async_copy(ref.at[slot], g_ref.at[table % sz.block], recv_sem).start()
-
-        @pl.when(jnp.logical_not(mine))
+            pltpu.make_async_copy(src, dst, recv).start()
+
+        @pl.when(dest != self.me)
         def _():
             pltpu.make_async_remote_copy(
-                src_ref=ref.at[slot],
-                dst_ref=g_ref.at[table % sz.block],
+                src_ref=src,
+                dst_ref=dst,
                 send_sem=sem,
-                recv_sem=recv_sem,
+                recv_sem=recv,
                 device_id=(dest // 8, dest % 8),
                 device_id_type=MESH,
             ).start()
 
-    def sent(ref, slot, table, sem):
-        @pl.when(table // sz.block != me)
+    def sent(self, src, dst, table, sem, recv):
+        @pl.when(table // self.sz.block != self.me)
         def _():
-            pltpu.make_async_copy(ref.at[slot], ref.at[slot], sem).wait()
+            pltpu.make_async_copy(src, src, sem).wait()
+
+    def received(self, first, count, view, recv):
+        block = self.sz.block
+        for device in range(first // block, -(-(first + count) // block)):
+            grains = min(first + count, (device + 1) * block) - max(first, device * block)
+
+            @pl.when(self.me == device)
+            def _():
+                pltpu.make_async_copy(view(grains), view(grains), recv).wait()
+
+
+def collect_mlp_kernel(sz, fc_ref, proj_ref, g_ref, send_sems, recv_sem):
+    to = Collector(sz)
+
+    def run(act):
+        for ref, base, turn, first_sem in (
+            (fc_ref, sz.fc_start, sz.fc_turn, 0), (proj_ref, sz.proj_start, sz.proj_turn, sz.mlp)
+        ):
+            r = range_of_spot(to.y, (to.z + 4 - turn) % 4)
+
+            def one(slot, _):
+                table = base + 4 * (r * sz.mlp + slot) + to.quarter
+                act(ref.at[slot], g_ref.at[table % sz.block], table, send_sems.at[first_sem + slot], recv_sem)
+                return 0
+
+            lax.fori_loop(0, sz.mlp, one, 0)
+
+    run(to.send)
+    run(to.sent)
+    to.received(sz.fc_start, 64 * sz.mlp, lambda n: g_ref.at[pl.ds(0, n)], recv_sem)
+
+
+def collect_mlp(sz, fc, proj):
+    return pl.pallas_call(
+        functools.partial(collect_mlp_kernel, sz),
+        out_shape=jax.ShapeDtypeStruct((sz.block, GRAIN, fc.shape[-1]), fc.dtype),
+        in_specs=[HBM] * 2,
+        out_specs=HBM,
+        scratch_shapes=[pltpu.SemaphoreType.DMA((2 * sz.mlp,)), pltpu.SemaphoreType.DMA],
+        cost_estimate=cost(30),
+        compiler_params=REMOTE,
+        name="collect_mlp",
+    )(fc, proj)
+
+
+def collect_rest_kernel(
+    sz, qkv_ref, out_ref, vec_ref, g_ref, outs_ref, vecs_ref, qkv_sems, out_sems, vec_sems, recv_sems
+):
+    to = Collector(sz)
+    out_share = out_ref.shape[0]
 
     def run(act):
         def heads(slot, _):
-            local = slot_qkv(y, z) * sz.qkv + slot
+            local = slot_qkv(to.y, to.z) * sz.qkv + slot
             inner = local % sz.part_grains
-            head = 4 * (inner // sz.head_grains) + quarter
+            head = 4 * (inner // sz.head_grains) + to.quarter
 
             @pl.when(head < sz.heads)
             def _():
                 table = (local // sz.part_grains) * sz.width_grains + head * sz.head_grains + inner % sz.head_grains
-                act(qkv_ref, slot, table, send_sems.at[slot])
+                act(qkv_ref.at[slot], g_ref.at[table % sz.block], table, qkv_sems.at[slot], recv_sems.at[0])
 
             return 0
 
         lax.fori_loop(0, sz.qkv, heads, 0)
 
         def outward(slot, _):
-            local = quarter * sz.part_grains + slot_out(y, z) * sz.out + slot
-
-            @pl.when(local < sz.width_grains)
-            def _():
-                act(out_ref, slot, sz.out_start + local, send_sems.at[sz.qkv + slot])
-
+            table = sz.out_start + slot_out(to.y, to.z) * out_share + slot
+            dst = outs_ref.at[to.quarter, table % sz.block]
+            act(out_ref.at[slot], dst, table, out_sems.at[slot], recv_sems.at[1])
             return 0
 
-        lax.fori_loop(0, sz.out, outward, 0)
-
-        def plain(ref, base, turn, first_sem):
-            r = range_of_spot(y, (z + 4 - turn) % 4)
-
-            def one(slot, _):
-                table = base + 4 * (r * sz.mlp + slot) + quarter
-                act(ref, slot, table, send_sems.at[first_sem + slot])
-                return 0
-
-            lax.fori_loop(0, sz.mlp, one, 0)
-
-        plain(fc_ref, sz.fc_start, sz.fc_turn, sz.qkv + sz.out)
-        plain(proj_ref, sz.proj_start, sz.proj_turn, sz.qkv + sz.out + sz.mlp)
+        lax.fori_loop(0, out_share, outward, 0)
 
     last = sz.vec_start // sz.block
     vec_copy = pltpu.make_async_remote_copy(
         src_ref=vec_ref,
-        dst_ref=vecs_ref.at[me],
+        dst_ref=vecs_ref.at[to.me],
         send_sem=vec_sems.at[0],
         recv_sem=vec_sems.at[1],
         device_id=(last // 8, last % 8),
         device_id_type=MESH,
     )
 
-    @pl.when(me != last)
+    @pl.when(to.me != last)
     def _():
         vec_copy.start()
 
-    @pl.when(me == last)
+    @pl.when(to.me == last)
     def _():
-        pltpu.make_async_copy(vec_ref, vecs_ref.at[me], vec_sems.at[1]).start()
-
-    run(send)
-    run(sent)
-
-    @pl.when(me != last)
+        pltpu.make_async_copy(vec_ref, vecs_ref.at[to.me], vec_sems.at[1]).start()
+
+    run(to.send)
+    run(to.sent)
+
+    @pl.when(to.me != last)
     def _():
         vec_copy.wait_send()
 
-    @pl.when(me == last)
+    @pl.when(to.me == last)
     def _():
-        view = g_ref.at[pl.ds(0, sz.vec_start % sz.block)]
-        pltpu.make_async_copy(view, view, recv_sem).wait()
         pltpu.make_async_copy(vecs_ref, vecs_ref, vec_sems.at[1]).wait()
 
-    @pl.when(me != last)
-    def _():
-        pltpu.make_async_copy(g_ref, g_ref, recv_sem).wait()
-
-
-def collect(sz, qkv, out, fc, proj, vectors):
-    width = qkv.shape[-1]
+    to.received(0, 3 * sz.width_grains, lambda n: g_ref.at[pl.ds(0, n)], recv_sems.at[0])
+    to.received(sz.out_start, sz.width_grains, lambda n: outs_ref.at[:, pl.ds(0, n)], recv_sems.at[1])
+
+
+def collect_rest(sz, qkv, out, vectors):
+    def like(value, *lead):
+        return jax.ShapeDtypeStruct(lead + value.shape[-2:], value.dtype)
+
     return pl.pallas_call(
-        functools.partial(collect_kernel, sz),
-        out_shape=(
-            jax.ShapeDtypeStruct((sz.block, GRAIN, width), qkv.dtype),
-            jax.ShapeDtypeStruct((32,) + vectors.shape, vectors.dtype),
-        ),
-        in_specs=[HBM] * 5,
-        out_specs=[HBM] * 2,
+        functools.partial(collect_rest_kernel, sz),
+        out_shape=(like(qkv, sz.block), like(out, 4, sz.block), like(vectors, 32, sz.vec)),
+        in_specs=[HBM] * 3,
+        out_specs=[HBM] * 3,
         scratch_shapes=[
-            pltpu.SemaphoreType.DMA((sz.qkv + sz.out + 2 * sz.mlp,)),
-            pltpu.SemaphoreType.DMA,
+            pltpu.SemaphoreType.DMA((sz.qkv,)),
+            pltpu.SemaphoreType.DMA((out.shape[0],)),
+            pltpu.SemaphoreType.DMA((2,)),
             pltpu.SemaphoreType.DMA((2,)),
         ],
+        cost_estimate=cost(30),
         compiler_params=REMOTE,
-        name="collect",
-    )(qkv, out, fc, proj, vectors)
+        name="collect_rest",
+    )(qkv, out, vectors)
 
 
 def attend_back_kernel(heads, size, own, *refs):
     if own:
-        q_ref, kv_ref, do_ref, mix_ref, lse_ref, seed_ref, term_ref, dq_ref, dkv_ref, sum_ref = refs[:10]
+        q_ref, kv_ref, do_ref, mix_ref, lse_ref, seed_ref, dq_ref, dkv_ref = refs
     else:
         q_ref, kv_ref, do_ref, mix_ref, lse_ref, term_ref, dq_ref, dkv_ref, sum_ref = refs[:9]
-    quad = QuadSum(term_ref, sum_ref, *refs[-5:])
-    quad.start()
+        quad = QuadSum(term_ref, sum_ref, *refs[-5:])
+        quad.start()
     _, _, z, _ = my_place()
     part = heads * size
     rows = q_ref.shape[0] // 2
@@ -1194,30 +1262,35 @@
             def _():
                 group(index)
 
-        @pl.when(index == 0)
-        def _():
-            quad.middle()
+            @pl.when(index == 0)
+            def _():
+                quad.middle()
 
         return 0
 
     lax.fori_loop(0, 2, one, 0)
-    quad.finish()
-
-
-def attend_back(sz, own, q, kv, grad_mix, mix, lse, seed, term, ident):
-    operands = [q, kv, grad_mix, mix, lse] + ([seed] if own else []) + [term]
+    if not own:
+        quad.finish()
+
+
+def attend_back(sz, q, kv, grad_mix, mix, lse, seed=None, term=None, ident=None):
+    own = term is None
+    operands = [q, kv, grad_mix, mix, lse, seed if own else term]
+    out_shape = [
+        jax.ShapeDtypeStruct(q.shape, jnp.bfloat16 if own else jnp.float32),
+        jax.ShapeDtypeStruct(kv.shape, jnp.float32),
+    ]
+    if not own:
+        out_shape.append(jax.ShapeDtypeStruct(term.shape[2:], jnp.float32))
+    params = pltpu.CompilerParams(vmem_limit_bytes=56 << 20) if own else remote_params(ident, 56 << 20)
     return pl.pallas_call(
         functools.partial(attend_back_kernel, sz.quarter_heads, sz.head_size, own),
-        out_shape=(
-            jax.ShapeDtypeStruct(q.shape, jnp.bfloat16 if own else jnp.float32),
-            jax.ShapeDtypeStruct(kv.shape, jnp.float32),
-            jax.ShapeDtypeStruct(term.shape[2:], jnp.float32),
-        ),
+        out_shape=out_shape,
         in_specs=[VMEM] * len(operands),
-        out_specs=[VMEM] * 3,
-        scratch_shapes=quad_scratch(term),
+        out_specs=[VMEM] * len(out_shape),
+        scratch_shapes=[] if own else quad_scratch(term),
         cost_estimate=cost(35),
-        compiler_params=remote_params(ident, 56 << 20),
+        compiler_params=params,
         name="attend_back_own" if own else "attend_back_before",
     )(*operands)
 
@@ -1289,6 +1362,9 @@
     q = (dot_nt(act_one, w_qkv[: sz.part]) + quarter_of(vectors[2])).astype(bf16)
     mix, lse, before, mixed, _, w_fc, w_proj, w_out = forward_call(sz, q, kv, w_out, w_fc, w_proj)
     w_fc, w_out = flat(w_fc), flat(w_out)[:width]
+    by_quarter = jnp.pad(w_out, ((0, 0), (0, 4 * sz.part - width)))
+    by_quarter = by_quarter.reshape(width, sz.quarter_heads, 4, sz.head_size)
+    w_out_own = lax.dynamic_index_in_dim(by_quarter, quarter, 2, keepdims=False).reshape(width, sz.part)
     by_head = (sz.quarter_heads, sz.head_size)
     mixed = jnp.transpose(mixed.reshape((4, rows) + by_head), (1, 2, 0, 3)).reshape(rows, 4 * sz.part)[:, :width]
     inputs = tokens.astype(f32)
@@ -1311,30 +1387,29 @@
     cot = out_grad.astype(f32)
     grad_res = cot + norm_back(normed_two, rs_two, grad_two, vectors[5])
     grad_attn = grad_res.astype(bf16)
-    grad_mix = dot_nn(grad_attn, w_out).astype(bf16)
-    grad_mix = jnp.pad(grad_mix, ((0, 0), (0, 4 * sz.part - width)))
-    grad_mix = jnp.transpose(grad_mix.reshape(rows, sz.quarter_heads, 4, sz.head_size), (2, 0, 1, 3))
-    grad_mix = grad_mix.reshape(4, rows, sz.part)
-    grad_mix = swap_call(grad_mix, 3).reshape(4 * rows, sz.part)
+    attn_all = flat(grads_call(grad_attn, 3))
+    grad_mix = rowwise(dot_nn(attn_all, w_out_own).astype(bf16))
     g_proj = to_places(dot_tn(hid_mine, cot_all), got_proj, sz.proj_turn)
     partial_out = rowwise(dot_nn(act_hidden, w_proj).astype(bf16)).reshape(2, 2, rows, width)
     dq_before, dkv_before, out_sum = attend_back(
-        sz, False, q, before, grad_mix, mix, lse, None, partial_out, 4
+        sz, q, before, grad_mix, mix, lse, term=partial_out, ident=4
     )
     output = (residual + out_sum + vectors[7]).astype(bf16)
     returned = permute(dkv_before.astype(bf16), lambda py, pc, pz, px: (py, pc, pz - 1, px) if pz % 2 == 1 else None)
+    g_out = rowwise(dot_tn(attn_all, mix.astype(bf16)).astype(bf16)).reshape(2, width // 2, sz.part)
+    got_out = to_other_y(pick(g_out, 1 - y))
     g_fc = to_places(dot_tn(fc_mine, act_two), got_fc, sz.fc_turn)
-    g_out = rowwise(dot_tn(jnp.pad(grad_attn, ((0, 0), (0, 4 * sz.part - width))), mixed).astype(bf16))
-    dq, dkv, g_out = attend_back(sz, True, q, kv, grad_mix, mix, lse, dq_before, g_out.reshape(2, 2, sz.part, width), 5)
-    g_out = g_out.reshape(2, sz.part // 2, width)
-    got_out = to_other_y(pick(g_out, 1 - y))
+    dq, dkv = attend_back(sz, q, kv, grad_mix, mix, lse, seed=dq_before)
     grad_qkv = jnp.concatenate([dq, (dkv + returned.astype(f32)).astype(bf16)], axis=1)
     g_qkv = rowwise(dot_tn(grad_qkv, act_one).astype(bf16)).reshape(4, 2, 3 * sz.part // 8, width)
     half_qkv = lambda index: lax.dynamic_index_in_dim(g_qkv, index, 1, keepdims=False).reshape(-1, width)
     got_qkv = to_other_y(half_qkv(1 - y))
-    grad_one = quad_sum(rowwise(dot_nn(grad_qkv, w_qkv).astype(bf16)).reshape(2, 2, rows, width), 6)
+    partial_one = rowwise(dot_nn(grad_qkv, w_qkv).astype(bf16))
+    grad_one = quad_sum(partial_one.reshape(2, 2, rows, width), 6)
     g_out = to_places(pick(g_out, y), got_out)
     g_qkv = to_places(half_qkv(y), got_qkv)
+    grains = lambda value: value.astype(bf16).reshape(-1, GRAIN, value.shape[-1])
+    table_mlp = collect_mlp(sz, grains(g_fc), grains(g_proj))
 
     normed_one, rs_one = norm_parts(inputs)
     input_grad = (grad_res + norm_back(normed_one, rs_one, grad_one, vectors[0])).astype(bf16)
@@ -1368,17 +1443,22 @@
     )
     count = grad_vectors.shape[0]
     grad_vectors = jnp.pad(grad_vectors, ((0, sz.vec * GRAIN - count), (0, 0)))
-    grains = lambda value: value.astype(bf16).reshape(-1, GRAIN, width)
-    table, all_vectors = collect(
-        sz, grains(g_qkv), grains(g_out), grains(g_fc), grains(g_proj), grad_vectors.reshape(sz.vec, GRAIN, width)
+    table_qkv, table_out, all_vectors = collect_rest(
+        sz, grains(g_qkv), grains(g_out), grad_vectors.reshape(sz.vec, GRAIN, width)
     )
     grad_vectors = jnp.sum(all_vectors.reshape(32, sz.vec * GRAIN, width), axis=0)[:count]
-    table = table.reshape(sz.block * GRAIN, width).astype(f32)
+    table_out = table_out.reshape((4, sz.block * GRAIN) + by_head)
+    table_out = jnp.transpose(table_out, (1, 2, 0, 3)).reshape(sz.block * GRAIN, 4 * sz.part)[:, :width]
+    me = flat_id(y, c, z, x)
+    row = me * (sz.block * GRAIN) + lax.broadcasted_iota(jnp.int32, (sz.block * GRAIN, 1), 0)
+    table = jnp.where(
+        row < sz.out_start * GRAIN,
+        flat(table_qkv),
+        jnp.where(row < sz.fc_start * GRAIN, table_out, flat(table_mlp)),
+    ).astype(f32)
     used = (sz.vec_start % sz.block) * GRAIN
-    tail = jnp.concatenate(
-        [grad_vectors, jnp.zeros((sz.block * GRAIN - used - grad_vectors.shape[0], width), f32)]
-    )
-    last = flat_id(y, c, z, x) == sz.vec_start // sz.block
+    tail = jnp.concatenate([grad_vectors, jnp.zeros((sz.block * GRAIN - used - count, width), f32)])
+    last = me == sz.vec_start // sz.block
     tail = jnp.where(last, tail, table[used:])
     param_grad = jnp.concatenate([table[:used], tail])
     return (output, input_grad, param_grad)

time: 954 us -> 956 us (level)
  the two profiles are of different devices: /device:TPU:0 before, /device:TPU:3 now
where the time goes in v3:
time: 956 us; the launch traced here: 951 us
  Pallas kernels  554 us (58%)
  waiting for transfers between devices  137 us (14%)
  matrix products  109 us (11%)
  local copies, waits for them, and re-layouts  74.6 us (8%)
  other arithmetic  43 us (4%)
  starting transfers between devices  31 us (3%)
    ppermute x17, waiting for transfers between devices, permute(): return lax.ppermute(value, ('dp', 'cp'), pairs)  137 us
    pallas_call x1, Pallas kernels, acts_call(): pl.pallas_call(functools.partial(acts_kernel, sz.proj_turn), out_shape=(j...  110 us
    pallas_call x1, Pallas kernels, forward_call(): pl.pallas_call(functools.partial(forward_kernel, sz.quarter_heads, sz.hea...  106 us
    pallas_call x1, Pallas kernels, open_call(): pl.pallas_call(functools.partial(open_kernel, sz), out_shape=(like(8, sz....  95.9 us
    pallas_call x1, Pallas kernels, collect_rest(): pl.pallas_call(functools.partial(collect_rest_kernel, sz), out_shape=(lik...  67.1 us
    pallas_call x2, Pallas kernels, attend_back(): pl.pallas_call(functools.partial(attend_back_kernel, sz.quarter_heads, sz...  63.3 us
    pallas_call x2, Pallas kernels, quad_sum(): pl.pallas_call(quad_sum_kernel, out_shape=jax.ShapeDtypeStruct(partial.sh...  59.4 us
    dot_general x5, matrix products, dot_nt(): return lax.dot_general(a, b, NT, preferred_element_type=jnp.float32)  38.2 us
  transfers between devices with their start and end apart: 17, of which 7 were waited for; matrix products, arithmetic and copies ran while one was open for 13% of the time, Pallas kernels for 18%

profile of v3, /device:TPU:3, one launch (start us, length us, event | category | flops | bytes accessed | tf_op | source)
XLA Modules:
  0.0 950.7 jit_solution(10481197804245613458)
XLA Ops:
  5.1 95.9 %open.1 = (bf16[8,21,8,1600]{3,2,1,0:T(8,128)(2,1)}, bf16[8,7,8,1600]{3,2,1,0:T(8,128)(2,1)}, bf16[8,25,8,1600]{3,2,1,0:T(8,128)(2,1)}, bf16[8,25,8,1600]{3,2,1,...) custom-call(bf16[76,8,1600]{2,1,0:T(8,128)(2,1)} %bitcast.181, ...), custom_call_target="tpu_custom_call" | custom-call | tf_op jit(solution)/shard_map/open/pallas_call | solution.py:724
  116.2 5.6 add_convert_fusion.2.q_ref.refs_0_
  121.8 5.1 add_convert_fusion.1.kv_ref.refs_1_
  126.9 106.3 %forward.1 = (f32[1024,448]{1,0:T(8,128)}, f32[1024,8]{1,0:T(8,128)}, bf16[1024,896]{1,0:T(8,128)(2,1)}, bf16[4,256,448]{2,1,0:T(8,128)(2,1)}, bf16[8,7,8,1600]{...) custom-call(bf16[1024,448]{1,0:T(8,128)(2,1)} %add_convert_fusion.2., ...), custom_call_target="tpu_custom_call", output_to_operand_aliasing={{4}: (2, {}), {5}: (3, {}), {6}: (4, {})} | custom-call | bytes 360000000 | tf_op jit(solution)/shard_map/forward/pallas_call | solution.py:880
  241.1 110.0 %acts.1 = (bf16[2,2,256,1600]{3,2,1,0:T(8,128)(2,1)}, bf16[8,25,8,1600]{3,2,1,0:T(8,128)(2,1)}) custom-call(bf16[256,1600]{1,0:T(8,128)(2,1)} %add_convert_fusion.4.act_ref, bf16[8,25,8,1600]{3,2,1,0:T(8,128)(2,1)} %get-tuple-element.36.proj_in), custom_call_target="tpu_custom_call", output_to_operand_aliasing={{1}: (1, {})} | custom-call | bytes 180000000 | tf_op jit(solution)/shard_map/acts/pallas_call | solution.py:942
  351.1 9.3 fusion.93
  360.4 13.7 %convert_reduce_fusion = (f32[1600]{0:T(1024)S(1)}, bf16[1024,1600]{0,1:T(8,128)(2,1)}, bf16[1024,1600]{0,1:T(8,128)(2,1)S(1)}) fusion(f32[1024,1600]{0,1:T(8,128)S(1)} %fusion.93, f32[1600]{0:T(1024)S(1)} %add.390, bf16[1024,1600]{1,0:T(8,128)(2,1)S(1)} %bitcast.200, bf16[1600,1600]{1,0:T(8,128)(2,1)S(1)} %bitcast.154), kind=kOutput, calls=%fused_computation.19 | convolution fusion | flops 5290392064 | bytes 21516800 | tf_op jit(solution)/shard_map/dot_general | solution.py:307
  378.8 11.2 %convolution_convert_fusion.3 = bf16[1024,1600]{1,0:T(8,128)(2,1)} fusion(bf16[1024,1600]{0,1:T(8,128)(2,1)} %get-tuple-element.86, bf16[1600,1600]{1,0:T(8,128)(2,1)} %bitcast.165), kind=kOutput, calls=%fused_computation.28 | convolution fusion | flops 5244518400 | bytes 11673600 | tf_op jit(solution)/shard_map/dot_general | solution.py:315
  390.0 30.7 %quad_sum.2 = f32[256,1600]{1,0:T(8,128)} custom-call(bf16[2,2,256,1600]{3,2,1,0:T(8,128)(2,1)} %bitcast.173), custom_call_target="tpu_custom_call" | custom-call | bytes 90000000 | tf_op jit(solution)/shard_map/quad_sum/pallas_call | solution.py:1027
  425.6 24.9 %grads.1 = bf16[2,2,256,1600]{3,2,1,0:T(8,128)(2,1)} custom-call(bf16[256,1600]{1,0:T(8,128)(2,1)} %get-tuple-element.88.act_ref), custom_call_target="tpu_custom_call" | custom-call | bytes 75000000 | tf_op jit(solution)/shard_map/grads/pallas_call | solution.py:929
  459.3 6.0 slice.129
  465.3 8.9 convolution_convert_fusion.2
  474.2 9.5 %copy.118 = bf16[1600,1600]{0,1:T(8,128)(2,1)} copy(bf16[1600,1600]{1,0:T(8,128)(2,1)} %slice.129) | data formatting | bytes 10240000
  490.4 31.9 %attend_back_before.1 = (f32[1024,448]{1,0:T(8,128)}, f32[1024,896]{1,0:T(8,128)}, f32[256,1600]{1,0:T(8,128)}) custom-call(bf16[1024,448]{1,0:T(8,128)(2,1)} %add_convert_fusion.2.q_ref.refs_0_, bf16[1024,896]{1,0:T(8,128)(2,1)} %get-tuple-element.35.refs_1_, bf16[1024,448]{1,0:T(8,128)(2,1)} %convolution_convert_fusion.7.refs_2_, ...), custom_call_target="tpu_custom_call" | custom-call | bytes 105000000 | tf_op jit(solution)/shard_map/attend_back_before/pallas_call | solution.py:1286
  534.0 31.4 %attend_back_own.1 = (bf16[1024,448]{1,0:T(8,128)(2,1)}, f32[1024,896]{1,0:T(8,128)}) custom-call(bf16[1024,448]{1,0:T(8,128)(2,1)} %add_convert_fusion.2.q_ref.refs_0_, bf16[1024,896]{1,0:T(8,128)(2,1)} %add_convert_fusion.1.kv_ref.refs_1_, bf16[1024,448]{1,0:T(8,128)(2,1)} %convolution_convert_fusion.7.refs_2_, f32[1024,448]{1,0:T(8,128)} %get-tuple-element.41.refs_3_, ...), custom_call_target="tpu_custom_call" | custom-call | bytes 105000000 | tf_op jit(solution)/shard_map/attend_back_own/pallas_call | solution.py:1286
  566.9 7.6 convolution_convert_fusion.5
  577.6 8.2 collective-permute-start.6
  585.8 7.3 collective-permute-start.8
  598.6 13.2 %collective-permute-done.7 = bf16[200,448]{1,0:T(8,128)(2,1)S(1)} collective-permute-done((bf16[200,448]{1,0:T(8,128)(2,1)S(1)}, bf16[200,448]{1,0:T(8,128)(2,1)S(1)}, u32[]{:S(2)}, u32[]{:S(2)}) %collective-permute-start.7) | collective-permute-done | bytes 179232 | tf_op jit(solution)/shard_map/ppermute | solution.py:331
  614.5 10.3 %convolution_convert_fusion.1 = bf16[1024,1600]{1,0:T(8,128)(2,1)} fusion(bf16[1344,1600]{1,0:T(8,128)(2,1)} %bitcast.195, bf16[1024,896]{1,0:T(8,128)(2,1)S(1)} %add_convert_fusion, bf16[1024,448]{1,0:T(8,128)(2,1)S(1)} %copy-done.13), kind=kOutput, calls=%fused_computation.26 | convolution fusion | flops 4411162624 | bytes 10330112 | tf_op jit(solution)/shard_map/dot_general | solution.py:315
  626.1 28.7 %quad_sum.3 = f32[256,1600]{1,0:T(8,128)} custom-call(bf16[2,2,256,1600]{3,2,1,0:T(8,128)(2,1)} %bitcast.172), custom_call_target="tpu_custom_call" | custom-call | bytes 90000000 | tf_op jit(solution)/shard_map/quad_sum/pallas_call | solution.py:1027
  661.3 8.3 convolution_convert_fusion
  673.1 7.0 convert_add_fusion
  692.4 29.2 %collective-permute-done.1 = bf16[672,1600]{1,0:T(8,128)(2,1)} collective-permute-done((bf16[672,1600]{1,0:T(8,128)(2,1)}, bf16[672,1600]{1,0:T(8,128)(2,1)}, u32[]{:S(2)}, u32[]{:S(2)}) %collective-permute-start.1) | collective-permute-done | bytes 2150432 | tf_op jit(solution)/shard_map/ppermute | solution.py:331
  726.9 13.5 %collective-permute-done.12 = bf16[200,1600]{1,0:T(8,128)(2,1)S(1)} collective-permute-done((bf16[200,1600]{1,0:T(8,128)(2,1)S(1)}, bf16[200,1600]{1,0:T(8,128)(2,1)S(1)}, u32[]{:S(2)}, u32[]{:S(2)}) %collective-permute-start.12) | collective-permute-done | bytes 640032 | tf_op jit(solution)/shard_map/ppermute | solution.py:331
  741.5 51.6 %collective-permute-done.11 = bf16[200,1600]{1,0:T(8,128)(2,1)S(1)} collective-permute-done((bf16[200,1600]{1,0:T(8,128)(2,1)S(1)}, bf16[200,1600]{1,0:T(8,128)(2,1)S(1)}, u32[]{:S(2)}, u32[]{:S(2)}) %collective-permute-start.11) | collective-permute-done | bytes 640032 | tf_op jit(solution)/shard_map/ppermute | solution.py:331
  794.2 25.0 %collective-permute-done.15 = bf16[200,1600]{1,0:T(8,128)(2,1)S(1)} collective-permute-done((bf16[200,1600]{1,0:T(8,128)(2,1)S(1)}, bf16[200,1600]{1,0:T(8,128)(2,1)S(1)}, u32[]{:S(2)}, u32[]{:S(2)}) %collective-permute-start.15) | collective-permute-done | bytes 640032 | tf_op jit(solution)/shard_map/ppermute | solution.py:331
  820.5 27.5 %collect_mlp.1 = bf16[76,8,1600]{2,1,0:T(8,128)(2,1)} custom-call(bf16[25,8,1600]{2,1,0:T(8,128)(2,1)} %fusion.69.fc_ref, bf16[25,8,1600]{2,1,0:T(8,128)(2,1)} %fusion.70.proj_ref), custom_call_target="tpu_custom_call" | custom-call | bytes 90000000 | tf_op jit(solution)/shard_map/collect_mlp/pallas_call | solution.py:1101
  854.4 67.1 %collect_rest.1 = (bf16[76,8,1600]{2,1,0:T(8,128)(2,1)}, bf16[4,76,8,448]{3,2,1,0:T(8,128)(2,1)}, f32[32,2,8,1600]{3,2,1,0:T(8,128)}) custom-call(bf16[21,8,1600]{2,1,0:T(8,128)(2,1)} %fusion.74.qkv_ref, bf16[25,8,448]{2,1,0:T(8,128)(2,1)} %fusion.81.out_ref, f32[2,8,1600]{2,1,0:T(8,128)} %pad_bitcast_fusion.vec_ref), custom_call_target="tpu_custom_call" | custom-call | bytes 90000000 | tf_op jit(solution)/shard_map/collect_rest/pallas_call | solution.py:1179
  926.2 7.5 reshape.299
  933.6 5.5 copy.109
  945.0 5.5 copy.115
  (189 shorter events, 125.4 us)
Async XLA Ops:
  2.8 99.8 %copy-start.17 = (s32[8]{0:T(128)S(1)}, s32[8]{0:T(128)}, u32[]{:S(2)}) copy-start(s32[8]{0:T(128)} %constant.265) | copy-start | bytes 100
  100.9 4.8 copy-start.1
  113.0 8.8 slice-start.2
  116.1 5.6 copy-start.11
  116.2 5.6 slice-start.3
  351.1 9.3 copy-start.2
  351.1 9.3 copy-start.18
  378.8 294.3 %collective-permute-start.13 = (bf16[800,1600]{1,0:T(8,128)(2,1)}, bf16[800,1600]{1,0:T(8,128)(2,1)}, u32[]{:S(2)}, u32[]{:S(2)}) collective-permute-start(bf16[800,1600]{1,0:T(8,128)(2,1)} %convolution_convert_fusion.4), channel_id=1, source_target_pairs={{0,16},{1,17},{2,18},{3,19},{4,20},{5,21},{6,22},{7,23},{8,24},{9,... | collective-permute-start | bytes 7680008 | tf_op jit(solution)/shard_map/ppermute | solution.py:331
  457.5 7.8 slice-start
  457.5 7.8 slice-start.1
  457.5 7.8 copy-start.22
  457.5 117.0 %collective-permute-start.5 = (bf16[800,448]{0,1:T(8,128)(2,1)}, bf16[800,448]{0,1:T(8,128)(2,1)}, u32[]{:S(2)}, u32[]{:S(2)}) collective-permute-start(bf16[800,448]{0,1:T(8,128)(2,1)} %bitcast.187), channel_id=1, source_target_pairs={{0,16},{1,17},{2,18},{3,19},{4,20},{5,21},{6,22},{7,23},{8,24},{9,... | collective-permute-start | bytes 2150408 | tf_op jit(solution)/shard_map/ppermute | solution.py:331
  522.3 5.0 copy-start.16
  525.8 86.7 %collective-permute-start = (bf16[1024,896]{1,0:T(8,128)(2,1)}, bf16[1024,896]{1,0:T(8,128)(2,1)}, u32[]{:S(2)}, u32[]{:S(2)}) collective-permute-start(bf16[1024,896]{1,0:T(8,128)(2,1)} %convert_element_type.266), channel_id=1, source_target_pairs={{2,0},{3,1},{6,4},{7,5},{10,8},{11,9},{14,12},{15,13},{18,16},{19,... | collective-permute-start | bytes 5505032 | tf_op jit(solution)/shard_map/ppermute | solution.py:331
  575.9 36.6 %copy-start.8 = (f32[1024,896]{1,0:T(8,128)S(1)}, f32[1024,896]{1,0:T(8,128)}, u32[]{:S(2)}) copy-start(f32[1024,896]{1,0:T(8,128)} %get-tuple-element.46) | copy-start | bytes 11010052
  577.6 20.0 %collective-permute-start.6 = (bf16[200,448]{1,0:T(8,128)(2,1)S(1)}, bf16[200,448]{1,0:T(8,128)(2,1)S(1)}, u32[]{:S(2)}, u32[]{:S(2)}) collective-permute-start(bf16[200,448]{1,0:T(8,128)(2,1)S(1)} %get-tuple-element.102), channel_id=1, source_target_pairs={{0,2},{1,3},{2,4},{3,5},{4,6},{5,7},{6,0},{7,1},{8,10},{9,11},{10,... | collective-permute-start | bytes 537608 | tf_op jit(solution)/shard_map/ppermute | solution.py:331
  585.8 12.7 %collective-permute-start.8 = (bf16[200,448]{1,0:T(8,128)(2,1)S(1)}, bf16[200,448]{1,0:T(8,128)(2,1)S(1)}, u32[]{:S(2)}, u32[]{:S(2)}) collective-permute-start(bf16[200,448]{1,0:T(8,128)(2,1)S(1)} %get-tuple-element.103), channel_id=1, source_target_pairs={{0,6},{1,7},{2,0},{3,1},{4,2},{5,3},{6,4},{7,5},{8,14},{9,15},{10,... | collective-permute-start | bytes 537608 | tf_op jit(solution)/shard_map/ppermute | solution.py:331
  593.1 18.6 %collective-permute-start.7 = (bf16[200,448]{1,0:T(8,128)(2,1)S(1)}, bf16[200,448]{1,0:T(8,128)(2,1)S(1)}, u32[]{:S(2)}, u32[]{:S(2)}) collective-permute-start(bf16[200,448]{1,0:T(8,128)(2,1)S(1)} %get-tuple-element.104), channel_id=1, source_target_pairs={{0,4},{1,5},{2,6},{3,7},{4,0},{5,1},{6,2},{7,3},{8,12},{9,13},{10,... | collective-permute-start | bytes 537608 | tf_op jit(solution)/shard_map/ppermute | solution.py:331
  597.5 86.2 %collective-permute-start.9 = (bf16[800,1600]{1,0:T(8,128)(2,1)}, bf16[800,1600]{1,0:T(8,128)(2,1)}, u32[]{:S(2)}, u32[]{:S(2)}) collective-permute-start(bf16[800,1600]{1,0:T(8,128)(2,1)} %convolution_convert_fusion.5), channel_id=1, source_target_pairs={{0,16},{1,17},{2,18},{3,19},{4,20},{5,21},{6,22},{7,23},{8,24},{9,... | collective-permute-start | bytes 7680008 | tf_op jit(solution)/shard_map/ppermute | solution.py:331
  614.5 10.3 %copy-start.7 = (bf16[1024,896]{1,0:T(8,128)(2,1)}, bf16[1024,896]{1,0:T(8,128)(2,1)S(1)}, u32[]{:S(2)}) copy-start(bf16[1024,896]{1,0:T(8,128)(2,1)S(1)} %add_convert_fusion) | copy-start | bytes 5505028
  671.4 50.3 %collective-permute-start.1 = (bf16[672,1600]{1,0:T(8,128)(2,1)}, bf16[672,1600]{1,0:T(8,128)(2,1)}, u32[]{:S(2)}, u32[]{:S(2)}) collective-permute-start(bf16[672,1600]{1,0:T(8,128)(2,1)} %bitcast.21), channel_id=1, source_target_pairs={{0,16},{1,17},{2,18},{3,19},{4,20},{5,21},{6,22},{7,23},{8,24},{9,... | collective-permute-start | bytes 6451208 | tf_op jit(solution)/shard_map/ppermute | solution.py:331
  673.1 10.7 %copy-start.20 = (bf16[1024,1600]{0,1:T(8,128)(2,1)S(1)}, bf16[1024,1600]{0,1:T(8,128)(2,1)}, u32[]{:S(2)}) copy-start(bf16[1024,1600]{0,1:T(8,128)(2,1)} %get-tuple-element.86) | copy-start | bytes 9830404
  680.4 43.3 %collective-permute-start.14 = (bf16[200,1600]{1,0:T(8,128)(2,1)S(1)}, bf16[200,1600]{1,0:T(8,128)(2,1)S(1)}, u32[]{:S(2)}, u32[]{:S(2)}) collective-permute-start(bf16[200,1600]{1,0:T(8,128)(2,1)S(1)} %get-tuple-element.91), channel_id=1, source_target_pairs={{0,2},{1,3},{2,4},{3,5},{4,6},{5,7},{6,0},{7,1},{8,10},{9,11},{10,... | collective-permute-start | bytes 1920008 | tf_op jit(solution)/shard_map/ppermute | solution.py:331
  680.5 113.8 %collective-permute-start.16 = (bf16[200,1600]{1,0:T(8,128)(2,1)S(1)}, bf16[200,1600]{1,0:T(8,128)(2,1)S(1)}, u32[]{:S(2)}, u32[]{:S(2)}) collective-permute-start(bf16[200,1600]{1,0:T(8,128)(2,1)S(1)} %get-tuple-element.92), channel_id=1, source_target_pairs={{0,6},{1,7},{2,0},{3,1},{4,2},{5,3},{6,4},{7,5},{8,14},{9,15},{10,... | collective-permute-start | bytes 1920008 | tf_op jit(solution)/shard_map/ppermute | solution.py:331
  689.0 37.9 %collective-permute-start.10 = (bf16[200,1600]{1,0:T(8,128)(2,1)S(1)}, bf16[200,1600]{1,0:T(8,128)(2,1)S(1)}, u32[]{:S(2)}, u32[]{:S(2)}) collective-permute-start(bf16[200,1600]{1,0:T(8,128)(2,1)S(1)} %get-tuple-element.94), channel_id=1, source_target_pairs={{0,2},{1,3},{2,4},{3,5},{4,6},{5,7},{6,0},{7,1},{8,10},{9,11},{10,... | collective-permute-start | bytes 1920008 | tf_op jit(solution)/shard_map/ppermute | solution.py:331
  689.0 51.4 %collective-permute-start.12 = (bf16[200,1600]{1,0:T(8,128)(2,1)S(1)}, bf16[200,1600]{1,0:T(8,128)(2,1)S(1)}, u32[]{:S(2)}, u32[]{:S(2)}) collective-permute-start(bf16[200,1600]{1,0:T(8,128)(2,1)S(1)} %get-tuple-element.95), channel_id=1, source_target_pairs={{0,6},{1,7},{2,0},{3,1},{4,2},{5,3},{6,4},{7,5},{8,14},{9,15},{10,... | collective-permute-start | bytes 1920008 | tf_op jit(solution)/shard_map/ppermute | solution.py:331
  721.7 71.4 %collective-permute-start.11 = (bf16[200,1600]{1,0:T(8,128)(2,1)S(1)}, bf16[200,1600]{1,0:T(8,128)(2,1)S(1)}, u32[]{:S(2)}, u32[]{:S(2)}) collective-permute-start(bf16[200,1600]{1,0:T(8,128)(2,1)S(1)} %get-tuple-element.96), channel_id=1, source_target_pairs={{0,4},{1,5},{2,6},{3,7},{4,0},{5,1},{6,2},{7,3},{8,12},{9,13},{10,... | collective-permute-start | bytes 1920008 | tf_op jit(solution)/shard_map/ppermute | solution.py:331
  723.7 70.5 %copy-start.5 = (f32[672,1600]{1,0:T(8,128)}, f32[672,1600]{1,0:T(8,128)S(1)}, u32[]{:S(2)}) copy-start(f32[672,1600]{1,0:T(8,128)S(1)} %convert_add_fusion.2) | copy-start | bytes 12902404
  723.8 95.5 %collective-permute-start.15 = (bf16[200,1600]{1,0:T(8,128)(2,1)S(1)}, bf16[200,1600]{1,0:T(8,128)(2,1)S(1)}, u32[]{:S(2)}, u32[]{:S(2)}) collective-permute-start(bf16[200,1600]{1,0:T(8,128)(2,1)S(1)} %get-tuple-element.93), channel_id=1, source_target_pairs={{0,4},{1,5},{2,6},{3,7},{4,0},{5,1},{6,2},{7,3},{8,12},{9,13},{10,... | collective-permute-start | bytes 1920008 | tf_op jit(solution)/shard_map/ppermute | solution.py:331
  726.9 125.1 %collective-permute-start.2 = (bf16[168,1600]{1,0:T(8,128)(2,1)S(1)}, bf16[168,1600]{1,0:T(8,128)(2,1)S(1)}, u32[]{:S(2)}, u32[]{:S(2)}) collective-permute-start(bf16[168,1600]{1,0:T(8,128)(2,1)S(1)} %get-tuple-element.97), channel_id=1, source_target_pairs={{0,2},{1,3},{2,4},{3,5},{4,6},{5,7},{6,0},{7,1},{8,10},{9,11},{10,... | collective-permute-start | bytes 1612808 | tf_op jit(solution)/shard_map/ppermute | solution.py:331
  740.4 111.6 %collective-permute-start.4 = (bf16[168,1600]{1,0:T(8,128)(2,1)S(1)}, bf16[168,1600]{1,0:T(8,128)(2,1)S(1)}, u32[]{:S(2)}, u32[]{:S(2)}) collective-permute-start(bf16[168,1600]{1,0:T(8,128)(2,1)S(1)} %get-tuple-element.98), channel_id=1, source_target_pairs={{0,6},{1,7},{2,0},{3,1},{4,2},{5,3},{6,4},{7,5},{8,14},{9,15},{10,... | collective-permute-start | bytes 1612808 | tf_op jit(solution)/shard_map/ppermute | solution.py:331
  793.0 59.0 %collective-permute-start.3 = (bf16[168,1600]{1,0:T(8,128)(2,1)S(1)}, bf16[168,1600]{1,0:T(8,128)(2,1)S(1)}, u32[]{:S(2)}, u32[]{:S(2)}) collective-permute-start(bf16[168,1600]{1,0:T(8,128)(2,1)S(1)} %get-tuple-element.99), channel_id=1, source_target_pairs={{0,4},{1,5},{2,6},{3,7},{4,0},{5,1},{6,2},{7,3},{8,12},{9,13},{10,... | collective-permute-start | bytes 1612808 | tf_op jit(solution)/shard_map/ppermute | solution.py:331
  (12 other events, 33.3 us)

commit v4 on v3

--- a/solution.py
+++ b/solution.py
@@ -580,13 +580,13 @@
         rest = inner % sz.head_grains
 
         def one(quarter, sem):
-            local = part * sz.part_grains + (head // 4) * sz.head_grains + rest
+            local = part * sz.part_grains + (2 * (head // 8) + head % 2) * sz.head_grains + rest
             spot = local // sz.qkv
             act(grain, qkv_ref, spot, local % sz.qkv, quarter, spot % 2, spot // 2, sem, kind_sems.at[0])
 
         @pl.when(table < sz.out_start)
         def _():
-            one(head % 4, spread_sems.at[grain])
+            one((head // 2) % 4, spread_sems.at[grain])
 
             @pl.when(head == sz.heads - 1)
             def _():
@@ -1076,8 +1076,10 @@
                 pltpu.make_async_copy(view(grains), view(grains), recv).wait()
 
 
-def collect_mlp_kernel(sz, fc_ref, proj_ref, g_ref, send_sems, recv_sem):
+def collect_mlp_kernel(sz, fc_ref, proj_ref, out_ref, g_ref, outs_ref, send_sems, out_sems, recv_sems):
     to = Collector(sz)
+    recv_sem = recv_sems.at[0]
+    out_share = out_ref.shape[0]
 
     def run(act):
         for ref, base, turn, first_sem in (
@@ -1092,45 +1094,6 @@
 
             lax.fori_loop(0, sz.mlp, one, 0)
 
-    run(to.send)
-    run(to.sent)
-    to.received(sz.fc_start, 64 * sz.mlp, lambda n: g_ref.at[pl.ds(0, n)], recv_sem)
-
-
-def collect_mlp(sz, fc, proj):
-    return pl.pallas_call(
-        functools.partial(collect_mlp_kernel, sz),
-        out_shape=jax.ShapeDtypeStruct((sz.block, GRAIN, fc.shape[-1]), fc.dtype),
-        in_specs=[HBM] * 2,
-        out_specs=HBM,
-        scratch_shapes=[pltpu.SemaphoreType.DMA((2 * sz.mlp,)), pltpu.SemaphoreType.DMA],
-        cost_estimate=cost(30),
-        compiler_params=REMOTE,
-        name="collect_mlp",
-    )(fc, proj)
-
-
-def collect_rest_kernel(
-    sz, qkv_ref, out_ref, vec_ref, g_ref, outs_ref, vecs_ref, qkv_sems, out_sems, vec_sems, recv_sems
-):
-    to = Collector(sz)
-    out_share = out_ref.shape[0]
-
-    def run(act):
-        def heads(slot, _):
-            local = slot_qkv(to.y, to.z) * sz.qkv + slot
-            inner = local % sz.part_grains
-            head = 4 * (inner // sz.head_grains) + to.quarter
-
-            @pl.when(head < sz.heads)
-            def _():
-                table = (local // sz.part_grains) * sz.width_grains + head * sz.head_grains + inner % sz.head_grains
-                act(qkv_ref.at[slot], g_ref.at[table % sz.block], table, qkv_sems.at[slot], recv_sems.at[0])
-
-            return 0
-
-        lax.fori_loop(0, sz.qkv, heads, 0)
-
         def outward(slot, _):
             table = sz.out_start + slot_out(to.y, to.z) * out_share + slot
             dst = outs_ref.at[to.quarter, table % sz.block]
@@ -1138,6 +1101,53 @@
             return 0
 
         lax.fori_loop(0, out_share, outward, 0)
+
+    run(to.send)
+    run(to.sent)
+    to.received(sz.fc_start, 64 * sz.mlp, lambda n: g_ref.at[pl.ds(0, n)], recv_sem)
+    to.received(sz.out_start, sz.width_grains, lambda n: outs_ref.at[:, pl.ds(0, n)], recv_sems.at[1])
+
+
+def collect_mlp(sz, fc, proj, out):
+    return pl.pallas_call(
+        functools.partial(collect_mlp_kernel, sz),
+        out_shape=(
+            jax.ShapeDtypeStruct((sz.block, GRAIN, fc.shape[-1]), fc.dtype),
+            jax.ShapeDtypeStruct((4, sz.block, GRAIN, out.shape[-1]), out.dtype),
+        ),
+        in_specs=[HBM] * 3,
+        out_specs=[HBM] * 2,
+        scratch_shapes=[
+            pltpu.SemaphoreType.DMA((2 * sz.mlp,)),
+            pltpu.SemaphoreType.DMA((out.shape[0],)),
+            pltpu.SemaphoreType.DMA((2,)),
+        ],
+        cost_estimate=cost(30),
+        compiler_params=REMOTE,
+        name="collect_mlp",
+    )(fc, proj, out)
+
+
+def collect_rest_kernel(
+    sz, qkv_ref, vec_ref, g_ref, vecs_ref, qkv_sems, vec_sems, recv_sem
+):
+    to = Collector(sz)
+
+    def run(act):
+        def heads(slot, _):
+            local = slot_qkv(to.y, to.z) * sz.qkv + slot
+            inner = local % sz.part_grains
+            index = inner // sz.head_grains
+            head = 8 * (index // 2) + 2 * to.quarter + index % 2
+
+            @pl.when(head < sz.heads)
+            def _():
+                table = (local // sz.part_grains) * sz.width_grains + head * sz.head_grains + inner % sz.head_grains
+                act(qkv_ref.at[slot], g_ref.at[table % sz.block], table, qkv_sems.at[slot], recv_sem)
+
+            return 0
+
+        lax.fori_loop(0, sz.qkv, heads, 0)
 
     last = sz.vec_start // sz.block
     vec_copy = pltpu.make_async_remote_copy(
@@ -1168,29 +1178,27 @@
     def _():
         pltpu.make_async_copy(vecs_ref, vecs_ref, vec_sems.at[1]).wait()
 
-    to.received(0, 3 * sz.width_grains, lambda n: g_ref.at[pl.ds(0, n)], recv_sems.at[0])
-    to.received(sz.out_start, sz.width_grains, lambda n: outs_ref.at[:, pl.ds(0, n)], recv_sems.at[1])
-
-
-def collect_rest(sz, qkv, out, vectors):
+    to.received(0, 3 * sz.width_grains, lambda n: g_ref.at[pl.ds(0, n)], recv_sem)
+
+
+def collect_rest(sz, qkv, vectors):
     def like(value, *lead):
         return jax.ShapeDtypeStruct(lead + value.shape[-2:], value.dtype)
 
     return pl.pallas_call(
         functools.partial(collect_rest_kernel, sz),
-        out_shape=(like(qkv, sz.block), like(out, 4, sz.block), like(vectors, 32, sz.vec)),
-        in_specs=[HBM] * 3,
-        out_specs=[HBM] * 3,
+        out_shape=(like(qkv, sz.block), like(vectors, 32, sz.vec)),
+        in_specs=[HBM] * 2,
+        out_specs=[HBM] * 2,
         scratch_shapes=[
             pltpu.SemaphoreType.DMA((sz.qkv,)),
-            pltpu.SemaphoreType.DMA((out.shape[0],)),
             pltpu.SemaphoreType.DMA((2,)),
-            pltpu.SemaphoreType.DMA((2,)),
+            pltpu.SemaphoreType.DMA,
         ],
         cost_estimate=cost(30),
         compiler_params=REMOTE,
         name="collect_rest",
-    )(qkv, out, vectors)
+    )(qkv, vectors)
 
 
 def attend_back_kernel(heads, size, own, *refs):
@@ -1353,20 +1361,26 @@
     normed_all, _ = norm_parts(flat(tok_all).astype(f32))
     act_one = (normed_all * vectors[0] + vectors[1]).astype(bf16)
 
-    def quarter_of(vector):
-        padded = jnp.pad(vector, (0, 4 * sz.part - width)).reshape(sz.quarter_heads, 4, sz.head_size)
-        return lax.dynamic_index_in_dim(padded, quarter, 1, keepdims=False).reshape(sz.part)
-
-    kv_bias = jnp.concatenate([jnp.zeros((sz.part,), f32), quarter_of(vectors[3])])
+    pair = 2 * sz.head_size
+    turns = width // (4 * pair)
+    rest = width - 4 * turns * pair
+
+    def quarter_of(value):
+        blocks = [lax.dynamic_slice_in_dim(value, (4 * j + quarter) * pair, pair, 1) for j in range(turns)]
+        end = value[:, width - rest :]
+        return jnp.concatenate(blocks + [jnp.where(quarter == 0, end, jnp.zeros_like(end))], axis=1)
+
+    def by_head(quarters):
+        blocks = [quarters[k][:, j * pair : (j + 1) * pair] for j in range(turns) for k in range(4)]
+        return jnp.concatenate(blocks + [quarters[0][:, turns * pair : turns * pair + rest]], axis=1)
+
+    biases = quarter_of(vectors[2:4])
+    kv_bias = jnp.concatenate([jnp.zeros((sz.part,), f32), biases[1]])
     kv = (dot_nt(act_one, w_qkv[sz.part :]) + kv_bias).astype(bf16)
-    q = (dot_nt(act_one, w_qkv[: sz.part]) + quarter_of(vectors[2])).astype(bf16)
+    q = (dot_nt(act_one, w_qkv[: sz.part]) + biases[0]).astype(bf16)
     mix, lse, before, mixed, _, w_fc, w_proj, w_out = forward_call(sz, q, kv, w_out, w_fc, w_proj)
     w_fc, w_out = flat(w_fc), flat(w_out)[:width]
-    by_quarter = jnp.pad(w_out, ((0, 0), (0, 4 * sz.part - width)))
-    by_quarter = by_quarter.reshape(width, sz.quarter_heads, 4, sz.head_size)
-    w_out_own = lax.dynamic_index_in_dim(by_quarter, quarter, 2, keepdims=False).reshape(width, sz.part)
-    by_head = (sz.quarter_heads, sz.head_size)
-    mixed = jnp.transpose(mixed.reshape((4, rows) + by_head), (1, 2, 0, 3)).reshape(rows, 4 * sz.part)[:, :width]
+    mixed = by_head(mixed)
     inputs = tokens.astype(f32)
     residual = inputs + (dot_nt(mixed, w_out) + vectors[4])
     normed_two, rs_two = norm_parts(residual)
@@ -1388,14 +1402,17 @@
     grad_res = cot + norm_back(normed_two, rs_two, grad_two, vectors[5])
     grad_attn = grad_res.astype(bf16)
     attn_all = flat(grads_call(grad_attn, 3))
-    grad_mix = rowwise(dot_nn(attn_all, w_out_own).astype(bf16))
+    grad_mix = rowwise(dot_nn(attn_all, w_out).astype(bf16))
+    grad_mix = rowwise(quarter_of(grad_mix))
     g_proj = to_places(dot_tn(hid_mine, cot_all), got_proj, sz.proj_turn)
     partial_out = rowwise(dot_nn(act_hidden, w_proj).astype(bf16)).reshape(2, 2, rows, width)
     dq_before, dkv_before, out_sum = attend_back(
         sz, q, before, grad_mix, mix, lse, term=partial_out, ident=4
     )
     output = (residual + out_sum + vectors[7]).astype(bf16)
-    returned = permute(dkv_before.astype(bf16), lambda py, pc, pz, px: (py, pc, pz - 1, px) if pz % 2 == 1 else None)
+    returned = permute(
+        dkv_before.astype(bf16), lambda py, pc, pz, px: (py, pc, pz - 1, px) if pz % 2 == 1 else None
+    )
     g_out = rowwise(dot_tn(attn_all, mix.astype(bf16)).astype(bf16)).reshape(2, width // 2, sz.part)
     got_out = to_other_y(pick(g_out, 1 - y))
     g_fc = to_places(dot_tn(fc_mine, act_two), got_fc, sz.fc_turn)
@@ -1409,15 +1426,19 @@
     g_out = to_places(pick(g_out, y), got_out)
     g_qkv = to_places(half_qkv(y), got_qkv)
     grains = lambda value: value.astype(bf16).reshape(-1, GRAIN, value.shape[-1])
-    table_mlp = collect_mlp(sz, grains(g_fc), grains(g_proj))
+    table_mlp, table_out = collect_mlp(sz, grains(g_fc), grains(g_proj), grains(g_out))
+    table_out = by_head(table_out.reshape(4, -1, sz.part))
 
     normed_one, rs_one = norm_parts(inputs)
     input_grad = (grad_res + norm_back(normed_one, rs_one, grad_one, vectors[0])).astype(bf16)
 
     def placed(vector):
-        spread = jnp.zeros((sz.quarter_heads, 4, sz.head_size), f32)
-        spread = lax.dynamic_update_slice_in_dim(spread, vector.reshape(-1, 1, sz.head_size), quarter, 1)
-        return spread.reshape(4 * sz.part)[:width]
+        spread = jnp.zeros((1, width), f32)
+        for j in range(turns):
+            block = vector[None, j * pair : (j + 1) * pair]
+            spread = lax.dynamic_update_slice_in_dim(spread, block, (4 * j + quarter) * pair, 1)
+        end = jnp.where(quarter == 0, vector[turns * pair : turns * pair + rest], 0.0)
+        return jnp.concatenate([spread[0, : width - rest], end])
 
     sums = jnp.sum(grad_qkv.astype(f32), axis=0)
     bias_sum = jnp.sum(grad_fc.astype(f32), axis=0).reshape(8, hidden // 32)[jnp.array(SPOTS)]
@@ -1443,12 +1464,8 @@
     )
     count = grad_vectors.shape[0]
     grad_vectors = jnp.pad(grad_vectors, ((0, sz.vec * GRAIN - count), (0, 0)))
-    table_qkv, table_out, all_vectors = collect_rest(
-        sz, grains(g_qkv), grains(g_out), grad_vectors.reshape(sz.vec, GRAIN, width)
-    )
+    table_qkv, all_vectors = collect_rest(sz, grains(g_qkv), grad_vectors.reshape(sz.vec, GRAIN, width))
     grad_vectors = jnp.sum(all_vectors.reshape(32, sz.vec * GRAIN, width), axis=0)[:count]
-    table_out = table_out.reshape((4, sz.block * GRAIN) + by_head)
-    table_out = jnp.transpose(table_out, (1, 2, 0, 3)).reshape(sz.block * GRAIN, 4 * sz.part)[:, :width]
     me = flat_id(y, c, z, x)
     row = me * (sz.block * GRAIN) + lax.broadcasted_iota(jnp.int32, (sz.block * GRAIN, 1), 0)
     table = jnp.where(

time: 956 us -> 937 us (0.980)
  the two profiles are of different devices: /device:TPU:3 before, /device:TPU:10 now
where the time goes in v4:
time: 937 us; the launch traced here: 924 us
  Pallas kernels  504 us (54%)
  waiting for transfers between devices  155 us (17%)
  matrix products  122 us (13%)
  starting transfers between devices  49.4 us (5%)
  other arithmetic  48 us (5%)
  local copies, waits for them, and re-layouts  43.1 us (5%)
    ppermute x17, waiting for transfers between devices, permute(): return lax.ppermute(value, ('dp', 'cp'), pairs)  155 us
    pallas_call x1, Pallas kernels, forward_call(): pl.pallas_call(functools.partial(forward_kernel, sz.quarter_heads, sz.hea...  124 us
    pallas_call x1, Pallas kernels, acts_call(): pl.pallas_call(functools.partial(acts_kernel, sz.proj_turn), out_shape=(j...  89.4 us
    pallas_call x1, Pallas kernels, open_call(): pl.pallas_call(functools.partial(open_kernel, sz), out_shape=(like(8, sz....  85.4 us
    pallas_call x2, Pallas kernels, attend_back(): pl.pallas_call(functools.partial(attend_back_kernel, sz.quarter_heads, sz...  75.6 us
    pallas_call x2, Pallas kernels, quad_sum(): pl.pallas_call(quad_sum_kernel, out_shape=jax.ShapeDtypeStruct(partial.sh...  54.4 us
    ppermute x17, starting transfers between devices, permute(): return lax.ppermute(value, ('dp', 'cp'), pairs)  49.4 us
    dot_general x5, matrix products, dot_nt(): return lax.dot_general(a, b, NT, preferred_element_type=jnp.float32)  43.7 us
  transfers between devices with their start and end apart: 17, of which 10 were waited for; matrix products, arithmetic and copies ran while one was open for 10% of the time, Pallas kernels for 9%

profile of v4, /device:TPU:10, one launch (start us, length us, event | category | flops | bytes accessed | tf_op | source)
XLA Modules:
  0.0 923.9 jit_solution(17836118400753958591)
XLA Ops:
  5.1 85.4 %open.1 = (bf16[8,21,8,1600]{3,2,1,0:T(8,128)(2,1)}, bf16[8,7,8,1600]{3,2,1,0:T(8,128)(2,1)}, bf16[8,25,8,1600]{3,2,1,0:T(8,128)(2,1)}, bf16[8,25,8,1600]{3,2,1,...) custom-call(bf16[76,8,1600]{2,1,0:T(8,128)(2,1)} %bitcast.198, ...), custom_call_target="tpu_custom_call" | custom-call | tf_op jit(solution)/shard_map/open/pallas_call | solution.py:724
  100.1 8.1 add_convert_fusion.1.kv_ref.refs_1_
  112.6 124.1 %forward.1 = (f32[1024,448]{1,0:T(8,128)}, f32[1024,8]{1,0:T(8,128)}, bf16[1024,896]{1,0:T(8,128)(2,1)}, bf16[4,256,448]{2,1,0:T(8,128)(2,1)}, bf16[8,7,8,1600]{...) custom-call(bf16[1024,448]{1,0:T(8,128)(2,1)} %add_convert_fusion.2., ...), custom_call_target="tpu_custom_call", output_to_operand_aliasing={{4}: (2, {}), {5}: (3, {}), {6}: (4, {})} | custom-call | bytes 360000000 | tf_op jit(solution)/shard_map/forward/pallas_call | solution.py:880
  246.0 89.4 %acts.1 = (bf16[2,2,256,1600]{3,2,1,0:T(8,128)(2,1)}, bf16[8,25,8,1600]{3,2,1,0:T(8,128)(2,1)}) custom-call(bf16[256,1600]{1,0:T(8,128)(2,1)} %add_convert_fusion.4.act_ref, bf16[8,25,8,1600]{3,2,1,0:T(8,128)(2,1)} %get-tuple-element.37.proj_in), custom_call_target="tpu_custom_call", output_to_operand_aliasing={{1}: (1, {})} | custom-call | bytes 180000000 | tf_op jit(solution)/shard_map/acts/pallas_call | solution.py:942
  335.5 11.0 %fusion.101 = f32[1024,1600]{0,1:T(8,128)} fusion(bf16[1024,1600]{1,0:T(8,128)(2,1)} %bitcast.218, bf16[1600,1600]{1,0:T(8,128)(2,1)} %bitcast.182), kind=kOutput, calls=%fused_computation.228 | convolution fusion | flops 5242880000 | bytes 14950400 | tf_op jit(solution)/shard_map/dot_general | solution.py:307
  346.4 15.7 %convert_reduce_fusion = (f32[1600]{0:T(1024)S(1)}, bf16[1024,1600]{0,1:T(8,128)(2,1)S(1)}, bf16[1024,1600]{0,1:T(8,128)(2,1)}) fusion(f32[1024,1600]{0,1:T(8,128)} %fusion.101, f32[1600]{0:T(1024)S(1)} %add.409, bf16[1024,1600]{1,0:T(8,128)(2,1)S(1)} %bitcast.216, bf16[1600,1600]{1,0:T(8,128)(2,1)S(1)} %bitcast.179), kind=kOutput, calls=%fused_computation.19 | convolution fusion | flops 5290392064 | bytes 21516800 | tf_op jit(solution)/shard_map/dot_general | solution.py:307
  362.2 8.5 convolution_convert_fusion.3
  370.7 25.7 %quad_sum.2 = f32[256,1600]{1,0:T(8,128)} custom-call(bf16[2,2,256,1600]{3,2,1,0:T(8,128)(2,1)} %bitcast.190), custom_call_target="tpu_custom_call" | custom-call | bytes 90000000 | tf_op jit(solution)/shard_map/quad_sum/pallas_call | solution.py:1027
  401.3 26.1 %grads.1 = bf16[2,2,256,1600]{3,2,1,0:T(8,128)(2,1)} custom-call(bf16[256,1600]{1,0:T(8,128)(2,1)} %get-tuple-element.85.act_ref), custom_call_target="tpu_custom_call" | custom-call | bytes 75000000 | tf_op jit(solution)/shard_map/grads/pallas_call | solution.py:929
  427.4 10.1 %fusion.14 = bf16[1024,1600]{1,0:T(8,128)(2,1)S(1)} fusion(bf16[1024,1600]{1,0:T(8,128)(2,1)} %bitcast.191, bf16[1792,1600]{1,0:T(8,128)(2,1)} %bitcast.209), kind=kOutput, calls=%fused_computation.30 | convolution fusion | flops 5244518400 | bytes 12009472 | tf_op jit(solution)/shard_map/dot_general | solution.py:315
  437.9 10.9 %convolution_convert_fusion.2 = bf16[1024,1600]{1,0:T(8,128)(2,1)} fusion(bf16[1024,1600]{0,1:T(8,128)(2,1)S(1)} %copy-done.23, bf16[1600,1600]{1,0:T(8,128)(2,1)} %bitcast.178), kind=kOutput, calls=%fused_computation.32 | convolution fusion | flops 5244518400 | bytes 11673600 | tf_op jit(solution)/shard_map/dot_general | solution.py:315
  449.9 43.8 %attend_back_before.1 = (f32[1024,448]{1,0:T(8,128)}, f32[1024,896]{1,0:T(8,128)}, f32[256,1600]{1,0:T(8,128)}) custom-call(bf16[1024,448]{1,0:T(8,128)(2,1)} %add_convert_fusion.2.q_ref.refs_0_, bf16[1024,896]{1,0:T(8,128)(2,1)} %get-tuple-element.36.refs_1_, bf16[1024,448]{1,0:T(8,128)(2,1)} %pad_maximum_fusion.2.refs_2_, ...), custom_call_target="tpu_custom_call" | custom-call | bytes 105000000 | tf_op jit(solution)/shard_map/attend_back_before/pallas_call | solution.py:1294
  499.8 5.7 convolution_convert_fusion.6
  509.7 7.7 convolution_convert_fusion.4
  520.0 31.8 %attend_back_own.1 = (bf16[1024,448]{1,0:T(8,128)(2,1)}, f32[1024,896]{1,0:T(8,128)}) custom-call(bf16[1024,448]{1,0:T(8,128)(2,1)} %add_convert_fusion.2.q_ref.refs_0_, bf16[1024,896]{1,0:T(8,128)(2,1)} %add_convert_fusion.1.kv_ref.refs_1_, bf16[1024,448]{1,0:T(8,128)(2,1)} %pad_maximum_fusion.2.refs_2_, f32[1024,448]{1,0:T(8,128)} %get-tuple-element.42.refs_3_, ...), custom_call_target="tpu_custom_call" | custom-call | bytes 105000000 | tf_op jit(solution)/shard_map/attend_back_own/pallas_call | solution.py:1294
  557.6 7.7 convolution_convert_fusion.5
  568.5 9.3 %collective-permute-start.15 = (bf16[200,448]{1,0:T(8,128)(2,1)S(1)}, bf16[200,448]{1,0:T(8,128)(2,1)S(1)}, u32[]{:S(2)}, u32[]{:S(2)}) collective-permute-start(bf16[200,448]{1,0:T(8,128)(2,1)S(1)} %get-tuple-element.108), channel_id=1, source_target_pairs={{0,4},{1,5},{2,6},{3,7},{4,0},{5,1},{6,2},{7,3},{8,12},{9,13},{10,... | collective-permute-start | bytes 537608 | tf_op jit(solution)/shard_map/ppermute | solution.py:331
  580.8 9.2 collective-permute-done.15
  599.2 7.4 convolution_convert_fusion.1
  607.6 28.7 %quad_sum.3 = f32[256,1600]{1,0:T(8,128)} custom-call(bf16[2,2,256,1600]{3,2,1,0:T(8,128)(2,1)} %bitcast.189), custom_call_target="tpu_custom_call" | custom-call | bytes 90000000 | tf_op jit(solution)/shard_map/quad_sum/pallas_call | solution.py:1027
  638.6 10.0 %convolution_convert_fusion = bf16[1344,1600]{1,0:T(8,128)(2,1)} fusion(bf16[1024,1600]{1,0:T(8,128)(2,1)} %copy-done.11, bf16[1024,896]{1,0:T(8,128)(2,1)} %copy-done.7, bf16[1024,448]{1,0:T(8,128)(2,1)S(1)} %copy-done.14), kind=kOutput, calls=%fused_computation.6 | convolution fusion | flops 4411674624 | bytes 10330112 | tf_op jit(solution)/shard_map/dot_general | solution.py:311
  657.1 5.1 convert_add_fusion.1
  683.2 38.7 %collective-permute-done.7 = bf16[200,1600]{1,0:T(8,128)(2,1)S(1)} collective-permute-done((bf16[200,1600]{1,0:T(8,128)(2,1)}, bf16[200,1600]{1,0:T(8,128)(2,1)S(1)}, u32[]{:S(2)}, u32[]{:S(2)}) %collective-permute-start.7) | collective-permute-done | bytes 640032 | tf_op jit(solution)/shard_map/ppermute | solution.py:331
  723.1 26.4 %collective-permute-done.8 = bf16[200,1600]{1,0:T(8,128)(2,1)S(1)} collective-permute-done((bf16[200,1600]{1,0:T(8,128)(2,1)}, bf16[200,1600]{1,0:T(8,128)(2,1)S(1)}, u32[]{:S(2)}, u32[]{:S(2)}) %collective-permute-start.8) | collective-permute-done | bytes 640032 | tf_op jit(solution)/shard_map/ppermute | solution.py:331
  751.9 12.6 %collective-permute-done.10 = bf16[200,1600]{1,0:T(8,128)(2,1)S(1)} collective-permute-done((bf16[200,1600]{1,0:T(8,128)(2,1)}, bf16[200,1600]{1,0:T(8,128)(2,1)S(1)}, u32[]{:S(2)}, u32[]{:S(2)}) %collective-permute-start.10) | collective-permute-done | bytes 640032 | tf_op jit(solution)/shard_map/ppermute | solution.py:331
  764.6 13.8 %collective-permute-done.11 = bf16[200,1600]{1,0:T(8,128)(2,1)} collective-permute-done((bf16[200,1600]{1,0:T(8,128)(2,1)}, bf16[200,1600]{1,0:T(8,128)(2,1)}, u32[]{:S(2)}, u32[]{:S(2)}) %collective-permute-start.11) | collective-permute-done | bytes 640032 | tf_op jit(solution)/shard_map/ppermute | solution.py:331
  781.2 20.8 %collect_mlp.1 = (bf16[76,8,1600]{2,1,0:T(8,128)(2,1)}, bf16[4,76,8,448]{3,2,1,0:T(8,128)(2,1)}) custom-call(bf16[25,8,1600]{2,1,0:T(8,128)(2,1)} %fusion.80.fc_ref, bf16[25,8,1600]{2,1,0:T(8,128)(2,1)} %fusion.81.proj_ref, bf16[25,8,448]{2,1,0:T(8,128)(2,1)} %fusion.92.out_ref), custom_call_target="tpu_custom_call" | custom-call | bytes 90000000 | tf_op jit(solution)/shard_map/collect_mlp/pallas_call | solution.py:1112
  809.1 23.8 %collective-permute-start.3 = (bf16[168,1600]{1,0:T(8,128)(2,1)S(1)}, bf16[168,1600]{1,0:T(8,128)(2,1)S(1)}, u32[]{:S(2)}, u32[]{:S(2)}) collective-permute-start(bf16[168,1600]{1,0:T(8,128)(2,1)S(1)} %get-tuple-element.96), channel_id=1, source_target_pairs={{0,4},{1,5},{2,6},{3,7},{4,0},{5,1},{6,2},{7,3},{8,12},{9,13},{10,... | collective-permute-start | bytes 1612808 | tf_op jit(solution)/shard_map/ppermute | solution.py:331
  833.0 11.0 %collective-permute-done.2 = bf16[168,1600]{1,0:T(8,128)(2,1)S(1)} collective-permute-done((bf16[168,1600]{1,0:T(8,128)(2,1)S(1)}, bf16[168,1600]{1,0:T(8,128)(2,1)S(1)}, u32[]{:S(2)}, u32[]{:S(2)}) %collective-permute-start.2) | collective-permute-done | bytes 537632 | tf_op jit(solution)/shard_map/ppermute | solution.py:331
  844.0 24.2 %collective-permute-done.3 = bf16[168,1600]{1,0:T(8,128)(2,1)S(1)} collective-permute-done((bf16[168,1600]{1,0:T(8,128)(2,1)S(1)}, bf16[168,1600]{1,0:T(8,128)(2,1)S(1)}, u32[]{:S(2)}, u32[]{:S(2)}) %collective-permute-start.3) | collective-permute-done | bytes 537632 | tf_op jit(solution)/shard_map/ppermute | solution.py:331
  868.2 11.9 %collective-permute-done.4 = bf16[168,1600]{1,0:T(8,128)(2,1)S(1)} collective-permute-done((bf16[168,1600]{1,0:T(8,128)(2,1)S(1)}, bf16[168,1600]{1,0:T(8,128)(2,1)S(1)}, u32[]{:S(2)}, u32[]{:S(2)}) %collective-permute-start.4) | collective-permute-done | bytes 537632 | tf_op jit(solution)/shard_map/ppermute | solution.py:331
  881.2 28.6 %collect_rest.1 = (bf16[76,8,1600]{2,1,0:T(8,128)(2,1)}, f32[32,2,8,1600]{3,2,1,0:T(8,128)}) custom-call(bf16[21,8,1600]{2,1,0:T(8,128)(2,1)} %fusion.85.qkv_ref, f32[2,8,1600]{2,1,0:T(8,128)} %pad_bitcast_fusion.vec_ref), custom_call_target="tpu_custom_call" | custom-call | bytes 90000000 | tf_op jit(solution)/shard_map/collect_rest/pallas_call | solution.py:1188
  (219 shorter events, 128.4 us)
Async XLA Ops:
  90.5 6.8 copy-start.1
  91.5 6.9 copy-start.16
  100.1 8.1 copy-start.11
  335.4 11.0 %copy-start.2 = (bf16[8,25,8,1600]{3,2,1,0:T(8,128)(2,1)S(1)}, bf16[8,25,8,1600]{3,2,1,0:T(8,128)(2,1)}, u32[]{:S(2)}) copy-start(bf16[8,25,8,1600]{3,2,1,0:T(8,128)(2,1)} %get-tuple-element.41) | copy-start | bytes 15360004
  335.4 11.0 %copy-start.20 = (bf16[2,2,256,1600]{3,2,1,0:T(8,128)(2,1)S(1)}, bf16[2,2,256,1600]{3,2,1,0:T(8,128)(2,1)}, u32[]{:S(2)}) copy-start(bf16[2,2,256,1600]{3,2,1,0:T(8,128)(2,1)} %get-tuple-element.40) | copy-start | bytes 9830404
  335.5 26.7 %slice-start = ((s8[5324800]{0:T(1024)(128)(4,1)}), s8[4194304]{0:T(1024)(128)(4,1)S(1)}, s32[]{:S(2)}) async-start(s8[5324800]{0:T(1024)(128)(4,1)} %bitcast.183), calls=%async_computation | async-start | bytes 8388608
  346.4 15.7 %slice-start.1 = ((s8[5324800]{0:T(1024)(128)(4,1)}), s8[1130496]{0:T(1024)(128)(4,1)S(1)}, s32[]{:S(2)}) async-start(s8[5324800]{0:T(1024)(128)(4,1)} %bitcast.183), calls=%async_computation.1 | async-start | bytes 2260992
  362.2 8.5 copy-start.25
  427.4 10.5 %copy-start.23 = (bf16[1024,1600]{0,1:T(8,128)(2,1)S(1)}, bf16[1024,1600]{0,1:T(8,128)(2,1)}, u32[]{:S(2)}) copy-start(bf16[1024,1600]{0,1:T(8,128)(2,1)} %get-tuple-element.87) | copy-start | bytes 9830404
  497.3 98.6 %collective-permute-start = (bf16[1024,896]{1,0:T(8,128)(2,1)}, bf16[1024,896]{1,0:T(8,128)(2,1)}, u32[]{:S(2)}, u32[]{:S(2)}) collective-permute-start(bf16[1024,896]{1,0:T(8,128)(2,1)} %convert_element_type.261), channel_id=1, source_target_pairs={{2,0},{3,1},{6,4},{7,5},{10,8},{11,9},{14,12},{15,13},{18,16},{19,... | collective-permute-start | bytes 5505032 | tf_op jit(solution)/shard_map/ppermute | solution.py:331
  507.9 57.4 %collective-permute-start.13 = (bf16[800,448]{0,1:T(8,128)(2,1)}, bf16[800,448]{0,1:T(8,128)(2,1)}, u32[]{:S(2)}, u32[]{:S(2)}) collective-permute-start(bf16[800,448]{0,1:T(8,128)(2,1)} %bitcast.201), channel_id=1, source_target_pairs={{0,16},{1,17},{2,18},{3,19},{4,20},{5,21},{6,22},{7,23},{8,24},{9,... | collective-permute-start | bytes 2150408 | tf_op jit(solution)/shard_map/ppermute | solution.py:331
  517.4 148.4 %collective-permute-start.9 = (bf16[800,1600]{1,0:T(8,128)(2,1)}, bf16[800,1600]{1,0:T(8,128)(2,1)}, u32[]{:S(2)}, u32[]{:S(2)}) collective-permute-start(bf16[800,1600]{1,0:T(8,128)(2,1)} %convolution_convert_fusion.4), channel_id=1, source_target_pairs={{0,16},{1,17},{2,18},{3,19},{4,20},{5,21},{6,22},{7,23},{8,24},{9,... | collective-permute-start | bytes 7680008 | tf_op jit(solution)/shard_map/ppermute | solution.py:331
  566.7 29.1 %copy-start.9 = (f32[1024,896]{1,0:T(8,128)S(1)}, f32[1024,896]{1,0:T(8,128)}, u32[]{:S(2)}) copy-start(f32[1024,896]{1,0:T(8,128)} %get-tuple-element.47) | copy-start | bytes 11010052
  566.7 32.4 %slice-start.3 = ((s8[4472832]{0:T(1024)(128)(4,1)}), s8[4194304]{0:T(1024)(128)(4,1)S(1)}, s32[]{:S(2)}) async-start(s8[4472832]{0:T(1024)(128)(4,1)} %bitcast.212), calls=%async_computation.3 | async-start | bytes 8388608
  568.4 11.3 %collective-permute-start.14 = (bf16[200,448]{1,0:T(8,128)(2,1)S(1)}, bf16[200,448]{1,0:T(8,128)(2,1)S(1)}, u32[]{:S(2)}, u32[]{:S(2)}) collective-permute-start(bf16[200,448]{1,0:T(8,128)(2,1)S(1)} %get-tuple-element.106), channel_id=1, source_target_pairs={{0,2},{1,3},{2,4},{3,5},{4,6},{5,7},{6,0},{7,1},{8,10},{9,11},{10,... | collective-permute-start | bytes 537608 | tf_op jit(solution)/shard_map/ppermute | solution.py:331
  568.5 21.6 %collective-permute-start.15 = (bf16[200,448]{1,0:T(8,128)(2,1)S(1)}, bf16[200,448]{1,0:T(8,128)(2,1)S(1)}, u32[]{:S(2)}, u32[]{:S(2)}) collective-permute-start(bf16[200,448]{1,0:T(8,128)(2,1)S(1)} %get-tuple-element.108), channel_id=1, source_target_pairs={{0,4},{1,5},{2,6},{3,7},{4,0},{5,1},{6,2},{7,3},{8,12},{9,13},{10,... | collective-permute-start | bytes 537608 | tf_op jit(solution)/shard_map/ppermute | solution.py:331
  577.8 17.3 %collective-permute-start.16 = (bf16[200,448]{1,0:T(8,128)(2,1)S(1)}, bf16[200,448]{1,0:T(8,128)(2,1)S(1)}, u32[]{:S(2)}, u32[]{:S(2)}) collective-permute-start(bf16[200,448]{1,0:T(8,128)(2,1)S(1)} %get-tuple-element.107), channel_id=1, source_target_pairs={{0,6},{1,7},{2,0},{3,1},{4,2},{5,3},{6,4},{7,5},{8,14},{9,15},{10,... | collective-permute-start | bytes 537608 | tf_op jit(solution)/shard_map/ppermute | solution.py:331
  579.7 75.9 %collective-permute-start.5 = (bf16[800,1600]{1,0:T(8,128)(2,1)}, bf16[800,1600]{1,0:T(8,128)(2,1)}, u32[]{:S(2)}, u32[]{:S(2)}) collective-permute-start(bf16[800,1600]{1,0:T(8,128)(2,1)} %convolution_convert_fusion.5), channel_id=1, source_target_pairs={{0,16},{1,17},{2,18},{3,19},{4,20},{5,21},{6,22},{7,23},{8,24},{9,... | collective-permute-start | bytes 7680008 | tf_op jit(solution)/shard_map/ppermute | solution.py:331
  597.8 8.8 copy-start.7
  657.1 8.7 copy-start.24
  662.1 9.2 %copy-start.12 = (f32[800,1600]{1,0:T(8,128)}, f32[800,1600]{1,0:T(8,128)S(1)}, u32[]{:S(2)}) copy-start(f32[800,1600]{1,0:T(8,128)S(1)} %convert_add_fusion.1) | copy-start | bytes 15360004
  663.5 17.8 %collective-permute-start.6 = (bf16[200,1600]{1,0:T(8,128)(2,1)S(1)}, bf16[200,1600]{1,0:T(8,128)(2,1)S(1)}, u32[]{:S(2)}, u32[]{:S(2)}) collective-permute-start(bf16[200,1600]{1,0:T(8,128)(2,1)S(1)} %get-tuple-element.91), channel_id=1, source_target_pairs={{0,2},{1,3},{2,4},{3,5},{4,6},{5,7},{6,0},{7,1},{8,10},{9,11},{10,... | collective-permute-start | bytes 1920008 | tf_op jit(solution)/shard_map/ppermute | solution.py:331
  663.5 58.4 %collective-permute-start.7 = (bf16[200,1600]{1,0:T(8,128)(2,1)}, bf16[200,1600]{1,0:T(8,128)(2,1)S(1)}, u32[]{:S(2)}, u32[]{:S(2)}) collective-permute-start(bf16[200,1600]{1,0:T(8,128)(2,1)} %get-tuple-element.93), channel_id=1, source_target_pairs={{0,4},{1,5},{2,6},{3,7},{4,0},{5,1},{6,2},{7,3},{8,12},{9,13},{10,... | collective-permute-start | bytes 1920008 | tf_op jit(solution)/shard_map/ppermute | solution.py:331
  663.5 85.9 %collective-permute-start.8 = (bf16[200,1600]{1,0:T(8,128)(2,1)}, bf16[200,1600]{1,0:T(8,128)(2,1)S(1)}, u32[]{:S(2)}, u32[]{:S(2)}) collective-permute-start(bf16[200,1600]{1,0:T(8,128)(2,1)} %get-tuple-element.92), channel_id=1, source_target_pairs={{0,6},{1,7},{2,0},{3,1},{4,2},{5,3},{6,4},{7,5},{8,14},{9,15},{10,... | collective-permute-start | bytes 1920008 | tf_op jit(solution)/shard_map/ppermute | solution.py:331
  671.4 10.0 %copy-start.15 = (f32[12,1600]{1,0:T(8,128)S(1)}, f32[12,1600]{1,0:T(8,128)}, u32[]{:S(2)}) copy-start(f32[12,1600]{1,0:T(8,128)} %concatenate.40) | copy-start | bytes 230404
  675.1 89.4 %collective-permute-start.10 = (bf16[200,1600]{1,0:T(8,128)(2,1)}, bf16[200,1600]{1,0:T(8,128)(2,1)S(1)}, u32[]{:S(2)}, u32[]{:S(2)}) collective-permute-start(bf16[200,1600]{1,0:T(8,128)(2,1)} %get-tuple-element.88), channel_id=1, source_target_pairs={{0,2},{1,3},{2,4},{3,5},{4,6},{5,7},{6,0},{7,1},{8,10},{9,11},{10,... | collective-permute-start | bytes 1920008 | tf_op jit(solution)/shard_map/ppermute | solution.py:331
  676.0 102.4 %collective-permute-start.11 = (bf16[200,1600]{1,0:T(8,128)(2,1)}, bf16[200,1600]{1,0:T(8,128)(2,1)}, u32[]{:S(2)}, u32[]{:S(2)}) collective-permute-start(bf16[200,1600]{1,0:T(8,128)(2,1)} %get-tuple-element.90), channel_id=1, source_target_pairs={{0,4},{1,5},{2,6},{3,7},{4,0},{5,1},{6,2},{7,3},{8,12},{9,13},{10,... | collective-permute-start | bytes 1920008 | tf_op jit(solution)/shard_map/ppermute | solution.py:331
  681.4 97.0 %collective-permute-start.12 = (bf16[200,1600]{1,0:T(8,128)(2,1)}, bf16[200,1600]{1,0:T(8,128)(2,1)}, u32[]{:S(2)}, u32[]{:S(2)}) collective-permute-start(bf16[200,1600]{1,0:T(8,128)(2,1)} %get-tuple-element.89), channel_id=1, source_target_pairs={{0,6},{1,7},{2,0},{3,1},{4,2},{5,3},{6,4},{7,5},{8,14},{9,15},{10,... | collective-permute-start | bytes 1920008 | tf_op jit(solution)/shard_map/ppermute | solution.py:331
  722.0 82.5 %collective-permute-start.1 = (bf16[672,1600]{1,0:T(8,128)(2,1)}, bf16[672,1600]{1,0:T(8,128)(2,1)}, u32[]{:S(2)}, u32[]{:S(2)}) collective-permute-start(bf16[672,1600]{1,0:T(8,128)(2,1)} %bitcast.22), channel_id=1, source_target_pairs={{0,16},{1,17},{2,18},{3,19},{4,20},{5,21},{6,22},{7,23},{8,24},{9,... | collective-permute-start | bytes 6451208 | tf_op jit(solution)/shard_map/ppermute | solution.py:331
  807.9 36.1 %collective-permute-start.2 = (bf16[168,1600]{1,0:T(8,128)(2,1)S(1)}, bf16[168,1600]{1,0:T(8,128)(2,1)S(1)}, u32[]{:S(2)}, u32[]{:S(2)}) collective-permute-start(bf16[168,1600]{1,0:T(8,128)(2,1)S(1)} %get-tuple-element.94), channel_id=1, source_target_pairs={{0,2},{1,3},{2,4},{3,5},{4,6},{5,7},{6,0},{7,1},{8,10},{9,11},{10,... | collective-permute-start | bytes 1612808 | tf_op jit(solution)/shard_map/ppermute | solution.py:331
  809.1 59.1 %collective-permute-start.3 = (bf16[168,1600]{1,0:T(8,128)(2,1)S(1)}, bf16[168,1600]{1,0:T(8,128)(2,1)S(1)}, u32[]{:S(2)}, u32[]{:S(2)}) collective-permute-start(bf16[168,1600]{1,0:T(8,128)(2,1)S(1)} %get-tuple-element.96), channel_id=1, source_target_pairs={{0,4},{1,5},{2,6},{3,7},{4,0},{5,1},{6,2},{7,3},{8,12},{9,13},{10,... | collective-permute-start | bytes 1612808 | tf_op jit(solution)/shard_map/ppermute | solution.py:331
  832.9 47.3 %collective-permute-start.4 = (bf16[168,1600]{1,0:T(8,128)(2,1)S(1)}, bf16[168,1600]{1,0:T(8,128)(2,1)S(1)}, u32[]{:S(2)}, u32[]{:S(2)}) collective-permute-start(bf16[168,1600]{1,0:T(8,128)(2,1)S(1)} %get-tuple-element.95), channel_id=1, source_target_pairs={{0,6},{1,7},{2,0},{3,1},{4,2},{5,3},{6,4},{7,5},{8,14},{9,15},{10,... | collective-permute-start | bytes 1612808 | tf_op jit(solution)/shard_map/ppermute | solution.py:331
  (17 other events, 58.8 us)

commit v5 on v4

--- a/solution.py
+++ b/solution.py
@@ -423,7 +423,7 @@
 
 
 class PlaceGather:
-    def __init__(self, wires, full, slot, along=True, over=True):
+    def __init__(self, wires, full, slot, steps=(1, 2, 3), over=(0, 1, 2, 3)):
         self.full = full
         self.dp, self.cp = lax.axis_index("dp"), lax.axis_index("cp")
         self.y, self.z, self.x = self.dp // 2, self.cp // 2, self.cp % 2
@@ -435,70 +435,71 @@
             view = full.at[slot(self.y, (self.z + 4 + by) % 4)]
             return wires.to(view, view, *to)
 
-        if along:
-            self.up = [share(1 - k, self.above) for k in (1, 2, 3)]
-            self.down = [share(k - 1, self.below) for k in (1, 2, 3)]
-        self.own_over = share(0, self.across) if over else None
-        self.over = [self.own_over] + [share(d, self.across) if along else None for d in (1, 2, 3)]
+        self.steps = steps
+        self.up = {k: share(1 - k, self.above) for k in steps}
+        self.down = {k: share(k - 1, self.below) for k in steps}
+        self.over = {d: share(d, self.across) for d in over}
 
     def partners(self):
         return [self.above, self.below, self.across]
 
-    def start_over(self):
-        self.own_over.start()
-
     def start(self):
-        @pl.when(self.z < 3)
-        def _():
-            self.up[0].start()
-
-        @pl.when(self.z > 0)
-        def _():
-            self.down[0].start()
-
-        if self.own_over is not None:
-            self.start_over()
+        if 1 in self.steps:
+
+            @pl.when(self.z < 3)
+            def _():
+                self.up[1].start()
+
+            @pl.when(self.z > 0)
+            def _():
+                self.down[1].start()
+
+        if 0 in self.over:
+            self.over[0].start()
 
     def forward(self, steps=(1, 2, 3)):
         for k in steps:
 
             @pl.when(self.z >= k)
             def _():
-                self.up[k - 1].wait_recv()
-                if k < 3:
+                if k in self.steps:
+                    self.up[k].wait_recv()
+                if k + 1 in self.steps:
 
                     @pl.when(self.z < 3)
                     def _():
-                        self.up[k].start()
-
-                self.over[4 - k].start()
+                        self.up[k + 1].start()
+
+                if 4 - k in self.over:
+                    self.over[4 - k].start()
 
             @pl.when(self.z <= 3 - k)
             def _():
-                self.down[k - 1].wait_recv()
-                if k < 3:
+                if k in self.steps:
+                    self.down[k].wait_recv()
+                if k + 1 in self.steps:
 
                     @pl.when(self.z > 0)
                     def _():
-                        self.down[k].start()
-
-                self.over[k].start()
+                        self.down[k + 1].start()
+
+                if k in self.over:
+                    self.over[k].start()
 
     def finish(self):
-        sent_over = [copy for copy in self.over if copy is not None]
-        for copy in sent_over:
+        for copy in self.over.values():
             copy.wait_recv()
-        for copy in sent_over:
+        for copy in self.over.values():
             copy.wait_send()
-        for k in (1, 2, 3):
+        for k in self.steps:
 
             @pl.when(jnp.logical_and(self.z >= k - 1, self.z < 3))
             def _():
-                self.up[k - 1].wait_send()
+                self.up[k].wait_send()
 
             @pl.when(jnp.logical_and(self.z <= 4 - k, self.z > 0))
             def _():
-                self.down[k - 1].wait_send()
+                self.down[k].wait_send()
 
 
 class QuadGather:
@@ -674,21 +675,27 @@
 
     others(send)
     cot.start()
+    tok.forward()
     weights.forward()
-    tok.forward()
+    early = []
+    for index, (ref, slot) in enumerate(((out_ref, slot_out), (fc_ref, slot_turned(sz.fc_turn)))):
+        view = ref.at[slot(y, z)]
+        pltpu.make_async_copy(view, view, kind_sems.at[index + 1]).wait()
+        early.append(PlaceGather(wires, ref, slot, steps=(1,), over=(0,)))
+        early[-1].start()
     cot.forward()
     heads(sent)
     others(sent)
     vector_sends(lambda copy: copy.wait_send())
-    for index, (ref, slot) in enumerate(
-        ((out_ref, slot_out), (fc_ref, slot_turned(sz.fc_turn)), (proj_ref, slot_turned(sz.proj_turn)))
-    ):
-        view = ref.at[slot(y, z)]
-        pltpu.make_async_copy(view, view, kind_sems.at[index + 1]).wait()
+    view = proj_ref.at[slot_turned(sz.proj_turn)(y, z)]
+    pltpu.make_async_copy(view, view, kind_sems.at[3]).wait()
     pltpu.make_async_copy(vec_ref, vec_ref, kind_sems.at[4]).wait()
     tok.finish()
     cot.finish()
     weights.finish()
+    for first in early:
+        first.forward((1,))
+        first.finish()
 
 
 HBM = pl.BlockSpec(memory_space=pl.ANY)
@@ -737,7 +744,7 @@
         scratch_shapes=[
             pltpu.SemaphoreType.DMA((sz.block + 3 * sz.head_grains + sz.spill + 32,)),
             pltpu.SemaphoreType.DMA((5,)),
-            *wire_sems(16),
+            *wire_sems(22),
             pltpu.SemaphoreType.DMA((2,)),
         ],
         compiler_params=REMOTE,
@@ -755,19 +762,24 @@
     wires = Wires(send_sems, recv_sems)
     part = heads * size
     rows = q_ref.shape[0] // 2
-    blk = 128
+    blk = 256
     scale = size**-0.5
     odd = z % 2 == 1
-    w_out = PlaceGather(wires, out_ref, slot_out)
-    w_fc = PlaceGather(wires, fc_ref, slot_turned(fc_turn))
-    w_proj = PlaceGather(wires, proj_ref, slot_turned(proj_turn), along=False)
+    w_out = PlaceGather(wires, out_ref, slot_out, steps=(2, 3), over=(1, 2, 3))
+    w_fc = PlaceGather(wires, fc_ref, slot_turned(fc_turn), steps=(2, 3), over=(1, 2, 3))
+    w_proj = PlaceGather(wires, proj_ref, slot_turned(proj_turn), steps=(1,), over=(0,))
     others = [(c, 1 - x), (1 - c, x), (1 - c, 1 - x)]
     quad = [(y * 2 + tc, z * 2 + tx) for tc, tx in others]
     greet(w_out.partners() + quad)
     keys = wires.to(kv_ref, before_ref, dp, (cp + 2) % 8)
 
-    w_out.start()
-    w_fc.start()
+    w_out.forward()
+
+    @pl.when(jnp.logical_not(odd))
+    def _():
+        keys.start()
+
+    w_fc.forward((1,))
 
     def own(group, _):
         start = group * rows
@@ -791,13 +803,6 @@
         return 0
 
     lax.fori_loop(0, 2, own, 0)
-    w_out.forward()
-
-    @pl.when(jnp.logical_not(odd))
-    def _():
-        keys.start()
-
-    w_fc.forward((1,))
 
     def add_before(index, _):
         here = pl.ds(pl.multiple_of(index * blk, blk), blk)
@@ -840,7 +845,6 @@
     def _():
         w_fc.forward((2,))
 
-    w_proj.start_over()
     mine = c * 2 + x
     each = rows // 2
     swaps = []
@@ -853,14 +857,15 @@
         stage.at[pl.ds(pl.multiple_of(mine * each, each), each)], mixed_ref.at[mine], local_sems.at[1]
     )
     local.start()
+    whole.forward()
     w_fc.forward((3,))
-    whole.forward()
+    w_proj.start()
     for copy in swaps:
         copy.wait_recv()
     whole.finish()
     w_fc.finish()
-    w_proj.over[0].wait_recv()
-    w_proj.over[0].wait_send()
+    w_proj.forward((1,))
+    w_proj.finish()
     for copy in swaps:
         copy.wait_send()
     local.wait()
@@ -906,12 +911,12 @@
 def acts_kernel(proj_turn, act_ref, proj_in, act_all, proj_ref, send_sems, recv_sems, local_sem):
     wires = Wires(send_sems, recv_sems)
     quad = QuadGather(wires, act_ref, act_all, local_sem)
-    places = PlaceGather(wires, proj_ref, slot_turned(proj_turn), over=False)
+    places = PlaceGather(wires, proj_ref, slot_turned(proj_turn), steps=(2, 3), over=(1, 2, 3))
     greet(places.partners() + [quad.over_x, quad.over_c])
     quad.start()
-    places.start()
+    places.forward((1, 2))
     quad.forward()
-    places.forward()
+    places.forward((3,))
     quad.finish()
     places.finish()
 
@@ -1211,7 +1216,7 @@
     _, _, z, _ = my_place()
     part = heads * size
     rows = q_ref.shape[0] // 2
-    blk = 128
+    blk = 256
     scale = size**-0.5
 
     def visit(here, start, seen, allowed):
@@ -1468,16 +1473,17 @@
     grad_vectors = jnp.sum(all_vectors.reshape(32, sz.vec * GRAIN, width), axis=0)[:count]
     me = flat_id(y, c, z, x)
     row = me * (sz.block * GRAIN) + lax.broadcasted_iota(jnp.int32, (sz.block * GRAIN, 1), 0)
-    table = jnp.where(
+    used = (sz.vec_start % sz.block) * GRAIN
+    tail = jnp.pad(grad_vectors, ((used, sz.block * GRAIN - used - count), (0, 0)))
+    param_grad = jnp.where(
         row < sz.out_start * GRAIN,
-        flat(table_qkv),
-        jnp.where(row < sz.fc_start * GRAIN, table_out, flat(table_mlp)),
-    ).astype(f32)
-    used = (sz.vec_start % sz.block) * GRAIN
-    tail = jnp.concatenate([grad_vectors, jnp.zeros((sz.block * GRAIN - used - count, width), f32)])
-    last = me == sz.vec_start // sz.block
-    tail = jnp.where(last, tail, table[used:])
-    param_grad = jnp.concatenate([table[:used], tail])
+        flat(table_qkv).astype(f32),
+        jnp.where(
+            row < sz.fc_start * GRAIN,
+            table_out.astype(f32),
+            jnp.where(row < sz.vec_start * GRAIN, flat(table_mlp).astype(f32), tail),
+        ),
+    )
     return (output, input_grad, param_grad)
 
 

time: 937 us -> 913 us (0.974)
  Pallas kernels: 504 us -> 451 us
  waiting for transfers between devices: 155 us -> 178 us
  starting transfers between devices: 49.4 us -> 61.1 us
    pallas_call x1, Pallas kernels: 124 us -> 90 us  [forward_call(): pl.pallas_call(functools.partial(forward_kernel, sz.quarter_heads, sz.hea...]
    pallas_call x1, Pallas kernels: 89.4 us -> 61.1 us  [acts_call(): pl.pallas_call(functools.partial(acts_kernel, sz.proj_turn), out_shape=(j...]
    ppermute x17, waiting for transfers between devices: 155 us -> 178 us  [permute(): return lax.ppermute(value, ('dp', 'cp'), pairs)]
    pallas_call x1, Pallas kernels: 85.4 us -> 104 us  [open_call(): pl.pallas_call(functools.partial(open_kernel, sz), out_shape=(like(8, sz....]
    pallas_call x2, Pallas kernels: 75.6 us -> 63.1 us  [attend_back(): pl.pallas_call(functools.partial(attend_back_kernel, sz.quarter_heads, sz...]
    ppermute x17, starting transfers between devices: 49.4 us -> 61.1 us  [permute(): return lax.ppermute(value, ('dp', 'cp'), pairs)]
  transfers between devices with their start and end apart: 17 -> 17, of which waited for: 10 -> 11; matrix products, arithmetic and copies ran while one was open for 10% -> 10% of each run, Pallas kernels for 9% -> 8%
where the time goes in v5:
time: 913 us; the launch traced here: 900 us
  Pallas kernels  451 us (49%)
  waiting for transfers between devices  178 us (19%)
  matrix products  123 us (13%)
  starting transfers between devices  61.1 us (7%)
  other arithmetic  44.8 us (5%)
  local copies, waits for them, and re-layouts  40.8 us (4%)
    ppermute x17, waiting for transfers between devices, permute(): return lax.ppermute(value, ('dp', 'cp'), pairs)  178 us
    pallas_call x1, Pallas kernels, open_call(): pl.pallas_call(functools.partial(open_kernel, sz), out_shape=(like(8, sz....  104 us
    pallas_call x1, Pallas kernels, forward_call(): pl.pallas_call(functools.partial(forward_kernel, sz.quarter_heads, sz.hea...  90 us
    pallas_call x2, Pallas kernels, attend_back(): pl.pallas_call(functools.partial(attend_back_kernel, sz.quarter_heads, sz...  63.1 us
    pallas_call x1, Pallas kernels, acts_call(): pl.pallas_call(functools.partial(acts_kernel, sz.proj_turn), out_shape=(j...  61.1 us
    ppermute x17, starting transfers between devices, permute(): return lax.ppermute(value, ('dp', 'cp'), pairs)  61.1 us
    pallas_call x2, Pallas kernels, quad_sum(): pl.pallas_call(quad_sum_kernel, out_shape=jax.ShapeDtypeStruct(partial.sh...  57.6 us
    dot_general x5, matrix products, dot_nt(): return lax.dot_general(a, b, NT, preferred_element_type=jnp.float32)  41.9 us
  transfers between devices with their start and end apart: 17, of which 11 were waited for; matrix products, arithmetic and copies ran while one was open for 10% of the time, Pallas kernels for 8%

profile of v5, /device:TPU:10, one launch (start us, length us, event | category | flops | bytes accessed | tf_op | source)
XLA Modules:
  0.0 900.2 jit_solution(18438890474180726733)
XLA Ops:
  5.0 103.8 %open.1 = (bf16[8,21,8,1600]{3,2,1,0:T(8,128)(2,1)}, bf16[8,7,8,1600]{3,2,1,0:T(8,128)(2,1)}, bf16[8,25,8,1600]{3,2,1,0:T(8,128)(2,1)}, bf16[8,25,8,1600]{3,2,1,...) custom-call(bf16[76,8,1600]{2,1,0:T(8,128)(2,1)} %bitcast.196, ...), custom_call_target="tpu_custom_call" | custom-call | tf_op jit(solution)/shard_map/open/pallas_call | solution.py:731
  131.1 90.0 %forward.1 = (f32[1024,448]{1,0:T(8,128)}, f32[1024,8]{1,0:T(8,128)}, bf16[1024,896]{1,0:T(8,128)(2,1)}, bf16[4,256,448]{2,1,0:T(8,128)(2,1)}, bf16[8,7,8,1600]{...) custom-call(bf16[1024,448]{1,0:T(8,128)(2,1)} %add_convert_fusion.2., ...), custom_call_target="tpu_custom_call", output_to_operand_aliasing={{4}: (2, {}), {5}: (3, {}), {6}: (4, {})} | custom-call | bytes 360000000 | tf_op jit(solution)/shard_map/forward/pallas_call | solution.py:885
  230.5 61.1 %acts.1 = (bf16[2,2,256,1600]{3,2,1,0:T(8,128)(2,1)}, bf16[8,25,8,1600]{3,2,1,0:T(8,128)(2,1)}) custom-call(bf16[256,1600]{1,0:T(8,128)(2,1)} %add_convert_fusion.4.act_ref, bf16[8,25,8,1600]{3,2,1,0:T(8,128)(2,1)} %get-tuple-element.37.proj_in), custom_call_target="tpu_custom_call", output_to_operand_aliasing={{1}: (1, {})} | custom-call | bytes 180000000 | tf_op jit(solution)/shard_map/acts/pallas_call | solution.py:947
  291.7 11.0 %fusion.102 = f32[1024,1600]{0,1:T(8,128)} fusion(bf16[1024,1600]{1,0:T(8,128)(2,1)} %bitcast.216, bf16[1600,1600]{1,0:T(8,128)(2,1)} %bitcast.180), kind=kOutput, calls=%fused_computation.227 | convolution fusion | flops 5242880000 | bytes 14950400 | tf_op jit(solution)/shard_map/dot_general | solution.py:307
  302.6 15.7 %convert_reduce_fusion = (f32[1600]{0:T(1024)S(1)}, bf16[1024,1600]{0,1:T(8,128)(2,1)S(1)}, bf16[1024,1600]{0,1:T(8,128)(2,1)}) fusion(f32[1024,1600]{0,1:T(8,128)} %fusion.102, f32[1600]{0:T(1024)S(1)} %add.412, bf16[1024,1600]{1,0:T(8,128)(2,1)S(1)} %bitcast.214, bf16[1600,1600]{1,0:T(8,128)(2,1)S(1)} %bitcast.177), kind=kOutput, calls=%fused_computation.19 | convolution fusion | flops 5290392064 | bytes 21516800 | tf_op jit(solution)/shard_map/dot_general | solution.py:307
  318.4 8.5 convolution_convert_fusion.3
  326.9 30.4 %quad_sum.2 = f32[256,1600]{1,0:T(8,128)} custom-call(bf16[2,2,256,1600]{3,2,1,0:T(8,128)(2,1)} %bitcast.188), custom_call_target="tpu_custom_call" | custom-call | bytes 90000000 | tf_op jit(solution)/shard_map/quad_sum/pallas_call | solution.py:1032
  362.2 24.5 %grads.1 = bf16[2,2,256,1600]{3,2,1,0:T(8,128)(2,1)} custom-call(bf16[256,1600]{1,0:T(8,128)(2,1)} %get-tuple-element.85.act_ref), custom_call_target="tpu_custom_call" | custom-call | bytes 75000000 | tf_op jit(solution)/shard_map/grads/pallas_call | solution.py:934
  386.6 10.1 %fusion.16 = bf16[1024,1600]{1,0:T(8,128)(2,1)S(1)} fusion(bf16[1024,1600]{1,0:T(8,128)(2,1)} %bitcast.189, bf16[1792,1600]{1,0:T(8,128)(2,1)} %bitcast.207), kind=kOutput, calls=%fused_computation.32 | convolution fusion | flops 5244518400 | bytes 12009472 | tf_op jit(solution)/shard_map/dot_general | solution.py:315
  397.1 10.9 %convolution_convert_fusion.2 = bf16[1024,1600]{1,0:T(8,128)(2,1)} fusion(bf16[1024,1600]{0,1:T(8,128)(2,1)S(1)} %copy-done.22, bf16[1600,1600]{1,0:T(8,128)(2,1)} %bitcast.176), kind=kOutput, calls=%fused_computation.34 | convolution fusion | flops 5244518400 | bytes 11673600 | tf_op jit(solution)/shard_map/dot_general | solution.py:315
  409.1 39.1 %attend_back_before.1 = (f32[1024,448]{1,0:T(8,128)}, f32[1024,896]{1,0:T(8,128)}, f32[256,1600]{1,0:T(8,128)}) custom-call(bf16[1024,448]{1,0:T(8,128)(2,1)} %add_convert_fusion.2.q_ref.refs_0_, bf16[1024,896]{1,0:T(8,128)(2,1)} %get-tuple-element.36.refs_1_, bf16[1024,448]{1,0:T(8,128)(2,1)} %pad_maximum_fusion.1.refs_2_, ...), custom_call_target="tpu_custom_call" | custom-call | bytes 105000000 | tf_op jit(solution)/shard_map/attend_back_before/pallas_call | solution.py:1299
  451.7 11.3 %collective-permute-start = (bf16[1024,896]{1,0:T(8,128)(2,1)}, bf16[1024,896]{1,0:T(8,128)(2,1)}, u32[]{:S(2)}, u32[]{:S(2)}) collective-permute-start(bf16[1024,896]{1,0:T(8,128)(2,1)} %convert_element_type.275), channel_id=1, source_target_pairs={{2,0},{3,1},{6,4},{7,5},{10,8},{11,9},{14,12},{15,13},{18,16},{19,... | collective-permute-start | bytes 5505032 | tf_op jit(solution)/shard_map/ppermute | solution.py:331
  462.9 7.6 convolution_convert_fusion.5
  472.8 5.7 convolution_convert_fusion.6
  484.9 24.0 %attend_back_own.1 = (bf16[1024,448]{1,0:T(8,128)(2,1)}, f32[1024,896]{1,0:T(8,128)}) custom-call(bf16[1024,448]{1,0:T(8,128)(2,1)} %add_convert_fusion.2.q_ref.refs_0_, bf16[1024,896]{1,0:T(8,128)(2,1)} %add_convert_fusion.1.kv_ref.refs_1_, bf16[1024,448]{1,0:T(8,128)(2,1)} %pad_maximum_fusion.1.refs_2_, f32[1024,448]{1,0:T(8,128)} %get-tuple-element.42.refs_3_, ...), custom_call_target="tpu_custom_call" | custom-call | bytes 105000000 | tf_op jit(solution)/shard_map/attend_back_own/pallas_call | solution.py:1299
  513.5 7.6 convolution_convert_fusion.4
  521.1 26.6 %collective-permute-done.13 = bf16[800,448]{0,1:T(8,128)(2,1)} collective-permute-done((bf16[800,448]{0,1:T(8,128)(2,1)}, bf16[800,448]{0,1:T(8,128)(2,1)}, u32[]{:S(2)}, u32[]{:S(2)}) %collective-permute-start.13) | collective-permute-done | bytes 716832 | tf_op jit(solution)/shard_map/ppermute | solution.py:331
  550.9 9.6 %collective-permute-start.15 = (bf16[200,448]{1,0:T(8,128)(2,1)S(1)}, bf16[200,448]{1,0:T(8,128)(2,1)S(1)}, u32[]{:S(2)}, u32[]{:S(2)}) collective-permute-start(bf16[200,448]{1,0:T(8,128)(2,1)S(1)} %get-tuple-element.108), channel_id=1, source_target_pairs={{0,4},{1,5},{2,6},{3,7},{4,0},{5,1},{6,2},{7,3},{8,12},{9,13},{10,... | collective-permute-start | bytes 537608 | tf_op jit(solution)/shard_map/ppermute | solution.py:331
  564.3 9.1 %collective-permute-done.15 = bf16[200,448]{1,0:T(8,128)(2,1)S(1)} collective-permute-done((bf16[200,448]{1,0:T(8,128)(2,1)S(1)}, bf16[200,448]{1,0:T(8,128)(2,1)S(1)}, u32[]{:S(2)}, u32[]{:S(2)}) %collective-permute-start.15) | collective-permute-done | bytes 179232 | tf_op jit(solution)/shard_map/ppermute | solution.py:331
  579.6 10.3 %convolution_convert_fusion.1 = bf16[1024,1600]{1,0:T(8,128)(2,1)} fusion(bf16[1344,1600]{1,0:T(8,128)(2,1)} %bitcast.209, bf16[1024,896]{1,0:T(8,128)(2,1)S(1)} %add_convert_fusion, bf16[1024,448]{1,0:T(8,128)(2,1)S(1)} %copy-done.13), kind=kOutput, calls=%fused_computation.33 | convolution fusion | flops 4411162624 | bytes 10330112 | tf_op jit(solution)/shard_map/dot_general | solution.py:315
  591.3 27.2 %quad_sum.3 = f32[256,1600]{1,0:T(8,128)} custom-call(bf16[2,2,256,1600]{3,2,1,0:T(8,128)(2,1)} %bitcast.187), custom_call_target="tpu_custom_call" | custom-call | bytes 90000000 | tf_op jit(solution)/shard_map/quad_sum/pallas_call | solution.py:1032
  622.0 10.0 %convolution_convert_fusion = bf16[1344,1600]{1,0:T(8,128)(2,1)} fusion(bf16[1024,1600]{1,0:T(8,128)(2,1)} %copy-done.10, bf16[1024,896]{1,0:T(8,128)(2,1)} %copy-done.7, bf16[1024,448]{1,0:T(8,128)(2,1)S(1)} %copy-done.13), kind=kOutput, calls=%fused_computation.6 | convolution fusion | flops 4411674624 | bytes 10330112 | tf_op jit(solution)/shard_map/dot_general | solution.py:311
  669.1 22.7 %collective-permute-done.7 = bf16[200,1600]{1,0:T(8,128)(2,1)S(1)} collective-permute-done((bf16[200,1600]{1,0:T(8,128)(2,1)}, bf16[200,1600]{1,0:T(8,128)(2,1)S(1)}, u32[]{:S(2)}, u32[]{:S(2)}) %collective-permute-start.7) | collective-permute-done | bytes 640032 | tf_op jit(solution)/shard_map/ppermute | solution.py:331
  692.8 41.7 %collective-permute-done.6 = bf16[200,1600]{1,0:T(8,128)(2,1)S(1)} collective-permute-done((bf16[200,1600]{1,0:T(8,128)(2,1)}, bf16[200,1600]{1,0:T(8,128)(2,1)S(1)}, u32[]{:S(2)}, u32[]{:S(2)}) %collective-permute-start.6) | collective-permute-done | bytes 640032 | tf_op jit(solution)/shard_map/ppermute | solution.py:331
  737.0 13.7 %collective-permute-done.12 = bf16[200,1600]{1,0:T(8,128)(2,1)S(1)} collective-permute-done((bf16[200,1600]{1,0:T(8,128)(2,1)}, bf16[200,1600]{1,0:T(8,128)(2,1)S(1)}, u32[]{:S(2)}, u32[]{:S(2)}) %collective-permute-start.12) | collective-permute-done | bytes 640032 | tf_op jit(solution)/shard_map/ppermute | solution.py:331
  750.7 12.3 %collective-permute-done.10 = bf16[200,1600]{1,0:T(8,128)(2,1)} collective-permute-done((bf16[200,1600]{1,0:T(8,128)(2,1)}, bf16[200,1600]{1,0:T(8,128)(2,1)}, u32[]{:S(2)}, u32[]{:S(2)}) %collective-permute-start.10) | collective-permute-done | bytes 640032 | tf_op jit(solution)/shard_map/ppermute | solution.py:331
  766.0 20.1 %collect_mlp.1 = (bf16[76,8,1600]{2,1,0:T(8,128)(2,1)}, bf16[4,76,8,448]{3,2,1,0:T(8,128)(2,1)}) custom-call(bf16[25,8,1600]{2,1,0:T(8,128)(2,1)} %fusion.80.fc_ref, bf16[25,8,1600]{2,1,0:T(8,128)(2,1)} %fusion.81.proj_ref, bf16[25,8,448]{2,1,0:T(8,128)(2,1)} %fusion.92.out_ref), custom_call_target="tpu_custom_call" | custom-call | bytes 90000000 | tf_op jit(solution)/shard_map/collect_mlp/pallas_call | solution.py:1117
  791.8 22.6 %collective-permute-start.4 = (bf16[168,1600]{1,0:T(8,128)(2,1)S(1)}, bf16[168,1600]{1,0:T(8,128)(2,1)S(1)}, u32[]{:S(2)}, u32[]{:S(2)}) collective-permute-start(bf16[168,1600]{1,0:T(8,128)(2,1)S(1)} %get-tuple-element.95), channel_id=1, source_target_pairs={{0,6},{1,7},{2,0},{3,1},{4,2},{5,3},{6,4},{7,5},{8,14},{9,15},{10,... | collective-permute-start | bytes 1612808 | tf_op jit(solution)/shard_map/ppermute | solution.py:331
  816.1 11.6 %collective-permute-done.4 = bf16[168,1600]{1,0:T(8,128)(2,1)S(1)} collective-permute-done((bf16[168,1600]{1,0:T(8,128)(2,1)S(1)}, bf16[168,1600]{1,0:T(8,128)(2,1)S(1)}, u32[]{:S(2)}, u32[]{:S(2)}) %collective-permute-start.4) | collective-permute-done | bytes 537632 | tf_op jit(solution)/shard_map/ppermute | solution.py:331
  827.7 22.2 %collective-permute-done.3 = bf16[168,1600]{1,0:T(8,128)(2,1)S(1)} collective-permute-done((bf16[168,1600]{1,0:T(8,128)(2,1)S(1)}, bf16[168,1600]{1,0:T(8,128)(2,1)S(1)}, u32[]{:S(2)}, u32[]{:S(2)}) %collective-permute-start.3) | collective-permute-done | bytes 537632 | tf_op jit(solution)/shard_map/ppermute | solution.py:331
  849.9 11.9 %collective-permute-done.2 = bf16[168,1600]{1,0:T(8,128)(2,1)S(1)} collective-permute-done((bf16[168,1600]{1,0:T(8,128)(2,1)S(1)}, bf16[168,1600]{1,0:T(8,128)(2,1)S(1)}, u32[]{:S(2)}, u32[]{:S(2)}) %collective-permute-start.2) | collective-permute-done | bytes 537632 | tf_op jit(solution)/shard_map/ppermute | solution.py:331
  862.9 30.5 %collect_rest.1 = (bf16[76,8,1600]{2,1,0:T(8,128)(2,1)}, f32[32,2,8,1600]{3,2,1,0:T(8,128)}) custom-call(bf16[21,8,1600]{2,1,0:T(8,128)(2,1)} %fusion.85.qkv_ref, f32[2,8,1600]{2,1,0:T(8,128)} %pad_bitcast_fusion.vec_ref), custom_call_target="tpu_custom_call" | custom-call | bytes 90000000 | tf_op jit(solution)/shard_map/collect_rest/pallas_call | solution.py:1193
  (215 shorter events, 134.5 us)
Async XLA Ops:
  109.8 6.1 copy-start.15
  118.0 8.0 slice-start.3
  120.4 5.6 copy-start.10
  120.4 5.6 slice-start.4
  291.6 11.0 %copy-start.2 = (bf16[8,25,8,1600]{3,2,1,0:T(8,128)(2,1)S(1)}, bf16[8,25,8,1600]{3,2,1,0:T(8,128)(2,1)}, u32[]{:S(2)}) copy-start(bf16[8,25,8,1600]{3,2,1,0:T(8,128)(2,1)} %get-tuple-element.41) | copy-start | bytes 15360004
  291.7 11.0 %copy-start.19 = (bf16[2,2,256,1600]{3,2,1,0:T(8,128)(2,1)S(1)}, bf16[2,2,256,1600]{3,2,1,0:T(8,128)(2,1)}, u32[]{:S(2)}) copy-start(bf16[2,2,256,1600]{3,2,1,0:T(8,128)(2,1)} %get-tuple-element.40) | copy-start | bytes 9830404
  291.7 26.7 %slice-start = ((s8[5324800]{0:T(1024)(128)(4,1)}), s8[4194304]{0:T(1024)(128)(4,1)S(1)}, s32[]{:S(2)}) async-start(s8[5324800]{0:T(1024)(128)(4,1)} %bitcast.181), calls=%async_computation | async-start | bytes 8388608
  302.6 15.7 %slice-start.1 = ((s8[5324800]{0:T(1024)(128)(4,1)}), s8[1130496]{0:T(1024)(128)(4,1)S(1)}, s32[]{:S(2)}) async-start(s8[5324800]{0:T(1024)(128)(4,1)} %bitcast.181), calls=%async_computation.1 | async-start | bytes 2260992
  318.4 8.5 copy-start.24
  386.6 10.5 %copy-start.22 = (bf16[1024,1600]{0,1:T(8,128)(2,1)S(1)}, bf16[1024,1600]{0,1:T(8,128)(2,1)}, u32[]{:S(2)}) copy-start(bf16[1024,1600]{0,1:T(8,128)(2,1)} %get-tuple-element.87) | copy-start | bytes 9830404
  451.7 126.0 %collective-permute-start = (bf16[1024,896]{1,0:T(8,128)(2,1)}, bf16[1024,896]{1,0:T(8,128)(2,1)}, u32[]{:S(2)}, u32[]{:S(2)}) collective-permute-start(bf16[1024,896]{1,0:T(8,128)(2,1)} %convert_element_type.275), channel_id=1, source_target_pairs={{2,0},{3,1},{6,4},{7,5},{10,8},{11,9},{14,12},{15,13},{18,16},{19,... | collective-permute-start | bytes 5505032 | tf_op jit(solution)/shard_map/ppermute | solution.py:331
  470.6 168.5 %collective-permute-start.5 = (bf16[800,1600]{1,0:T(8,128)(2,1)}, bf16[800,1600]{1,0:T(8,128)(2,1)}, u32[]{:S(2)}, u32[]{:S(2)}) collective-permute-start(bf16[800,1600]{1,0:T(8,128)(2,1)} %convolution_convert_fusion.5), channel_id=1, source_target_pairs={{0,16},{1,17},{2,18},{3,19},{4,20},{5,21},{6,22},{7,23},{8,24},{9,... | collective-permute-start | bytes 7680008 | tf_op jit(solution)/shard_map/ppermute | solution.py:331
  481.3 66.5 %collective-permute-start.13 = (bf16[800,448]{0,1:T(8,128)(2,1)}, bf16[800,448]{0,1:T(8,128)(2,1)}, u32[]{:S(2)}, u32[]{:S(2)}) collective-permute-start(bf16[800,448]{0,1:T(8,128)(2,1)} %bitcast.199), channel_id=1, source_target_pairs={{0,16},{1,17},{2,18},{3,19},{4,20},{5,21},{6,22},{7,23},{8,24},{9,... | collective-permute-start | bytes 2150408 | tf_op jit(solution)/shard_map/ppermute | solution.py:331
  549.1 28.5 %copy-start.9 = (f32[1024,896]{1,0:T(8,128)S(1)}, f32[1024,896]{1,0:T(8,128)}, u32[]{:S(2)}) copy-start(f32[1024,896]{1,0:T(8,128)} %get-tuple-element.47) | copy-start | bytes 11010052
  550.8 12.6 %collective-permute-start.16 = (bf16[200,448]{1,0:T(8,128)(2,1)S(1)}, bf16[200,448]{1,0:T(8,128)(2,1)S(1)}, u32[]{:S(2)}, u32[]{:S(2)}) collective-permute-start(bf16[200,448]{1,0:T(8,128)(2,1)S(1)} %get-tuple-element.107), channel_id=1, source_target_pairs={{0,6},{1,7},{2,0},{3,1},{4,2},{5,3},{6,4},{7,5},{8,14},{9,15},{10,... | collective-permute-start | bytes 537608 | tf_op jit(solution)/shard_map/ppermute | solution.py:331
  550.9 22.5 %collective-permute-start.15 = (bf16[200,448]{1,0:T(8,128)(2,1)S(1)}, bf16[200,448]{1,0:T(8,128)(2,1)S(1)}, u32[]{:S(2)}, u32[]{:S(2)}) collective-permute-start(bf16[200,448]{1,0:T(8,128)(2,1)S(1)} %get-tuple-element.108), channel_id=1, source_target_pairs={{0,4},{1,5},{2,6},{3,7},{4,0},{5,1},{6,2},{7,3},{8,12},{9,13},{10,... | collective-permute-start | bytes 537608 | tf_op jit(solution)/shard_map/ppermute | solution.py:331
  560.5 16.4 %collective-permute-start.14 = (bf16[200,448]{1,0:T(8,128)(2,1)S(1)}, bf16[200,448]{1,0:T(8,128)(2,1)S(1)}, u32[]{:S(2)}, u32[]{:S(2)}) collective-permute-start(bf16[200,448]{1,0:T(8,128)(2,1)S(1)} %get-tuple-element.106), channel_id=1, source_target_pairs={{0,2},{1,3},{2,4},{3,5},{4,6},{5,7},{6,0},{7,1},{8,10},{9,11},{10,... | collective-permute-start | bytes 537608 | tf_op jit(solution)/shard_map/ppermute | solution.py:331
  563.4 87.8 %collective-permute-start.9 = (bf16[800,1600]{1,0:T(8,128)(2,1)}, bf16[800,1600]{1,0:T(8,128)(2,1)}, u32[]{:S(2)}, u32[]{:S(2)}) collective-permute-start(bf16[800,1600]{1,0:T(8,128)(2,1)} %convolution_convert_fusion.4), channel_id=1, source_target_pairs={{0,16},{1,17},{2,18},{3,19},{4,20},{5,21},{6,22},{7,23},{8,24},{9,... | collective-permute-start | bytes 7680008 | tf_op jit(solution)/shard_map/ppermute | solution.py:331
  579.6 10.3 %copy-start.7 = (bf16[1024,896]{1,0:T(8,128)(2,1)}, bf16[1024,896]{1,0:T(8,128)(2,1)S(1)}, u32[]{:S(2)}) copy-start(bf16[1024,896]{1,0:T(8,128)(2,1)S(1)} %add_convert_fusion) | copy-start | bytes 5505028
  640.5 10.7 %copy-start.23 = (bf16[1024,1600]{0,1:T(8,128)(2,1)S(1)}, bf16[1024,1600]{0,1:T(8,128)(2,1)}, u32[]{:S(2)}) copy-start(bf16[1024,1600]{0,1:T(8,128)(2,1)} %get-tuple-element.87) | copy-start | bytes 9830404
  645.5 10.5 %copy-start.11 = (f32[800,1600]{1,0:T(8,128)}, f32[800,1600]{1,0:T(8,128)S(1)}, u32[]{:S(2)}) copy-start(f32[800,1600]{1,0:T(8,128)S(1)} %convert_add_fusion.1) | copy-start | bytes 15360004
  647.0 18.1 %collective-permute-start.8 = (bf16[200,1600]{1,0:T(8,128)(2,1)S(1)}, bf16[200,1600]{1,0:T(8,128)(2,1)S(1)}, u32[]{:S(2)}, u32[]{:S(2)}) collective-permute-start(bf16[200,1600]{1,0:T(8,128)(2,1)S(1)} %get-tuple-element.92), channel_id=1, source_target_pairs={{0,6},{1,7},{2,0},{3,1},{4,2},{5,3},{6,4},{7,5},{8,14},{9,15},{10,... | collective-permute-start | bytes 1920008 | tf_op jit(solution)/shard_map/ppermute | solution.py:331
  647.0 44.8 %collective-permute-start.7 = (bf16[200,1600]{1,0:T(8,128)(2,1)}, bf16[200,1600]{1,0:T(8,128)(2,1)S(1)}, u32[]{:S(2)}, u32[]{:S(2)}) collective-permute-start(bf16[200,1600]{1,0:T(8,128)(2,1)} %get-tuple-element.93), channel_id=1, source_target_pairs={{0,4},{1,5},{2,6},{3,7},{4,0},{5,1},{6,2},{7,3},{8,12},{9,13},{10,... | collective-permute-start | bytes 1920008 | tf_op jit(solution)/shard_map/ppermute | solution.py:331
  650.9 83.6 %collective-permute-start.6 = (bf16[200,1600]{1,0:T(8,128)(2,1)}, bf16[200,1600]{1,0:T(8,128)(2,1)S(1)}, u32[]{:S(2)}, u32[]{:S(2)}) collective-permute-start(bf16[200,1600]{1,0:T(8,128)(2,1)} %get-tuple-element.91), channel_id=1, source_target_pairs={{0,2},{1,3},{2,4},{3,5},{4,6},{5,7},{6,0},{7,1},{8,10},{9,11},{10,... | collective-permute-start | bytes 1920008 | tf_op jit(solution)/shard_map/ppermute | solution.py:331
  656.1 11.2 %copy-start.14 = (f32[12,1600]{1,0:T(8,128)S(1)}, f32[12,1600]{1,0:T(8,128)}, u32[]{:S(2)}) copy-start(f32[12,1600]{1,0:T(8,128)} %concatenate.34) | copy-start | bytes 230404
  659.8 90.9 %collective-permute-start.12 = (bf16[200,1600]{1,0:T(8,128)(2,1)}, bf16[200,1600]{1,0:T(8,128)(2,1)S(1)}, u32[]{:S(2)}, u32[]{:S(2)}) collective-permute-start(bf16[200,1600]{1,0:T(8,128)(2,1)} %get-tuple-element.89), channel_id=1, source_target_pairs={{0,6},{1,7},{2,0},{3,1},{4,2},{5,3},{6,4},{7,5},{8,14},{9,15},{10,... | collective-permute-start | bytes 1920008 | tf_op jit(solution)/shard_map/ppermute | solution.py:331
  661.8 88.9 %collective-permute-start.11 = (bf16[200,1600]{1,0:T(8,128)(2,1)}, bf16[200,1600]{1,0:T(8,128)(2,1)}, u32[]{:S(2)}, u32[]{:S(2)}) collective-permute-start(bf16[200,1600]{1,0:T(8,128)(2,1)} %get-tuple-element.90), channel_id=1, source_target_pairs={{0,4},{1,5},{2,6},{3,7},{4,0},{5,1},{6,2},{7,3},{8,12},{9,13},{10,... | collective-permute-start | bytes 1920008 | tf_op jit(solution)/shard_map/ppermute | solution.py:331
  665.1 98.0 %collective-permute-start.10 = (bf16[200,1600]{1,0:T(8,128)(2,1)}, bf16[200,1600]{1,0:T(8,128)(2,1)}, u32[]{:S(2)}, u32[]{:S(2)}) collective-permute-start(bf16[200,1600]{1,0:T(8,128)(2,1)} %get-tuple-element.88), channel_id=1, source_target_pairs={{0,2},{1,3},{2,4},{3,5},{4,6},{5,7},{6,0},{7,1},{8,10},{9,11},{10,... | collective-permute-start | bytes 1920008 | tf_op jit(solution)/shard_map/ppermute | solution.py:331
  691.8 96.5 %collective-permute-start.1 = (bf16[672,1600]{1,0:T(8,128)(2,1)}, bf16[672,1600]{1,0:T(8,128)(2,1)}, u32[]{:S(2)}, u32[]{:S(2)}) collective-permute-start(bf16[672,1600]{1,0:T(8,128)(2,1)} %bitcast.22), channel_id=1, source_target_pairs={{0,16},{1,17},{2,18},{3,19},{4,20},{5,21},{6,22},{7,23},{8,24},{9,... | collective-permute-start | bytes 6451208 | tf_op jit(solution)/shard_map/ppermute | solution.py:331
  791.8 35.9 %collective-permute-start.4 = (bf16[168,1600]{1,0:T(8,128)(2,1)S(1)}, bf16[168,1600]{1,0:T(8,128)(2,1)S(1)}, u32[]{:S(2)}, u32[]{:S(2)}) collective-permute-start(bf16[168,1600]{1,0:T(8,128)(2,1)S(1)} %get-tuple-element.95), channel_id=1, source_target_pairs={{0,6},{1,7},{2,0},{3,1},{4,2},{5,3},{6,4},{7,5},{8,14},{9,15},{10,... | collective-permute-start | bytes 1612808 | tf_op jit(solution)/shard_map/ppermute | solution.py:331
  814.4 35.5 %collective-permute-start.3 = (bf16[168,1600]{1,0:T(8,128)(2,1)S(1)}, bf16[168,1600]{1,0:T(8,128)(2,1)S(1)}, u32[]{:S(2)}, u32[]{:S(2)}) collective-permute-start(bf16[168,1600]{1,0:T(8,128)(2,1)S(1)} %get-tuple-element.96), channel_id=1, source_target_pairs={{0,4},{1,5},{2,6},{3,7},{4,0},{5,1},{6,2},{7,3},{8,12},{9,13},{10,... | collective-permute-start | bytes 1612808 | tf_op jit(solution)/shard_map/ppermute | solution.py:331
  814.4 47.3 %collective-permute-start.2 = (bf16[168,1600]{1,0:T(8,128)(2,1)S(1)}, bf16[168,1600]{1,0:T(8,128)(2,1)S(1)}, u32[]{:S(2)}, u32[]{:S(2)}) collective-permute-start(bf16[168,1600]{1,0:T(8,128)(2,1)S(1)} %get-tuple-element.94), channel_id=1, source_target_pairs={{0,2},{1,3},{2,4},{3,5},{4,6},{5,7},{6,0},{7,1},{8,10},{9,11},{10,... | collective-permute-start | bytes 1612808 | tf_op jit(solution)/shard_map/ppermute | solution.py:331
  (16 other events, 58.1 us)

commit v6 on v5

--- a/solution.py
+++ b/solution.py
@@ -423,7 +423,7 @@
 
 
 class PlaceGather:
-    def __init__(self, wires, full, slot, steps=(1, 2, 3), over=(0, 1, 2, 3)):
+    def __init__(self, wires, full, slot, steps=(1, 2, 3), over=(0, 1, 2, 3), rows=None):
         self.full = full
         self.dp, self.cp = lax.axis_index("dp"), lax.axis_index("cp")
         self.y, self.z, self.x = self.dp // 2, self.cp // 2, self.cp % 2
@@ -432,7 +432,8 @@
         self.across = ((self.dp + 2) % 4, self.cp)
 
         def share(by, to):
-            view = full.at[slot(self.y, (self.z + 4 + by) % 4)]
+            spot = slot(self.y, (self.z + 4 + by) % 4)
+            view = full.at[spot] if rows is None else full.at[pl.ds(pl.multiple_of(spot * rows, GRAIN), rows)]
             return wires.to(view, view, *to)
 
         self.steps = steps
@@ -513,8 +514,14 @@
         self.over_c = (self.dp + 1 - 2 * self.c, self.cp)
         self.local_sem = local_sem
 
+    def spot(self, c, x):
+        if len(self.full.shape) > len(self.block.shape):
+            return self.full.at[c, x]
+        rows = self.block.shape[0]
+        return self.full.at[pl.ds(pl.multiple_of((c * 2 + x) * rows, rows), rows)]
+
     def start(self):
-        spot = self.full.at[self.c, self.x]
+        spot = self.spot(self.c, self.x)
         self.by_x = self.wires.to(self.block, spot, *self.over_x)
         self.by_c = self.wires.to(self.block, spot, *self.over_c)
         self.by_x.start()
@@ -524,7 +531,7 @@
 
     def forward(self):
         self.by_x.wait_recv()
-        spot = self.full.at[self.c, 1 - self.x]
+        spot = self.spot(self.c, 1 - self.x)
         self.pass_on = self.wires.to(spot, spot, *self.over_c)
         self.pass_on.start()
 
@@ -908,58 +915,6 @@
     )(q, kv, w_out, w_fc, w_proj)
 
 
-def acts_kernel(proj_turn, act_ref, proj_in, act_all, proj_ref, send_sems, recv_sems, local_sem):
-    wires = Wires(send_sems, recv_sems)
-    quad = QuadGather(wires, act_ref, act_all, local_sem)
-    places = PlaceGather(wires, proj_ref, slot_turned(proj_turn), steps=(2, 3), over=(1, 2, 3))
-    greet(places.partners() + [quad.over_x, quad.over_c])
-    quad.start()
-    places.forward((1, 2))
-    quad.forward()
-    places.forward((3,))
-    quad.finish()
-    places.finish()
-
-
-def grads_kernel(act_ref, act_all, send_sems, recv_sems, local_sem):
-    wires = Wires(send_sems, recv_sems)
-    quad = QuadGather(wires, act_ref, act_all, local_sem)
-    greet([quad.over_x, quad.over_c])
-    quad.start()
-    quad.forward()
-    quad.finish()
-
-
-def grads_call(act, ident):
-    return pl.pallas_call(
-        grads_kernel,
-        out_shape=jax.ShapeDtypeStruct((2, 2) + act.shape, act.dtype),
-        in_specs=[VMEM],
-        out_specs=HBM,
-        scratch_shapes=[*wire_sems(3), pltpu.SemaphoreType.DMA],
-        cost_estimate=cost(25),
-        compiler_params=remote_params(ident),
-        name="grads",
-    )(act)
-
-
-def acts_call(sz, act, w_proj):
-    return pl.pallas_call(
-        functools.partial(acts_kernel, sz.proj_turn),
-        out_shape=(
-            jax.ShapeDtypeStruct((2, 2) + act.shape, act.dtype),
-            jax.ShapeDtypeStruct(w_proj.shape, w_proj.dtype),
-        ),
-        in_specs=[VMEM, HBM],
-        out_specs=[HBM] * 2,
-        input_output_aliases={1: 1},
-        scratch_shapes=[*wire_sems(13), pltpu.SemaphoreType.DMA],
-        cost_estimate=cost(60),
-        compiler_params=remote_params(2),
-        name="acts",
-    )(act, w_proj)
-
-
 class QuadSum:
     step = 32
 
@@ -979,8 +934,9 @@
 
         lax.fori_loop(0, self.out_ref.shape[0] // self.step, one, 0)
 
-    def start(self):
-        greet(self.partners)
+    def start(self, greeting=True):
+        if greeting:
+            greet(self.partners)
         self.by_c.start()
 
     def middle(self):
@@ -1009,13 +965,6 @@
         self.each(to_add)
         self.by_c.wait_send()
         self.by_x.wait_send()
-
-
-def quad_sum_kernel(*refs):
-    quad = QuadSum(*refs)
-    quad.start()
-    quad.middle()
-    quad.finish()
 
 
 def quad_scratch(partial):
@@ -1028,17 +977,232 @@
     ]
 
 
-def quad_sum(partial, ident):
+def fill_rows(left, first, right, out, step=160):
+    def one(index, _):
+        here = pl.ds(pl.multiple_of(index * step, step), step)
+        rows = pl.ds(pl.multiple_of(first + index * step, 32), step)
+        out[here, :] = dot_nn(left[rows, :], right[...]).astype(out.dtype)
+        return 0
+
+    lax.fori_loop(0, out.shape[0] // step, one, 0)
+
+
+def fill_columns(left, right, out, step=256):
+    def one(index, _):
+        here = pl.ds(pl.multiple_of(index * step, step), step)
+        out[here, :] = dot_tn(left[:, here], right[...]).astype(out.dtype)
+        return 0
+
+    lax.fori_loop(0, out.shape[0] // step, one, 0)
+
+
+def gelu_parts(f):
+    t = jnp.tanh(GELU_SCALE * (f + 0.044715 * f * f * f))
+    return t, 0.5 * f * (1.0 + t)
+
+
+def gelu_slope(f, t):
+    return 0.5 * (1.0 + t) + 0.5 * f * (1.0 - t * t) * GELU_SCALE * (1.0 + 3.0 * 0.044715 * f * f)
+
+
+def middle_kernel(
+    proj_turn, act_ref, cot, w_fc, bias, proj_in,
+    total, act_all, hid_t, proj_sum, fc_sent, fc_kept, bias_grad, proj_ref,
+    f_all, df_t, w_proj, proj_sent, proj_got, term, got_c, stage, got_x,
+    send_sems, recv_sems, sum_send, sum_recv, local_sems,
+):
+    y, c, _, _ = my_place()
+    wires = Wires(send_sems, recv_sems)
+    hidden = w_fc.shape[0]
+    half = hidden // 2
+    step = 160
+    quad = QuadGather(wires, act_ref, act_all, local_sems.at[0])
+    places = PlaceGather(
+        wires, proj_ref, slot_turned(proj_turn), steps=(2, 3), over=(1, 2, 3), rows=hidden // 8
+    )
+    across = wires.to(proj_sent, proj_got, *places.across)
+    summed = QuadSum(term, total, got_c, stage, got_x, sum_send, sum_recv)
+    greet(places.partners() + [quad.over_x, quad.over_c])
+    quad.start()
+    places.forward((1, 2))
+    quad.forward()
+    quad.finish()
+
+    def hidden_rows(first):
+        def one(index, _):
+            rows = pl.ds(pl.multiple_of(first + index * step, 32), step)
+            f = dot_nt(w_fc[rows, :], act_all[...]) + bias[rows, :]
+            f_all[rows, :] = f
+            hid_t[rows, :] = gelu_parts(f)[1].astype(hid_t.dtype)
+            return 0
+
+        lax.fori_loop(0, half // step, one, 0)
+
+    hidden_rows((1 - y) * half)
+    places.forward((3,))
+    fill_rows(hid_t, (1 - y) * half, cot, proj_sent)
+    across.start()
+    hidden_rows(y * half)
+    fill_rows(hid_t, y * half, cot, proj_sum)
+    places.finish()
+    load = pltpu.make_async_copy(proj_ref, w_proj, local_sems.at[1])
+    load.start()
+    load.wait()
+
+    def back_rows(index, _):
+        rows = pl.ds(pl.multiple_of(index * step, 32), step)
+        f = f_all[rows, :]
+        grad = dot_nt(w_proj[rows, :], cot[...])
+        df = (grad * gelu_slope(f, gelu_parts(f)[0])).astype(df_t.dtype)
+        df_t[rows, :] = df
+        bias_grad[rows, :] = jnp.sum(df.astype(jnp.float32), axis=1, keepdims=True)
+        return 0
+
+    lax.fori_loop(0, hidden // step, back_rows, 0)
+    block = term.shape[2]
+
+    def tokens_of(core):
+        for side in range(2):
+            columns = pl.ds(pl.multiple_of((core * 2 + side) * block, block), block)
+            term[core, side, :, :] = dot_tn(df_t[:, columns], w_fc[...]).astype(term.dtype)
+
+    tokens_of(1 - c)
+    summed.start(greeting=False)
+    tokens_of(c)
+    summed.middle()
+    fill_rows(df_t, (1 - y) * half, act_all, fc_sent)
+    fill_rows(df_t, y * half, act_all, fc_kept)
+    across.wait_recv()
+
+    def add(index, _):
+        rows = pl.ds(pl.multiple_of(index * step, 32), step)
+        proj_sum[rows, :] = (
+            proj_sum[rows, :].astype(jnp.float32) + proj_got[rows, :].astype(jnp.float32)
+        ).astype(proj_sum.dtype)
+        return 0
+
+    lax.fori_loop(0, half // step, add, 0)
+    summed.finish()
+    across.wait_send()
+
+
+def middle_call(sz, act, cot, w_fc, bias, w_proj):
+    rows, width = act.shape
+    hidden = w_fc.shape[0]
+    bf16, f32 = act.dtype, jnp.float32
+    half = jax.ShapeDtypeStruct((hidden // 2, width), bf16)
     return pl.pallas_call(
-        quad_sum_kernel,
-        out_shape=jax.ShapeDtypeStruct(partial.shape[2:], jnp.float32),
-        in_specs=[VMEM],
-        out_specs=VMEM,
-        scratch_shapes=quad_scratch(partial),
-        compiler_params=remote_params(ident),
-        cost_estimate=cost(30),
-        name="quad_sum",
-    )(partial)
+        functools.partial(middle_kernel, sz.proj_turn),
+        out_shape=(
+            jax.ShapeDtypeStruct((rows, width), f32),
+            jax.ShapeDtypeStruct((4 * rows, width), bf16),
+            jax.ShapeDtypeStruct((hidden, 4 * rows), bf16),
+            half,
+            half,
+            half,
+            jax.ShapeDtypeStruct((hidden, 1), f32),
+            jax.ShapeDtypeStruct((hidden, width), bf16),
+        ),
+        in_specs=[VMEM] * 4 + [HBM],
+        out_specs=[VMEM] * 7 + [HBM],
+        input_output_aliases={4: 7},
+        scratch_shapes=[
+            pltpu.VMEM((hidden, 4 * rows), f32),
+            pltpu.VMEM((hidden, 4 * rows), bf16),
+            pltpu.VMEM((hidden, width), bf16),
+            pltpu.VMEM((hidden // 2, width), bf16),
+            pltpu.VMEM((hidden // 2, width), bf16),
+            pltpu.VMEM((2, 2, rows, width), bf16),
+            pltpu.VMEM((2, rows, width), bf16),
+            pltpu.VMEM((rows, width), bf16),
+            pltpu.VMEM((rows, width), bf16),
+            *wire_sems(11),
+            *wire_sems(2),
+            pltpu.SemaphoreType.DMA((2,)),
+        ],
+        cost_estimate=cost(110),
+        compiler_params=remote_params(2, 63 << 20),
+        name="middle",
+    )(act, cot, w_fc, bias, w_proj)
+
+
+def grads_kernel(act_ref, hid_t, w_proj, act_all, partial_out, send_sems, recv_sems, local_sem):
+    wires = Wires(send_sems, recv_sems)
+    quad = QuadGather(wires, act_ref, act_all, local_sem)
+    greet([quad.over_x, quad.over_c])
+    quad.start()
+    fill_columns(hid_t, w_proj, partial_out)
+    quad.forward()
+    quad.finish()
+
+
+def grads_call(act, hid_t, w_proj, ident):
+    width = w_proj.shape[1]
+    return pl.pallas_call(
+        grads_kernel,
+        out_shape=(
+            jax.ShapeDtypeStruct((2, 2) + act.shape, act.dtype),
+            jax.ShapeDtypeStruct((hid_t.shape[1], width), jnp.bfloat16),
+        ),
+        in_specs=[VMEM] * 3,
+        out_specs=[HBM, VMEM],
+        scratch_shapes=[*wire_sems(3), pltpu.SemaphoreType.DMA],
+        cost_estimate=cost(25),
+        compiler_params=remote_params(ident, 60 << 20),
+        name="grads",
+    )(act, hid_t, w_proj)
+
+
+def row_steps(rows, step=64):
+    return [slice(start, min(start + step, rows)) for start in range(0, rows, step)]
+
+
+class PlaceSum:
+    def __init__(self, out, got, turn, send_sems, recv_sems, filled=False):
+        self.y, self.c, self.z, self.x = my_place()
+        self.dp = lax.axis_index("dp")
+        self.filled = filled
+        self.out, self.got, self.turn = out, got, turn
+        self.send_sems, self.recv_sems = send_sems, recv_sems
+
+    def place(self, k):
+        return (k + self.turn) % 4
+
+    def put(self, k, store):
+        @pl.when(self.z == self.place(k))
+        def _():
+            store(self.got.at[self.place(k)])
+
+        @pl.when(self.z != self.place(k))
+        def _():
+            if not self.filled:
+                store(self.out.at[k])
+            pltpu.make_async_remote_copy(
+                src_ref=self.out.at[k],
+                dst_ref=self.got.at[self.z],
+                send_sem=self.send_sems.at[k],
+                recv_sem=self.recv_sems.at[self.z],
+                device_id=(self.dp, self.place(k) * 2 + self.x),
+                device_id_type=MESH,
+            ).start()
+
+    def total(self, into):
+        for s in range(4):
+
+            @pl.when(self.z != s)
+            def _():
+                pltpu.make_async_copy(self.got.at[s], self.got.at[s], self.recv_sems.at[s]).wait()
+
+        for rows in row_steps(self.got.shape[1]):
+            terms = [self.got[s, rows, :].astype(jnp.float32) for s in range(4)]
+            into[rows, :] = (terms[0] + terms[1] + (terms[2] + terms[3])).astype(into.dtype)
+
+    def finish(self):
+        for k in range(4):
+
+            @pl.when(self.z != self.place(k))
+            def _():
+                pltpu.make_async_copy(self.out.at[k], self.out.at[k], self.send_sems.at[k]).wait()
 
 
 class Collector:
@@ -1081,66 +1245,53 @@
                 pltpu.make_async_copy(view(grains), view(grains), recv).wait()
 
 
-def collect_mlp_kernel(sz, fc_ref, proj_ref, out_ref, g_ref, outs_ref, send_sems, out_sems, recv_sems):
-    to = Collector(sz)
-    recv_sem = recv_sems.at[0]
-    out_share = out_ref.shape[0]
-
-    def run(act):
-        for ref, base, turn, first_sem in (
-            (fc_ref, sz.fc_start, sz.fc_turn, 0), (proj_ref, sz.proj_start, sz.proj_turn, sz.mlp)
-        ):
-            r = range_of_spot(to.y, (to.z + 4 - turn) % 4)
-
-            def one(slot, _):
-                table = base + 4 * (r * sz.mlp + slot) + to.quarter
-                act(ref.at[slot], g_ref.at[table % sz.block], table, send_sems.at[first_sem + slot], recv_sem)
-                return 0
-
-            lax.fori_loop(0, sz.mlp, one, 0)
-
-        def outward(slot, _):
-            table = sz.out_start + slot_out(to.y, to.z) * out_share + slot
-            dst = outs_ref.at[to.quarter, table % sz.block]
-            act(out_ref.at[slot], dst, table, out_sems.at[slot], recv_sems.at[1])
-            return 0
-
-        lax.fori_loop(0, out_share, outward, 0)
-
-    run(to.send)
-    run(to.sent)
-    to.received(sz.fc_start, 64 * sz.mlp, lambda n: g_ref.at[pl.ds(0, n)], recv_sem)
-    to.received(sz.out_start, sz.width_grains, lambda n: outs_ref.at[:, pl.ds(0, n)], recv_sems.at[1])
-
-
-def collect_mlp(sz, fc, proj, out):
-    return pl.pallas_call(
-        functools.partial(collect_mlp_kernel, sz),
-        out_shape=(
-            jax.ShapeDtypeStruct((sz.block, GRAIN, fc.shape[-1]), fc.dtype),
-            jax.ShapeDtypeStruct((4, sz.block, GRAIN, out.shape[-1]), out.dtype),
-        ),
-        in_specs=[HBM] * 3,
-        out_specs=[HBM] * 2,
-        scratch_shapes=[
-            pltpu.SemaphoreType.DMA((2 * sz.mlp,)),
-            pltpu.SemaphoreType.DMA((out.shape[0],)),
-            pltpu.SemaphoreType.DMA((2,)),
-        ],
-        cost_estimate=cost(30),
-        compiler_params=REMOTE,
-        name="collect_mlp",
-    )(fc, proj, out)
-
-
-def collect_rest_kernel(
-    sz, qkv_ref, vec_ref, g_ref, vecs_ref, qkv_sems, vec_sems, recv_sem
+def close_kernel(
+    sz, dqkv, act, w_qkv, normed, vec_in, fc_sum, out_sum, proj_share,
+    total, g_qkv, g_mlp, g_outs, vecs, qkv_share, fc_share, out_share,
+    grads, got_y, qkv_out, qkv_got, fc_got, out_got, share_v, out_v, vec_v, term, got_c, stage, got_x,
+    y_send, y_recv, z_send, z_recv, sum_send, sum_recv, grain_sems, kind_sems, local_sems, vec_sems,
 ):
     to = Collector(sz)
-
-    def run(act):
-        def heads(slot, _):
-            local = slot_qkv(to.y, to.z) * sz.qkv + slot
+    y, c, z = to.y, to.c, to.z
+    dp, cp = lax.axis_index("dp"), lax.axis_index("cp")
+    rows = got_y.shape[1]
+    block = term.shape[2]
+    fc = PlaceSum(fc_sum, fc_got, sz.fc_turn, z_send.at[0], z_recv.at[0], True)
+    out = PlaceSum(out_sum, out_got, 0, z_send.at[1], z_recv.at[1], True)
+    qkv = PlaceSum(qkv_out, qkv_got, 0, z_send.at[2], z_recv.at[2])
+    summed = QuadSum(term, total, got_c, stage, got_x, sum_send, sum_recv)
+
+    for part in (out, fc):
+        for k in range(4):
+            part.put(k, lambda ref, k=k, part=part: store_same(part.out.at[k], ref, local_sems.at[0]))
+
+    def mlp_grains(act_on, ref, base, turn, first_sem):
+        r = range_of_spot(y, (z + 4 - turn) % 4)
+
+        def one(slot, _):
+            table = base + 4 * (r * sz.mlp + slot) + to.quarter
+            act_on(ref(slot), g_mlp.at[table % sz.block], table, grain_sems.at[first_sem + slot], kind_sems.at[0])
+            return 0
+
+        lax.fori_loop(0, sz.mlp, one, 0)
+
+    def grain_of(ref):
+        return lambda slot: ref.at[pl.ds(pl.multiple_of(slot * GRAIN, GRAIN), GRAIN)]
+
+    def out_grains(act_on, first_sem):
+        count = out_share.shape[0] // GRAIN
+
+        def one(slot, _):
+            table = sz.out_start + slot_out(y, z) * count + slot
+            dst = g_outs.at[to.quarter, table % sz.block]
+            act_on(grain_of(out_share)(slot), dst, table, grain_sems.at[first_sem + slot], kind_sems.at[1])
+            return 0
+
+        lax.fori_loop(0, count, one, 0)
+
+    def head_grains(act_on, first_sem):
+        def one(slot, _):
+            local = slot_qkv(y, z) * sz.qkv + slot
             inner = local % sz.part_grains
             index = inner // sz.head_grains
             head = 8 * (index // 2) + 2 * to.quarter + index % 2
@@ -1148,16 +1299,77 @@
             @pl.when(head < sz.heads)
             def _():
                 table = (local // sz.part_grains) * sz.width_grains + head * sz.head_grains + inner % sz.head_grains
-                act(qkv_ref.at[slot], g_ref.at[table % sz.block], table, qkv_sems.at[slot], recv_sem)
+                act_on(
+                    grain_of(qkv_share)(slot), g_qkv.at[table % sz.block], table,
+                    grain_sems.at[first_sem + slot], kind_sems.at[2],
+                )
 
             return 0
 
-        lax.fori_loop(0, sz.qkv, heads, 0)
-
+        lax.fori_loop(0, sz.qkv, one, 0)
+
+    counts = (0, sz.mlp, 2 * sz.mlp, 3 * sz.mlp)
+    mlp_grains(to.send, lambda slot: proj_share.at[slot], sz.proj_start, sz.proj_turn, counts[0])
+
+    across = []
+    for k in range(4):
+        for s in (2 * k, 2 * k + 1):
+            grads[s, :, :] = dot_tn(dqkv[:, s * rows : (s + 1) * rows], act[...]).astype(grads.dtype)
+        copy = pltpu.make_async_remote_copy(
+            src_ref=grads.at[2 * k + 1 - y],
+            dst_ref=got_y.at[k],
+            send_sem=y_send.at[k],
+            recv_sem=y_recv.at[k],
+            device_id=((dp + 2) % 4, cp),
+            device_id_type=MESH,
+        )
+        copy.start()
+        across.append(copy)
+
+    def tokens_of(core):
+        for side in range(2):
+            here = pl.ds(pl.multiple_of((core * 2 + side) * block, block), block)
+            term[core, side, :, :] = dot_nn(dqkv[here, :], w_qkv[...]).astype(term.dtype)
+
+    tokens_of(1 - c)
+    summed.start(greeting=False)
+    tokens_of(c)
+    summed.middle()
+
+    def share_sum(k):
+        def store(ref):
+            for step in row_steps(rows):
+                ref[step, :] = (
+                    grads[2 * k + y, step, :].astype(jnp.float32) + got_y[k, step, :].astype(jnp.float32)
+                ).astype(ref.dtype)
+
+        return store
+
+    def settle(part, value, share):
+        part.total(value)
+        copy = pltpu.make_async_copy(value, share, local_sems.at[1])
+        copy.start()
+        copy.wait()
+
+    settle(out, out_v, out_share)
+    out_grains(to.send, counts[2])
+    for k in range(2):
+        across[k].wait_recv()
+        qkv.put(k, share_sum(k))
+    settle(fc, share_v, fc_share)
+    mlp_grains(to.send, grain_of(fc_share), sz.fc_start, sz.fc_turn, counts[1])
+    for k in range(2, 4):
+        across[k].wait_recv()
+        qkv.put(k, share_sum(k))
+    summed.finish()
+
+    vec_v[...] = vec_in[...]
+    vec_v[0:1, :] = jnp.sum(total[...] * normed[...], axis=0, keepdims=True)
+    vec_v[1:2, :] = jnp.sum(total[...], axis=0, keepdims=True)
     last = sz.vec_start // sz.block
     vec_copy = pltpu.make_async_remote_copy(
-        src_ref=vec_ref,
-        dst_ref=vecs_ref.at[to.me],
+        src_ref=vec_v,
+        dst_ref=vecs.at[to.me],
         send_sem=vec_sems.at[0],
         recv_sem=vec_sems.at[1],
         device_id=(last // 8, last % 8),
@@ -1170,10 +1382,19 @@
 
     @pl.when(to.me == last)
     def _():
-        pltpu.make_async_copy(vec_ref, vecs_ref.at[to.me], vec_sems.at[1]).start()
-
-    run(to.send)
-    run(to.sent)
+        pltpu.make_async_copy(vec_v, vecs.at[to.me], vec_sems.at[1]).start()
+
+    settle(qkv, share_v.at[0:rows], qkv_share)
+    head_grains(to.send, counts[3])
+
+    for copy in across:
+        copy.wait_send()
+    for part in (out, fc, qkv):
+        part.finish()
+    mlp_grains(to.sent, lambda slot: proj_share.at[slot], sz.proj_start, sz.proj_turn, counts[0])
+    mlp_grains(to.sent, grain_of(fc_share), sz.fc_start, sz.fc_turn, counts[1])
+    out_grains(to.sent, counts[2])
+    head_grains(to.sent, counts[3])
 
     @pl.when(to.me != last)
     def _():
@@ -1181,29 +1402,71 @@
 
     @pl.when(to.me == last)
     def _():
-        pltpu.make_async_copy(vecs_ref, vecs_ref, vec_sems.at[1]).wait()
-
-    to.received(0, 3 * sz.width_grains, lambda n: g_ref.at[pl.ds(0, n)], recv_sem)
-
-
-def collect_rest(sz, qkv, vectors):
-    def like(value, *lead):
-        return jax.ShapeDtypeStruct(lead + value.shape[-2:], value.dtype)
+        pltpu.make_async_copy(vecs, vecs, vec_sems.at[1]).wait()
+
+    to.received(sz.fc_start, 64 * sz.mlp, lambda n: g_mlp.at[pl.ds(0, n)], kind_sems.at[0])
+    to.received(sz.out_start, sz.width_grains, lambda n: g_outs.at[:, pl.ds(0, n)], kind_sems.at[1])
+    to.received(0, 3 * sz.width_grains, lambda n: g_qkv.at[pl.ds(0, n)], kind_sems.at[2])
+
+
+def store_same(src, ref, sem):
+    copy = pltpu.make_async_copy(src, ref, sem)
+    copy.start()
+    copy.wait()
+
+
+def close_call(sz, dqkv, act, w_qkv, normed, vectors, fc_sum, out_sum, proj_share):
+    rows, width = normed.shape
+    bf16, f32 = act.dtype, jnp.float32
+    qkv_rows, out_rows, mlp_rows = sz.qkv * GRAIN, out_sum.shape[1], fc_sum.shape[1]
+
+    def like(*shape, dtype=bf16):
+        return jax.ShapeDtypeStruct(shape, dtype)
+
+    def vmem(*shape):
+        return pltpu.VMEM(shape, bf16)
 
     return pl.pallas_call(
-        functools.partial(collect_rest_kernel, sz),
-        out_shape=(like(qkv, sz.block), like(vectors, 32, sz.vec)),
-        in_specs=[HBM] * 2,
-        out_specs=[HBM] * 2,
+        functools.partial(close_kernel, sz),
+        out_shape=(
+            like(rows, width, dtype=f32),
+            like(sz.block, GRAIN, width),
+            like(sz.block, GRAIN, width),
+            like(4, sz.block, GRAIN, sz.part),
+            like(32, *vectors.shape, dtype=f32),
+            like(qkv_rows, width),
+            like(mlp_rows, width),
+            like(out_rows, sz.part),
+        ),
+        in_specs=[VMEM] * 7 + [HBM],
+        out_specs=[VMEM] + [HBM] * 7,
         scratch_shapes=[
-            pltpu.SemaphoreType.DMA((sz.qkv,)),
+            vmem(8, qkv_rows, width),
+            vmem(4, qkv_rows, width),
+            vmem(4, qkv_rows, width),
+            vmem(4, qkv_rows, width),
+            vmem(4, mlp_rows, width),
+            vmem(4, out_rows, sz.part),
+            vmem(mlp_rows, width),
+            vmem(out_rows, sz.part),
+            pltpu.VMEM(vectors.shape, f32),
+            vmem(2, 2, rows, width),
+            vmem(2, rows, width),
+            vmem(rows, width),
+            vmem(rows, width),
+            *wire_sems(4),
+            pltpu.SemaphoreType.DMA((3, 4)),
+            pltpu.SemaphoreType.DMA((3, 4)),
+            *wire_sems(2),
+            pltpu.SemaphoreType.DMA((3 * sz.mlp + sz.qkv,)),
+            pltpu.SemaphoreType.DMA((3,)),
             pltpu.SemaphoreType.DMA((2,)),
-            pltpu.SemaphoreType.DMA,
+            pltpu.SemaphoreType.DMA((2,)),
         ],
-        cost_estimate=cost(30),
-        compiler_params=REMOTE,
-        name="collect_rest",
-    )(qkv, vectors)
+        cost_estimate=cost(120),
+        compiler_params=remote_params(None, 62 << 20),
+        name="close",
+    )(dqkv, act, w_qkv, normed, vectors, fc_sum, out_sum, proj_share)
 
 
 def attend_back_kernel(heads, size, own, *refs):
@@ -1339,16 +1602,11 @@
     def pick(value, index):
         return lax.dynamic_index_in_dim(value, index, 0, keepdims=False)
 
-    def halves_of(value):
-        half = value.shape[1] // 2
-        first, second = value[:, :half], value[:, half:]
-        return jnp.where(y == 0, first, second), jnp.where(y == 0, second, first)
-
     def to_other_y(sent):
         return over_y(sent.astype(bf16))
 
     def to_places(kept, got, turn=0):
-        summed = kept.astype(f32) + got.astype(f32)
+        summed = kept.astype(f32) if got is None else kept.astype(f32) + got.astype(f32)
         summed = summed.reshape(4, summed.shape[0] // 4, -1)
         total = pick(summed, (z + 4 - turn) % 4)
         for d in (1, 2, 3):
@@ -1389,28 +1647,23 @@
     inputs = tokens.astype(f32)
     residual = inputs + (dot_nt(mixed, w_out) + vectors[4])
     normed_two, rs_two = norm_parts(residual)
-    act_two, w_proj = acts_call(sz, (normed_two * vectors[5] + vectors[6]).astype(bf16), w_proj)
-    act_two, w_proj = flat(act_two), flat(w_proj)
+    act_two = (normed_two * vectors[5] + vectors[6]).astype(bf16)
     bias = lax.dynamic_index_in_dim(fc_bias.reshape(-1, 4, GRAIN), quarter, 1, keepdims=False)
-    bias = bias.reshape(8, hidden // 32)[jnp.array(RANGES)].reshape(hidden // 4)
-    pre_act = dot_nt(act_two, w_fc) + bias
-    act_hidden, pull_gelu = jax.vjp(gelu_tanh, pre_act)
-    act_hidden = act_hidden.astype(bf16)
-    hid_mine, hid_other = halves_of(act_hidden)
-    got_proj = to_other_y(dot_tn(hid_other, cot_all))
-    grad_fc = pull_gelu(dot_nt(cot_all, w_proj))[0].astype(bf16)
-    fc_mine, fc_other = halves_of(grad_fc)
-    got_fc = to_other_y(dot_tn(fc_other, act_two))
-    grad_two = quad_sum(rowwise(dot_nn(grad_fc, w_fc).astype(bf16)).reshape(2, 2, rows, width), 7)
+    bias = bias.reshape(8, hidden // 32)[jnp.array(RANGES)].reshape(hidden // 4, 1)
+    grad_two, act_two, hid_t, proj_sum, fc_sent, fc_kept, bias_sum, w_proj = middle_call(
+        sz, act_two, cot_all, w_fc, bias, flat(w_proj)
+    )
+    got_fc = to_other_y(fc_sent)
 
     cot = out_grad.astype(f32)
     grad_res = cot + norm_back(normed_two, rs_two, grad_two, vectors[5])
     grad_attn = grad_res.astype(bf16)
-    attn_all = flat(grads_call(grad_attn, 3))
+    attn_all, partial_out = grads_call(grad_attn, hid_t, w_proj, 3)
+    attn_all = flat(attn_all)
     grad_mix = rowwise(dot_nn(attn_all, w_out).astype(bf16))
     grad_mix = rowwise(quarter_of(grad_mix))
-    g_proj = to_places(dot_tn(hid_mine, cot_all), got_proj, sz.proj_turn)
-    partial_out = rowwise(dot_nn(act_hidden, w_proj).astype(bf16)).reshape(2, 2, rows, width)
+    g_proj = to_places(proj_sum, None, sz.proj_turn)
+    partial_out = partial_out.reshape(2, 2, rows, width)
     dq_before, dkv_before, out_sum = attend_back(
         sz, q, before, grad_mix, mix, lse, term=partial_out, ident=4
     )
@@ -1420,22 +1673,12 @@
     )
     g_out = rowwise(dot_tn(attn_all, mix.astype(bf16)).astype(bf16)).reshape(2, width // 2, sz.part)
     got_out = to_other_y(pick(g_out, 1 - y))
-    g_fc = to_places(dot_tn(fc_mine, act_two), got_fc, sz.fc_turn)
+    fc_sum = (fc_kept.astype(f32) + got_fc.astype(f32)).astype(bf16).reshape(4, hidden // 32, width)
+    out_sum = (pick(g_out, y).astype(f32) + got_out.astype(f32)).astype(bf16).reshape(4, width // 8, sz.part)
     dq, dkv = attend_back(sz, q, kv, grad_mix, mix, lse, seed=dq_before)
     grad_qkv = jnp.concatenate([dq, (dkv + returned.astype(f32)).astype(bf16)], axis=1)
-    g_qkv = rowwise(dot_tn(grad_qkv, act_one).astype(bf16)).reshape(4, 2, 3 * sz.part // 8, width)
-    half_qkv = lambda index: lax.dynamic_index_in_dim(g_qkv, index, 1, keepdims=False).reshape(-1, width)
-    got_qkv = to_other_y(half_qkv(1 - y))
-    partial_one = rowwise(dot_nn(grad_qkv, w_qkv).astype(bf16))
-    grad_one = quad_sum(partial_one.reshape(2, 2, rows, width), 6)
-    g_out = to_places(pick(g_out, y), got_out)
-    g_qkv = to_places(half_qkv(y), got_qkv)
+    normed_one, rs_one = norm_parts(inputs)
     grains = lambda value: value.astype(bf16).reshape(-1, GRAIN, value.shape[-1])
-    table_mlp, table_out = collect_mlp(sz, grains(g_fc), grains(g_proj), grains(g_out))
-    table_out = by_head(table_out.reshape(4, -1, sz.part))
-
-    normed_one, rs_one = norm_parts(inputs)
-    input_grad = (grad_res + norm_back(normed_one, rs_one, grad_one, vectors[0])).astype(bf16)
 
     def placed(vector):
         spread = jnp.zeros((1, width), f32)
@@ -1446,7 +1689,7 @@
         return jnp.concatenate([spread[0, : width - rest], end])
 
     sums = jnp.sum(grad_qkv.astype(f32), axis=0)
-    bias_sum = jnp.sum(grad_fc.astype(f32), axis=0).reshape(8, hidden // 32)[jnp.array(SPOTS)]
+    bias_sum = bias_sum.reshape(8, hidden // 32)[jnp.array(SPOTS)]
     fc_rows = lax.dynamic_update_slice_in_dim(
         jnp.zeros((hidden // 4 // GRAIN, 4, GRAIN), f32), bias_sum.reshape(-1, 1, GRAIN), quarter, 1
     )
@@ -1454,8 +1697,8 @@
         [
             jnp.stack(
                 [
-                    jnp.sum(grad_one * normed_one, axis=0),
-                    jnp.sum(grad_one, axis=0),
+                    jnp.zeros((width,), f32),
+                    jnp.zeros((width,), f32),
                     placed(sums[: sz.part]),
                     placed(sums[2 * sz.part :]),
                     jnp.sum(grad_attn.astype(f32), axis=0),
@@ -1469,8 +1712,12 @@
     )
     count = grad_vectors.shape[0]
     grad_vectors = jnp.pad(grad_vectors, ((0, sz.vec * GRAIN - count), (0, 0)))
-    table_qkv, all_vectors = collect_rest(sz, grains(g_qkv), grad_vectors.reshape(sz.vec, GRAIN, width))
-    grad_vectors = jnp.sum(all_vectors.reshape(32, sz.vec * GRAIN, width), axis=0)[:count]
+    grad_one, table_qkv, table_mlp, table_out, all_vectors = close_call(
+        sz, grad_qkv, act_one, w_qkv, normed_one, grad_vectors, fc_sum, out_sum, grains(g_proj)
+    )[:5]
+    input_grad = (grad_res + norm_back(normed_one, rs_one, grad_one, vectors[0])).astype(bf16)
+    grad_vectors = jnp.sum(all_vectors, axis=0)[:count]
+    table_out = by_head(table_out.reshape(4, -1, sz.part))
     me = flat_id(y, c, z, x)
     row = me * (sz.block * GRAIN) + lax.broadcasted_iota(jnp.int32, (sz.block * GRAIN, 1), 0)
     used = (sz.vec_start % sz.block) * GRAIN

time: 913 us -> 790 us (0.87)
  the two profiles are of different devices: /device:TPU:10 before, /device:TPU:24 now
where the time goes in v6:
time: 790 us; the launch traced here: 780 us
  Pallas kernels  612 us (77%)
  other arithmetic  51.6 us (7%)
  waiting for transfers between devices  41.9 us (5%)
  local copies, waits for them, and re-layouts  33.5 us (4%)
  matrix products  32.6 us (4%)
    pallas_call x1, Pallas kernels, close_call(): pl.pallas_call(functools.partial(close_kernel, sz), out_shape=(like(rows,...  178 us
    pallas_call x1, Pallas kernels, middle_call(): pl.pallas_call(functools.partial(middle_kernel, sz.proj_turn), out_shape=...  118 us
    pallas_call x1, Pallas kernels, open_call(): pl.pallas_call(functools.partial(open_kernel, sz), out_shape=(like(8, sz....  116 us
    pallas_call x1, Pallas kernels, forward_call(): pl.pallas_call(functools.partial(forward_kernel, sz.quarter_heads, sz.hea...  108 us
    pallas_call x2, Pallas kernels, attend_back(): pl.pallas_call(functools.partial(attend_back_kernel, sz.quarter_heads, sz...  62.9 us
    ppermute x6, waiting for transfers between devices, permute(): return lax.ppermute(value, ('dp', 'cp'), pairs)  41.9 us
    pallas_call x1, Pallas kernels, grads_call(): pl.pallas_call(grads_kernel, out_shape=(jax.ShapeDtypeStruct((2, 2) + act...  28.5 us
    dot_general x3, matrix products, dot_nt(): return lax.dot_general(a, b, NT, preferred_element_type=jnp.float32)  17 us
  transfers between devices with their start and end apart: 6, of which 1 were waited for; matrix products, arithmetic and copies ran while one was open for 7% of the time, Pallas kernels for 12%

profile of v6, /device:TPU:24, one launch (start us, length us, event | category | flops | bytes accessed | tf_op | source)
XLA Modules:
  0.0 780.0 jit_solution(16212396615605597576)
XLA Ops:
  0.7 2.3 copy.32.tok_ref
  4.3 115.7 %open.1 = (bf16[8,21,8,1600]{3,2,1,0:T(8,128)(2,1)}, bf16[8,7,8,1600]{3,2,1,0:T(8,128)(2,1)}, bf16[8,25,8,1600]{3,2,1,0:T(8,128)(2,1)}, bf16[8,25,8,1600]{3,2,1,...) custom-call(bf16[76,8,1600]{2,1,0:T(8,128)(2,1)} %bitcast.107, ...), custom_call_target="tpu_custom_call" | custom-call | tf_op jit(solution)/shard_map/open/pallas_call | solution.py:738
  124.4 2.5 convert_reduce_fusion.1
  129.7 8.1 %add_convert_fusion.2.kv_ref.refs_1_ = bf16[1024,896]{1,0:T(8,128)(2,1)} fusion(f32[896]{0:T(1024)S(1)} %concatenate.31, bf16[1024,1600]{1,0:T(8,128)(2,1)S(1)} %fusion.3.act, bf16[1344,1600]{1,0:T(8,128)(2,1)} %bitcast.100), kind=kOutput, calls=%fused_computation.19 | convolution fusion | flops 2937847808 | bytes 8097280 | tf_op jit(solution)/shard_map/dot_general | solution.py:307
  137.8 4.4 add_convert_fusion.3.q_ref.refs_0_
  142.2 107.7 %forward.1 = (f32[1024,448]{1,0:T(8,128)}, f32[1024,8]{1,0:T(8,128)}, bf16[1024,896]{1,0:T(8,128)(2,1)}, bf16[4,256,448]{2,1,0:T(8,128)(2,1)}, bf16[8,7,8,1600]{...) custom-call(bf16[1024,448]{1,0:T(8,128)(2,1)} %add_convert_fusion.3., ...), custom_call_target="tpu_custom_call", output_to_operand_aliasing={{4}: (2, {}), {5}: (3, {}), {6}: (4, {})} | custom-call | bytes 360000000 | tf_op jit(solution)/shard_map/forward/pallas_call | solution.py:892
  251.7 4.5 fusion.41
  260.5 118.5 %middle.1 = (f32[256,1600]{1,0:T(8,128)}, bf16[1024,1600]{1,0:T(8,128)(2,1)}, bf16[1600,1024]{1,0:T(8,128)(2,1)}, bf16[800,1600]{1,0:T(8,128)(2,1)}, bf16[800,16...) custom-call(bf16[256,1600]{1,0:T(8,128)(2,1)} %add_convert_fusion.6., ...), custom_call_target="tpu_custom_call", output_to_operand_aliasing={{7}: (4, {})} | custom-call | bytes 330000000 | tf_op jit(solution)/shard_map/middle/pallas_call | solution.py:1094
  379.0 4.4 convert.7
  383.4 3.6 fusion.32
  387.0 2.0 collective-permute-start.5
  389.0 2.2 multiply_reduce_fusion.2
  391.2 3.9 convert_reduce_fusion.4
  395.2 28.5 %grads.1 = (bf16[2,2,256,1600]{3,2,1,0:T(8,128)(2,1)}, bf16[1024,1600]{1,0:T(8,128)(2,1)}) custom-call(bf16[256,1600]{1,0:T(8,128)(2,1)} %get-tuple-element.91.act_ref, bf16[1600,1024]{1,0:T(8,128)(2,1)} %get-tuple-element.49.hid_t, bf16[1600,1600]{1,0:T(8,128)(2,1)} %get-tuple-element.50.w_proj), custom_call_target="tpu_custom_call" | custom-call | bytes 75000000 | tf_op jit(solution)/shard_map/grads/pallas_call | solution.py:1141
  423.7 5.7 convolution_convert_fusion
  429.4 2.4 constant_dynamic-slice_fusion.1
  433.5 10.0 %fusion.10 = bf16[1024,1600]{1,0:T(8,128)(2,1)S(1)} fusion(bf16[1024,1600]{1,0:T(8,128)(2,1)} %bitcast.119, bf16[1792,1600]{1,0:T(8,128)(2,1)} %bitcast.117), kind=kOutput, calls=%fused_computation.17 | convolution fusion | flops 5244518400 | bytes 12009472 | tf_op jit(solution)/shard_map/dot_general | solution.py:315
  445.0 38.9 %attend_back_before.1 = (f32[1024,448]{1,0:T(8,128)}, f32[1024,896]{1,0:T(8,128)}, f32[256,1600]{1,0:T(8,128)}) custom-call(bf16[1024,448]{1,0:T(8,128)(2,1)} %add_convert_fusion.3.q_ref.refs_0_, bf16[1024,896]{1,0:T(8,128)(2,1)} %get-tuple-element.44.refs_1_, bf16[1024,448]{1,0:T(8,128)(2,1)} %pad_maximum_fusion.1.refs_2_, ...), custom_call_target="tpu_custom_call" | custom-call | bytes 105000000 | tf_op jit(solution)/shard_map/attend_back_before/pallas_call | solution.py:1562
  483.9 3.6 convert_element_type.152
  487.6 2.7 collective-permute-start
  491.1 1.7 copy.47
  492.9 24.0 %attend_back_own.1 = (bf16[1024,448]{1,0:T(8,128)(2,1)}, f32[1024,896]{1,0:T(8,128)}) custom-call(bf16[1024,448]{1,0:T(8,128)(2,1)} %add_convert_fusion.3.q_ref.refs_0_, bf16[1024,896]{1,0:T(8,128)(2,1)} %add_convert_fusion.2.kv_ref.refs_1_, bf16[1024,448]{1,0:T(8,128)(2,1)} %pad_maximum_fusion.1.refs_2_, f32[1024,448]{1,0:T(8,128)} %get-tuple-element.52.refs_3_, ...), custom_call_target="tpu_custom_call" | custom-call | bytes 105000000 | tf_op jit(solution)/shard_map/attend_back_own/pallas_call | solution.py:1562
  518.0 3.2 dynamic_update_slice.27
  525.8 3.1 fusion.35.proj_share
  531.6 3.0 add_convert_fusion.1
  537.9 4.1 pad_maximum_fusion.dqkv
  542.0 41.9 %collective-permute-done.1 = bf16[800,1600]{1,0:T(8,128)(2,1)} collective-permute-done((bf16[800,1600]{1,0:T(8,128)(2,1)}, bf16[800,1600]{1,0:T(8,128)(2,1)}, u32[]{:S(2)}, u32[]{:S(2)}) %collective-permute-start.1) | collective-permute-done | bytes 2560032 | tf_op jit(solution)/shard_map/ppermute | solution.py:331
  583.9 4.0 add_convert_fusion
  587.8 178.4 %close.1 = (f32[256,1600]{1,0:T(8,128)}, bf16[76,8,1600]{2,1,0:T(8,128)(2,1)}, bf16[76,8,1600]{2,1,0:T(8,128)(2,1)}, bf16[4,76,8,448]{3,2,1,0:T(8,128)(2,1)}, f3...) custom-call(bf16[1024,1344]{1,0:T(8,128)(2,1)} %pad_maximum_fusion.dqkv, ...), custom_call_target="tpu_custom_call" | custom-call | bytes 360000000 | tf_op jit(solution)/shard_map/close/pallas_call | solution.py:1429
  766.3 1.8 slice_bitcast_fusion
  772.8 2.3 reduce_sum.159
  775.4 4.2 fusion.9
  (155 shorter events, 34.7 us)
Async XLA Ops:
  0.6 2.3 copy-start.13
  120.0 6.9 copy-start.3
  121.0 6.9 copy-start.15
  129.7 8.1 %copy-start.4 = (bf16[1024,1600]{1,0:T(8,128)(2,1)}, bf16[1024,1600]{1,0:T(8,128)(2,1)S(1)}, u32[]{:S(2)}) copy-start(bf16[1024,1600]{1,0:T(8,128)(2,1)S(1)} %fusion.3.act) | copy-start | bytes 9830404
  249.9 1.7 copy-start.2
  249.9 1.7 copy-start.17
  251.7 4.9 slice-start
  256.2 4.3 copy-start
  256.2 1.1 copy-start.18
  256.2 1.1 copy-start.19
  256.2 2.9 copy-start.16
  383.4 5.7 copy-start.1
  387.0 4.2 copy-start.5
  387.0 137.4 %collective-permute-start.3 = (bf16[200,1600]{1,0:T(8,128)(2,1)}, bf16[200,1600]{1,0:T(8,128)(2,1)}, u32[]{:S(2)}, u32[]{:S(2)}) collective-permute-start(bf16[200,1600]{1,0:T(8,128)(2,1)} %get-tuple-element.93), channel_id=1, source_target_pairs={{0,2},{1,3},{2,4},{3,5},{4,6},{5,7},{6,0},{7,1},{8,10},{9,11},{10,... | collective-permute-start | bytes 1920008 | tf_op jit(solution)/shard_map/ppermute | solution.py:331
  387.0 138.8 %collective-permute-start.4 = (bf16[200,1600]{1,0:T(8,128)(2,1)}, bf16[200,1600]{1,0:T(8,128)(2,1)}, u32[]{:S(2)}, u32[]{:S(2)}) collective-permute-start(bf16[200,1600]{1,0:T(8,128)(2,1)} %get-tuple-element.95), channel_id=1, source_target_pairs={{0,4},{1,5},{2,6},{3,7},{4,0},{5,1},{6,2},{7,3},{8,12},{9,13},{10,... | collective-permute-start | bytes 1920008 | tf_op jit(solution)/shard_map/ppermute | solution.py:331
  387.0 138.7 %collective-permute-start.5 = (bf16[200,1600]{1,0:T(8,128)(2,1)}, bf16[200,1600]{1,0:T(8,128)(2,1)}, u32[]{:S(2)}, u32[]{:S(2)}) collective-permute-start(bf16[200,1600]{1,0:T(8,128)(2,1)} %get-tuple-element.94), channel_id=1, source_target_pairs={{0,6},{1,7},{2,0},{3,1},{4,2},{5,3},{6,4},{7,5},{8,14},{9,15},{10,... | collective-permute-start | bytes 1920008 | tf_op jit(solution)/shard_map/ppermute | solution.py:331
  433.0 95.8 %collective-permute-start.2 = (bf16[800,448]{0,1:T(8,128)(2,1)}, bf16[800,448]{0,1:T(8,128)(2,1)}, u32[]{:S(2)}, u32[]{:S(2)}) collective-permute-start(bf16[800,448]{0,1:T(8,128)(2,1)} %bitcast.109), channel_id=1, source_target_pairs={{0,16},{1,17},{2,18},{3,19},{4,20},{5,21},{6,22},{7,23},{8,24},{9,... | collective-permute-start | bytes 2150408 | tf_op jit(solution)/shard_map/ppermute | solution.py:331
  483.9 6.5 copy-start.12
  487.6 44.0 %collective-permute-start = (bf16[1024,896]{1,0:T(8,128)(2,1)}, bf16[1024,896]{1,0:T(8,128)(2,1)}, u32[]{:S(2)}, u32[]{:S(2)}) collective-permute-start(bf16[1024,896]{1,0:T(8,128)(2,1)} %convert_element_type.152), channel_id=1, source_target_pairs={{2,0},{3,1},{6,4},{7,5},{10,8},{11,9},{14,12},{15,13},{18,16},{19,... | collective-permute-start | bytes 5505032 | tf_op jit(solution)/shard_map/ppermute | solution.py:331
  492.8 24.1 %copy-start.14 = (f32[1600,1]{1,0:T(8,128)S(1)}, f32[1600,1]{1,0:T(8,128)}, u32[]{:S(2)}) copy-start(f32[1600,1]{1,0:T(8,128)} %get-tuple-element.60) | copy-start | bytes 19204
  524.4 59.5 %collective-permute-start.1 = (bf16[800,1600]{1,0:T(8,128)(2,1)}, bf16[800,1600]{1,0:T(8,128)(2,1)}, u32[]{:S(2)}, u32[]{:S(2)}) collective-permute-start(bf16[800,1600]{1,0:T(8,128)(2,1)} %get-tuple-element.62), channel_id=1, source_target_pairs={{0,16},{1,17},{2,18},{3,19},{4,20},{5,21},{6,22},{7,23},{8,24},{9,... | collective-permute-start | bytes 7680008 | tf_op jit(solution)/shard_map/ppermute | solution.py:331
  531.6 3.0 copy-start.8
  537.9 46.0 %copy-start.9 = (bf16[800,1600]{1,0:T(8,128)(2,1)S(1)}, bf16[800,1600]{1,0:T(8,128)(2,1)}, u32[]{:S(2)}) copy-start(bf16[800,1600]{1,0:T(8,128)(2,1)} %get-tuple-element.61) | copy-start | bytes 7680004
  768.1 2.0 copy-start.6
  768.5 2.4 copy-start.7
  768.8 1.3 copy-start.10
  772.8 2.6 copy-start.11

commit v7 on v6

--- a/solution.py
+++ b/solution.py
@@ -335,10 +335,6 @@
     return permute(value, lambda y, c, z, x: (1 - y, c, z, x))
 
 
-def over_z(value, by):
-    return permute(value, lambda y, c, z, x: (y, c, (z + by) % 4, x))
-
-
 class Sizes:
     def __init__(self, width, hidden, heads, head_size, rows):
         self.heads = heads
@@ -423,7 +419,7 @@
 
 
 class PlaceGather:
-    def __init__(self, wires, full, slot, steps=(1, 2, 3), over=(0, 1, 2, 3), rows=None):
+    def __init__(self, wires, full, slot, steps=(1, 2, 3), over=(0, 1, 2, 3)):
         self.full = full
         self.dp, self.cp = lax.axis_index("dp"), lax.axis_index("cp")
         self.y, self.z, self.x = self.dp // 2, self.cp // 2, self.cp % 2
@@ -433,7 +429,7 @@
 
         def share(by, to):
             spot = slot(self.y, (self.z + 4 + by) % 4)
-            view = full.at[spot] if rows is None else full.at[pl.ds(pl.multiple_of(spot * rows, GRAIN), rows)]
+            view = full.at[spot]
             return wires.to(view, view, *to)
 
         self.steps = steps
@@ -967,33 +963,57 @@
         self.by_x.wait_send()
 
 
-def quad_scratch(partial):
-    rows, width = partial.shape[2:]
-    return [
-        pltpu.VMEM((2, rows, width), partial.dtype),
-        pltpu.VMEM((rows, width), partial.dtype),
-        pltpu.VMEM((rows, width), partial.dtype),
-        *wire_sems(2),
-    ]
-
-
-def fill_rows(left, first, right, out, step=160):
-    def one(index, _):
-        here = pl.ds(pl.multiple_of(index * step, step), step)
-        rows = pl.ds(pl.multiple_of(first + index * step, 32), step)
-        out[here, :] = dot_nn(left[rows, :], right[...]).astype(out.dtype)
-        return 0
-
-    lax.fori_loop(0, out.shape[0] // step, one, 0)
-
-
-def fill_columns(left, right, out, step=256):
-    def one(index, _):
-        here = pl.ds(pl.multiple_of(index * step, step), step)
-        out[here, :] = dot_tn(left[:, here], right[...]).astype(out.dtype)
-        return 0
-
-    lax.fori_loop(0, out.shape[0] // step, one, 0)
+def row_steps(rows, step=64):
+    return [slice(start, min(start + step, rows)) for start in range(0, rows, step)]
+
+
+class PlaceSum:
+    def __init__(self, out, got, turn, send_sems, recv_sems, filled=False):
+        self.y, self.c, self.z, self.x = my_place()
+        self.dp = lax.axis_index("dp")
+        self.out, self.got, self.turn, self.filled = out, got, turn, filled
+        self.send_sems, self.recv_sems = send_sems, recv_sems
+
+    def chunk(self, i):
+        return (self.z + 5 + i - self.turn) % 4
+
+    def put(self, i, store):
+        if i == 3:
+            store(self.got.at[self.z])
+            return
+        k = self.chunk(i)
+        if not self.filled:
+            store(self.out.at[k])
+        pltpu.make_async_remote_copy(
+            src_ref=self.out.at[k],
+            dst_ref=self.got.at[self.z],
+            send_sem=self.send_sems.at[i],
+            recv_sem=self.recv_sems.at[self.z],
+            device_id=(self.dp, ((self.z + 1 + i) % 4) * 2 + self.x),
+            device_id_type=MESH,
+        ).start()
+
+    def total(self, into):
+        for s in range(4):
+
+            @pl.when(self.z != s)
+            def _():
+                pltpu.make_async_copy(self.got.at[s], self.got.at[s], self.recv_sems.at[s]).wait()
+
+        for rows in row_steps(self.got.shape[1]):
+            terms = [self.got[s, rows, :].astype(jnp.float32) for s in range(4)]
+            into[rows, :] = (terms[0] + terms[1] + (terms[2] + terms[3])).astype(into.dtype)
+
+    def finish(self):
+        for i in range(3):
+            view = self.out.at[self.chunk(i)]
+            pltpu.make_async_copy(view, view, self.send_sems.at[i]).wait()
+
+
+def copy_and_wait(src, dst, sem):
+    copy = pltpu.make_async_copy(src, dst, sem)
+    copy.start()
+    copy.wait()
 
 
 def gelu_parts(f):
@@ -1005,118 +1025,185 @@
     return 0.5 * (1.0 + t) + 0.5 * f * (1.0 - t * t) * GELU_SCALE * (1.0 + 3.0 * 0.044715 * f * f)
 
 
+class Crossing:
+    def __init__(self, sent, kept, got_y, got_z, turn, y_sems, z_sems, out=None):
+        dp, cp = lax.axis_index("dp"), lax.axis_index("cp")
+        self.kept, self.got_y = kept, got_y
+        self.places = PlaceSum(out, got_z, turn, *z_sems)
+        self.copies = []
+        for i in range(4):
+            k = self.places.chunk(i)
+            self.copies.append(
+                pltpu.make_async_remote_copy(
+                    src_ref=sent(k),
+                    dst_ref=got_y.at[k],
+                    send_sem=y_sems[0].at[i],
+                    recv_sem=y_sems[1].at[i],
+                    device_id=((dp + 2) % 4, cp),
+                    device_id_type=MESH,
+                )
+            )
+
+    def partners(self):
+        dp, cp = lax.axis_index("dp"), lax.axis_index("cp")
+        z, x = cp // 2, cp % 2
+        return [((dp + 2) % 4, cp)] + [(dp, ((z + d) % 4) * 2 + x) for d in (1, 2, 3)]
+
+    def start(self, i):
+        self.copies[i].start()
+
+    def settle(self, i):
+        self.copies[i].wait_recv()
+        k = self.places.chunk(i)
+        kept = self.kept(k)
+
+        def store(ref):
+            for rows in row_steps(self.got_y.shape[1]):
+                ref[rows, :] = (
+                    kept[rows, :].astype(jnp.float32) + self.got_y[k, rows, :].astype(jnp.float32)
+                ).astype(ref.dtype)
+
+        self.places.put(i, store)
+
+    def finish(self, value, share, sem):
+        self.places.total(value)
+        copy_and_wait(value, share, sem)
+
+    def close(self):
+        for copy in self.copies:
+            copy.wait_send()
+        self.places.finish()
+
+
 def middle_kernel(
     proj_turn, act_ref, cot, w_fc, bias, proj_in,
-    total, act_all, hid_t, proj_sum, fc_sent, fc_kept, bias_grad, proj_ref,
-    f_all, df_t, w_proj, proj_sent, proj_got, term, got_c, stage, got_x,
-    send_sems, recv_sems, sum_send, sum_recv, local_sems,
+    total, act_all, hid_t, fc_sent, fc_kept, bias_grad, proj_ref, proj_share,
+    f_all, df_t, w_proj, proj_sent, proj_kept, got_y, got_z, share_v, term, got_c, stage, got_x,
+    send_sems, recv_sems, y_send, y_recv, z_send, z_recv, sum_send, sum_recv, local_sems,
 ):
     y, c, _, _ = my_place()
     wires = Wires(send_sems, recv_sems)
-    hidden = w_fc.shape[0]
-    half = hidden // 2
-    step = 160
     quad = QuadGather(wires, act_ref, act_all, local_sems.at[0])
-    places = PlaceGather(
-        wires, proj_ref, slot_turned(proj_turn), steps=(2, 3), over=(1, 2, 3), rows=hidden // 8
-    )
-    across = wires.to(proj_sent, proj_got, *places.across)
+    places = PlaceGather(wires, proj_ref, slot_turned(proj_turn), steps=(2, 3), over=(1, 2, 3))
+    cross = Crossing(
+        lambda k: proj_sent.at[k], lambda k: proj_kept.at[k], got_y, got_z, proj_turn,
+        (y_send, y_recv), (z_send, z_recv), proj_kept,
+    )
     summed = QuadSum(term, total, got_c, stage, got_x, sum_send, sum_recv)
-    greet(places.partners() + [quad.over_x, quad.over_c])
+    greet(cross.partners() + [quad.over_x, quad.over_c])
     quad.start()
     places.forward((1, 2))
     quad.forward()
     quad.finish()
 
-    def hidden_rows(first):
-        def one(index, _):
-            rows = pl.ds(pl.multiple_of(first + index * step, 32), step)
-            f = dot_nt(w_fc[rows, :], act_all[...]) + bias[rows, :]
-            f_all[rows, :] = f
-            hid_t[rows, :] = gelu_parts(f)[1].astype(hid_t.dtype)
+    def hidden_of(side):
+        def one(k, _):
+            at = side * 4 + k
+            f = dot_nt(w_fc[at], act_all[...]) + bias[at]
+            f_all[at] = f.astype(f_all.dtype)
+            hid_t[at] = gelu_parts(f)[1].astype(hid_t.dtype)
             return 0
 
-        lax.fori_loop(0, half // step, one, 0)
-
-    hidden_rows((1 - y) * half)
+        lax.fori_loop(0, 4, one, 0)
+
+    hidden_of(1 - y)
     places.forward((3,))
-    fill_rows(hid_t, (1 - y) * half, cot, proj_sent)
-    across.start()
-    hidden_rows(y * half)
-    fill_rows(hid_t, y * half, cot, proj_sum)
+
+    for i in range(4):
+        k = cross.places.chunk(i)
+        proj_sent[k] = dot_nn(hid_t[(1 - y) * 4 + k], cot[...]).astype(proj_sent.dtype)
+        cross.start(i)
+    hidden_of(y)
+
+    def keep(k, _):
+        proj_kept[k] = dot_nn(hid_t[y * 4 + k], cot[...]).astype(proj_kept.dtype)
+        return 0
+
+    lax.fori_loop(0, 4, keep, 0)
     places.finish()
-    load = pltpu.make_async_copy(proj_ref, w_proj, local_sems.at[1])
-    load.start()
-    load.wait()
-
-    def back_rows(index, _):
-        rows = pl.ds(pl.multiple_of(index * step, 32), step)
-        f = f_all[rows, :]
-        grad = dot_nt(w_proj[rows, :], cot[...])
+    copy_and_wait(proj_ref, w_proj, local_sems.at[1])
+
+    def back(at, _):
+        f = f_all[at].astype(jnp.float32)
+        grad = dot_nt(w_proj[at], cot[...])
         df = (grad * gelu_slope(f, gelu_parts(f)[0])).astype(df_t.dtype)
-        df_t[rows, :] = df
-        bias_grad[rows, :] = jnp.sum(df.astype(jnp.float32), axis=1, keepdims=True)
+        df_t[at] = df
+        bias_grad[at] = jnp.sum(df.astype(jnp.float32), axis=1, keepdims=True)
         return 0
 
-    lax.fori_loop(0, hidden // step, back_rows, 0)
+    lax.fori_loop(0, 8, back, 0)
+    cross.settle(0)
     block = term.shape[2]
 
     def tokens_of(core):
         for side in range(2):
             columns = pl.ds(pl.multiple_of((core * 2 + side) * block, block), block)
-            term[core, side, :, :] = dot_tn(df_t[:, columns], w_fc[...]).astype(term.dtype)
+            value = dot_tn(df_t[0, :, columns], w_fc[0])
+            for at in range(1, 8):
+                value = value + dot_tn(df_t[at, :, columns], w_fc[at])
+            term[core, side, :, :] = value.astype(term.dtype)
 
     tokens_of(1 - c)
     summed.start(greeting=False)
     tokens_of(c)
     summed.middle()
-    fill_rows(df_t, (1 - y) * half, act_all, fc_sent)
-    fill_rows(df_t, y * half, act_all, fc_kept)
-    across.wait_recv()
-
-    def add(index, _):
-        rows = pl.ds(pl.multiple_of(index * step, 32), step)
-        proj_sum[rows, :] = (
-            proj_sum[rows, :].astype(jnp.float32) + proj_got[rows, :].astype(jnp.float32)
-        ).astype(proj_sum.dtype)
+    cross.settle(1)
+
+    def fc_terms(k, _):
+        fc_sent[k] = dot_nn(df_t[(1 - y) * 4 + k], act_all[...]).astype(fc_sent.dtype)
+        fc_kept[k] = dot_nn(df_t[y * 4 + k], act_all[...]).astype(fc_kept.dtype)
         return 0
 
-    lax.fori_loop(0, half // step, add, 0)
+    lax.fori_loop(0, 4, fc_terms, 0)
+    cross.settle(2)
     summed.finish()
-    across.wait_send()
+    cross.settle(3)
+    cross.finish(share_v, proj_share, local_sems.at[1])
+    cross.close()
 
 
 def middle_call(sz, act, cot, w_fc, bias, w_proj):
     rows, width = act.shape
-    hidden = w_fc.shape[0]
+    share = w_fc.shape[1]
     bf16, f32 = act.dtype, jnp.float32
-    half = jax.ShapeDtypeStruct((hidden // 2, width), bf16)
+
+    def like(*shape, dtype=bf16):
+        return jax.ShapeDtypeStruct(shape, dtype)
+
+    def vmem(*shape):
+        return pltpu.VMEM(shape, bf16)
+
     return pl.pallas_call(
         functools.partial(middle_kernel, sz.proj_turn),
         out_shape=(
-            jax.ShapeDtypeStruct((rows, width), f32),
-            jax.ShapeDtypeStruct((4 * rows, width), bf16),
-            jax.ShapeDtypeStruct((hidden, 4 * rows), bf16),
-            half,
-            half,
-            half,
-            jax.ShapeDtypeStruct((hidden, 1), f32),
-            jax.ShapeDtypeStruct((hidden, width), bf16),
+            like(rows, width, dtype=f32),
+            like(4 * rows, width),
+            like(8, share, 4 * rows),
+            like(4, share, width),
+            like(4, share, width),
+            like(8, share, 1, dtype=f32),
+            like(8, share, width),
+            like(share, width),
         ),
         in_specs=[VMEM] * 4 + [HBM],
-        out_specs=[VMEM] * 7 + [HBM],
-        input_output_aliases={4: 7},
+        out_specs=[VMEM] * 6 + [HBM] * 2,
+        input_output_aliases={4: 6},
         scratch_shapes=[
-            pltpu.VMEM((hidden, 4 * rows), f32),
-            pltpu.VMEM((hidden, 4 * rows), bf16),
-            pltpu.VMEM((hidden, width), bf16),
-            pltpu.VMEM((hidden // 2, width), bf16),
-            pltpu.VMEM((hidden // 2, width), bf16),
-            pltpu.VMEM((2, 2, rows, width), bf16),
-            pltpu.VMEM((2, rows, width), bf16),
-            pltpu.VMEM((rows, width), bf16),
-            pltpu.VMEM((rows, width), bf16),
-            *wire_sems(11),
+            vmem(8, share, 4 * rows),
+            vmem(8, share, 4 * rows),
+            vmem(8, share, width),
+            vmem(4, share, width),
+            vmem(4, share, width),
+            vmem(4, share, width),
+            vmem(4, share, width),
+            vmem(share, width),
+            vmem(2, 2, rows, width),
+            vmem(2, rows, width),
+            vmem(rows, width),
+            vmem(rows, width),
+            *wire_sems(10),
+            *wire_sems(4),
+            *wire_sems(4),
             *wire_sems(2),
             pltpu.SemaphoreType.DMA((2,)),
         ],
@@ -1126,83 +1213,157 @@
     )(act, cot, w_fc, bias, w_proj)
 
 
-def grads_kernel(act_ref, hid_t, w_proj, act_all, partial_out, send_sems, recv_sems, local_sem):
+def turn_kernel(
+    heads, size, fc_turn, act_ref, w_out, hid_t, w_proj, fc_sent, fc_kept, q_ref, kv_ref, mix_ref, lse_ref,
+    act_all, do_ref, dq_ref, dkv_ref, total, fc_share,
+    dkv_sum, got_y, got_z, share_v, term, got_c, stage, got_x,
+    send_sems, recv_sems, y_send, y_recv, z_send, z_recv, sum_send, sum_recv, local_sems,
+):
+    _, c, z, x = my_place()
     wires = Wires(send_sems, recv_sems)
-    quad = QuadGather(wires, act_ref, act_all, local_sem)
-    greet([quad.over_x, quad.over_c])
+    quad = QuadGather(wires, act_ref, act_all, local_sems.at[0])
+    cross = Crossing(
+        lambda k: fc_sent.at[k], lambda k: fc_kept.at[k], got_y, got_z, fc_turn,
+        (y_send, y_recv), (z_send, z_recv), fc_kept,
+    )
+    summed = QuadSum(term, total, got_c, stage, got_x, sum_send, sum_recv)
+    greet(cross.partners() + [quad.over_x, quad.over_c])
     quad.start()
-    fill_columns(hid_t, w_proj, partial_out)
+    for k in range(4):
+        cross.start(k)
+    block = term.shape[2]
+
+    def tokens_of(core):
+        for side in range(2):
+            columns = pl.ds(pl.multiple_of((core * 2 + side) * block, block), block)
+            value = dot_tn(hid_t[0, :, columns], w_proj[0])
+            for at in range(1, 8):
+                value = value + dot_tn(hid_t[at, :, columns], w_proj[at])
+            term[core, side, :, :] = value.astype(term.dtype)
+
+    tokens_of(1 - c)
+    summed.start(greeting=False)
+    tokens_of(c)
     quad.forward()
+    cross.settle(0)
     quad.finish()
-
-
-def grads_call(act, hid_t, w_proj, ident):
-    width = w_proj.shape[1]
+    summed.middle()
+    pair = 2 * size
+    turns = heads * size // pair
+    quarter = c * 2 + x
+
+    def mix_rows(index, _):
+        here = pl.ds(pl.multiple_of(index * block, block), block)
+        for j in range(turns):
+            columns = pl.ds(pl.multiple_of((4 * j + quarter) * pair, pair), pair)
+            do_ref[here, j * pair : (j + 1) * pair] = dot_nn(act_all[here, :], w_out[:, columns]).astype(do_ref.dtype)
+
+        @pl.when(quarter == 0)
+        def _():
+            last = w_out.shape[1] - size
+            do_ref[here, turns * pair :] = dot_nn(act_all[here, :], w_out[:, last:]).astype(do_ref.dtype)
+
+        @pl.when(quarter != 0)
+        def _():
+            do_ref[here, turns * pair :] = jnp.zeros((block, size), do_ref.dtype)
+
+        return 0
+
+    lax.fori_loop(0, 4, mix_rows, 0)
+    part = heads * size
+    rows = q_ref.shape[0] // 2
+    blk = 256
+    scale = size**-0.5
+    odd = z % 2 == 1
+
+    def group(index):
+        start = pl.multiple_of(index * rows, rows)
+        keys_at = pl.ds(start, rows)
+        dkv_sum[...] = jnp.zeros_like(dkv_sum)
+
+        def one(i, _):
+            here = pl.ds(pl.multiple_of(start + i * blk, blk), blk)
+            for h in range(heads):
+                cols = slice(h * size, (h + 1) * size)
+                vals = slice(part + h * size, part + (h + 1) * size)
+                q = q_ref[here, cols]
+                k = kv_ref[keys_at, cols]
+                do = do_ref[here, cols]
+                p = jnp.exp(dot_nt(q, k) * scale - lse_ref[here, h : h + 1])
+                dp = dot_nt(do, kv_ref[keys_at, vals])
+                delta = jnp.sum(do.astype(jnp.float32) * mix_ref[here, cols], axis=-1, keepdims=True)
+                ds = (p * (dp - delta)).astype(jnp.bfloat16)
+                dq_ref[here, cols] = dot_nn(ds, k) * scale
+                dkv_sum[:, cols] += dot_tn(ds, q) * scale
+                dkv_sum[:, vals] += dot_tn(p.astype(jnp.bfloat16), do)
+            return 0
+
+        lax.fori_loop(0, rows // blk, one, 0)
+        dkv_ref[keys_at, :] = dkv_sum[...].astype(dkv_ref.dtype)
+
+    @pl.when(jnp.logical_not(odd))
+    def _():
+        dq_ref[...] = jnp.zeros_like(dq_ref)
+
+    def one_group(index, _):
+        @pl.when(odd)
+        def _():
+            group(index)
+
+        return 0
+
+    lax.fori_loop(0, 1, one_group, 0)
+    cross.settle(1)
+    cross.settle(2)
+    summed.finish()
+    lax.fori_loop(1, 2, one_group, 0)
+    cross.settle(3)
+    cross.finish(share_v, fc_share, local_sems.at[1])
+    cross.close()
+
+
+def turn_call(sz, act, w_out, hid_t, w_proj, fc_sent, fc_kept, q, before, mix, lse):
+    rows, width = act.shape
+    share = w_proj.shape[1]
+    bf16, f32 = act.dtype, jnp.float32
+
+    def like(*shape, dtype=bf16):
+        return jax.ShapeDtypeStruct(shape, dtype)
+
+    def vmem(*shape):
+        return pltpu.VMEM(shape, bf16)
+
     return pl.pallas_call(
-        grads_kernel,
+        functools.partial(turn_kernel, sz.quarter_heads, sz.head_size, sz.fc_turn),
         out_shape=(
-            jax.ShapeDtypeStruct((2, 2) + act.shape, act.dtype),
-            jax.ShapeDtypeStruct((hid_t.shape[1], width), jnp.bfloat16),
+            like(4 * rows, width),
+            like(4 * rows, sz.part),
+            like(4 * rows, sz.part, dtype=f32),
+            like(4 * rows, 2 * sz.part),
+            like(rows, width, dtype=f32),
+            like(share, width),
         ),
-        in_specs=[VMEM] * 3,
-        out_specs=[HBM, VMEM],
-        scratch_shapes=[*wire_sems(3), pltpu.SemaphoreType.DMA],
-        cost_estimate=cost(25),
-        compiler_params=remote_params(ident, 60 << 20),
-        name="grads",
-    )(act, hid_t, w_proj)
-
-
-def row_steps(rows, step=64):
-    return [slice(start, min(start + step, rows)) for start in range(0, rows, step)]
-
-
-class PlaceSum:
-    def __init__(self, out, got, turn, send_sems, recv_sems, filled=False):
-        self.y, self.c, self.z, self.x = my_place()
-        self.dp = lax.axis_index("dp")
-        self.filled = filled
-        self.out, self.got, self.turn = out, got, turn
-        self.send_sems, self.recv_sems = send_sems, recv_sems
-
-    def place(self, k):
-        return (k + self.turn) % 4
-
-    def put(self, k, store):
-        @pl.when(self.z == self.place(k))
-        def _():
-            store(self.got.at[self.place(k)])
-
-        @pl.when(self.z != self.place(k))
-        def _():
-            if not self.filled:
-                store(self.out.at[k])
-            pltpu.make_async_remote_copy(
-                src_ref=self.out.at[k],
-                dst_ref=self.got.at[self.z],
-                send_sem=self.send_sems.at[k],
-                recv_sem=self.recv_sems.at[self.z],
-                device_id=(self.dp, self.place(k) * 2 + self.x),
-                device_id_type=MESH,
-            ).start()
-
-    def total(self, into):
-        for s in range(4):
-
-            @pl.when(self.z != s)
-            def _():
-                pltpu.make_async_copy(self.got.at[s], self.got.at[s], self.recv_sems.at[s]).wait()
-
-        for rows in row_steps(self.got.shape[1]):
-            terms = [self.got[s, rows, :].astype(jnp.float32) for s in range(4)]
-            into[rows, :] = (terms[0] + terms[1] + (terms[2] + terms[3])).astype(into.dtype)
-
-    def finish(self):
-        for k in range(4):
-
-            @pl.when(self.z != self.place(k))
-            def _():
-                pltpu.make_async_copy(self.out.at[k], self.out.at[k], self.send_sems.at[k]).wait()
+        in_specs=[VMEM] * 4 + [HBM] + [VMEM] * 5,
+        out_specs=[VMEM] * 5 + [HBM],
+        scratch_shapes=[
+            pltpu.VMEM((2 * rows, 2 * sz.part), f32),
+            vmem(4, share, width),
+            vmem(4, share, width),
+            vmem(share, width),
+            vmem(2, 2, rows, width),
+            vmem(2, rows, width),
+            vmem(rows, width),
+            vmem(rows, width),
+            *wire_sems(3),
+            *wire_sems(4),
+            *wire_sems(4),
+            *wire_sems(2),
+            pltpu.SemaphoreType.DMA((2,)),
+        ],
+        cost_estimate=cost(80),
+        compiler_params=remote_params(3, 62 << 20),
+        name="turn",
+    )(act, w_out, hid_t, w_proj, fc_sent, fc_kept, q, before, mix, lse)
 
 
 class Collector:
@@ -1246,24 +1407,24 @@
 
 
 def close_kernel(
-    sz, dqkv, act, w_qkv, normed, vec_in, fc_sum, out_sum, proj_share,
-    total, g_qkv, g_mlp, g_outs, vecs, qkv_share, fc_share, out_share,
-    grads, got_y, qkv_out, qkv_got, fc_got, out_got, share_v, out_v, vec_v, term, got_c, stage, got_x,
+    sz, dqkv, act, w_qkv, normed, vec_in, out_sum, fc_share, proj_share,
+    total, g_qkv, g_mlp, g_outs, vecs, qkv_share, out_share,
+    grads, got_y, qkv_out, qkv_got, out_got, share_v, out_v, vec_v, term, got_c, stage, got_x,
     y_send, y_recv, z_send, z_recv, sum_send, sum_recv, grain_sems, kind_sems, local_sems, vec_sems,
 ):
     to = Collector(sz)
     y, c, z = to.y, to.c, to.z
-    dp, cp = lax.axis_index("dp"), lax.axis_index("cp")
     rows = got_y.shape[1]
     block = term.shape[2]
-    fc = PlaceSum(fc_sum, fc_got, sz.fc_turn, z_send.at[0], z_recv.at[0], True)
     out = PlaceSum(out_sum, out_got, 0, z_send.at[1], z_recv.at[1], True)
-    qkv = PlaceSum(qkv_out, qkv_got, 0, z_send.at[2], z_recv.at[2])
+    cross = Crossing(
+        lambda k: grads.at[2 * k + 1 - y], lambda k: grads.at[2 * k + y], got_y, qkv_got, 0,
+        (y_send, y_recv), (z_send.at[2], z_recv.at[2]), qkv_out,
+    )
     summed = QuadSum(term, total, got_c, stage, got_x, sum_send, sum_recv)
 
-    for part in (out, fc):
-        for k in range(4):
-            part.put(k, lambda ref, k=k, part=part: store_same(part.out.at[k], ref, local_sems.at[0]))
+    for i in range(4):
+        out.put(i, lambda ref, i=i: copy_and_wait(out_sum.at[out.chunk(i)], ref, local_sems.at[0]))
 
     def mlp_grains(act_on, ref, base, turn, first_sem):
         r = range_of_spot(y, (z + 4 - turn) % 4)
@@ -1309,22 +1470,13 @@
         lax.fori_loop(0, sz.qkv, one, 0)
 
     counts = (0, sz.mlp, 2 * sz.mlp, 3 * sz.mlp)
-    mlp_grains(to.send, lambda slot: proj_share.at[slot], sz.proj_start, sz.proj_turn, counts[0])
-
-    across = []
-    for k in range(4):
-        for s in (2 * k, 2 * k + 1):
-            grads[s, :, :] = dot_tn(dqkv[:, s * rows : (s + 1) * rows], act[...]).astype(grads.dtype)
-        copy = pltpu.make_async_remote_copy(
-            src_ref=grads.at[2 * k + 1 - y],
-            dst_ref=got_y.at[k],
-            send_sem=y_send.at[k],
-            recv_sem=y_recv.at[k],
-            device_id=((dp + 2) % 4, cp),
-            device_id_type=MESH,
-        )
-        copy.start()
-        across.append(copy)
+    mlp_grains(to.send, grain_of(proj_share), sz.proj_start, sz.proj_turn, counts[0])
+    mlp_grains(to.send, grain_of(fc_share), sz.fc_start, sz.fc_turn, counts[1])
+
+    for s in range(8):
+        grads[s, :, :] = dot_tn(dqkv[:, s * rows : (s + 1) * rows], act[...]).astype(grads.dtype)
+    for i in range(4):
+        cross.start(i)
 
     def tokens_of(core):
         for side in range(2):
@@ -1336,31 +1488,14 @@
     tokens_of(c)
     summed.middle()
 
-    def share_sum(k):
-        def store(ref):
-            for step in row_steps(rows):
-                ref[step, :] = (
-                    grads[2 * k + y, step, :].astype(jnp.float32) + got_y[k, step, :].astype(jnp.float32)
-                ).astype(ref.dtype)
-
-        return store
-
     def settle(part, value, share):
         part.total(value)
-        copy = pltpu.make_async_copy(value, share, local_sems.at[1])
-        copy.start()
-        copy.wait()
+        copy_and_wait(value, share, local_sems.at[1])
 
     settle(out, out_v, out_share)
     out_grains(to.send, counts[2])
-    for k in range(2):
-        across[k].wait_recv()
-        qkv.put(k, share_sum(k))
-    settle(fc, share_v, fc_share)
-    mlp_grains(to.send, grain_of(fc_share), sz.fc_start, sz.fc_turn, counts[1])
-    for k in range(2, 4):
-        across[k].wait_recv()
-        qkv.put(k, share_sum(k))
+    for i in range(4):
+        cross.settle(i)
     summed.finish()
 
     vec_v[...] = vec_in[...]
@@ -1384,14 +1519,12 @@
     def _():
         pltpu.make_async_copy(vec_v, vecs.at[to.me], vec_sems.at[1]).start()
 
-    settle(qkv, share_v.at[0:rows], qkv_share)
+    cross.finish(share_v, qkv_share, local_sems.at[1])
     head_grains(to.send, counts[3])
 
-    for copy in across:
-        copy.wait_send()
-    for part in (out, fc, qkv):
-        part.finish()
-    mlp_grains(to.sent, lambda slot: proj_share.at[slot], sz.proj_start, sz.proj_turn, counts[0])
+    cross.close()
+    out.finish()
+    mlp_grains(to.sent, grain_of(proj_share), sz.proj_start, sz.proj_turn, counts[0])
     mlp_grains(to.sent, grain_of(fc_share), sz.fc_start, sz.fc_turn, counts[1])
     out_grains(to.sent, counts[2])
     head_grains(to.sent, counts[3])
@@ -1409,16 +1542,10 @@
     to.received(0, 3 * sz.width_grains, lambda n: g_qkv.at[pl.ds(0, n)], kind_sems.at[2])
 
 
-def store_same(src, ref, sem):
-    copy = pltpu.make_async_copy(src, ref, sem)
-    copy.start()
-    copy.wait()
-
-
-def close_call(sz, dqkv, act, w_qkv, normed, vectors, fc_sum, out_sum, proj_share):
+def close_call(sz, dqkv, act, w_qkv, normed, vectors, out_sum, fc_share, proj_share):
     rows, width = normed.shape
     bf16, f32 = act.dtype, jnp.float32
-    qkv_rows, out_rows, mlp_rows = sz.qkv * GRAIN, out_sum.shape[1], fc_sum.shape[1]
+    qkv_rows, out_rows = sz.qkv * GRAIN, out_sum.shape[1]
 
     def like(*shape, dtype=bf16):
         return jax.ShapeDtypeStruct(shape, dtype)
@@ -1435,19 +1562,17 @@
             like(4, sz.block, GRAIN, sz.part),
             like(32, *vectors.shape, dtype=f32),
             like(qkv_rows, width),
-            like(mlp_rows, width),
             like(out_rows, sz.part),
         ),
-        in_specs=[VMEM] * 7 + [HBM],
-        out_specs=[VMEM] + [HBM] * 7,
+        in_specs=[VMEM] * 6 + [HBM] * 2,
+        out_specs=[VMEM] + [HBM] * 6,
         scratch_shapes=[
             vmem(8, qkv_rows, width),
             vmem(4, qkv_rows, width),
             vmem(4, qkv_rows, width),
             vmem(4, qkv_rows, width),
-            vmem(4, mlp_rows, width),
             vmem(4, out_rows, sz.part),
-            vmem(mlp_rows, width),
+            vmem(qkv_rows, width),
             vmem(out_rows, sz.part),
             pltpu.VMEM(vectors.shape, f32),
             vmem(2, 2, rows, width),
@@ -1466,109 +1591,57 @@
         cost_estimate=cost(120),
         compiler_params=remote_params(None, 62 << 20),
         name="close",
-    )(dqkv, act, w_qkv, normed, vectors, fc_sum, out_sum, proj_share)
-
-
-def attend_back_kernel(heads, size, own, *refs):
-    if own:
-        q_ref, kv_ref, do_ref, mix_ref, lse_ref, seed_ref, dq_ref, dkv_ref = refs
-    else:
-        q_ref, kv_ref, do_ref, mix_ref, lse_ref, term_ref, dq_ref, dkv_ref, sum_ref = refs[:9]
-        quad = QuadSum(term_ref, sum_ref, *refs[-5:])
-        quad.start()
-    _, _, z, _ = my_place()
+    )(dqkv, act, w_qkv, normed, vectors, out_sum, fc_share, proj_share)
+
+
+def attend_back_kernel(heads, size, q_ref, kv_ref, do_ref, mix_ref, lse_ref, seed_ref, dq_ref, dkv_ref):
     part = heads * size
     rows = q_ref.shape[0] // 2
     blk = 256
     scale = size**-0.5
 
-    def visit(here, start, seen, allowed):
-        keys_at = pl.ds(start, seen)
-        for h in range(heads):
-            cols = slice(h * size, (h + 1) * size)
-            vals = slice(part + h * size, part + (h + 1) * size)
-            q = q_ref[here, cols]
-            k = kv_ref[keys_at, cols]
-            do = do_ref[here, cols]
-            s = dot_nt(q, k) * scale
-            p = jnp.exp(s - lse_ref[here, h : h + 1])
-            if own:
-                p = jnp.where(allowed, p, 0.0)
-            dp = dot_nt(do, kv_ref[keys_at, vals])
-            delta = jnp.sum(do.astype(jnp.float32) * mix_ref[here, cols], axis=-1, keepdims=True)
-            ds = (p * (dp - delta)).astype(jnp.bfloat16)
-            dq = dot_nn(ds, k) * scale
-            if own:
-                dq = dq + seed_ref[here, cols]
-            dq_ref[here, cols] = dq.astype(dq_ref.dtype)
-            dkv_ref[keys_at, cols] += dot_tn(ds, q) * scale
-            dkv_ref[keys_at, vals] += dot_tn(p.astype(jnp.bfloat16), do)
-
-    def group(index):
+    def group(index, _):
         start = pl.multiple_of(index * rows, rows)
-        if not own:
-
-            def block(i, _):
-                visit(pl.ds(pl.multiple_of(start + i * blk, blk), blk), start, rows, None)
-                return 0
-
-            lax.fori_loop(0, rows // blk, block, 0)
-            return
+        dkv_ref[pl.ds(start, rows), :] = jnp.zeros((rows, 2 * part), dkv_ref.dtype)
         for i in range(rows // blk):
             seen = (i + 1) * blk
+            here = pl.ds(pl.multiple_of(start + i * blk, blk), blk)
+            keys_at = pl.ds(start, seen)
             lane = lax.broadcasted_iota(jnp.int32, (blk, seen), 1)
             line = lax.broadcasted_iota(jnp.int32, (blk, seen), 0)
-            visit(pl.ds(pl.multiple_of(start + i * blk, blk), blk), start, seen, lane <= line + i * blk)
-
-    def clear(index, _):
-        here = pl.ds(pl.multiple_of(index * blk, blk), blk)
-        dkv_ref[here, :] = jnp.zeros((blk, dkv_ref.shape[1]), dkv_ref.dtype)
-        if not own:
-            dq_ref[here, :] = jnp.zeros((blk, dq_ref.shape[1]), dq_ref.dtype)
+            allowed = lane <= line + i * blk
+            for h in range(heads):
+                cols = slice(h * size, (h + 1) * size)
+                vals = slice(part + h * size, part + (h + 1) * size)
+                q = q_ref[here, cols]
+                k = kv_ref[keys_at, cols]
+                do = do_ref[here, cols]
+                p = jnp.exp(dot_nt(q, k) * scale - lse_ref[here, h : h + 1])
+                p = jnp.where(allowed, p, 0.0)
+                dp = dot_nt(do, kv_ref[keys_at, vals])
+                delta = jnp.sum(do.astype(jnp.float32) * mix_ref[here, cols], axis=-1, keepdims=True)
+                ds = (p * (dp - delta)).astype(jnp.bfloat16)
+                dq_ref[here, cols] = (dot_nn(ds, k) * scale + seed_ref[here, cols]).astype(dq_ref.dtype)
+                dkv_ref[keys_at, cols] += dot_tn(ds, q) * scale
+                dkv_ref[keys_at, vals] += dot_tn(p.astype(jnp.bfloat16), do)
         return 0
 
-    lax.fori_loop(0, 2 * rows // blk, clear, 0)
-
-    def one(index, _):
-        if own:
-            group(index)
-        else:
-
-            @pl.when(z % 2 == 1)
-            def _():
-                group(index)
-
-            @pl.when(index == 0)
-            def _():
-                quad.middle()
-
-        return 0
-
-    lax.fori_loop(0, 2, one, 0)
-    if not own:
-        quad.finish()
-
-
-def attend_back(sz, q, kv, grad_mix, mix, lse, seed=None, term=None, ident=None):
-    own = term is None
-    operands = [q, kv, grad_mix, mix, lse, seed if own else term]
-    out_shape = [
-        jax.ShapeDtypeStruct(q.shape, jnp.bfloat16 if own else jnp.float32),
-        jax.ShapeDtypeStruct(kv.shape, jnp.float32),
-    ]
-    if not own:
-        out_shape.append(jax.ShapeDtypeStruct(term.shape[2:], jnp.float32))
-    params = pltpu.CompilerParams(vmem_limit_bytes=56 << 20) if own else remote_params(ident, 56 << 20)
+    lax.fori_loop(0, 2, group, 0)
+
+
+def attend_back(sz, q, kv, grad_mix, mix, lse, seed):
     return pl.pallas_call(
-        functools.partial(attend_back_kernel, sz.quarter_heads, sz.head_size, own),
-        out_shape=out_shape,
-        in_specs=[VMEM] * len(operands),
-        out_specs=[VMEM] * len(out_shape),
-        scratch_shapes=[] if own else quad_scratch(term),
+        functools.partial(attend_back_kernel, sz.quarter_heads, sz.head_size),
+        out_shape=(
+            jax.ShapeDtypeStruct(q.shape, jnp.bfloat16),
+            jax.ShapeDtypeStruct(kv.shape, jnp.float32),
+        ),
+        in_specs=[VMEM] * 6,
+        out_specs=[VMEM] * 2,
         cost_estimate=cost(35),
-        compiler_params=params,
-        name="attend_back_own" if own else "attend_back_before",
-    )(*operands)
+        compiler_params=pltpu.CompilerParams(vmem_limit_bytes=56 << 20),
+        name="attend_back",
+    )(q, kv, grad_mix, mix, lse, seed)
 
 
 def rowwise(value):
@@ -1592,7 +1665,7 @@
 
 
 def per_device_quad(tokens, params, out_grad, lengths):
-    rows, width = tokens.shape
+    _, width = tokens.shape
     hidden = FF
     sz = Sizes(width, hidden, HEADS, HEAD_DIM, params.shape[0])
     y, c, z, x = my_place()
@@ -1604,15 +1677,6 @@
 
     def to_other_y(sent):
         return over_y(sent.astype(bf16))
-
-    def to_places(kept, got, turn=0):
-        summed = kept.astype(f32) if got is None else kept.astype(f32) + got.astype(f32)
-        summed = summed.reshape(4, summed.shape[0] // 4, -1)
-        total = pick(summed, (z + 4 - turn) % 4)
-        for d in (1, 2, 3):
-            got = over_z(pick(summed, (z + d + 4 - turn) % 4).astype(bf16), d)
-            total = total + got.astype(f32)
-        return total
 
     w_qkv, w_out, w_fc, w_proj, vec, tok_all, cot_all = open_call(
         sz, params.reshape(sz.block, GRAIN, width), tokens, out_grad
@@ -1649,36 +1713,28 @@
     normed_two, rs_two = norm_parts(residual)
     act_two = (normed_two * vectors[5] + vectors[6]).astype(bf16)
     bias = lax.dynamic_index_in_dim(fc_bias.reshape(-1, 4, GRAIN), quarter, 1, keepdims=False)
-    bias = bias.reshape(8, hidden // 32)[jnp.array(RANGES)].reshape(hidden // 4, 1)
-    grad_two, act_two, hid_t, proj_sum, fc_sent, fc_kept, bias_sum, w_proj = middle_call(
-        sz, act_two, cot_all, w_fc, bias, flat(w_proj)
-    )
-    got_fc = to_other_y(fc_sent)
+    bias = bias.reshape(8, hidden // 32)[jnp.array(RANGES)][:, :, None]
+    shares = lambda value: value.reshape(8, hidden // 32, width)
+    grad_two, _, hid_t, fc_sent, fc_kept, bias_sum, w_proj, proj_share = middle_call(
+        sz, act_two, cot_all, shares(w_fc), bias, shares(w_proj)
+    )
 
     cot = out_grad.astype(f32)
     grad_res = cot + norm_back(normed_two, rs_two, grad_two, vectors[5])
     grad_attn = grad_res.astype(bf16)
-    attn_all, partial_out = grads_call(grad_attn, hid_t, w_proj, 3)
-    attn_all = flat(attn_all)
-    grad_mix = rowwise(dot_nn(attn_all, w_out).astype(bf16))
-    grad_mix = rowwise(quarter_of(grad_mix))
-    g_proj = to_places(proj_sum, None, sz.proj_turn)
-    partial_out = partial_out.reshape(2, 2, rows, width)
-    dq_before, dkv_before, out_sum = attend_back(
-        sz, q, before, grad_mix, mix, lse, term=partial_out, ident=4
+    attn_all, grad_mix, dq_before, dkv_before, out_sum, fc_share = turn_call(
+        sz, grad_attn, w_out, hid_t, w_proj, fc_sent, fc_kept, q, before, mix, lse
     )
     output = (residual + out_sum + vectors[7]).astype(bf16)
     returned = permute(
-        dkv_before.astype(bf16), lambda py, pc, pz, px: (py, pc, pz - 1, px) if pz % 2 == 1 else None
+        dkv_before, lambda py, pc, pz, px: (py, pc, pz - 1, px) if pz % 2 == 1 else None
     )
     g_out = rowwise(dot_tn(attn_all, mix.astype(bf16)).astype(bf16)).reshape(2, width // 2, sz.part)
     got_out = to_other_y(pick(g_out, 1 - y))
-    fc_sum = (fc_kept.astype(f32) + got_fc.astype(f32)).astype(bf16).reshape(4, hidden // 32, width)
     out_sum = (pick(g_out, y).astype(f32) + got_out.astype(f32)).astype(bf16).reshape(4, width // 8, sz.part)
-    dq, dkv = attend_back(sz, q, kv, grad_mix, mix, lse, seed=dq_before)
+    dq, dkv = attend_back(sz, q, kv, grad_mix, mix, lse, dq_before)
     grad_qkv = jnp.concatenate([dq, (dkv + returned.astype(f32)).astype(bf16)], axis=1)
     normed_one, rs_one = norm_parts(inputs)
-    grains = lambda value: value.astype(bf16).reshape(-1, GRAIN, value.shape[-1])
 
     def placed(vector):
         spread = jnp.zeros((1, width), f32)
@@ -1713,7 +1769,7 @@
     count = grad_vectors.shape[0]
     grad_vectors = jnp.pad(grad_vectors, ((0, sz.vec * GRAIN - count), (0, 0)))
     grad_one, table_qkv, table_mlp, table_out, all_vectors = close_call(
-        sz, grad_qkv, act_one, w_qkv, normed_one, grad_vectors, fc_sum, out_sum, grains(g_proj)
+        sz, grad_qkv, act_one, w_qkv, normed_one, grad_vectors, out_sum, fc_share, proj_share
     )[:5]
     input_grad = (grad_res + norm_back(normed_one, rs_one, grad_one, vectors[0])).astype(bf16)
     grad_vectors = jnp.sum(all_vectors, axis=0)[:count]

time: 790 us -> 705 us (0.89)
  the two profiles are of different devices: /device:TPU:24 before, /device:TPU:26 now
where the time goes in v7:
time: 705 us; the launch traced here: 696 us
  Pallas kernels  599 us (85%)
  other arithmetic  35.9 us (5%)
  local copies, waits for them, and re-layouts  34.9 us (5%)
  matrix products  20.4 us (3%)
    pallas_call x1, Pallas kernels, middle_call(): pl.pallas_call(functools.partial(middle_kernel, sz.proj_turn), out_shape=...  128 us
    pallas_call x1, Pallas kernels, close_call(): pl.pallas_call(functools.partial(close_kernel, sz), out_shape=(like(rows,...  123 us
    pallas_call x1, Pallas kernels, open_call(): pl.pallas_call(functools.partial(open_kernel, sz), out_shape=(like(8, sz....  116 us
    pallas_call x1, Pallas kernels, forward_call(): pl.pallas_call(functools.partial(forward_kernel, sz.quarter_heads, sz.hea...  110 us
    pallas_call x1, Pallas kernels, turn_call(): pl.pallas_call(functools.partial(turn_kernel, sz.quarter_heads, sz.head_s...  97.2 us
    pallas_call x1, Pallas kernels, attend_back(): pl.pallas_call(functools.partial(attend_back_kernel, sz.quarter_heads, sz...  24.1 us
    dot_general x3, matrix products, dot_nt(): return lax.dot_general(a, b, NT, preferred_element_type=jnp.float32)  14.7 us
  transfers between devices with their start and end apart: 2, of which 0 were waited for; matrix products, arithmetic and copies ran while one was open for 2% of the time, Pallas kernels for 3%

profile of v7, /device:TPU:26, one launch (start us, length us, event | category | flops | bytes accessed | tf_op | source)
XLA Modules:
  0.0 695.6 jit_solution(1975260835223408571)
XLA Ops:
  0.7 2.3 copy.32.tok_ref
  3.0 1.3 copy.34.cot_ref
  4.3 115.7 %open.1 = (bf16[8,21,8,1600]{3,2,1,0:T(8,128)(2,1)}, bf16[8,7,8,1600]{3,2,1,0:T(8,128)(2,1)}, bf16[8,25,8,1600]{3,2,1,0:T(8,128)(2,1)}, bf16[8,25,8,1600]{3,2,1,...) custom-call(bf16[76,8,1600]{2,1,0:T(8,128)(2,1)} %bitcast.85, ...), custom_call_target="tpu_custom_call" | custom-call | tf_op jit(solution)/shard_map/open/pallas_call | solution.py:734
  124.4 2.5 convert_reduce_fusion.1
  128.1 1.6 fusion.3.act
  129.7 8.1 %add_convert_fusion.1.kv_ref = bf16[1024,896]{1,0:T(8,128)(2,1)} fusion(f32[896]{0:T(1024)S(1)} %concatenate.28, bf16[1024,1600]{1,0:T(8,128)(2,1)S(1)} %fusion.3.act, bf16[1344,1600]{1,0:T(8,128)(2,1)} %bitcast.80), kind=kOutput, calls=%fused_computation.13 | convolution fusion | flops 2937847808 | bytes 8097280 | tf_op jit(solution)/shard_map/dot_general | solution.py:307
  137.8 4.4 add_convert_fusion.2.q_ref
  142.2 110.4 %forward.1 = (f32[1024,448]{1,0:T(8,128)}, f32[1024,8]{1,0:T(8,128)}, bf16[1024,896]{1,0:T(8,128)(2,1)}, bf16[4,256,448]{2,1,0:T(8,128)(2,1)}, bf16[8,7,8,1600]{...) custom-call(bf16[1024,448]{1,0:T(8,128)(2,1)} %add_convert_fusion.2., ...), custom_call_target="tpu_custom_call", output_to_operand_aliasing={{4}: (2, {}), {5}: (3, {}), {6}: (4, {})} | custom-call | bytes 360000000 | tf_op jit(solution)/shard_map/forward/pallas_call | solution.py:888
  254.2 5.5 slice.296.w_out
  259.8 2.1 fusion.23
  264.9 1.3 add_convert_fusion.5.act_ref
  266.2 128.1 %middle.1 = (f32[256,1600]{1,0:T(8,128)}, bf16[1024,1600]{1,0:T(8,128)(2,1)}, bf16[8,200,1024]{2,1,0:T(8,128)(2,1)}, bf16[4,200,1600]{2,1,0:T(8,128)(2,1)}, bf16...) custom-call(bf16[256,1600]{1,0:T(8,128)(2,1)} %add_convert_fusion.5., ...), custom_call_target="tpu_custom_call", output_to_operand_aliasing={{6}: (4, {})} | custom-call | bytes 330000000 | tf_op jit(solution)/shard_map/middle/pallas_call | solution.py:1176
  394.3 2.8 multiply_reduce_fusion.2
  397.2 4.0 convert_reduce_fusion.4
  401.1 97.2 %turn.1 = (bf16[1024,1600]{1,0:T(8,128)(2,1)}, bf16[1024,448]{1,0:T(8,128)(2,1)}, f32[1024,448]{1,0:T(8,128)}, bf16[1024,896]{1,0:T(8,128)(2,1)}, f32[256,1600]{1,0:T(8,128)}, /*index=5*/bf16[200,1600]{1,0:T(8,128)(2,1)}) custom-call(bf16[256,1600]{1,0:T(8,128)(2,1)} %get-tuple-element.93.act_ref, bf16[1600,1600]{1,0:T(8,128)(2,1)} %slice.296.w_out, ...), custom_call_target="tpu_custom_call" | custom-call | bytes 240000000 | tf_op jit(solution)/shard_map/turn/pallas_call | solution.py:1336
  498.4 5.7 convolution_convert_fusion
  504.0 2.4 constant_dynamic-slice_fusion
  508.8 2.7 collective-permute-start
  511.5 1.6 add_convert_fusion.4
  513.1 1.8 copy.47
  516.0 3.2 dynamic_update_slice.27
  520.8 24.1 %attend_back.1 = (bf16[1024,448]{1,0:T(8,128)(2,1)}, f32[1024,896]{1,0:T(8,128)}) custom-call(bf16[1024,448]{1,0:T(8,128)(2,1)} %add_convert_fusion.2.q_ref, bf16[1024,896]{1,0:T(8,128)(2,1)} %add_convert_fusion.1.kv_ref, bf16[1024,448]{1,0:T(8,128)(2,1)} %get-tuple-element.57.do_ref, f32[1024,448]{1,0:T(8,128)} %get-tuple-element.54.mix_ref, ...), custom_call_target="tpu_custom_call" | custom-call | bytes 105000000 | tf_op jit(solution)/shard_map/attend_back/pallas_call | solution.py:1633
  545.5 1.6 fusion.9.normed
  547.1 1.3 fusion.12
  548.4 1.4 copy.42
  549.9 3.0 add_convert_fusion
  552.9 1.3 convert_reduce_fusion
  554.2 2.7 pad_maximum_fusion.dqkv
  558.7 123.1 %close.1 = (f32[256,1600]{1,0:T(8,128)}, bf16[76,8,1600]{2,1,0:T(8,128)(2,1)}, bf16[76,8,1600]{2,1,0:T(8,128)(2,1)}, bf16[4,76,8,448]{3,2,1,0:T(8,128)(2,1)}, f3...) custom-call(bf16[1024,1344]{1,0:T(8,128)(2,1)} %pad_maximum_fusion.dqkv, ...), custom_call_target="tpu_custom_call" | custom-call | bytes 360000000 | tf_op jit(solution)/shard_map/close/pallas_call | solution.py:1556
  681.9 1.8 slice_bitcast_fusion
  688.4 2.3 reduce_sum.159
  691.0 4.2 fusion.5
  (138 shorter events, 22.2 us)
Async XLA Ops:
  0.6 2.3 copy-start.12
  120.0 6.9 copy-start.4
  121.0 6.9 copy-start.14
  129.7 8.1 %copy-start.5 = (bf16[1024,1600]{1,0:T(8,128)(2,1)}, bf16[1024,1600]{1,0:T(8,128)(2,1)S(1)}, u32[]{:S(2)}) copy-start(bf16[1024,1600]{1,0:T(8,128)(2,1)S(1)} %fusion.3.act) | copy-start | bytes 9830404
  254.0 5.8 slice-start
  254.2 5.5 copy-start.2
  254.2 5.5 slice-start.1
  254.2 5.5 copy-start.15
  259.8 2.5 slice-start.2
  261.9 4.3 copy-start
  261.9 1.1 copy-start.16
  261.9 1.1 copy-start.17
  394.3 2.9 copy-start.1
  394.3 2.9 copy-start.6
  507.7 39.4 %collective-permute-start.1 = (bf16[800,448]{0,1:T(8,128)(2,1)}, bf16[800,448]{0,1:T(8,128)(2,1)}, u32[]{:S(2)}, u32[]{:S(2)}) collective-permute-start(bf16[800,448]{0,1:T(8,128)(2,1)} %bitcast.87), channel_id=1, source_target_pairs={{0,16},{1,17},{2,18},{3,19},{4,20},{5,21},{6,22},{7,23},{8,24},{9,... | collective-permute-start | bytes 2150408 | tf_op jit(solution)/shard_map/ppermute | solution.py:331
  508.8 41.1 %collective-permute-start = (bf16[1024,896]{1,0:T(8,128)(2,1)}, bf16[1024,896]{1,0:T(8,128)(2,1)}, u32[]{:S(2)}, u32[]{:S(2)}) collective-permute-start(bf16[1024,896]{1,0:T(8,128)(2,1)} %get-tuple-element.61), channel_id=1, source_target_pairs={{2,0},{3,1},{6,4},{7,5},{10,8},{11,9},{14,12},{15,13},{18,16},{19,... | collective-permute-start | bytes 5505032 | tf_op jit(solution)/shard_map/ppermute | solution.py:331
  513.1 1.8 copy-start.13
  520.8 24.1 %copy-start.3 = (bf16[256,1600]{1,0:T(8,128)(2,1)S(1)}, bf16[256,1600]{1,0:T(8,128)(2,1)}, u32[]{:S(2)}) copy-start(bf16[256,1600]{1,0:T(8,128)(2,1)} %copy.32.tok_ref) | copy-start | bytes 2457604
  549.9 3.0 copy-start.9
  683.7 2.0 copy-start.7
  684.1 2.4 copy-start.8
  684.3 1.3 copy-start.10
  688.4 2.6 copy-start.11
